TPU v7x, 32 devices: a whole 2x2x4 slice. The times are simulated.
32 devices in a mesh: row: 4 (over z), col: 8 (over y, x, core).
Axes of the slice: x: 2, y: 2, z: 4, core: 2. Of those that a mesh axis runs over, the one named last changes fastest.
Arguments:
- obj: float32 [2, 1536, 3072], P(None, 'row', 'col'), may hold values from -6 to 6
- probe: float32 [4, 2, 128, 128], replicated, may hold values from -3 to 3
- positions: int32 [4, 8, 8, 2], P('row', 'col'), may hold values from 0 to 383
- counts: int32 [4, 8], P('row', 'col'), may hold values from 2 to 8, as said below
- offsets: int32 [8, 4], replicated, may hold values from 0 to 3, each once within a row
- measured: float32 [4, 8, 8, 128, 128], P('row', 'col'), may hold values from 0.3 to 5
Outputs:
- new_object: float32 [2, 1536, 3072], P(None, 'row', 'col')
Inputs may be any that keep to these rules, and one draw needn't show every extreme that they name: `counts`: some device uses all 8 slots. At each scan slot the beams have different offsets.
All inputs are finite; a program needn't handle non-finite values.
Results may differ from a plain program's by a relative error of at most 0.0003.
Values sent between devices are 32-bit elements; how exact they have to be, the bound alone decides.
No kernel may reach another device: no remote copies, remote signals or barrier semaphores. Data moves between devices by JAX's collectives and lax.ppermute only.
A program may use at most 128 MiB of HBM per device.

v0:
```python
import functools
import math

import jax
import jax.numpy as jnp
import numpy as np
from jax import lax
from jax.experimental import pallas as pl
from jax.experimental.pallas import tpu as pltpu
from jax.sharding import PartitionSpec as P

EPSILON = 0.5
DAMPING = 0.5


SMEM = pl.BlockSpec(memory_space=pltpu.SMEM)
VMEM = pl.BlockSpec(memory_space=pltpu.VMEM)
F32 = jnp.float32
BF16 = jnp.bfloat16


def call(kernel, outs, specs, args, flops, scratch=(), aliases=None):
    return pl.pallas_call(
        kernel,
        out_shape=[jax.ShapeDtypeStruct(s, F32) for s in outs],
        in_specs=specs,
        out_specs=[VMEM] * len(outs),
        scratch_shapes=list(scratch),
        input_output_aliases=aliases or {},
        compiler_params=pltpu.CompilerParams(vmem_limit_bytes=16 * 2**20),
        cost_estimate=pl.CostEstimate(flops=flops, bytes_accessed=2**20, transcendentals=0),
    )(*args)


def dft_tables(length):
    index = np.arange(length)
    angle = (index[:, None] * index[None, :] % length) * (2.0 * math.pi / length)
    cos, sin = np.cos(angle) / math.sqrt(length), np.sin(angle) / math.sqrt(length)
    right = np.block([[cos, -sin], [sin, cos]])
    tables = []
    for table in (right, right.T):
        high = table.astype(BF16)
        tables += [high, (table - high.astype(np.float64)).astype(BF16)]
    return jnp.asarray(np.stack(tables))


def split(x):
    high = x.astype(BF16)
    return high, (x - high.astype(F32)).astype(BF16)


def dot3(a_high, a_low, b_high, b_low):
    dot = functools.partial(jnp.dot, preferred_element_type=F32)
    return dot(a_high, b_high) + (dot(a_low, b_high) + dot(a_high, b_low))


def lanes(rows, size):
    return lax.broadcasted_iota(jnp.int32, (rows, size), 1)


def turn(x):
    return pltpu.roll(x, x.shape[-1] // 2, 1)


def place(metas, which, slot, size):
    y, x = metas[which, 2 * slot], metas[which, 2 * slot + 1]
    return y, x // size, x % size


def edge_kernel(obj, up, down, edge_l, edge_r):
    _, rows, columns = obj.shape
    half, size = up.shape[1], edge_l.shape[1]
    low = lanes(rows, size) < half
    for ch in range(2):
        down[ch] = obj[ch, :half, :]
        up[ch] = obj[ch, rows - half :, :]
    near, far = slice(0, size), slice(columns - size, columns)
    edge_l[...] = jnp.where(low, obj[0, :, near], turn(obj[1, :, near]))
    edge_r[...] = jnp.where(low, turn(obj[0, :, far]), obj[1, :, far])


def frame_kernel(obj, top, bot, left, right, out):
    tiles, rows, size = out.shape[1:]
    half = size // 2
    low = lanes(half, size) < half
    for at in range(0, rows, half):
        body, src = obj, pl.ds(at - half, half)
        if at == 0:
            body, src = top, pl.ds(0, half)
        elif at == rows - half:
            body, src = bot, pl.ds(0, half)
        here = pl.ds(at, half)
        for ch in range(2):
            parts = [turn(body[ch, src, t * size : (t + 1) * size]) for t in range(tiles - 1)]
            edge_l, edge_r = left[here, :], right[here, :]
            edge_l = edge_l if ch == 0 else turn(edge_l)
            edge_r = turn(edge_r) if ch == 0 else edge_r
            parts = [edge_l, *parts, edge_r]
            for t in range(tiles):
                out[ch, t, here, :] = jnp.where(low, parts[t], parts[t + 1])


def forward_kernel(parts, *refs):
    metas, beams, frame, probe, tables = refs[:5]
    outs, (x_high, x_low, y_high, y_low) = refs[5:-4], refs[-4:]
    size = probe.shape[-1]
    lane = lanes(size, size)
    for at, (which, start, slots) in enumerate(parts):
        far, wave, power = outs[3 * at : 3 * at + 3]
        for index in range(slots):
            slot = start + index
            y, tile, shift = place(metas, which, slot, size)
            beam = beams[which, slot]
            back = lax.rem(size - shift, size)
            patch = []
            for ch in range(2):
                near = pltpu.roll(frame[ch, tile, pl.ds(y, size), :], back, 1)
                rest = pltpu.roll(frame[ch, tile + 1, pl.ds(y, size), :], back, 1)
                patch.append(jnp.where(lane < size - shift, near, rest))
            probe_re, probe_im = probe[beam, 0], probe[beam, 1]
            waves = (
                probe_re * patch[0] - probe_im * patch[1],
                probe_re * patch[1] + probe_im * patch[0],
            )
            rows = slice(index * size, (index + 1) * size)
            for ch in range(2):
                wave[index, ch] = waves[ch]
                columns = slice(ch * size, (ch + 1) * size)
                x_high[rows, columns], x_low[rows, columns] = split(waves[ch])
        for slot in range(0, slots, 2):
            rows = slice(slot * size, (slot + 2) * size)
            mid = dot3(x_high[rows, :], x_low[rows, :], tables[0], tables[1])
            for sub in range(2):
                columns = slice((slot + sub) * size, (slot + sub + 1) * size)
                for ch in range(2):
                    piece = mid[sub * size : (sub + 1) * size, ch * size : (ch + 1) * size]
                    into = slice(ch * size, (ch + 1) * size)
                    y_high[into, columns], y_low[into, columns] = split(piece)
            columns = slice(slot * size, (slot + 2) * size)
            result = dot3(tables[2], tables[3], y_high[:, columns], y_low[:, columns])
            far[:, columns] = result
            for sub in range(2):
                inside = slice(sub * size, (sub + 1) * size)
                re, im = result[:size, inside], result[size:, inside]
                power[slot + sub] = re * re + im * im


def add_patch(total, channel, y, tile, shift, value, lane):
    moved = pltpu.roll(value, shift, 1)
    rows = pl.ds(y, value.shape[0])
    total[channel, tile, rows, :] += jnp.where(lane >= shift, moved, 0.0)
    total[channel, tile + 1, rows, :] += jnp.where(lane < shift, moved, 0.0)


def write_sides(total, side_l, side_r):
    channels, tiles, rows, size = total.shape
    half = size // 2
    low = lanes(rows, size) < half
    if channels == 1:
        side_l[...] = total[0, 0]
        side_r[...] = turn(total[0, tiles - 1])
    else:
        side_l[...] = jnp.where(low, total[0, 0], turn(total[1, 0]))
        side_r[...] = jnp.where(low, turn(total[0, tiles - 1]), total[1, tiles - 1])


def own_columns(total, channel, rows, low):
    tiles = total.shape[1]
    turned = [turn(total[channel, t, rows, :]) for t in range(tiles)]
    return [jnp.where(low, turned[t], turned[t + 1]) for t in range(tiles - 1)]


def write_rims(total, rim_top, rim_bot):
    channels, _, rows, size = total.shape
    half = size // 2
    low = lanes(half, size) < half
    for ch in range(channels):
        for start, out in ((0, rim_top), (rows - half, rim_bot)):
            for t, value in enumerate(own_columns(total, ch, pl.ds(start, half), low)):
                out[ch, :, t * size : (t + 1) * size] = value


def backward_kernel(parts, fresh, last, *refs):
    metas, beams, probe, tables = refs[:4]
    inputs, refs = refs[4 : 4 + 3 * len(parts)], refs[4 + 3 * len(parts) :]
    if not fresh:
        refs = refs[1:]
    total, refs = refs[0], refs[1:]
    if last:
        (side_l, side_r, rim_top, rim_bot), refs = refs[:4], refs[4:]
    x_high, x_low, y_high, y_low = refs
    size = probe.shape[-1]
    scans = beams.shape[1]
    lane = lanes(size, size)
    if fresh:
        total[...] = jnp.zeros_like(total)
    for at, (which, start, slots) in enumerate(parts):
        far, wave, factor = inputs[3 * at : 3 * at + 3]
        for slot in range(0, slots, 2):
            for sub in range(2):
                columns = slice((slot + sub) * size, (slot + sub + 1) * size)
                scale = factor[slot + sub]
                for ch in range(2):
                    into = slice(ch * size, (ch + 1) * size)
                    y_high[into, columns], y_low[into, columns] = split(far[into, columns] * scale)
            columns = slice(slot * size, (slot + 2) * size)
            mid = dot3(tables[0], tables[1], y_high[:, columns], y_low[:, columns])
            for sub in range(2):
                rows = slice((slot + sub) * size, (slot + sub + 1) * size)
                for ch in range(2):
                    piece = mid[ch * size : (ch + 1) * size, sub * size : (sub + 1) * size]
                    into = slice(ch * size, (ch + 1) * size)
                    x_high[rows, into], x_low[rows, into] = split(piece)
            rows = slice(slot * size, (slot + 2) * size)
            result = dot3(x_high[rows, :], x_low[rows, :], tables[2], tables[3])
            for sub in range(2):
                true_slot = start + slot + sub
                live = (true_slot < metas[which, 2 * scans]).astype(F32)
                beam = beams[which, true_slot]
                probe_re, probe_im = probe[beam, 0], probe[beam, 1]
                inside = slice(sub * size, (sub + 1) * size)
                change_re = (result[inside, :size] - wave[slot + sub, 0]) * live
                change_im = (result[inside, size:] - wave[slot + sub, 1]) * live
                grad_re = probe_re * change_re + probe_im * change_im
                grad_im = probe_re * change_im - probe_im * change_re
                spot = place(metas, which, true_slot, size)
                add_patch(total, 0, *spot, grad_re, lane)
                add_patch(total, 1, *spot, grad_im, lane)
    if last:
        write_sides(total, side_l, side_r)
        write_rims(total, rim_top, rim_bot)


def weight_kernel(steps, spans, fresh, *refs):
    metas, (inside, beams, probe) = refs[: len(spans)], refs[len(spans) : len(spans) + 3]
    total = refs[-1]
    _, tiles, rows, size = total.shape
    half, scans = size // 2, beams.shape[1]
    own_rows, own_columns = rows - 2 * size, (tiles - 2) * size
    lane = lanes(size, size)
    if fresh:
        total[...] = jnp.zeros_like(total)
    else:
        total[...] = refs[-2][...]
    for meta, across in zip(metas, spans):
        for row, down, which in steps:

            def add(slot, carry, meta=meta, across=across, row=row, down=down, which=which):
                y = meta[row, 2 * slot] + (down * own_rows + half)
                x = meta[row, 2 * slot + 1] + (across * own_columns + half)
                near = (y > 0) & (y < rows - size) & (x > 0) & (x < (tiles - 1) * size)
                live = (slot < meta[row, 2 * scans]) & (inside[down + 1] > 0)

                @pl.when(near & live)
                def _():
                    beam = beams[which, slot]
                    probe_re, probe_im = probe[beam, 0], probe[beam, 1]
                    value = probe_re * probe_re + probe_im * probe_im
                    add_patch(total, 0, y, x // size, x % size, value, lane)

                return carry

            lax.fori_loop(0, scans, add, 0)


def gathered(total, side_l, side_r, in_top, in_bot, in_ctop, in_cbot, channel, chunk, half):
    _, tiles, rows, size = total.shape
    chunks = (rows - size) // half
    low = lanes(half, size) < half
    ext = pl.ds((chunk + 1) * half, half)
    values = own_columns(total, channel, ext, low)

    def add_sides(from_l, from_r):
        from_l = from_l if channel == 0 else turn(from_l)
        from_r = turn(from_r) if channel == 0 else from_r
        values[0] += jnp.where(low, from_l, 0.0)
        values[-1] += jnp.where(low, 0.0, from_r)

    add_sides(side_l[ext, :], side_r[ext, :])
    for at, rim, corner in ((0, in_top, in_ctop), (chunks - 1, in_bot, in_cbot)):
        if chunk == at:
            for t in range(tiles - 1):
                values[t] += rim[channel, :, t * size : (t + 1) * size]
            add_sides(corner[0], corner[1])
    return values


def final_kernel(*refs):
    obj, weight, out = refs[0], refs[1], refs[-1]
    grads = refs[2:9]
    size = grads[0].shape[-1]
    half = size // 2
    tiles = obj.shape[2] // size
    for chunk in range(obj.shape[1] // half):
        wide = pl.ds(size + chunk * half, half)
        scale = [1.0 / (weight[0, t + 1, wide, :] + DAMPING) for t in range(tiles)]
        rows = slice(chunk * half, (chunk + 1) * half)
        for ch in range(2):
            for t, value in enumerate(gathered(*grads, ch, chunk, half)):
                columns = slice(t * size, (t + 1) * size)
                out[ch, rows, columns] = obj[ch, rows, columns] + value * scale[t]


def line(axis, by):
    count = lax.axis_size(axis)
    return [(i, i + by) for i in range(count) if 0 <= i + by < count]


def ring(axis, by):
    count = lax.axis_size(axis)
    return [(i, (i + by) % count) for i in range(count)]


def send_rims(side_l, side_r, rim_top, rim_bot):
    rows, size = side_l.shape
    half = size // 2
    in_r = lax.ppermute(side_l, "col", line("col", -1))
    in_l = lax.ppermute(side_r, "col", line("col", 1))
    in_bot = lax.ppermute(rim_top, "row", line("row", -1))
    in_top = lax.ppermute(rim_bot, "row", line("row", 1))
    corner_top = jnp.stack([in_l[:half], in_r[:half]])
    corner_bot = jnp.stack([in_l[rows - half :], in_r[rows - half :]])
    in_cbot = lax.ppermute(corner_top, "row", line("row", -1))
    in_ctop = lax.ppermute(corner_bot, "row", line("row", 1))
    return in_l, in_r, in_top, in_bot, in_ctop, in_cbot


def on_device(obj, probe, positions, counts, offsets, measured):
    offsets_count, _, size, _ = probe.shape
    scans = positions.shape[2]
    half = size // 2
    tile_rows, tile_columns = obj.shape[1:]
    rows, tiles = tile_rows + size, tile_columns // size + 1
    row_count = lax.axis_size("row")
    tables = dft_tables(size)

    def packed(x):
        return jnp.concatenate([x[0], x[1]], axis=1)

    up, down, edge_l, edge_r = call(
        edge_kernel, [(2, half, tile_columns)] * 2 + [(tile_rows, size)] * 2, [VMEM], (obj,), 10**6
    )
    top = lax.ppermute(up, "row", line("row", 1))
    bot = lax.ppermute(down, "row", line("row", -1))

    meta = jnp.concatenate([positions.reshape(1, -1), counts.reshape(1, -1)], axis=1)
    kept = min(row_count, offsets_count + 2)
    shifts = [k if k <= offsets_count else k - kept for k in range(kept)]
    metas = [meta] + [lax.ppermute(meta, "row", ring("row", k)) for k in shifts[1:]]
    metas = jnp.concatenate(metas)
    beams = jnp.argmax(offsets[None] == jnp.arange(offsets_count)[:, None, None], axis=2).astype(jnp.int32)
    most = offsets_count - 1

    edge_l, edge_r = (
        jnp.concatenate([packed(top[:, :, part]), edge, packed(bot[:, :, part])])
        for part, edge in ((slice(0, half), edge_l), (slice(tile_columns - half, None), edge_r))
    )
    left = lax.ppermute(edge_r, "col", line("col", 1))
    right = lax.ppermute(edge_l, "col", line("col", -1))
    (frame,) = call(
        frame_kernel, [(2, tiles, rows, size)], [VMEM] * 5, (obj, top, bot, left, right), 10**6
    )

    slots = scans // 2
    halves = ((0, slots), (slots, scans - slots))
    work = [
        pltpu.VMEM((slots * size, 2 * size), BF16),
        pltpu.VMEM((slots * size, 2 * size), BF16),
        pltpu.VMEM((2 * size, slots * size), BF16),
        pltpu.VMEM((2 * size, slots * size), BF16),
    ]
    flops = slots * 2 * 3 * 2 * size * (2 * size) ** 2

    far, wave, power = {}, {}, {}

    def forward(parts):
        outs = []
        for _, _, count in parts:
            outs += [(2 * size, count * size), (count, 2, size, size), (count, size, size)]
        results = call(
            functools.partial(forward_kernel, parts),
            outs,
            [SMEM, SMEM, VMEM, VMEM, VMEM],
            (metas, beams, frame, probe, tables),
            flops * len(parts),
            work,
        )
        for at, (which, start, _) in enumerate(parts):
            far[which, start], wave[which, start], power[which, start] = results[3 * at : 3 * at + 3]

    at_row = lax.axis_index("row")
    inside = jnp.stack([at_row > 0, at_row >= 0, at_row < row_count - 1]).astype(jnp.int32)
    spans = {
        0: metas,
        -1: lax.ppermute(metas, "col", line("col", 1)),
        1: lax.ppermute(metas, "col", line("col", -1)),
    }
    everything = [(which, down) for down in (-1, 0, 1) for which in range(offsets_count)]
    pieces = [(0, everything[::2]), (0, everything[1::2]), (-1, everything), (1, everything)]
    weight = None

    def add_weight(after):
        nonlocal weight
        across, chosen = pieces.pop(0)
        steps = [((which - down) % kept, down, which) for which, down in chosen]
        span, _ = lax.optimization_barrier((spans[across], after))
        (weight,) = call(
            functools.partial(weight_kernel, steps, (across,), weight is None),
            [(1, tiles + 1, tile_rows + 2 * size, size)],
            [SMEM, SMEM, SMEM, VMEM] + ([] if weight is None else [VMEM]),
            (span, inside, beams, probe) + (() if weight is None else (weight,)),
            flops,
            aliases={} if weight is None else {4: 0},
        )

    forward([(most, *halves[0])])
    forward([(most, *halves[1])])
    sums = {start: power[most, start] for start, _ in halves}
    for which in reversed(range(most)):
        for start, _ in halves:
            arrived = lax.ppermute(sums[start], "row", ring("row", -1))
            if which == most - 1 and start == halves[-1][0]:
                forward([(w, *part) for w in reversed(range(most)) for part in halves])
            if which < most - 1 and pieces:
                add_weight(sums[start])
                arrived, weight = lax.optimization_barrier((arrived, weight))
            sums[start] = arrived
        for start, _ in halves:
            sums[start] = sums[start] + power[which, start]
    factors = {
        start: measured[0, 0, start : start + count] / jnp.sqrt(sums[start] + EPSILON) for start, count in halves
    }
    while pieces:
        add_weight(factors[0])

    total = None
    for which in range(offsets_count):
        if which:
            for start, _ in halves:
                value = lax.ppermute(factors[start], "row", ring("row", 1))
                if start == halves[-1][0] and which < most:
                    value, total = lax.optimization_barrier((value, total))
                factors[start] = value
        groups = [[part] for part in halves] if which == most else [list(halves)]
        for group in groups:
            fresh, last = total is None, which == most and group[-1] == halves[-1]
            outs = [(2, tiles, rows, size)]
            if last:
                outs += [(rows, size), (rows, size), (2, half, tile_columns), (2, half, tile_columns)]
            args = [metas, beams, probe, tables]
            for start, _ in group:
                args += [far[which, start], wave[which, start], factors[start]]
            specs = [SMEM, SMEM] + [VMEM] * (len(args) - 2)
            if not fresh:
                args, specs = args + [total], specs + [VMEM]
            total, *sides = call(
                functools.partial(backward_kernel, [(which, *part) for part in group], fresh, last),
                outs,
                specs,
                args,
                flops * len(group),
                work,
                {} if fresh else {len(args) - 1: 0},
            )
    grad_in = send_rims(*sides)

    (new_object,) = call(
        final_kernel, [obj.shape], [VMEM] * 9, (obj, weight, total, *grad_in), 10**6
    )
    return new_object


def solution(mesh):
    return jax.shard_map(
        on_device,
        mesh=mesh,
        in_specs=(
            P(None, "row", "col"),
            P(),
            P("row", "col", None, None),
            P("row", "col"),
            P(),
            P("row", "col", None, None, None),
        ),
        out_specs=P(None, "row", "col"),
        check_vma=False,
    )
```

profile of v0, /device:TPU:1, one launch (start us, length us, event | category | flops | bytes accessed | tf_op | source)
XLA Modules:
  0.0 143.0 jit_solution(11132799065960258177)
XLA Ops:
  1.4 4.2 %collective-permute-start.3 = (f32[2,64,384]{2,1,0:T(8,128)S(1)}, f32[2,64,384]{2,1,0:T(8,128)S(1)}, u32[]{:S(2)}, u32[]{:S(2)}) collective-permute-start(f32[2,64,384]{2,1,0:T(8,128)S(1)} %get-tuple-element.56), channel_id=1, source_target_pairs={{0,8},{8,16},{16,24},{1,9},{9,17},{17,25},{2,10},{10,18},{18,26},{... | collective-permute-start | bytes 589832 | tf_op jit(solution)/shard_map/ppermute | solution.py:343
  7.2 1.4 collective-permute-start.2
  12.3 5.0 %collective-permute-done.4.bot = f32[2,64,384]{2,1,0:T(8,128)S(1)} collective-permute-done((f32[2,64,384]{2,1,0:T(8,128)S(1)}, f32[2,64,384]{2,1,0:T(8,128)S(1)}, u32[]{:S(2)}, u32[]{:S(2)}) %collective-permute-start.4) | collective-permute-done | bytes 196640 | tf_op jit(solution)/shard_map/ppermute | solution.py:344
  17.5 4.8 %collective-permute-start.6 = (f32[512,128]{1,0:T(8,128)S(1)}, f32[512,128]{1,0:T(8,128)S(1)}, u32[]{:S(2)}, u32[]{:S(2)}) collective-permute-start(f32[512,128]{1,0:T(8,128)S(1)} %maximum_maximum_fusion.1), channel_id=1, source_target_pairs={{1,0},{2,1},{3,2},{4,3},{5,4},{6,5},{7,6},{9,8},{10,9},{11,10},{12... | collective-permute-start | bytes 786440 | tf_op jit(solution)/shard_map/ppermute | solution.py:359
  22.5 3.0 %collective-permute-start.5 = (f32[512,128]{1,0:T(8,128)S(1)}, f32[512,128]{1,0:T(8,128)S(1)}, u32[]{:S(2)}, u32[]{:S(2)}) collective-permute-start(f32[512,128]{1,0:T(8,128)S(1)} %maximum_maximum_fusion), channel_id=1, source_target_pairs={{0,1},{1,2},{2,3},{3,4},{4,5},{5,6},{6,7},{8,9},{9,10},{10,11},{11... | collective-permute-start | bytes 786440 | tf_op jit(solution)/shard_map/ppermute | solution.py:358
  26.2 1.4 collective-permute-done.6.right
  29.4 1.7 %shard_map.77 = (f32[256,512]{1,0:T(8,128)S(1)}, f32[4,2,128,128]{3,2,1,0:T(8,128)S(1)}, f32[4,128,128]{2,1,0:T(8,128)S(1)}) custom-call(s32[4,17]{1,0:T(4,128)S(1)} %pad_add_fusion.refs_0_, s32[4,8]{1,0:T(4,128)S(1)} %get-tuple-element.55.refs_1_.refs_2_, f32[2,4,512,128]{3,2,1,0:T(8,128)S(1)} %shard_map.74.refs_2_, f32[4,2,128,128]{3,2,1,0:T(8,128)S(1)} %copy-done, ...), custom_call_target="tpu_custom_call" | custom-call | flops 402653184 | bytes 1048576 | tf_op jit(solution)/shard_map/pallas_call | solution.py:23
  31.2 1.7 %shard_map.75 = (f32[256,512]{1,0:T(8,128)S(1)}, f32[4,2,128,128]{3,2,1,0:T(8,128)S(1)}, f32[4,128,128]{2,1,0:T(8,128)S(1)}) custom-call(s32[4,17]{1,0:T(4,128)S(1)} %pad_add_fusion.refs_0_, s32[4,8]{1,0:T(4,128)S(1)} %get-tuple-element.55.refs_1_.refs_2_, f32[2,4,512,128]{3,2,1,0:T(8,128)S(1)} %shard_map.74.refs_2_, f32[4,2,128,128]{3,2,1,0:T(8,128)S(1)} %copy-done, ...), custom_call_target="tpu_custom_call" | custom-call | flops 402653184 | bytes 1048576 | tf_op jit(solution)/shard_map/pallas_call | solution.py:23
  34.2 4.1 %shard_map.76 = (f32[256,512]{1,0:T(8,128)S(1)}, f32[4,2,128,128]{3,2,1,0:T(8,128)S(1)}, f32[4,128,128]{2,1,0:T(8,128)S(1)}, f32[256,512]{1,0:T(8,128)S(1)}, f32...) custom-call(s32[4,17]{1,0:T(4,128)S(1)} %pad_add_fusion.refs_0_, ...), custom_call_target="tpu_custom_call" | custom-call | flops 2415919104 | bytes 1048576 | tf_op jit(solution)/shard_map/pallas_call | solution.py:23
  52.8 2.7 %shard_map.78.refs_4_ = f32[1,5,640,128]{3,2,1,0:T(8,128)S(1)} custom-call(s32[4,17]{1,0:T(4,128)S(1)} %pad_add_fusion.refs_0_, s32[3]{0:T(128)S(1)} %add_convert_fusion.refs_1_, s32[4,8]{1,0:T(4,128)S(1)} %get-tuple-element.55.refs_1_.refs_2_, f32[4,2,128,128]{3,2,1,0:T(8,128)S(1)} %copy-done), custom_call_target="tpu_custom_call" | custom-call | flops 402653184 | bytes 1048576 | tf_op jit(solution)/shard_map/pallas_call | solution.py:23
  55.6 2.5 %collective-permute-done.10 = f32[4,128,128]{2,1,0:T(8,128)} collective-permute-done((f32[4,128,128]{2,1,0:T(8,128)}, f32[4,128,128]{2,1,0:T(8,128)}, u32[]{:S(2)}, u32[]{:S(2)}) %collective-permute-start.10) | collective-permute-done | bytes 262176 | tf_op jit(solution)/shard_map/ppermute | solution.py:421
  59.0 3.1 %collective-permute-start.13 = (f32[4,128,128]{2,1,0:T(8,128)S(1)}, f32[4,128,128]{2,1,0:T(8,128)S(1)}, u32[]{:S(2)}, u32[]{:S(2)}) collective-permute-start(f32[4,128,128]{2,1,0:T(8,128)S(1)} %add.27), channel_id=1, source_target_pairs={{0,24},{8,0},{16,8},{24,16},{1,25},{9,1},{17,9},{25,17},{2,26},{10... | collective-permute-start | bytes 786440 | tf_op jit(solution)/shard_map/ppermute | solution.py:421
  62.1 2.8 %shard_map.79.refs_4_ = f32[1,5,640,128]{3,2,1,0:T(8,128)S(1)} custom-call(s32[4,17]{1,0:T(4,128)S(1)} %pad_add_fusion.refs_0_, s32[3]{0:T(128)S(1)} %add_convert_fusion.refs_1_, s32[4,8]{1,0:T(4,128)S(1)} %get-tuple-element.55.refs_1_.refs_2_, f32[4,2,128,128]{3,2,1,0:T(8,128)S(1)} %copy-done, ...), custom_call_target="tpu_custom_call", output_to_operand_aliasing={{}: (4, {})} | custom-call | flops 402653184 | bytes 1048576 | tf_op jit(solution)/shard_map/pallas_call | solution.py:23
  66.8 1.9 %collective-permute-start.12 = (s32[4,17]{1,0:T(4,128)S(1)}, s32[4,17]{1,0:T(4,128)S(1)}, u32[]{:S(2)}, u32[]{:S(2)}) collective-permute-start(s32[4,17]{1,0:T(4,128)S(1)} %pad_add_fusion.refs_0_), channel_id=1, source_target_pairs={{1,0},{2,1},{3,2},{4,3},{5,4},{6,5},{7,6},{9,8},{10,9},{11,10},{12... | collective-permute-start | bytes 824 | tf_op jit(solution)/shard_map/ppermute | solution.py:396
  68.7 7.0 %collective-permute-start.14 = (s32[4,17]{1,0:T(4,128)S(1)}, s32[4,17]{1,0:T(4,128)S(1)}, u32[]{:S(2)}, u32[]{:S(2)}) collective-permute-start(s32[4,17]{1,0:T(4,128)S(1)} %pad_add_fusion.refs_0_), channel_id=1, source_target_pairs={{0,1},{1,2},{2,3},{3,4},{4,5},{5,6},{6,7},{8,9},{9,10},{10,11},{11... | collective-permute-start | bytes 824 | tf_op jit(solution)/shard_map/ppermute | solution.py:395
  76.5 3.0 %shard_map.80.refs_4_ = f32[1,5,640,128]{3,2,1,0:T(8,128)S(1)} custom-call(s32[4,17]{1,0:T(4,128)S(1)} %collective-permute-done.14.refs_0_, s32[3]{0:T(128)S(1)} %add_convert_fusion.refs_1_, s32[4,8]{1,0:T(4,128)S(1)} %get-tuple-element.55.refs_1_.refs_2_, f32[4,2,128,128]{3,2,1,0:T(8,128)S(1)} %copy-done, ...), custom_call_target="tpu_custom_call", output_to_operand_aliasing={{}: (4, {})} | custom-call | flops 402653184 | bytes 1048576 | tf_op jit(solution)/shard_map/pallas_call | solution.py:23
  79.6 2.9 %shard_map.81.refs_1_ = f32[1,5,640,128]{3,2,1,0:T(8,128)S(1)} custom-call(s32[4,17]{1,0:T(4,128)S(1)} %collective-permute-done.12.refs_0_, s32[3]{0:T(128)S(1)} %add_convert_fusion.refs_1_, s32[4,8]{1,0:T(4,128)S(1)} %get-tuple-element.55.refs_1_.refs_2_, f32[4,2,128,128]{3,2,1,0:T(8,128)S(1)} %copy-done, ...), custom_call_target="tpu_custom_call", output_to_operand_aliasing={{}: (4, {})} | custom-call | flops 402653184 | bytes 1048576 | tf_op jit(solution)/shard_map/pallas_call | solution.py:23
  83.1 8.8 %collective-permute-done.17.refs_6_ = f32[4,128,128]{2,1,0:T(8,128)S(1)} collective-permute-done((f32[4,128,128]{2,1,0:T(8,128)S(1)}, f32[4,128,128]{2,1,0:T(8,128)S(1)}, u32[]{:S(2)}, u32[]{:S(2)}) %collective-permute-start.17) | collective-permute-done | bytes 262176 | tf_op jit(solution)/shard_map/ppermute | solution.py:440
  92.0 2.3 %shard_map.82.refs_10_ = f32[2,4,512,128]{3,2,1,0:T(8,128)S(1)} custom-call(s32[4,17]{1,0:T(4,128)S(1)} %pad_add_fusion.refs_0_, s32[4,8]{1,0:T(4,128)S(1)} %get-tuple-element.55.refs_1_.refs_2_, f32[4,2,128,128]{3,2,1,0:T(8,128)S(1)} %copy-done, bf16[4,256,256]{2,1,0:T(8,128)(2,1)S(1)} %copy-done.1, f32[256,512]{1,0:T(8,128)S(1)} %copy-done.21, ...), custom_call_target="tpu_custom_call" | custom-call | flops 805306368 | bytes 1048576 | tf_op jit(solution)/shard_map/pallas_call | solution.py:23
  94.3 3.2 %collective-permute-done.15.refs_9_ = f32[4,128,128]{2,1,0:T(8,128)S(1)} collective-permute-done((f32[4,128,128]{2,1,0:T(8,128)S(1)}, f32[4,128,128]{2,1,0:T(8,128)S(1)}, u32[]{:S(2)}, u32[]{:S(2)}) %collective-permute-start.15) | collective-permute-done | bytes 262176 | tf_op jit(solution)/shard_map/ppermute | solution.py:440
  97.5 5.6 %collective-permute-done.19.refs_6_ = f32[4,128,128]{2,1,0:T(8,128)S(1)} collective-permute-done((f32[4,128,128]{2,1,0:T(8,128)S(1)}, f32[4,128,128]{2,1,0:T(8,128)S(1)}, u32[]{:S(2)}, u32[]{:S(2)}) %collective-permute-start.19) | collective-permute-done | bytes 262176 | tf_op jit(solution)/shard_map/ppermute | solution.py:440
  103.2 2.2 %shard_map.83.refs_10_ = f32[2,4,512,128]{3,2,1,0:T(8,128)S(1)} custom-call(s32[4,17]{1,0:T(4,128)S(1)} %pad_add_fusion.refs_0_, s32[4,8]{1,0:T(4,128)S(1)} %get-tuple-element.55.refs_1_.refs_2_, f32[4,2,128,128]{3,2,1,0:T(8,128)S(1)} %copy-done, bf16[4,256,256]{2,1,0:T(8,128)(2,1)S(1)} %copy-done.1, ...), custom_call_target="tpu_custom_call", output_to_operand_aliasing={{}: (10, {})} | custom-call | flops 805306368 | bytes 1048576 | tf_op jit(solution)/shard_map/pallas_call | solution.py:23
  105.4 3.4 %collective-permute-done.16.refs_9_ = f32[4,128,128]{2,1,0:T(8,128)S(1)} collective-permute-done((f32[4,128,128]{2,1,0:T(8,128)S(1)}, f32[4,128,128]{2,1,0:T(8,128)S(1)}, u32[]{:S(2)}, u32[]{:S(2)}) %collective-permute-start.16) | collective-permute-done | bytes 262176 | tf_op jit(solution)/shard_map/ppermute | solution.py:440
  108.8 2.2 %shard_map.84.refs_7_ = f32[2,4,512,128]{3,2,1,0:T(8,128)S(1)} custom-call(s32[4,17]{1,0:T(4,128)S(1)} %pad_add_fusion.refs_0_, s32[4,8]{1,0:T(4,128)S(1)} %get-tuple-element.55.refs_1_.refs_2_, f32[4,2,128,128]{3,2,1,0:T(8,128)S(1)} %copy-done, bf16[4,256,256]{2,1,0:T(8,128)(2,1)S(1)} %copy-done.1, ...), custom_call_target="tpu_custom_call", output_to_operand_aliasing={{}: (10, {})} | custom-call | flops 805306368 | bytes 1048576 | tf_op jit(solution)/shard_map/pallas_call | solution.py:23
  111.0 2.9 %collective-permute-done.20.refs_6_ = f32[4,128,128]{2,1,0:T(8,128)S(1)} collective-permute-done((f32[4,128,128]{2,1,0:T(8,128)S(1)}, f32[4,128,128]{2,1,0:T(8,128)S(1)}, u32[]{:S(2)}, u32[]{:S(2)}) %collective-permute-start.20) | collective-permute-done | bytes 262176 | tf_op jit(solution)/shard_map/ppermute | solution.py:440
  113.9 1.6 %shard_map.85.refs_7_ = f32[2,4,512,128]{3,2,1,0:T(8,128)S(1)} custom-call(s32[4,17]{1,0:T(4,128)S(1)} %pad_add_fusion.refs_0_, s32[4,8]{1,0:T(4,128)S(1)} %get-tuple-element.55.refs_1_.refs_2_, f32[4,2,128,128]{3,2,1,0:T(8,128)S(1)} %copy-done, bf16[4,256,256]{2,1,0:T(8,128)(2,1)S(1)} %copy-done.1, ...), custom_call_target="tpu_custom_call", output_to_operand_aliasing={{}: (7, {})} | custom-call | flops 402653184 | bytes 1048576 | tf_op jit(solution)/shard_map/pallas_call | solution.py:23
  116.6 1.9 %shard_map.86 = (f32[2,4,512,128]{3,2,1,0:T(8,128)S(1)}, f32[512,128]{1,0:T(8,128)S(1)}, f32[512,128]{1,0:T(8,128)S(1)}, f32[2,64,384]{2,1,0:T(8,128)S(1)}, f32[2,64,384]{2,1,0:T(8,128)S(1)}) custom-call(s32[4,17]{1,0:T(4,128)S(1)} %pad_add_fusion.refs_0_, s32[4,8]{1,0:T(4,128)S(1)} %get-tuple-element.55.refs_1_.refs_2_, ...), custom_call_target="tpu_custom_call", output_to_operand_aliasing={{0}: (7, {})} | custom-call | flops 402653184 | bytes 1048576 | tf_op jit(solution)/shard_map/pallas_call | solution.py:23
  118.5 8.8 %collective-permute-start.21 = (f32[512,128]{1,0:T(8,128)S(1)}, f32[512,128]{1,0:T(8,128)S(1)}, u32[]{:S(2)}, u32[]{:S(2)}) collective-permute-start(f32[512,128]{1,0:T(8,128)S(1)} %get-tuple-element.101), channel_id=1, source_target_pairs={{0,1},{1,2},{2,3},{3,4},{4,5},{5,6},{6,7},{8,9},{9,10},{10,11},{11... | collective-permute-start | bytes 786440 | tf_op jit(solution)/shard_map/ppermute | solution.py:318
  127.4 1.9 %collective-permute-start.22 = (f32[512,128]{1,0:T(8,128)S(1)}, f32[512,128]{1,0:T(8,128)S(1)}, u32[]{:S(2)}, u32[]{:S(2)}) collective-permute-start(f32[512,128]{1,0:T(8,128)S(1)} %get-tuple-element.102), channel_id=1, source_target_pairs={{1,0},{2,1},{3,2},{4,3},{5,4},{6,5},{7,6},{9,8},{10,9},{11,10},{12... | collective-permute-start | bytes 786440 | tf_op jit(solution)/shard_map/ppermute | solution.py:317
  132.0 3.1 %collective-permute-done.22.refs_4_ = f32[512,128]{1,0:T(8,128)S(1)} collective-permute-done((f32[512,128]{1,0:T(8,128)S(1)}, f32[512,128]{1,0:T(8,128)S(1)}, u32[]{:S(2)}, u32[]{:S(2)}) %collective-permute-start.22) | collective-permute-done | bytes 262176 | tf_op jit(solution)/shard_map/ppermute | solution.py:317
  137.7 3.7 %collective-permute-done.26.refs_8_ = f32[2,64,128]{2,1,0:T(8,128)S(1)} collective-permute-done((f32[2,64,128]{2,1,0:T(8,128)S(1)}, f32[2,64,128]{2,1,0:T(8,128)S(1)}, u32[]{:S(2)}, u32[]{:S(2)}) %collective-permute-start.26) | collective-permute-done | bytes 65568 | tf_op jit(solution)/shard_map/ppermute | solution.py:323
  141.4 1.6 %shard_map.87 = f32[2,384,384]{2,1,0:T(8,128)} custom-call(f32[2,384,384]{2,1,0:T(8,128)S(1)} %copy-done.3, f32[1,5,640,128]{3,2,1,0:T(8,128)S(1)} %shard_map.81.refs_1_, f32[2,4,512,128]{3,2,1,0:T(8,128)S(1)} %get-tuple-element.100.refs_2_, f32[512,128]{1,0:T(8,128)S(1)} %collective-permute-done.21.refs_3_, f32[512,128]{1,0:T(8,128)S(1)} %collective-permute-done.22.refs_4_, ...), custom_call_target="tpu_custom_call" | custom-call | flops 1000000 | bytes 1048576 | tf_op jit(solution)/shard_map/pallas_call | solution.py:23
  (136 shorter events, 35.2 us)
Async XLA Ops:
  1.3 24.2 %copy-start.39 = (s32[8,4]{0,1:T(4,128)S(1)}, s32[8,4]{0,1:T(4,128)}, u32[]{:S(2)}) copy-start(s32[8,4]{0,1:T(4,128)} %param.11) | copy-start | bytes 388
  1.3 27.5 %copy-start.3 = (f32[2,384,384]{2,1,0:T(8,128)S(1)}, f32[2,384,384]{2,1,0:T(8,128)}, u32[]{:S(2)}) copy-start(f32[2,384,384]{2,1,0:T(8,128)} %refs_0_.1) | copy-start | bytes 3538948
  1.4 10.8 %collective-permute-start.3 = (f32[2,64,384]{2,1,0:T(8,128)S(1)}, f32[2,64,384]{2,1,0:T(8,128)S(1)}, u32[]{:S(2)}, u32[]{:S(2)}) collective-permute-start(f32[2,64,384]{2,1,0:T(8,128)S(1)} %get-tuple-element.56), channel_id=1, source_target_pairs={{0,8},{8,16},{16,24},{1,9},{9,17},{17,25},{2,10},{10,18},{18,26},{... | collective-permute-start | bytes 589832 | tf_op jit(solution)/shard_map/ppermute | solution.py:343
  7.2 18.9 %collective-permute-start.2 = (s32[1,17]{1,0:T(1,128)S(1)}, s32[1,17]{1,0:T(1,128)S(1)}, u32[]{:S(2)}, u32[]{:S(2)}) collective-permute-start(s32[1,17]{1,0:T(1,128)S(1)} %pad_add_fusion.1), channel_id=1, source_target_pairs={{0,24},{8,0},{16,8},{24,16},{1,25},{9,1},{17,9},{25,17},{2,26},{10... | collective-permute-start | bytes 212 | tf_op jit(solution)/shard_map/ppermute | solution.py:349
  8.6 17.5 %collective-permute-start.1 = (s32[1,17]{1,0:T(1,128)S(1)}, s32[1,17]{1,0:T(1,128)S(1)}, u32[]{:S(2)}, u32[]{:S(2)}) collective-permute-start(s32[1,17]{1,0:T(1,128)S(1)} %pad_add_fusion.1), channel_id=1, source_target_pairs={{0,16},{8,24},{16,0},{24,8},{1,17},{9,25},{17,1},{25,9},{2,18},{10... | collective-permute-start | bytes 212 | tf_op jit(solution)/shard_map/ppermute | solution.py:349
  9.7 16.4 %collective-permute-start = (s32[1,17]{1,0:T(1,128)S(1)}, s32[1,17]{1,0:T(1,128)S(1)}, u32[]{:S(2)}, u32[]{:S(2)}) collective-permute-start(s32[1,17]{1,0:T(1,128)S(1)} %pad_add_fusion.1), channel_id=1, source_target_pairs={{0,8},{8,16},{16,24},{24,0},{1,9},{9,17},{17,25},{25,1},{2,10},{10... | collective-permute-start | bytes 212 | tf_op jit(solution)/shard_map/ppermute | solution.py:349
  10.9 6.4 %collective-permute-start.4 = (f32[2,64,384]{2,1,0:T(8,128)S(1)}, f32[2,64,384]{2,1,0:T(8,128)S(1)}, u32[]{:S(2)}, u32[]{:S(2)}) collective-permute-start(f32[2,64,384]{2,1,0:T(8,128)S(1)} %get-tuple-element.57), channel_id=1, source_target_pairs={{8,0},{16,8},{24,16},{9,1},{17,9},{25,17},{10,2},{18,10},{26,18},{... | collective-permute-start | bytes 589832 | tf_op jit(solution)/shard_map/ppermute | solution.py:344
  17.5 10.0 %collective-permute-start.6 = (f32[512,128]{1,0:T(8,128)S(1)}, f32[512,128]{1,0:T(8,128)S(1)}, u32[]{:S(2)}, u32[]{:S(2)}) collective-permute-start(f32[512,128]{1,0:T(8,128)S(1)} %maximum_maximum_fusion.1), channel_id=1, source_target_pairs={{1,0},{2,1},{3,2},{4,3},{5,4},{6,5},{7,6},{9,8},{10,9},{11,10},{12... | collective-permute-start | bytes 786440 | tf_op jit(solution)/shard_map/ppermute | solution.py:359
  22.5 6.3 %collective-permute-start.5 = (f32[512,128]{1,0:T(8,128)S(1)}, f32[512,128]{1,0:T(8,128)S(1)}, u32[]{:S(2)}, u32[]{:S(2)}) collective-permute-start(f32[512,128]{1,0:T(8,128)S(1)} %maximum_maximum_fusion), channel_id=1, source_target_pairs={{0,1},{1,2},{2,3},{3,4},{4,5},{5,6},{6,7},{8,9},{9,10},{10,11},{11... | collective-permute-start | bytes 786440 | tf_op jit(solution)/shard_map/ppermute | solution.py:358
  31.1 17.5 %collective-permute-start.9 = (f32[4,128,128]{2,1,0:T(8,128)S(1)}, f32[4,128,128]{2,1,0:T(8,128)S(1)}, u32[]{:S(2)}, u32[]{:S(2)}) collective-permute-start(f32[4,128,128]{2,1,0:T(8,128)S(1)} %get-tuple-element.63), channel_id=1, source_target_pairs={{0,24},{8,0},{16,8},{24,16},{1,25},{9,1},{17,9},{25,17},{2,26},{10... | collective-permute-start | bytes 786440 | tf_op jit(solution)/shard_map/ppermute | solution.py:421
  32.9 17.8 %collective-permute-start.7 = (f32[4,128,128]{2,1,0:T(8,128)S(1)}, f32[4,128,128]{2,1,0:T(8,128)S(1)}, u32[]{:S(2)}, u32[]{:S(2)}) collective-permute-start(f32[4,128,128]{2,1,0:T(8,128)S(1)} %get-tuple-element.60), channel_id=1, source_target_pairs={{0,24},{8,0},{16,8},{24,16},{1,25},{9,1},{17,9},{25,17},{2,26},{10... | collective-permute-start | bytes 786440 | tf_op jit(solution)/shard_map/ppermute | solution.py:421
  49.4 8.6 %collective-permute-start.10 = (f32[4,128,128]{2,1,0:T(8,128)}, f32[4,128,128]{2,1,0:T(8,128)}, u32[]{:S(2)}, u32[]{:S(2)}) collective-permute-start(f32[4,128,128]{2,1,0:T(8,128)} %add.25), channel_id=1, source_target_pairs={{0,24},{8,0},{16,8},{24,16},{1,25},{9,1},{17,9},{25,17},{2,26},{10... | collective-permute-start | bytes 786440 | tf_op jit(solution)/shard_map/ppermute | solution.py:421
  51.4 13.6 %collective-permute-start.8 = (f32[4,128,128]{2,1,0:T(8,128)}, f32[4,128,128]{2,1,0:T(8,128)}, u32[]{:S(2)}, u32[]{:S(2)}) collective-permute-start(f32[4,128,128]{2,1,0:T(8,128)} %add.24), channel_id=1, source_target_pairs={{0,24},{8,0},{16,8},{24,16},{1,25},{9,1},{17,9},{25,17},{2,26},{10... | collective-permute-start | bytes 786440 | tf_op jit(solution)/shard_map/ppermute | solution.py:421
  59.0 20.5 %collective-permute-start.13 = (f32[4,128,128]{2,1,0:T(8,128)S(1)}, f32[4,128,128]{2,1,0:T(8,128)S(1)}, u32[]{:S(2)}, u32[]{:S(2)}) collective-permute-start(f32[4,128,128]{2,1,0:T(8,128)S(1)} %add.27), channel_id=1, source_target_pairs={{0,24},{8,0},{16,8},{24,16},{1,25},{9,1},{17,9},{25,17},{2,26},{10... | collective-permute-start | bytes 786440 | tf_op jit(solution)/shard_map/ppermute | solution.py:421
  66.0 16.5 %collective-permute-start.11 = (f32[4,128,128]{2,1,0:T(8,128)S(1)}, f32[4,128,128]{2,1,0:T(8,128)S(1)}, u32[]{:S(2)}, u32[]{:S(2)}) collective-permute-start(f32[4,128,128]{2,1,0:T(8,128)S(1)} %add.26), channel_id=1, source_target_pairs={{0,24},{8,0},{16,8},{24,16},{1,25},{9,1},{17,9},{25,17},{2,26},{10... | collective-permute-start | bytes 786440 | tf_op jit(solution)/shard_map/ppermute | solution.py:421
  66.8 9.0 %collective-permute-start.12 = (s32[4,17]{1,0:T(4,128)S(1)}, s32[4,17]{1,0:T(4,128)S(1)}, u32[]{:S(2)}, u32[]{:S(2)}) collective-permute-start(s32[4,17]{1,0:T(4,128)S(1)} %pad_add_fusion.refs_0_), channel_id=1, source_target_pairs={{1,0},{2,1},{3,2},{4,3},{5,4},{6,5},{7,6},{9,8},{10,9},{11,10},{12... | collective-permute-start | bytes 824 | tf_op jit(solution)/shard_map/ppermute | solution.py:396
  68.7 7.8 %collective-permute-start.14 = (s32[4,17]{1,0:T(4,128)S(1)}, s32[4,17]{1,0:T(4,128)S(1)}, u32[]{:S(2)}, u32[]{:S(2)}) collective-permute-start(s32[4,17]{1,0:T(4,128)S(1)} %pad_add_fusion.refs_0_), channel_id=1, source_target_pairs={{0,1},{1,2},{2,3},{3,4},{4,5},{5,6},{6,7},{8,9},{9,10},{10,11},{11... | collective-permute-start | bytes 824 | tf_op jit(solution)/shard_map/ppermute | solution.py:395
  79.5 12.4 %copy-start.21 = (f32[256,512]{1,0:T(8,128)S(1)}, f32[256,512]{1,0:T(8,128)}, u32[]{:S(2)}) copy-start(f32[256,512]{1,0:T(8,128)} %copy-done.20) | copy-start | bytes 1572868
  79.5 12.4 %copy-start.23 = (f32[4,2,128,128]{3,2,1,0:T(8,128)S(1)}, f32[4,2,128,128]{3,2,1,0:T(8,128)}, u32[]{:S(2)}) copy-start(f32[4,2,128,128]{3,2,1,0:T(8,128)} %copy-done.22) | copy-start | bytes 1572868
  79.5 12.4 %copy-start.25 = (f32[256,512]{1,0:T(8,128)S(1)}, f32[256,512]{1,0:T(8,128)}, u32[]{:S(2)}) copy-start(f32[256,512]{1,0:T(8,128)} %copy-done.24) | copy-start | bytes 1572868
  82.6 9.2 %collective-permute-start.17 = (f32[4,128,128]{2,1,0:T(8,128)S(1)}, f32[4,128,128]{2,1,0:T(8,128)S(1)}, u32[]{:S(2)}, u32[]{:S(2)}) collective-permute-start(f32[4,128,128]{2,1,0:T(8,128)S(1)} %get-tuple-element.105.refs_6_), channel_id=1, source_target_pairs={{0,8},{8,16},{16,24},{24,0},{1,9},{9,17},{17,25},{25,1},{2,10},{10... | collective-permute-start | bytes 786440 | tf_op jit(solution)/shard_map/ppermute | solution.py:440
  83.0 14.5 %collective-permute-start.15 = (f32[4,128,128]{2,1,0:T(8,128)S(1)}, f32[4,128,128]{2,1,0:T(8,128)S(1)}, u32[]{:S(2)}, u32[]{:S(2)}) collective-permute-start(f32[4,128,128]{2,1,0:T(8,128)S(1)} %get-tuple-element.106.refs_9_), channel_id=1, source_target_pairs={{0,8},{8,16},{16,24},{24,0},{1,9},{9,17},{17,25},{25,1},{2,10},{10... | collective-permute-start | bytes 786440 | tf_op jit(solution)/shard_map/ppermute | solution.py:440
  91.9 11.2 %collective-permute-start.19 = (f32[4,128,128]{2,1,0:T(8,128)S(1)}, f32[4,128,128]{2,1,0:T(8,128)S(1)}, u32[]{:S(2)}, u32[]{:S(2)}) collective-permute-start(f32[4,128,128]{2,1,0:T(8,128)S(1)} %collective-permute-done.17.refs_6_), channel_id=1, source_target_pairs={{0,8},{8,16},{16,24},{24,0},{1,9},{9,17},{17,25},{25,1},{2,10},{10... | collective-permute-start | bytes 786440 | tf_op jit(solution)/shard_map/ppermute | solution.py:440
  97.5 11.2 %collective-permute-start.16 = (f32[4,128,128]{2,1,0:T(8,128)S(1)}, f32[4,128,128]{2,1,0:T(8,128)S(1)}, u32[]{:S(2)}, u32[]{:S(2)}) collective-permute-start(f32[4,128,128]{2,1,0:T(8,128)S(1)} %collective-permute-done.15.refs_9_), channel_id=1, source_target_pairs={{0,8},{8,16},{16,24},{24,0},{1,9},{9,17},{17,25},{25,1},{2,10},{10... | collective-permute-start | bytes 786440 | tf_op jit(solution)/shard_map/ppermute | solution.py:440
  103.1 10.7 %collective-permute-start.20 = (f32[4,128,128]{2,1,0:T(8,128)S(1)}, f32[4,128,128]{2,1,0:T(8,128)S(1)}, u32[]{:S(2)}, u32[]{:S(2)}) collective-permute-start(f32[4,128,128]{2,1,0:T(8,128)S(1)} %collective-permute-done.19.refs_6_), channel_id=1, source_target_pairs={{0,8},{8,16},{16,24},{24,0},{1,9},{9,17},{17,25},{25,1},{2,10},{10... | collective-permute-start | bytes 786440 | tf_op jit(solution)/shard_map/ppermute | solution.py:440
  108.7 7.9 %collective-permute-start.18 = (f32[4,128,128]{2,1,0:T(8,128)S(1)}, f32[4,128,128]{2,1,0:T(8,128)S(1)}, u32[]{:S(2)}, u32[]{:S(2)}) collective-permute-start(f32[4,128,128]{2,1,0:T(8,128)S(1)} %collective-permute-done.16.refs_9_), channel_id=1, source_target_pairs={{0,8},{8,16},{16,24},{24,0},{1,9},{9,17},{17,25},{25,1},{2,10},{10... | collective-permute-start | bytes 786440 | tf_op jit(solution)/shard_map/ppermute | solution.py:440
  118.5 13.4 %collective-permute-start.21 = (f32[512,128]{1,0:T(8,128)S(1)}, f32[512,128]{1,0:T(8,128)S(1)}, u32[]{:S(2)}, u32[]{:S(2)}) collective-permute-start(f32[512,128]{1,0:T(8,128)S(1)} %get-tuple-element.101), channel_id=1, source_target_pairs={{0,1},{1,2},{2,3},{3,4},{4,5},{5,6},{6,7},{8,9},{9,10},{10,11},{11... | collective-permute-start | bytes 786440 | tf_op jit(solution)/shard_map/ppermute | solution.py:318
  127.4 7.7 %collective-permute-start.22 = (f32[512,128]{1,0:T(8,128)S(1)}, f32[512,128]{1,0:T(8,128)S(1)}, u32[]{:S(2)}, u32[]{:S(2)}) collective-permute-start(f32[512,128]{1,0:T(8,128)S(1)} %get-tuple-element.102), channel_id=1, source_target_pairs={{1,0},{2,1},{3,2},{4,3},{5,4},{6,5},{7,6},{9,8},{10,9},{11,10},{12... | collective-permute-start | bytes 786440 | tf_op jit(solution)/shard_map/ppermute | solution.py:317
  129.3 8.4 %collective-permute-start.23 = (f32[2,64,384]{2,1,0:T(8,128)S(1)}, f32[2,64,384]{2,1,0:T(8,128)S(1)}, u32[]{:S(2)}, u32[]{:S(2)}) collective-permute-start(f32[2,64,384]{2,1,0:T(8,128)S(1)} %get-tuple-element.103), channel_id=1, source_target_pairs={{0,8},{8,16},{16,24},{1,9},{9,17},{17,25},{2,10},{10,18},{18,26},{... | collective-permute-start | bytes 589832 | tf_op jit(solution)/shard_map/ppermute | solution.py:320
  130.6 7.1 %collective-permute-start.24 = (f32[2,64,384]{2,1,0:T(8,128)S(1)}, f32[2,64,384]{2,1,0:T(8,128)S(1)}, u32[]{:S(2)}, u32[]{:S(2)}) collective-permute-start(f32[2,64,384]{2,1,0:T(8,128)S(1)} %get-tuple-element.104), channel_id=1, source_target_pairs={{8,0},{16,8},{24,16},{9,1},{17,9},{25,17},{10,2},{18,10},{26,18},{... | collective-permute-start | bytes 589832 | tf_op jit(solution)/shard_map/ppermute | solution.py:319
  135.1 2.6 %collective-permute-start.25 = (f32[2,64,128]{2,1,0:T(8,128)S(1)}, f32[2,64,128]{2,1,0:T(8,128)S(1)}, u32[]{:S(2)}, u32[]{:S(2)}) collective-permute-start(f32[2,64,128]{2,1,0:T(8,128)S(1)} %pad_maximum_fusion), channel_id=1, source_target_pairs={{0,8},{8,16},{16,24},{1,9},{9,17},{17,25},{2,10},{10,18},{18,26},{... | collective-permute-start | bytes 196616 | tf_op jit(solution)/shard_map/ppermute | solution.py:324
  136.4 5.0 %collective-permute-start.26 = (f32[2,64,128]{2,1,0:T(8,128)S(1)}, f32[2,64,128]{2,1,0:T(8,128)S(1)}, u32[]{:S(2)}, u32[]{:S(2)}) collective-permute-start(f32[2,64,128]{2,1,0:T(8,128)S(1)} %pad_maximum_fusion.1), channel_id=1, source_target_pairs={{8,0},{16,8},{24,16},{9,1},{17,9},{25,17},{10,2},{18,10},{26,18},{... | collective-permute-start | bytes 196616 | tf_op jit(solution)/shard_map/ppermute | solution.py:323
  (35 other events, 132.7 us)
where the time goes:
time: 144 us; the launch traced here: 143 us
  starting transfers between devices  50.3 us (35%)
  waiting for transfers between devices  42.7 us (30%)
  Pallas kernels  31.5 us (22%)
  local copies, waits for them, and re-layouts  12.7 us (9%)
  other arithmetic  4.58 us (3%)
    pallas_call x15, Pallas kernels, call(): pl.pallas_call(kernel, out_shape=[jax.ShapeDtypeStruct(s, F32) for s in o...  31.5 us
    ppermute x6, waiting for transfers between devices, on_device(): value = lax.ppermute(factors[start], 'row', ring('row', 1))  25 us
    unnamed x81, local copies, waits for them, and re-layouts  12.4 us
    ppermute x1, starting transfers between devices, send_rims(): in_l = lax.ppermute(side_r, 'col', line('col', 1))  8.85 us
    ppermute x6, starting transfers between devices, on_device(): arrived = lax.ppermute(sums[start], 'row', ring('row', -1))  7.84 us
    ppermute x1, starting transfers between devices, on_device(): lax.ppermute(metas, 'col', line('col', 1))  7.04 us
    ppermute x1, waiting for transfers between devices, on_device(): bot = lax.ppermute(down, 'row', line('row', -1))  5.03 us
    ppermute x1, starting transfers between devices, on_device(): right = lax.ppermute(edge_l, 'col', line('col', -1))  4.85 us
  transfers between devices with their start and end apart: 27, of which 13 were waited for; matrix products, arithmetic and copies ran while one was open for 4% of the time, Pallas kernels for 18%

commit v1 on v0

--- a/solution.py
+++ b/solution.py
@@ -22,7 +22,7 @@
 def call(kernel, outs, specs, args, flops, scratch=(), aliases=None):
     return pl.pallas_call(
         kernel,
-        out_shape=[jax.ShapeDtypeStruct(s, F32) for s in outs],
+        out_shape=[s if hasattr(s, "dtype") else jax.ShapeDtypeStruct(s, F32) for s in outs],
         in_specs=specs,
         out_specs=[VMEM] * len(outs),
         scratch_shapes=list(scratch),
@@ -62,12 +62,27 @@
     return pltpu.roll(x, x.shape[-1] // 2, 1)
 
 
+def beam_of(offsets, which, slot):
+    beam = jnp.int32(0)
+    for index in range(1, offsets.shape[1]):
+        beam = jnp.where(offsets[slot, index] == which, index, beam)
+    return beam
+
+
 def place(metas, which, slot, size):
     y, x = metas[which, 2 * slot], metas[which, 2 * slot + 1]
     return y, x // size, x % size
 
 
-def edge_kernel(obj, up, down, edge_l, edge_r):
+def edge_kernel(obj, positions, counts, place_of, up, down, edge_l, edge_r, meta):
+    scans = positions.shape[2]
+    values = [positions[0, 0, slot, axis] for slot in range(scans) for axis in range(2)]
+    values += [counts[0, 0], place_of[0]]
+    lane = lax.broadcasted_iota(jnp.int32, meta.shape, 1)
+    row = jnp.zeros(meta.shape, jnp.int32)
+    for at, value in enumerate(values):
+        row = jnp.where(lane == at, value, row)
+    meta[...] = row
     _, rows, columns = obj.shape
     half, size = up.shape[1], edge_l.shape[1]
     low = lanes(rows, size) < half
@@ -101,7 +116,7 @@
 
 
 def forward_kernel(parts, *refs):
-    metas, beams, frame, probe, tables = refs[:5]
+    metas, offsets, frame, probe, tables = refs[:5]
     outs, (x_high, x_low, y_high, y_low) = refs[5:-4], refs[-4:]
     size = probe.shape[-1]
     lane = lanes(size, size)
@@ -110,7 +125,7 @@
         for index in range(slots):
             slot = start + index
             y, tile, shift = place(metas, which, slot, size)
-            beam = beams[which, slot]
+            beam = beam_of(offsets, which, slot)
             back = lax.rem(size - shift, size)
             patch = []
             for ch in range(2):
@@ -181,7 +196,7 @@
 
 
 def backward_kernel(parts, fresh, last, *refs):
-    metas, beams, probe, tables = refs[:4]
+    metas, offsets, probe, tables = refs[:4]
     inputs, refs = refs[4 : 4 + 3 * len(parts)], refs[4 + 3 * len(parts) :]
     if not fresh:
         refs = refs[1:]
@@ -190,7 +205,7 @@
         (side_l, side_r, rim_top, rim_bot), refs = refs[:4], refs[4:]
     x_high, x_low, y_high, y_low = refs
     size = probe.shape[-1]
-    scans = beams.shape[1]
+    scans = offsets.shape[0]
     lane = lanes(size, size)
     if fresh:
         total[...] = jnp.zeros_like(total)
@@ -216,7 +231,7 @@
             for sub in range(2):
                 true_slot = start + slot + sub
                 live = (true_slot < metas[which, 2 * scans]).astype(F32)
-                beam = beams[which, true_slot]
+                beam = beam_of(offsets, which, true_slot)
                 probe_re, probe_im = probe[beam, 0], probe[beam, 1]
                 inside = slice(sub * size, (sub + 1) * size)
                 change_re = (result[inside, :size] - wave[slot + sub, 0]) * live
@@ -231,11 +246,11 @@
         write_rims(total, rim_top, rim_bot)
 
 
-def weight_kernel(steps, spans, fresh, *refs):
-    metas, (inside, beams, probe) = refs[: len(spans)], refs[len(spans) : len(spans) + 3]
+def weight_kernel(steps, spans, row_count, fresh, *refs):
+    metas, (offsets, probe) = refs[: len(spans)], refs[len(spans) : len(spans) + 2]
     total = refs[-1]
     _, tiles, rows, size = total.shape
-    half, scans = size // 2, beams.shape[1]
+    half, scans = size // 2, offsets.shape[0]
     own_rows, own_columns = rows - 2 * size, (tiles - 2) * size
     lane = lanes(size, size)
     if fresh:
@@ -249,11 +264,12 @@
                 y = meta[row, 2 * slot] + (down * own_rows + half)
                 x = meta[row, 2 * slot + 1] + (across * own_columns + half)
                 near = (y > 0) & (y < rows - size) & (x > 0) & (x < (tiles - 1) * size)
-                live = (slot < meta[row, 2 * scans]) & (inside[down + 1] > 0)
+                below = meta[0, 2 * scans + 1] + down
+                live = (slot < meta[row, 2 * scans]) & (below >= 0) & (below < row_count)
 
                 @pl.when(near & live)
                 def _():
-                    beam = beams[which, slot]
+                    beam = beam_of(offsets, which, slot)
                     probe_re, probe_im = probe[beam, 0], probe[beam, 1]
                     value = probe_re * probe_re + probe_im * probe_im
                     add_patch(total, 0, y, x // size, x % size, value, lane)
@@ -337,18 +353,20 @@
     def packed(x):
         return jnp.concatenate([x[0], x[1]], axis=1)
 
-    up, down, edge_l, edge_r = call(
-        edge_kernel, [(2, half, tile_columns)] * 2 + [(tile_rows, size)] * 2, [VMEM], (obj,), 10**6
+    up, down, edge_l, edge_r, meta = call(
+        edge_kernel,
+        [(2, half, tile_columns)] * 2 + [(tile_rows, size)] * 2 + [jax.ShapeDtypeStruct((1, size), jnp.int32)],
+        [VMEM, SMEM, SMEM, SMEM],
+        (obj, positions, counts, lax.axis_index("row").astype(jnp.int32).reshape(1)),
+        10**6,
     )
     top = lax.ppermute(up, "row", line("row", 1))
     bot = lax.ppermute(down, "row", line("row", -1))
 
-    meta = jnp.concatenate([positions.reshape(1, -1), counts.reshape(1, -1)], axis=1)
     kept = min(row_count, offsets_count + 2)
     shifts = [k if k <= offsets_count else k - kept for k in range(kept)]
     metas = [meta] + [lax.ppermute(meta, "row", ring("row", k)) for k in shifts[1:]]
     metas = jnp.concatenate(metas)
-    beams = jnp.argmax(offsets[None] == jnp.arange(offsets_count)[:, None, None], axis=2).astype(jnp.int32)
     most = offsets_count - 1
 
     edge_l, edge_r = (
@@ -381,15 +399,13 @@
             functools.partial(forward_kernel, parts),
             outs,
             [SMEM, SMEM, VMEM, VMEM, VMEM],
-            (metas, beams, frame, probe, tables),
+            (metas, offsets, frame, probe, tables),
             flops * len(parts),
             work,
         )
         for at, (which, start, _) in enumerate(parts):
             far[which, start], wave[which, start], power[which, start] = results[3 * at : 3 * at + 3]
 
-    at_row = lax.axis_index("row")
-    inside = jnp.stack([at_row > 0, at_row >= 0, at_row < row_count - 1]).astype(jnp.int32)
     spans = {
         0: metas,
         -1: lax.ppermute(metas, "col", line("col", 1)),
@@ -405,12 +421,12 @@
         steps = [((which - down) % kept, down, which) for which, down in chosen]
         span, _ = lax.optimization_barrier((spans[across], after))
         (weight,) = call(
-            functools.partial(weight_kernel, steps, (across,), weight is None),
+            functools.partial(weight_kernel, steps, (across,), row_count, weight is None),
             [(1, tiles + 1, tile_rows + 2 * size, size)],
-            [SMEM, SMEM, SMEM, VMEM] + ([] if weight is None else [VMEM]),
-            (span, inside, beams, probe) + (() if weight is None else (weight,)),
+            [SMEM, SMEM, VMEM] + ([] if weight is None else [VMEM]),
+            (span, offsets, probe) + (() if weight is None else (weight,)),
             flops,
-            aliases={} if weight is None else {4: 0},
+            aliases={} if weight is None else {3: 0},
         )
 
     forward([(most, *halves[0])])
@@ -447,7 +463,7 @@
             outs = [(2, tiles, rows, size)]
             if last:
                 outs += [(rows, size), (rows, size), (2, half, tile_columns), (2, half, tile_columns)]
-            args = [metas, beams, probe, tables]
+            args = [metas, offsets, probe, tables]
             for start, _ in group:
                 args += [far[which, start], wave[which, start], factors[start]]
             specs = [SMEM, SMEM] + [VMEM] * (len(args) - 2)

time: 144 us -> 134 us (0.931)
  local copies, waits for them, and re-layouts: 12.7 us -> 2.84 us
  waiting for transfers between devices: 42.7 us -> 50.8 us
  starting transfers between devices: 50.3 us -> 44.9 us
  other arithmetic: 4.58 us -> 0.42 us
    unnamed x81 -> x14, local copies, waits for them, and re-layouts: 12.4 us -> 2.66 us
    ppermute x1, starting transfers between devices: 8.85 us -> 3.96 us  [send_rims(): in_l = lax.ppermute(side_r, 'col', line('col', 1))]
    ppermute x6, waiting for transfers between devices: 25 us -> 29.6 us  [on_device(): value = lax.ppermute(factors[start], 'row', ring('row', 1))]
    ppermute x1, starting transfers between devices: 7.04 us -> 3.01 us  [on_device(): lax.ppermute(metas, 'col', line('col', 1))]
    add x4, other arithmetic: 3.52 us -> 0.13 us  [on_device(): sums[start] = sums[start] + power[which, start]]
    ppermute x1, starting transfers between devices: 1.91 us -> 5.18 us  [on_device(): lax.ppermute(metas, 'col', line('col', -1))]
    ppermute x3, waiting for transfers between devices: 0.01 us -> 2.84 us  [on_device(): lax.ppermute(meta, 'row', ring('row', k))]
    ppermute x1, waiting for transfers between devices: 0.01 us -> 2.26 us  [on_device(): top = lax.ppermute(up, 'row', line('row', 1))]
  transfers between devices with their start and end apart: 27 -> 27, of which waited for: 13 -> 17; matrix products, arithmetic and copies ran while one was open for 4% -> 0% of each run, Pallas kernels for 18% -> 20%
where the time goes in v1:
time: 134 us; the launch traced here: 133 us
  waiting for transfers between devices  50.8 us (38%)
  starting transfers between devices  44.9 us (34%)
  Pallas kernels  32.9 us (25%)
  local copies, waits for them, and re-layouts  2.84 us (2%)
    pallas_call x15, Pallas kernels, call(): pl.pallas_call(kernel, out_shape=[s if hasattr(s, 'dtype') else jax.Shape...  32.9 us
    ppermute x6, waiting for transfers between devices, on_device(): value = lax.ppermute(factors[start], 'row', ring('row', 1))  29.6 us
    ppermute x6, starting transfers between devices, on_device(): arrived = lax.ppermute(sums[start], 'row', ring('row', -1))  9.64 us
    ppermute x1, starting transfers between devices, on_device(): lax.ppermute(metas, 'col', line('col', -1))  5.18 us
    ppermute x6, waiting for transfers between devices, on_device(): arrived = lax.ppermute(sums[start], 'row', ring('row', -1))  4.49 us
    ppermute x1, starting transfers between devices, on_device(): top = lax.ppermute(up, 'row', line('row', 1))  4.03 us
    ppermute x1, starting transfers between devices, send_rims(): in_l = lax.ppermute(side_r, 'col', line('col', 1))  3.96 us
    ppermute x3, starting transfers between devices, on_device(): lax.ppermute(meta, 'row', ring('row', k))  3.82 us
  transfers between devices with their start and end apart: 27, of which 17 were waited for; matrix products, arithmetic and copies ran while one was open for 0% of the time, Pallas kernels for 20%

profile of v1, /device:TPU:1, one launch (start us, length us, event | category | flops | bytes accessed | tf_op | source)
XLA Modules:
  0.0 132.9 jit_solution(9588921841921976544)
XLA Ops:
  3.5 4.0 %collective-permute-start.3 = (f32[2,64,384]{2,1,0:T(8,128)S(1)}, f32[2,64,384]{2,1,0:T(8,128)S(1)}, u32[]{:S(2)}, u32[]{:S(2)}) collective-permute-start(f32[2,64,384]{2,1,0:T(8,128)S(1)} %get-tuple-element.56), channel_id=1, source_target_pairs={{0,8},{8,16},{16,24},{1,9},{9,17},{17,25},{2,10},{10,18},{18,26},{... | collective-permute-start | bytes 589832 | tf_op jit(solution)/shard_map/ppermute | solution.py:363
  8.8 2.3 %collective-permute-done.3.top = f32[2,64,384]{2,1,0:T(8,128)S(1)} collective-permute-done((f32[2,64,384]{2,1,0:T(8,128)S(1)}, f32[2,64,384]{2,1,0:T(8,128)S(1)}, u32[]{:S(2)}, u32[]{:S(2)}) %collective-permute-start.3) | collective-permute-done | bytes 196640 | tf_op jit(solution)/shard_map/ppermute | solution.py:363
  11.1 3.8 %collective-permute-done.4.bot = f32[2,64,384]{2,1,0:T(8,128)S(1)} collective-permute-done((f32[2,64,384]{2,1,0:T(8,128)S(1)}, f32[2,64,384]{2,1,0:T(8,128)S(1)}, u32[]{:S(2)}, u32[]{:S(2)}) %collective-permute-start.4) | collective-permute-done | bytes 196640 | tf_op jit(solution)/shard_map/ppermute | solution.py:364
  15.1 3.7 %collective-permute-start.6 = (f32[512,128]{1,0:T(8,128)S(1)}, f32[512,128]{1,0:T(8,128)S(1)}, u32[]{:S(2)}, u32[]{:S(2)}) collective-permute-start(f32[512,128]{1,0:T(8,128)S(1)} %maximum_maximum_fusion.1), channel_id=1, source_target_pairs={{1,0},{2,1},{3,2},{4,3},{5,4},{6,5},{7,6},{9,8},{10,9},{11,10},{12... | collective-permute-start | bytes 786440 | tf_op jit(solution)/shard_map/ppermute | solution.py:377
  18.9 3.0 %collective-permute-start.5 = (f32[512,128]{1,0:T(8,128)S(1)}, f32[512,128]{1,0:T(8,128)S(1)}, u32[]{:S(2)}, u32[]{:S(2)}) collective-permute-start(f32[512,128]{1,0:T(8,128)S(1)} %maximum_maximum_fusion), channel_id=1, source_target_pairs={{0,1},{1,2},{2,3},{3,4},{4,5},{5,6},{6,7},{8,9},{9,10},{10,11},{11... | collective-permute-start | bytes 786440 | tf_op jit(solution)/shard_map/ppermute | solution.py:376
  26.6 2.1 %collective-permute-done = s32[1,128]{1,0:T(1,128)S(1)} collective-permute-done((s32[1,128]{1,0:T(1,128)S(1)}, s32[1,128]{1,0:T(1,128)S(1)}, u32[]{:S(2)}, u32[]{:S(2)}) %collective-permute-start) | collective-permute-done | bytes 544 | tf_op jit(solution)/shard_map/ppermute | solution.py:368
  34.0 4.2 %shard_map.76 = (f32[256,512]{1,0:T(8,128)S(1)}, f32[4,2,128,128]{3,2,1,0:T(8,128)S(1)}, f32[4,128,128]{2,1,0:T(8,128)S(1)}, f32[256,512]{1,0:T(8,128)S(1)}, f32...) custom-call(s32[4,128]{1,0:T(4,128)S(1)} %pad_add_fusion.refs_0_, ...), custom_call_target="tpu_custom_call" | custom-call | flops 2415919104 | bytes 1048576 | tf_op jit(solution)/shard_map/pallas_call | solution.py:23
  38.4 2.2 %collective-permute-start.10 = (f32[4,128,128]{2,1,0:T(8,128)S(1)}, f32[4,128,128]{2,1,0:T(8,128)S(1)}, u32[]{:S(2)}, u32[]{:S(2)}) collective-permute-start(f32[4,128,128]{2,1,0:T(8,128)S(1)} %add.25), channel_id=1, source_target_pairs={{0,24},{8,0},{16,8},{24,16},{1,25},{9,1},{17,9},{25,17},{2,26},{10... | collective-permute-start | bytes 786440 | tf_op jit(solution)/shard_map/ppermute | solution.py:437
  40.7 3.3 %collective-permute-done.7 = f32[4,128,128]{2,1,0:T(8,128)S(1)} collective-permute-done((f32[4,128,128]{2,1,0:T(8,128)S(1)}, f32[4,128,128]{2,1,0:T(8,128)S(1)}, u32[]{:S(2)}, u32[]{:S(2)}) %collective-permute-start.7) | collective-permute-done | bytes 262176 | tf_op jit(solution)/shard_map/ppermute | solution.py:437
  44.0 2.2 %collective-permute-start.8 = (f32[4,128,128]{2,1,0:T(8,128)S(1)}, f32[4,128,128]{2,1,0:T(8,128)S(1)}, u32[]{:S(2)}, u32[]{:S(2)}) collective-permute-start(f32[4,128,128]{2,1,0:T(8,128)S(1)} %add.24), channel_id=1, source_target_pairs={{0,24},{8,0},{16,8},{24,16},{1,25},{9,1},{17,9},{25,17},{2,26},{10... | collective-permute-start | bytes 786440 | tf_op jit(solution)/shard_map/ppermute | solution.py:437
  46.3 2.8 %shard_map.78.refs_3_ = f32[1,5,640,128]{3,2,1,0:T(8,128)S(1)} custom-call(s32[4,128]{1,0:T(4,128)S(1)} %pad_add_fusion.refs_0_, s32[8,4]{1,0:T(8,128)S(1)} %copy.16.refs_1_, f32[4,2,128,128]{3,2,1,0:T(8,128)S(1)} %copy-done), custom_call_target="tpu_custom_call" | custom-call | flops 402653184 | bytes 1048576 | tf_op jit(solution)/shard_map/pallas_call | solution.py:23
  49.7 2.2 %collective-permute-start.13 = (f32[4,128,128]{2,1,0:T(8,128)S(1)}, f32[4,128,128]{2,1,0:T(8,128)S(1)}, u32[]{:S(2)}, u32[]{:S(2)}) collective-permute-start(f32[4,128,128]{2,1,0:T(8,128)S(1)} %add.27), channel_id=1, source_target_pairs={{0,24},{8,0},{16,8},{24,16},{1,25},{9,1},{17,9},{25,17},{2,26},{10... | collective-permute-start | bytes 786440 | tf_op jit(solution)/shard_map/ppermute | solution.py:437
  51.9 2.9 %shard_map.79.refs_3_ = f32[1,5,640,128]{3,2,1,0:T(8,128)S(1)} custom-call(s32[4,128]{1,0:T(4,128)S(1)} %pad_add_fusion.refs_0_, s32[8,4]{1,0:T(8,128)S(1)} %copy.16.refs_1_, f32[4,2,128,128]{3,2,1,0:T(8,128)S(1)} %copy-done, f32[1,5,640,128]{3,2,1,0:T(8,128)S(1)} %shard_map.78.refs_3_), custom_call_target="tpu_custom_call", output_to_operand_aliasing={{}: (3, {})} | custom-call | flops 402653184 | bytes 1048576 | tf_op jit(solution)/shard_map/pallas_call | solution.py:23
  55.3 2.2 %collective-permute-start.11 = (f32[4,128,128]{2,1,0:T(8,128)S(1)}, f32[4,128,128]{2,1,0:T(8,128)S(1)}, u32[]{:S(2)}, u32[]{:S(2)}) collective-permute-start(f32[4,128,128]{2,1,0:T(8,128)S(1)} %add.26), channel_id=1, source_target_pairs={{0,24},{8,0},{16,8},{24,16},{1,25},{9,1},{17,9},{25,17},{2,26},{10... | collective-permute-start | bytes 786440 | tf_op jit(solution)/shard_map/ppermute | solution.py:437
  57.5 5.2 %collective-permute-start.12 = (s32[4,128]{1,0:T(4,128)S(1)}, s32[4,128]{1,0:T(4,128)S(1)}, u32[]{:S(2)}, u32[]{:S(2)}) collective-permute-start(s32[4,128]{1,0:T(4,128)S(1)} %pad_add_fusion.refs_0_), channel_id=1, source_target_pairs={{1,0},{2,1},{3,2},{4,3},{5,4},{6,5},{7,6},{9,8},{10,9},{11,10},{12... | collective-permute-start | bytes 6152 | tf_op jit(solution)/shard_map/ppermute | solution.py:412
  62.7 3.0 %collective-permute-start.14 = (s32[4,128]{1,0:T(4,128)S(1)}, s32[4,128]{1,0:T(4,128)S(1)}, u32[]{:S(2)}, u32[]{:S(2)}) collective-permute-start(s32[4,128]{1,0:T(4,128)S(1)} %pad_add_fusion.refs_0_), channel_id=1, source_target_pairs={{0,1},{1,2},{2,3},{3,4},{4,5},{5,6},{6,7},{8,9},{9,10},{10,11},{11... | collective-permute-start | bytes 6152 | tf_op jit(solution)/shard_map/ppermute | solution.py:411
  66.4 3.1 %shard_map.80.refs_3_ = f32[1,5,640,128]{3,2,1,0:T(8,128)S(1)} custom-call(s32[4,128]{1,0:T(4,128)S(1)} %collective-permute-done.14.refs_0_, s32[8,4]{1,0:T(8,128)S(1)} %copy.16.refs_1_, f32[4,2,128,128]{3,2,1,0:T(8,128)S(1)} %copy-done, f32[1,5,640,128]{3,2,1,0:T(8,128)S(1)} %shard_map.79.refs_3_), custom_call_target="tpu_custom_call", output_to_operand_aliasing={{}: (3, {})} | custom-call | flops 402653184 | bytes 1048576 | tf_op jit(solution)/shard_map/pallas_call | solution.py:23
  69.6 3.0 %shard_map.81.refs_1_ = f32[1,5,640,128]{3,2,1,0:T(8,128)S(1)} custom-call(s32[4,128]{1,0:T(4,128)S(1)} %collective-permute-done.12.refs_0_, s32[8,4]{1,0:T(8,128)S(1)} %copy.16.refs_1_, f32[4,2,128,128]{3,2,1,0:T(8,128)S(1)} %copy-done, f32[1,5,640,128]{3,2,1,0:T(8,128)S(1)} %shard_map.80.refs_3_), custom_call_target="tpu_custom_call", output_to_operand_aliasing={{}: (3, {})} | custom-call | flops 402653184 | bytes 1048576 | tf_op jit(solution)/shard_map/pallas_call | solution.py:23
  72.9 10.0 %collective-permute-done.17.refs_6_ = f32[4,128,128]{2,1,0:T(8,128)S(1)} collective-permute-done((f32[4,128,128]{2,1,0:T(8,128)S(1)}, f32[4,128,128]{2,1,0:T(8,128)S(1)}, u32[]{:S(2)}, u32[]{:S(2)}) %collective-permute-start.17) | collective-permute-done | bytes 262176 | tf_op jit(solution)/shard_map/ppermute | solution.py:456
  82.9 2.3 %shard_map.82.refs_10_ = f32[2,4,512,128]{3,2,1,0:T(8,128)S(1)} custom-call(s32[4,128]{1,0:T(4,128)S(1)} %pad_add_fusion.refs_0_, s32[8,4]{1,0:T(8,128)S(1)} %copy.16.refs_1_, f32[4,2,128,128]{3,2,1,0:T(8,128)S(1)} %copy-done, bf16[4,256,256]{2,1,0:T(8,128)(2,1)S(1)} %copy-done.1, f32[256,512]{1,0:T(8,128)S(1)} %get-tuple-element.80.refs_4_, ...), custom_call_target="tpu_custom_call" | custom-call | flops 805306368 | bytes 1048576 | tf_op jit(solution)/shard_map/pallas_call | solution.py:23
  85.2 3.3 %collective-permute-done.15.refs_9_ = f32[4,128,128]{2,1,0:T(8,128)S(1)} collective-permute-done((f32[4,128,128]{2,1,0:T(8,128)S(1)}, f32[4,128,128]{2,1,0:T(8,128)S(1)}, u32[]{:S(2)}, u32[]{:S(2)}) %collective-permute-start.15) | collective-permute-done | bytes 262176 | tf_op jit(solution)/shard_map/ppermute | solution.py:456
  88.5 5.6 %collective-permute-done.19.refs_6_ = f32[4,128,128]{2,1,0:T(8,128)S(1)} collective-permute-done((f32[4,128,128]{2,1,0:T(8,128)S(1)}, f32[4,128,128]{2,1,0:T(8,128)S(1)}, u32[]{:S(2)}, u32[]{:S(2)}) %collective-permute-start.19) | collective-permute-done | bytes 262176 | tf_op jit(solution)/shard_map/ppermute | solution.py:456
  94.1 2.2 %shard_map.83.refs_10_ = f32[2,4,512,128]{3,2,1,0:T(8,128)S(1)} custom-call(s32[4,128]{1,0:T(4,128)S(1)} %pad_add_fusion.refs_0_, s32[8,4]{1,0:T(8,128)S(1)} %copy.16.refs_1_, f32[4,2,128,128]{3,2,1,0:T(8,128)S(1)} %copy-done, bf16[4,256,256]{2,1,0:T(8,128)(2,1)S(1)} %copy-done.1, ...), custom_call_target="tpu_custom_call", output_to_operand_aliasing={{}: (10, {})} | custom-call | flops 805306368 | bytes 1048576 | tf_op jit(solution)/shard_map/pallas_call | solution.py:23
  96.4 3.4 %collective-permute-done.16.refs_9_ = f32[4,128,128]{2,1,0:T(8,128)S(1)} collective-permute-done((f32[4,128,128]{2,1,0:T(8,128)S(1)}, f32[4,128,128]{2,1,0:T(8,128)S(1)}, u32[]{:S(2)}, u32[]{:S(2)}) %collective-permute-start.16) | collective-permute-done | bytes 262176 | tf_op jit(solution)/shard_map/ppermute | solution.py:456
  99.7 2.2 %shard_map.84.refs_7_ = f32[2,4,512,128]{3,2,1,0:T(8,128)S(1)} custom-call(s32[4,128]{1,0:T(4,128)S(1)} %pad_add_fusion.refs_0_, s32[8,4]{1,0:T(8,128)S(1)} %copy.16.refs_1_, f32[4,2,128,128]{3,2,1,0:T(8,128)S(1)} %copy-done, bf16[4,256,256]{2,1,0:T(8,128)(2,1)S(1)} %copy-done.1, ...), custom_call_target="tpu_custom_call", output_to_operand_aliasing={{}: (10, {})} | custom-call | flops 805306368 | bytes 1048576 | tf_op jit(solution)/shard_map/pallas_call | solution.py:23
  102.0 3.4 %collective-permute-done.20.refs_6_ = f32[4,128,128]{2,1,0:T(8,128)S(1)} collective-permute-done((f32[4,128,128]{2,1,0:T(8,128)S(1)}, f32[4,128,128]{2,1,0:T(8,128)S(1)}, u32[]{:S(2)}, u32[]{:S(2)}) %collective-permute-start.20) | collective-permute-done | bytes 262176 | tf_op jit(solution)/shard_map/ppermute | solution.py:456
  107.0 4.0 %collective-permute-done.18.refs_6_ = f32[4,128,128]{2,1,0:T(8,128)S(1)} collective-permute-done((f32[4,128,128]{2,1,0:T(8,128)S(1)}, f32[4,128,128]{2,1,0:T(8,128)S(1)}, u32[]{:S(2)}, u32[]{:S(2)}) %collective-permute-start.18) | collective-permute-done | bytes 262176 | tf_op jit(solution)/shard_map/ppermute | solution.py:456
  111.0 2.0 %shard_map.86 = (f32[2,4,512,128]{3,2,1,0:T(8,128)S(1)}, f32[512,128]{1,0:T(8,128)S(1)}, f32[512,128]{1,0:T(8,128)S(1)}, f32[2,64,384]{2,1,0:T(8,128)S(1)}, f32[2,64,384]{2,1,0:T(8,128)S(1)}) custom-call(s32[4,128]{1,0:T(4,128)S(1)} %pad_add_fusion.refs_0_, s32[8,4]{1,0:T(8,128)S(1)} %copy.16.refs_1_, ...), custom_call_target="tpu_custom_call", output_to_operand_aliasing={{0}: (7, {})} | custom-call | flops 402653184 | bytes 1048576 | tf_op jit(solution)/shard_map/pallas_call | solution.py:23
  112.9 4.0 %collective-permute-start.21 = (f32[512,128]{1,0:T(8,128)S(1)}, f32[512,128]{1,0:T(8,128)S(1)}, u32[]{:S(2)}, u32[]{:S(2)}) collective-permute-start(f32[512,128]{1,0:T(8,128)S(1)} %get-tuple-element.101), channel_id=1, source_target_pairs={{0,1},{1,2},{2,3},{3,4},{4,5},{5,6},{6,7},{8,9},{9,10},{10,11},{11... | collective-permute-start | bytes 786440 | tf_op jit(solution)/shard_map/ppermute | solution.py:334
  116.9 1.9 %collective-permute-start.22 = (f32[512,128]{1,0:T(8,128)S(1)}, f32[512,128]{1,0:T(8,128)S(1)}, u32[]{:S(2)}, u32[]{:S(2)}) collective-permute-start(f32[512,128]{1,0:T(8,128)S(1)} %get-tuple-element.102), channel_id=1, source_target_pairs={{1,0},{2,1},{3,2},{4,3},{5,4},{6,5},{7,6},{9,8},{10,9},{11,10},{12... | collective-permute-start | bytes 786440 | tf_op jit(solution)/shard_map/ppermute | solution.py:333
  121.5 3.4 %collective-permute-done.22.refs_4_ = f32[512,128]{1,0:T(8,128)S(1)} collective-permute-done((f32[512,128]{1,0:T(8,128)S(1)}, f32[512,128]{1,0:T(8,128)S(1)}, u32[]{:S(2)}, u32[]{:S(2)}) %collective-permute-start.22) | collective-permute-done | bytes 262176 | tf_op jit(solution)/shard_map/ppermute | solution.py:333
  127.6 3.7 %collective-permute-done.26.refs_8_ = f32[2,64,128]{2,1,0:T(8,128)S(1)} collective-permute-done((f32[2,64,128]{2,1,0:T(8,128)S(1)}, f32[2,64,128]{2,1,0:T(8,128)S(1)}, u32[]{:S(2)}, u32[]{:S(2)}) %collective-permute-start.26) | collective-permute-done | bytes 65568 | tf_op jit(solution)/shard_map/ppermute | solution.py:339
  (65 shorter events, 25.0 us)
Async XLA Ops:
  0.0 25.7 %copy-start.5 = (s32[8,4]{0,1:T(4,128)S(1)}, s32[8,4]{0,1:T(4,128)}, u32[]{:S(2)}) copy-start(s32[8,4]{0,1:T(4,128)} %param.11) | copy-start | bytes 388
  1.4 1.3 copy-start.2
  2.7 26.0 %copy-start.3 = (f32[2,384,384]{2,1,0:T(8,128)S(1)}, f32[2,384,384]{2,1,0:T(8,128)}, u32[]{:S(2)}) copy-start(f32[2,384,384]{2,1,0:T(8,128)} %refs_0_.1) | copy-start | bytes 3538948
  3.5 7.6 %collective-permute-start.3 = (f32[2,64,384]{2,1,0:T(8,128)S(1)}, f32[2,64,384]{2,1,0:T(8,128)S(1)}, u32[]{:S(2)}, u32[]{:S(2)}) collective-permute-start(f32[2,64,384]{2,1,0:T(8,128)S(1)} %get-tuple-element.56), channel_id=1, source_target_pairs={{0,8},{8,16},{16,24},{1,9},{9,17},{17,25},{2,10},{10,18},{18,26},{... | collective-permute-start | bytes 589832 | tf_op jit(solution)/shard_map/ppermute | solution.py:363
  7.5 7.4 %collective-permute-start.4 = (f32[2,64,384]{2,1,0:T(8,128)S(1)}, f32[2,64,384]{2,1,0:T(8,128)S(1)}, u32[]{:S(2)}, u32[]{:S(2)}) collective-permute-start(f32[2,64,384]{2,1,0:T(8,128)S(1)} %get-tuple-element.57), channel_id=1, source_target_pairs={{8,0},{16,8},{24,16},{9,1},{17,9},{25,17},{10,2},{18,10},{26,18},{... | collective-permute-start | bytes 589832 | tf_op jit(solution)/shard_map/ppermute | solution.py:364
  15.1 13.6 %collective-permute-start.6 = (f32[512,128]{1,0:T(8,128)S(1)}, f32[512,128]{1,0:T(8,128)S(1)}, u32[]{:S(2)}, u32[]{:S(2)}) collective-permute-start(f32[512,128]{1,0:T(8,128)S(1)} %maximum_maximum_fusion.1), channel_id=1, source_target_pairs={{1,0},{2,1},{3,2},{4,3},{5,4},{6,5},{7,6},{9,8},{10,9},{11,10},{12... | collective-permute-start | bytes 786440 | tf_op jit(solution)/shard_map/ppermute | solution.py:377
  18.9 9.8 %collective-permute-start.5 = (f32[512,128]{1,0:T(8,128)S(1)}, f32[512,128]{1,0:T(8,128)S(1)}, u32[]{:S(2)}, u32[]{:S(2)}) collective-permute-start(f32[512,128]{1,0:T(8,128)S(1)} %maximum_maximum_fusion), channel_id=1, source_target_pairs={{0,1},{1,2},{2,3},{3,4},{4,5},{5,6},{6,7},{8,9},{9,10},{10,11},{11... | collective-permute-start | bytes 786440 | tf_op jit(solution)/shard_map/ppermute | solution.py:376
  21.9 3.9 %collective-permute-start.2 = (s32[1,128]{1,0:T(1,128)S(1)}, s32[1,128]{1,0:T(1,128)S(1)}, u32[]{:S(2)}, u32[]{:S(2)}) collective-permute-start(s32[1,128]{1,0:T(1,128)S(1)} %get-tuple-element.55), channel_id=1, source_target_pairs={{0,24},{8,0},{16,8},{24,16},{1,25},{9,1},{17,9},{25,17},{2,26},{10... | collective-permute-start | bytes 1544 | tf_op jit(solution)/shard_map/ppermute | solution.py:368
  23.3 3.3 %collective-permute-start.1 = (s32[1,128]{1,0:T(1,128)S(1)}, s32[1,128]{1,0:T(1,128)S(1)}, u32[]{:S(2)}, u32[]{:S(2)}) collective-permute-start(s32[1,128]{1,0:T(1,128)S(1)} %get-tuple-element.55), channel_id=1, source_target_pairs={{0,16},{8,24},{16,0},{24,8},{1,17},{9,25},{17,1},{25,9},{2,18},{10... | collective-permute-start | bytes 1544 | tf_op jit(solution)/shard_map/ppermute | solution.py:368
  24.4 4.2 %collective-permute-start = (s32[1,128]{1,0:T(1,128)S(1)}, s32[1,128]{1,0:T(1,128)S(1)}, u32[]{:S(2)}, u32[]{:S(2)}) collective-permute-start(s32[1,128]{1,0:T(1,128)S(1)} %get-tuple-element.55), channel_id=1, source_target_pairs={{0,8},{8,16},{16,24},{24,0},{1,9},{9,17},{17,25},{25,1},{2,10},{10... | collective-permute-start | bytes 1544 | tf_op jit(solution)/shard_map/ppermute | solution.py:368
  28.7 1.2 copy-start.1
  31.6 6.8 %collective-permute-start.9 = (f32[4,128,128]{2,1,0:T(8,128)S(1)}, f32[4,128,128]{2,1,0:T(8,128)S(1)}, u32[]{:S(2)}, u32[]{:S(2)}) collective-permute-start(f32[4,128,128]{2,1,0:T(8,128)S(1)} %get-tuple-element.63), channel_id=1, source_target_pairs={{0,24},{8,0},{16,8},{24,16},{1,25},{9,1},{17,9},{25,17},{2,26},{10... | collective-permute-start | bytes 786440 | tf_op jit(solution)/shard_map/ppermute | solution.py:437
  33.5 10.5 %collective-permute-start.7 = (f32[4,128,128]{2,1,0:T(8,128)S(1)}, f32[4,128,128]{2,1,0:T(8,128)S(1)}, u32[]{:S(2)}, u32[]{:S(2)}) collective-permute-start(f32[4,128,128]{2,1,0:T(8,128)S(1)} %get-tuple-element.60), channel_id=1, source_target_pairs={{0,24},{8,0},{16,8},{24,16},{1,25},{9,1},{17,9},{25,17},{2,26},{10... | collective-permute-start | bytes 786440 | tf_op jit(solution)/shard_map/ppermute | solution.py:437
  38.4 11.2 %collective-permute-start.10 = (f32[4,128,128]{2,1,0:T(8,128)S(1)}, f32[4,128,128]{2,1,0:T(8,128)S(1)}, u32[]{:S(2)}, u32[]{:S(2)}) collective-permute-start(f32[4,128,128]{2,1,0:T(8,128)S(1)} %add.25), channel_id=1, source_target_pairs={{0,24},{8,0},{16,8},{24,16},{1,25},{9,1},{17,9},{25,17},{2,26},{10... | collective-permute-start | bytes 786440 | tf_op jit(solution)/shard_map/ppermute | solution.py:437
  44.0 11.2 %collective-permute-start.8 = (f32[4,128,128]{2,1,0:T(8,128)S(1)}, f32[4,128,128]{2,1,0:T(8,128)S(1)}, u32[]{:S(2)}, u32[]{:S(2)}) collective-permute-start(f32[4,128,128]{2,1,0:T(8,128)S(1)} %add.24), channel_id=1, source_target_pairs={{0,24},{8,0},{16,8},{24,16},{1,25},{9,1},{17,9},{25,17},{2,26},{10... | collective-permute-start | bytes 786440 | tf_op jit(solution)/shard_map/ppermute | solution.py:437
  49.7 19.9 %collective-permute-start.13 = (f32[4,128,128]{2,1,0:T(8,128)S(1)}, f32[4,128,128]{2,1,0:T(8,128)S(1)}, u32[]{:S(2)}, u32[]{:S(2)}) collective-permute-start(f32[4,128,128]{2,1,0:T(8,128)S(1)} %add.27), channel_id=1, source_target_pairs={{0,24},{8,0},{16,8},{24,16},{1,25},{9,1},{17,9},{25,17},{2,26},{10... | collective-permute-start | bytes 786440 | tf_op jit(solution)/shard_map/ppermute | solution.py:437
  55.3 17.4 %collective-permute-start.11 = (f32[4,128,128]{2,1,0:T(8,128)S(1)}, f32[4,128,128]{2,1,0:T(8,128)S(1)}, u32[]{:S(2)}, u32[]{:S(2)}) collective-permute-start(f32[4,128,128]{2,1,0:T(8,128)S(1)} %add.26), channel_id=1, source_target_pairs={{0,24},{8,0},{16,8},{24,16},{1,25},{9,1},{17,9},{25,17},{2,26},{10... | collective-permute-start | bytes 786440 | tf_op jit(solution)/shard_map/ppermute | solution.py:437
  57.5 8.2 %collective-permute-start.12 = (s32[4,128]{1,0:T(4,128)S(1)}, s32[4,128]{1,0:T(4,128)S(1)}, u32[]{:S(2)}, u32[]{:S(2)}) collective-permute-start(s32[4,128]{1,0:T(4,128)S(1)} %pad_add_fusion.refs_0_), channel_id=1, source_target_pairs={{1,0},{2,1},{3,2},{4,3},{5,4},{6,5},{7,6},{9,8},{10,9},{11,10},{12... | collective-permute-start | bytes 6152 | tf_op jit(solution)/shard_map/ppermute | solution.py:412
  62.7 3.7 %collective-permute-start.14 = (s32[4,128]{1,0:T(4,128)S(1)}, s32[4,128]{1,0:T(4,128)S(1)}, u32[]{:S(2)}, u32[]{:S(2)}) collective-permute-start(s32[4,128]{1,0:T(4,128)S(1)} %pad_add_fusion.refs_0_), channel_id=1, source_target_pairs={{0,1},{1,2},{2,3},{3,4},{4,5},{5,6},{6,7},{8,9},{9,10},{10,11},{11... | collective-permute-start | bytes 6152 | tf_op jit(solution)/shard_map/ppermute | solution.py:411
  69.6 3.1 %copy-start.4 = (f32[1,1,8,128,128]{4,3,2,1,0:T(8,128)S(1)}, f32[1,1,8,128,128]{4,3,2,1,0:T(8,128)}, u32[]{:S(2)}) copy-start(f32[1,1,8,128,128]{4,3,2,1,0:T(8,128)} %param.12) | copy-start | bytes 1572868
  72.8 10.1 %collective-permute-start.17 = (f32[4,128,128]{2,1,0:T(8,128)S(1)}, f32[4,128,128]{2,1,0:T(8,128)S(1)}, u32[]{:S(2)}, u32[]{:S(2)}) collective-permute-start(f32[4,128,128]{2,1,0:T(8,128)S(1)} %get-tuple-element.105.refs_6_), channel_id=1, source_target_pairs={{0,8},{8,16},{16,24},{24,0},{1,9},{9,17},{17,25},{25,1},{2,10},{10... | collective-permute-start | bytes 786440 | tf_op jit(solution)/shard_map/ppermute | solution.py:456
  72.8 15.7 %collective-permute-start.15 = (f32[4,128,128]{2,1,0:T(8,128)S(1)}, f32[4,128,128]{2,1,0:T(8,128)S(1)}, u32[]{:S(2)}, u32[]{:S(2)}) collective-permute-start(f32[4,128,128]{2,1,0:T(8,128)S(1)} %get-tuple-element.106.refs_9_), channel_id=1, source_target_pairs={{0,8},{8,16},{16,24},{24,0},{1,9},{9,17},{17,25},{25,1},{2,10},{10... | collective-permute-start | bytes 786440 | tf_op jit(solution)/shard_map/ppermute | solution.py:456
  82.9 11.2 %collective-permute-start.19 = (f32[4,128,128]{2,1,0:T(8,128)S(1)}, f32[4,128,128]{2,1,0:T(8,128)S(1)}, u32[]{:S(2)}, u32[]{:S(2)}) collective-permute-start(f32[4,128,128]{2,1,0:T(8,128)S(1)} %collective-permute-done.17.refs_6_), channel_id=1, source_target_pairs={{0,8},{8,16},{16,24},{24,0},{1,9},{9,17},{17,25},{25,1},{2,10},{10... | collective-permute-start | bytes 786440 | tf_op jit(solution)/shard_map/ppermute | solution.py:456
  88.5 11.2 %collective-permute-start.16 = (f32[4,128,128]{2,1,0:T(8,128)S(1)}, f32[4,128,128]{2,1,0:T(8,128)S(1)}, u32[]{:S(2)}, u32[]{:S(2)}) collective-permute-start(f32[4,128,128]{2,1,0:T(8,128)S(1)} %collective-permute-done.15.refs_9_), channel_id=1, source_target_pairs={{0,8},{8,16},{16,24},{24,0},{1,9},{9,17},{17,25},{25,1},{2,10},{10... | collective-permute-start | bytes 786440 | tf_op jit(solution)/shard_map/ppermute | solution.py:456
  94.1 11.2 %collective-permute-start.20 = (f32[4,128,128]{2,1,0:T(8,128)S(1)}, f32[4,128,128]{2,1,0:T(8,128)S(1)}, u32[]{:S(2)}, u32[]{:S(2)}) collective-permute-start(f32[4,128,128]{2,1,0:T(8,128)S(1)} %collective-permute-done.19.refs_6_), channel_id=1, source_target_pairs={{0,8},{8,16},{16,24},{24,0},{1,9},{9,17},{17,25},{25,1},{2,10},{10... | collective-permute-start | bytes 786440 | tf_op jit(solution)/shard_map/ppermute | solution.py:456
  99.7 11.2 %collective-permute-start.18 = (f32[4,128,128]{2,1,0:T(8,128)S(1)}, f32[4,128,128]{2,1,0:T(8,128)S(1)}, u32[]{:S(2)}, u32[]{:S(2)}) collective-permute-start(f32[4,128,128]{2,1,0:T(8,128)S(1)} %collective-permute-done.16.refs_9_), channel_id=1, source_target_pairs={{0,8},{8,16},{16,24},{24,0},{1,9},{9,17},{17,25},{25,1},{2,10},{10... | collective-permute-start | bytes 786440 | tf_op jit(solution)/shard_map/ppermute | solution.py:456
  112.9 8.5 %collective-permute-start.21 = (f32[512,128]{1,0:T(8,128)S(1)}, f32[512,128]{1,0:T(8,128)S(1)}, u32[]{:S(2)}, u32[]{:S(2)}) collective-permute-start(f32[512,128]{1,0:T(8,128)S(1)} %get-tuple-element.101), channel_id=1, source_target_pairs={{0,1},{1,2},{2,3},{3,4},{4,5},{5,6},{6,7},{8,9},{9,10},{10,11},{11... | collective-permute-start | bytes 786440 | tf_op jit(solution)/shard_map/ppermute | solution.py:334
  116.9 8.0 %collective-permute-start.22 = (f32[512,128]{1,0:T(8,128)S(1)}, f32[512,128]{1,0:T(8,128)S(1)}, u32[]{:S(2)}, u32[]{:S(2)}) collective-permute-start(f32[512,128]{1,0:T(8,128)S(1)} %get-tuple-element.102), channel_id=1, source_target_pairs={{1,0},{2,1},{3,2},{4,3},{5,4},{6,5},{7,6},{9,8},{10,9},{11,10},{12... | collective-permute-start | bytes 786440 | tf_op jit(solution)/shard_map/ppermute | solution.py:333
  118.8 8.7 %collective-permute-start.23 = (f32[2,64,384]{2,1,0:T(8,128)S(1)}, f32[2,64,384]{2,1,0:T(8,128)S(1)}, u32[]{:S(2)}, u32[]{:S(2)}) collective-permute-start(f32[2,64,384]{2,1,0:T(8,128)S(1)} %get-tuple-element.103), channel_id=1, source_target_pairs={{0,8},{8,16},{16,24},{1,9},{9,17},{17,25},{2,10},{10,18},{18,26},{... | collective-permute-start | bytes 589832 | tf_op jit(solution)/shard_map/ppermute | solution.py:336
  120.1 7.4 %collective-permute-start.24 = (f32[2,64,384]{2,1,0:T(8,128)S(1)}, f32[2,64,384]{2,1,0:T(8,128)S(1)}, u32[]{:S(2)}, u32[]{:S(2)}) collective-permute-start(f32[2,64,384]{2,1,0:T(8,128)S(1)} %get-tuple-element.104), channel_id=1, source_target_pairs={{8,0},{16,8},{24,16},{9,1},{17,9},{25,17},{10,2},{18,10},{26,18},{... | collective-permute-start | bytes 589832 | tf_op jit(solution)/shard_map/ppermute | solution.py:335
  124.9 2.6 %collective-permute-start.25 = (f32[2,64,128]{2,1,0:T(8,128)S(1)}, f32[2,64,128]{2,1,0:T(8,128)S(1)}, u32[]{:S(2)}, u32[]{:S(2)}) collective-permute-start(f32[2,64,128]{2,1,0:T(8,128)S(1)} %pad_maximum_fusion), channel_id=1, source_target_pairs={{0,8},{8,16},{16,24},{1,9},{9,17},{17,25},{2,10},{10,18},{18,26},{... | collective-permute-start | bytes 196616 | tf_op jit(solution)/shard_map/ppermute | solution.py:340
  126.2 5.0 %collective-permute-start.26 = (f32[2,64,128]{2,1,0:T(8,128)S(1)}, f32[2,64,128]{2,1,0:T(8,128)S(1)}, u32[]{:S(2)}, u32[]{:S(2)}) collective-permute-start(f32[2,64,128]{2,1,0:T(8,128)S(1)} %pad_maximum_fusion.1), channel_id=1, source_target_pairs={{8,0},{16,8},{24,16},{9,1},{17,9},{25,17},{10,2},{18,10},{26,18},{... | collective-permute-start | bytes 196616 | tf_op jit(solution)/shard_map/ppermute | solution.py:339
  (1 other events, 1.0 us)

commit v2 on v1

--- a/solution.py
+++ b/solution.py
@@ -74,7 +74,7 @@
     return y, x // size, x % size
 
 
-def edge_kernel(obj, positions, counts, place_of, up, down, edge_l, edge_r, meta):
+def edge_kernel(obj, positions, counts, place_of, edge_l, edge_r, meta):
     scans = positions.shape[2]
     values = [positions[0, 0, slot, axis] for slot in range(scans) for axis in range(2)]
     values += [counts[0, 0], place_of[0]]
@@ -84,11 +84,8 @@
         row = jnp.where(lane == at, value, row)
     meta[...] = row
     _, rows, columns = obj.shape
-    half, size = up.shape[1], edge_l.shape[1]
-    low = lanes(rows, size) < half
-    for ch in range(2):
-        down[ch] = obj[ch, :half, :]
-        up[ch] = obj[ch, rows - half :, :]
+    size = edge_l.shape[1]
+    low = lanes(rows, size) < size // 2
     near, far = slice(0, size), slice(columns - size, columns)
     edge_l[...] = jnp.where(low, obj[0, :, near], turn(obj[1, :, near]))
     edge_r[...] = jnp.where(low, turn(obj[0, :, far]), obj[1, :, far])
@@ -353,15 +350,15 @@
     def packed(x):
         return jnp.concatenate([x[0], x[1]], axis=1)
 
-    up, down, edge_l, edge_r, meta = call(
+    edge_l, edge_r, meta = call(
         edge_kernel,
-        [(2, half, tile_columns)] * 2 + [(tile_rows, size)] * 2 + [jax.ShapeDtypeStruct((1, size), jnp.int32)],
+        [(tile_rows, size)] * 2 + [jax.ShapeDtypeStruct((1, size), jnp.int32)],
         [VMEM, SMEM, SMEM, SMEM],
         (obj, positions, counts, lax.axis_index("row").astype(jnp.int32).reshape(1)),
         10**6,
     )
-    top = lax.ppermute(up, "row", line("row", 1))
-    bot = lax.ppermute(down, "row", line("row", -1))
+    top = lax.ppermute(obj[:, tile_rows - half :], "row", line("row", 1))
+    bot = lax.ppermute(obj[:, :half], "row", line("row", -1))
 
     kept = min(row_count, offsets_count + 2)
     shifts = [k if k <= offsets_count else k - kept for k in range(kept)]
@@ -369,8 +366,9 @@
     metas = jnp.concatenate(metas)
     most = offsets_count - 1
 
+    extra = metas.astype(F32)
     edge_l, edge_r = (
-        jnp.concatenate([packed(top[:, :, part]), edge, packed(bot[:, :, part])])
+        jnp.concatenate([packed(top[:, :, part]), edge, packed(bot[:, :, part]), extra])
         for part, edge in ((slice(0, half), edge_l), (slice(tile_columns - half, None), edge_r))
     )
     left = lax.ppermute(edge_r, "col", line("col", 1))
@@ -408,8 +406,8 @@
 
     spans = {
         0: metas,
-        -1: lax.ppermute(metas, "col", line("col", 1)),
-        1: lax.ppermute(metas, "col", line("col", -1)),
+        -1: left[rows : rows + kept].astype(jnp.int32),
+        1: right[rows : rows + kept].astype(jnp.int32),
     }
     everything = [(which, down) for down in (-1, 0, 1) for which in range(offsets_count)]
     pieces = [(0, everything[::2]), (0, everything[1::2]), (-1, everything), (1, everything)]

time: 134 us -> 133 us (level)
    ppermute x4 -> x2, starting transfers between devices: 13.5 us -> 5.4 us  [the longest x1 4.11 us: on_device(): top = lax.ppermute(obj[:, tile_rows - half:], 'row', line('row', 1))]
    ppermute x6, waiting for transfers between devices: 4.49 us -> 8.85 us  [on_device(): arrived = lax.ppermute(sums[start], 'row', ring('row', -1))]
    ppermute x4 -> x2, waiting for transfers between devices: 6.72 us -> 2.45 us  [the longest x1 2.44 us: on_device(): top = lax.ppermute(obj[:, tile_rows - half:], 'row', line('row', 1))]
    ppermute x6, starting transfers between devices: 9.64 us -> 13.9 us  [on_device(): arrived = lax.ppermute(sums[start], 'row', ring('row', -1))]
    ppermute x3, waiting for transfers between devices: 2.84 us -> 0.01 us  [on_device(): lax.ppermute(meta, 'row', ring('row', k))]
    ppermute x1, waiting for transfers between devices: 0.01 us -> 2.08 us  [on_device(): right = lax.ppermute(edge_l, 'col', line('col', -1))]
    ppermute x3, starting transfers between devices: 3.82 us -> 5.43 us  [on_device(): lax.ppermute(meta, 'row', ring('row', k))]
  transfers between devices with their start and end apart: 27 -> 25, of which waited for: 17 -> 13; matrix products, arithmetic and copies ran while one was open for 0% -> 1% of each run, Pallas kernels for 20% -> 20%
where the time goes in v2:
time: 133 us; the launch traced here: 132 us
  waiting for transfers between devices  51 us (38%)
  starting transfers between devices  43.6 us (33%)
  Pallas kernels  32.9 us (25%)
  local copies, waits for them, and re-layouts  3.35 us (3%)
    pallas_call x15, Pallas kernels, call(): pl.pallas_call(kernel, out_shape=[s if hasattr(s, 'dtype') else jax.Shape...  32.9 us
    ppermute x6, waiting for transfers between devices, on_device(): value = lax.ppermute(factors[start], 'row', ring('row', 1))  29.3 us
    ppermute x6, starting transfers between devices, on_device(): arrived = lax.ppermute(sums[start], 'row', ring('row', -1))  13.9 us
    ppermute x6, waiting for transfers between devices, on_device(): arrived = lax.ppermute(sums[start], 'row', ring('row', -1))  8.85 us
    ppermute x3, starting transfers between devices, on_device(): lax.ppermute(meta, 'row', ring('row', k))  5.43 us
    ppermute x1, starting transfers between devices, on_device(): right = lax.ppermute(edge_l, 'col', line('col', -1))  4.56 us
    ppermute x1, starting transfers between devices, on_device(): top = lax.ppermute(obj[:, tile_rows - half:], 'row', line('row', 1))  4.11 us
    ppermute x1, waiting for transfers between devices, send_rims(): in_cbot = lax.ppermute(corner_top, 'row', line('row', -1))  3.68 us
  transfers between devices with their start and end apart: 25, of which 13 were waited for; matrix products, arithmetic and copies ran while one was open for 1% of the time, Pallas kernels for 20%

profile of v2, /device:TPU:1, one launch (start us, length us, event | category | flops | bytes accessed | tf_op | source)
XLA Modules:
  0.0 132.3 jit_solution(11917212442027813223)
XLA Ops:
  5.8 5.0 %collective-permute-start.2 = (s32[1,128]{1,0:T(1,128)S(1)}, s32[1,128]{1,0:T(1,128)S(1)}, u32[]{:S(2)}, u32[]{:S(2)}) collective-permute-start(s32[1,128]{1,0:T(1,128)S(1)} %get-tuple-element.53), channel_id=1, source_target_pairs={{0,24},{8,0},{16,8},{24,16},{1,25},{9,1},{17,9},{25,17},{2,26},{10... | collective-permute-start | bytes 1544 | tf_op jit(solution)/shard_map/ppermute | solution.py:365
  11.2 4.1 %collective-permute-start.3 = (f32[2,64,384]{2,1,0:T(8,128)S(1)}, f32[2,64,384]{2,1,0:T(8,128)S(1)}, u32[]{:S(2)}, u32[]{:S(2)}) collective-permute-start(f32[2,64,384]{2,1,0:T(8,128)S(1)} %get-tuple-element.102), channel_id=1, source_target_pairs={{0,8},{8,16},{16,24},{1,9},{9,17},{17,25},{2,10},{10,18},{18,26},{... | collective-permute-start | bytes 589832 | tf_op jit(solution)/shard_map/ppermute | solution.py:360
  15.5 2.4 %collective-permute-done.3.top = f32[2,64,384]{2,1,0:T(8,128)S(1)} collective-permute-done((f32[2,64,384]{2,1,0:T(8,128)S(1)}, f32[2,64,384]{2,1,0:T(8,128)S(1)}, u32[]{:S(2)}, u32[]{:S(2)}) %collective-permute-start.3) | collective-permute-done | bytes 196640 | tf_op jit(solution)/shard_map/ppermute | solution.py:360
  18.1 4.6 %collective-permute-start.6 = (f32[516,128]{1,0:T(8,128)S(1)}, f32[516,128]{1,0:T(8,128)S(1)}, u32[]{:S(2)}, u32[]{:S(2)}) collective-permute-start(f32[516,128]{1,0:T(8,128)S(1)} %get-tuple-element.117), channel_id=1, source_target_pairs={{1,0},{2,1},{3,2},{4,3},{5,4},{6,5},{7,6},{9,8},{10,9},{11,10},{12... | collective-permute-start | bytes 792584 | tf_op jit(solution)/shard_map/ppermute | solution.py:375
  22.7 3.0 %collective-permute-start.5 = (f32[516,128]{1,0:T(8,128)S(1)}, f32[516,128]{1,0:T(8,128)S(1)}, u32[]{:S(2)}, u32[]{:S(2)}) collective-permute-start(f32[516,128]{1,0:T(8,128)S(1)} %get-tuple-element.118), channel_id=1, source_target_pairs={{0,1},{1,2},{2,3},{3,4},{4,5},{5,6},{6,7},{8,9},{9,10},{10,11},{11... | collective-permute-start | bytes 792584 | tf_op jit(solution)/shard_map/ppermute | solution.py:374
  25.8 2.1 %collective-permute-done.6.right = f32[516,128]{1,0:T(8,128)S(1)} collective-permute-done((f32[516,128]{1,0:T(8,128)S(1)}, f32[516,128]{1,0:T(8,128)S(1)}, u32[]{:S(2)}, u32[]{:S(2)}) %collective-permute-start.6) | collective-permute-done | bytes 264224 | tf_op jit(solution)/shard_map/ppermute | solution.py:375
  29.7 1.7 %shard_map.77 = (f32[256,512]{1,0:T(8,128)S(1)}, f32[4,2,128,128]{3,2,1,0:T(8,128)S(1)}, f32[4,128,128]{2,1,0:T(8,128)S(1)}) custom-call(s32[4,128]{1,0:T(4,128)S(1)} %get-tuple-element.61.refs_0_, s32[8,4]{1,0:T(8,128)S(1)} %copy.16.refs_1_, f32[2,4,512,128]{3,2,1,0:T(8,128)S(1)} %shard_map.74.refs_2_, f32[4,2,128,128]{3,2,1,0:T(8,128)S(1)} %copy-done, ...), custom_call_target="tpu_custom_call" | custom-call | flops 402653184 | bytes 1048576 | tf_op jit(solution)/shard_map/pallas_call | solution.py:23
  31.4 2.7 %collective-permute-start.9 = (f32[4,128,128]{2,1,0:T(8,128)S(1)}, f32[4,128,128]{2,1,0:T(8,128)S(1)}, u32[]{:S(2)}, u32[]{:S(2)}) collective-permute-start(f32[4,128,128]{2,1,0:T(8,128)S(1)} %get-tuple-element.59), channel_id=1, source_target_pairs={{0,24},{8,0},{16,8},{24,16},{1,25},{9,1},{17,9},{25,17},{2,26},{10... | collective-permute-start | bytes 786440 | tf_op jit(solution)/shard_map/ppermute | solution.py:435
  34.2 1.7 %shard_map.75 = (f32[256,512]{1,0:T(8,128)S(1)}, f32[4,2,128,128]{3,2,1,0:T(8,128)S(1)}, f32[4,128,128]{2,1,0:T(8,128)S(1)}) custom-call(s32[4,128]{1,0:T(4,128)S(1)} %get-tuple-element.61.refs_0_, s32[8,4]{1,0:T(8,128)S(1)} %copy.16.refs_1_, f32[2,4,512,128]{3,2,1,0:T(8,128)S(1)} %shard_map.74.refs_2_, f32[4,2,128,128]{3,2,1,0:T(8,128)S(1)} %copy-done, ...), custom_call_target="tpu_custom_call" | custom-call | flops 402653184 | bytes 1048576 | tf_op jit(solution)/shard_map/pallas_call | solution.py:23
  36.2 4.2 %shard_map.76 = (f32[256,512]{1,0:T(8,128)S(1)}, f32[4,2,128,128]{3,2,1,0:T(8,128)S(1)}, f32[4,128,128]{2,1,0:T(8,128)S(1)}, f32[256,512]{1,0:T(8,128)S(1)}, f32...) custom-call(s32[4,128]{1,0:T(4,128)S(1)} %get-tuple-element.61.refs_, ...), custom_call_target="tpu_custom_call" | custom-call | flops 2415919104 | bytes 1048576 | tf_op jit(solution)/shard_map/pallas_call | solution.py:23
  40.4 3.9 %collective-permute-start.10 = (f32[4,128,128]{2,1,0:T(8,128)S(1)}, f32[4,128,128]{2,1,0:T(8,128)S(1)}, u32[]{:S(2)}, u32[]{:S(2)}) collective-permute-start(f32[4,128,128]{2,1,0:T(8,128)S(1)} %add.25), channel_id=1, source_target_pairs={{0,24},{8,0},{16,8},{24,16},{1,25},{9,1},{17,9},{25,17},{2,26},{10... | collective-permute-start | bytes 786440 | tf_op jit(solution)/shard_map/ppermute | solution.py:435
  45.9 4.1 %collective-permute-start.8 = (f32[4,128,128]{2,1,0:T(8,128)S(1)}, f32[4,128,128]{2,1,0:T(8,128)S(1)}, u32[]{:S(2)}, u32[]{:S(2)}) collective-permute-start(f32[4,128,128]{2,1,0:T(8,128)S(1)} %add.24), channel_id=1, source_target_pairs={{0,24},{8,0},{16,8},{24,16},{1,25},{9,1},{17,9},{25,17},{2,26},{10... | collective-permute-start | bytes 786440 | tf_op jit(solution)/shard_map/ppermute | solution.py:435
  50.0 2.8 %shard_map.78.refs_3_ = f32[1,5,640,128]{3,2,1,0:T(8,128)S(1)} custom-call(s32[4,128]{1,0:T(4,128)S(1)} %get-tuple-element.61.refs_0_, s32[8,4]{1,0:T(8,128)S(1)} %copy.16.refs_1_, f32[4,2,128,128]{3,2,1,0:T(8,128)S(1)} %copy-done), custom_call_target="tpu_custom_call" | custom-call | flops 402653184 | bytes 1048576 | tf_op jit(solution)/shard_map/pallas_call | solution.py:23
  52.8 2.9 %shard_map.79.refs_3_ = f32[1,5,640,128]{3,2,1,0:T(8,128)S(1)} custom-call(s32[4,128]{1,0:T(4,128)S(1)} %get-tuple-element.61.refs_0_, s32[8,4]{1,0:T(8,128)S(1)} %copy.16.refs_1_, f32[4,2,128,128]{3,2,1,0:T(8,128)S(1)} %copy-done, f32[1,5,640,128]{3,2,1,0:T(8,128)S(1)} %shard_map.78.refs_3_), custom_call_target="tpu_custom_call", output_to_operand_aliasing={{}: (3, {})} | custom-call | flops 402653184 | bytes 1048576 | tf_op jit(solution)/shard_map/pallas_call | solution.py:23
  55.8 2.8 %collective-permute-start.11 = (f32[4,128,128]{2,1,0:T(8,128)S(1)}, f32[4,128,128]{2,1,0:T(8,128)S(1)}, u32[]{:S(2)}, u32[]{:S(2)}) collective-permute-start(f32[4,128,128]{2,1,0:T(8,128)S(1)} %add.26), channel_id=1, source_target_pairs={{0,24},{8,0},{16,8},{24,16},{1,25},{9,1},{17,9},{25,17},{2,26},{10... | collective-permute-start | bytes 786440 | tf_op jit(solution)/shard_map/ppermute | solution.py:435
  58.7 3.1 %shard_map.80.refs_3_ = f32[1,5,640,128]{3,2,1,0:T(8,128)S(1)} custom-call(s32[4,128]{1,0:T(4,128)S(1)} %slice_convert_fusion.refs_0_, s32[8,4]{1,0:T(8,128)S(1)} %copy.16.refs_1_, f32[4,2,128,128]{3,2,1,0:T(8,128)S(1)} %copy-done, f32[1,5,640,128]{3,2,1,0:T(8,128)S(1)} %shard_map.79.refs_3_), custom_call_target="tpu_custom_call", output_to_operand_aliasing={{}: (3, {})} | custom-call | flops 402653184 | bytes 1048576 | tf_op jit(solution)/shard_map/pallas_call | solution.py:23
  61.9 7.3 %collective-permute-done.12 = f32[4,128,128]{2,1,0:T(8,128)S(1)} collective-permute-done((f32[4,128,128]{2,1,0:T(8,128)S(1)}, f32[4,128,128]{2,1,0:T(8,128)S(1)}, u32[]{:S(2)}, u32[]{:S(2)}) %collective-permute-start.12) | collective-permute-done | bytes 262176 | tf_op jit(solution)/shard_map/ppermute | solution.py:435
  69.2 3.0 %shard_map.81.refs_1_ = f32[1,5,640,128]{3,2,1,0:T(8,128)S(1)} custom-call(s32[4,128]{1,0:T(4,128)S(1)} %slice_convert_fusion.1.refs_0_, s32[8,4]{1,0:T(8,128)S(1)} %copy.16.refs_1_, f32[4,2,128,128]{3,2,1,0:T(8,128)S(1)} %copy-done, f32[1,5,640,128]{3,2,1,0:T(8,128)S(1)} %shard_map.80.refs_3_), custom_call_target="tpu_custom_call", output_to_operand_aliasing={{}: (3, {})} | custom-call | flops 402653184 | bytes 1048576 | tf_op jit(solution)/shard_map/pallas_call | solution.py:23
  73.1 9.8 %collective-permute-done.15.refs_6_ = f32[4,128,128]{2,1,0:T(8,128)S(1)} collective-permute-done((f32[4,128,128]{2,1,0:T(8,128)S(1)}, f32[4,128,128]{2,1,0:T(8,128)S(1)}, u32[]{:S(2)}, u32[]{:S(2)}) %collective-permute-start.15) | collective-permute-done | bytes 262176 | tf_op jit(solution)/shard_map/ppermute | solution.py:454
  83.0 2.4 %shard_map.82.refs_10_ = f32[2,4,512,128]{3,2,1,0:T(8,128)S(1)} custom-call(s32[4,128]{1,0:T(4,128)S(1)} %get-tuple-element.61.refs_0_, s32[8,4]{1,0:T(8,128)S(1)} %copy.16.refs_1_, f32[4,2,128,128]{3,2,1,0:T(8,128)S(1)} %copy-done, bf16[4,256,256]{2,1,0:T(8,128)(2,1)S(1)} %copy-done.1, f32[256,512]{1,0:T(8,128)S(1)} %get-tuple-element.76.refs_4_, ...), custom_call_target="tpu_custom_call" | custom-call | flops 805306368 | bytes 1048576 | tf_op jit(solution)/shard_map/pallas_call | solution.py:23
  85.3 3.3 %collective-permute-done.13.refs_9_ = f32[4,128,128]{2,1,0:T(8,128)S(1)} collective-permute-done((f32[4,128,128]{2,1,0:T(8,128)S(1)}, f32[4,128,128]{2,1,0:T(8,128)S(1)}, u32[]{:S(2)}, u32[]{:S(2)}) %collective-permute-start.13) | collective-permute-done | bytes 262176 | tf_op jit(solution)/shard_map/ppermute | solution.py:454
  88.6 5.6 %collective-permute-done.17.refs_6_ = f32[4,128,128]{2,1,0:T(8,128)S(1)} collective-permute-done((f32[4,128,128]{2,1,0:T(8,128)S(1)}, f32[4,128,128]{2,1,0:T(8,128)S(1)}, u32[]{:S(2)}, u32[]{:S(2)}) %collective-permute-start.17) | collective-permute-done | bytes 262176 | tf_op jit(solution)/shard_map/ppermute | solution.py:454
  94.2 2.2 %shard_map.83.refs_10_ = f32[2,4,512,128]{3,2,1,0:T(8,128)S(1)} custom-call(s32[4,128]{1,0:T(4,128)S(1)} %get-tuple-element.61.refs_0_, s32[8,4]{1,0:T(8,128)S(1)} %copy.16.refs_1_, f32[4,2,128,128]{3,2,1,0:T(8,128)S(1)} %copy-done, bf16[4,256,256]{2,1,0:T(8,128)(2,1)S(1)} %copy-done.1, ...), custom_call_target="tpu_custom_call", output_to_operand_aliasing={{}: (10, {})} | custom-call | flops 805306368 | bytes 1048576 | tf_op jit(solution)/shard_map/pallas_call | solution.py:23
  96.4 3.4 %collective-permute-done.14.refs_9_ = f32[4,128,128]{2,1,0:T(8,128)S(1)} collective-permute-done((f32[4,128,128]{2,1,0:T(8,128)S(1)}, f32[4,128,128]{2,1,0:T(8,128)S(1)}, u32[]{:S(2)}, u32[]{:S(2)}) %collective-permute-start.14) | collective-permute-done | bytes 262176 | tf_op jit(solution)/shard_map/ppermute | solution.py:454
  99.8 2.2 %shard_map.84.refs_7_ = f32[2,4,512,128]{3,2,1,0:T(8,128)S(1)} custom-call(s32[4,128]{1,0:T(4,128)S(1)} %get-tuple-element.61.refs_0_, s32[8,4]{1,0:T(8,128)S(1)} %copy.16.refs_1_, f32[4,2,128,128]{3,2,1,0:T(8,128)S(1)} %copy-done, bf16[4,256,256]{2,1,0:T(8,128)(2,1)S(1)} %copy-done.1, ...), custom_call_target="tpu_custom_call", output_to_operand_aliasing={{}: (10, {})} | custom-call | flops 805306368 | bytes 1048576 | tf_op jit(solution)/shard_map/pallas_call | solution.py:23
  102.0 3.4 %collective-permute-done.18.refs_6_ = f32[4,128,128]{2,1,0:T(8,128)S(1)} collective-permute-done((f32[4,128,128]{2,1,0:T(8,128)S(1)}, f32[4,128,128]{2,1,0:T(8,128)S(1)}, u32[]{:S(2)}, u32[]{:S(2)}) %collective-permute-start.18) | collective-permute-done | bytes 262176 | tf_op jit(solution)/shard_map/ppermute | solution.py:454
  107.1 3.9 %collective-permute-done.16.refs_6_ = f32[4,128,128]{2,1,0:T(8,128)S(1)} collective-permute-done((f32[4,128,128]{2,1,0:T(8,128)S(1)}, f32[4,128,128]{2,1,0:T(8,128)S(1)}, u32[]{:S(2)}, u32[]{:S(2)}) %collective-permute-start.16) | collective-permute-done | bytes 262176 | tf_op jit(solution)/shard_map/ppermute | solution.py:454
  110.9 2.0 %shard_map.86 = (f32[2,4,512,128]{3,2,1,0:T(8,128)S(1)}, f32[512,128]{1,0:T(8,128)S(1)}, f32[512,128]{1,0:T(8,128)S(1)}, f32[2,64,384]{2,1,0:T(8,128)S(1)}, f32[2,64,384]{2,1,0:T(8,128)S(1)}) custom-call(s32[4,128]{1,0:T(4,128)S(1)} %get-tuple-element.61.refs_0_, s32[8,4]{1,0:T(8,128)S(1)} %copy.16.refs_1_, ...), custom_call_target="tpu_custom_call", output_to_operand_aliasing={{0}: (7, {})} | custom-call | flops 402653184 | bytes 1048576 | tf_op jit(solution)/shard_map/pallas_call | solution.py:23
  112.9 3.4 %collective-permute-start.19 = (f32[512,128]{1,0:T(8,128)S(1)}, f32[512,128]{1,0:T(8,128)S(1)}, u32[]{:S(2)}, u32[]{:S(2)}) collective-permute-start(f32[512,128]{1,0:T(8,128)S(1)} %get-tuple-element.97), channel_id=1, source_target_pairs={{0,1},{1,2},{2,3},{3,4},{4,5},{5,6},{6,7},{8,9},{9,10},{10,11},{11... | collective-permute-start | bytes 786440 | tf_op jit(solution)/shard_map/ppermute | solution.py:331
  116.3 1.9 %collective-permute-start.20 = (f32[512,128]{1,0:T(8,128)S(1)}, f32[512,128]{1,0:T(8,128)S(1)}, u32[]{:S(2)}, u32[]{:S(2)}) collective-permute-start(f32[512,128]{1,0:T(8,128)S(1)} %get-tuple-element.98), channel_id=1, source_target_pairs={{1,0},{2,1},{3,2},{4,3},{5,4},{6,5},{7,6},{9,8},{10,9},{11,10},{12... | collective-permute-start | bytes 786440 | tf_op jit(solution)/shard_map/ppermute | solution.py:330
  120.9 3.4 %collective-permute-done.20.refs_4_ = f32[512,128]{1,0:T(8,128)S(1)} collective-permute-done((f32[512,128]{1,0:T(8,128)S(1)}, f32[512,128]{1,0:T(8,128)S(1)}, u32[]{:S(2)}, u32[]{:S(2)}) %collective-permute-start.20) | collective-permute-done | bytes 262176 | tf_op jit(solution)/shard_map/ppermute | solution.py:330
  127.0 3.7 %collective-permute-done.24.refs_8_ = f32[2,64,128]{2,1,0:T(8,128)S(1)} collective-permute-done((f32[2,64,128]{2,1,0:T(8,128)S(1)}, f32[2,64,128]{2,1,0:T(8,128)S(1)}, u32[]{:S(2)}, u32[]{:S(2)}) %collective-permute-start.24) | collective-permute-done | bytes 65568 | tf_op jit(solution)/shard_map/ppermute | solution.py:336
  (63 shorter events, 19.2 us)
Async XLA Ops:
  1.1 24.7 %copy-start.5 = (s32[8,4]{0,1:T(4,128)S(1)}, s32[8,4]{0,1:T(4,128)}, u32[]{:S(2)}) copy-start(s32[8,4]{0,1:T(4,128)} %param.11) | copy-start | bytes 388
  1.1 14.3 %collective-permute-start.4 = (f32[2,64,384]{2,1,0:T(8,128)S(1)}, f32[2,64,384]{2,1,0:T(8,128)S(1)}, u32[]{:S(2)}, u32[]{:S(2)}) collective-permute-start(f32[2,64,384]{2,1,0:T(8,128)S(1)} %get-tuple-element.101), channel_id=1, source_target_pairs={{8,0},{16,8},{24,16},{9,1},{17,9},{25,17},{10,2},{18,10},{26,18},{... | collective-permute-start | bytes 589832 | tf_op jit(solution)/shard_map/ppermute | solution.py:361
  3.8 1.3 copy-start.2
  5.0 24.0 %copy-start.3 = (f32[2,384,384]{2,1,0:T(8,128)S(1)}, f32[2,384,384]{2,1,0:T(8,128)}, u32[]{:S(2)}) copy-start(f32[2,384,384]{2,1,0:T(8,128)} %refs_0_.1) | copy-start | bytes 3538948
  5.8 9.5 %collective-permute-start.2 = (s32[1,128]{1,0:T(1,128)S(1)}, s32[1,128]{1,0:T(1,128)S(1)}, u32[]{:S(2)}, u32[]{:S(2)}) collective-permute-start(s32[1,128]{1,0:T(1,128)S(1)} %get-tuple-element.53), channel_id=1, source_target_pairs={{0,24},{8,0},{16,8},{24,16},{1,25},{9,1},{17,9},{25,17},{2,26},{10... | collective-permute-start | bytes 1544 | tf_op jit(solution)/shard_map/ppermute | solution.py:365
  10.8 4.6 %collective-permute-start.1 = (s32[1,128]{1,0:T(1,128)S(1)}, s32[1,128]{1,0:T(1,128)S(1)}, u32[]{:S(2)}, u32[]{:S(2)}) collective-permute-start(s32[1,128]{1,0:T(1,128)S(1)} %get-tuple-element.53), channel_id=1, source_target_pairs={{0,16},{8,24},{16,0},{24,8},{1,17},{9,25},{17,1},{25,9},{2,18},{10... | collective-permute-start | bytes 1544 | tf_op jit(solution)/shard_map/ppermute | solution.py:365
  10.8 4.6 %collective-permute-start = (s32[1,128]{1,0:T(1,128)S(1)}, s32[1,128]{1,0:T(1,128)S(1)}, u32[]{:S(2)}, u32[]{:S(2)}) collective-permute-start(s32[1,128]{1,0:T(1,128)S(1)} %get-tuple-element.53), channel_id=1, source_target_pairs={{0,8},{8,16},{16,24},{24,0},{1,9},{9,17},{17,25},{25,1},{2,10},{10... | collective-permute-start | bytes 1544 | tf_op jit(solution)/shard_map/ppermute | solution.py:365
  11.2 6.7 %collective-permute-start.3 = (f32[2,64,384]{2,1,0:T(8,128)S(1)}, f32[2,64,384]{2,1,0:T(8,128)S(1)}, u32[]{:S(2)}, u32[]{:S(2)}) collective-permute-start(f32[2,64,384]{2,1,0:T(8,128)S(1)} %get-tuple-element.102), channel_id=1, source_target_pairs={{0,8},{8,16},{16,24},{1,9},{9,17},{17,25},{2,10},{10,18},{18,26},{... | collective-permute-start | bytes 589832 | tf_op jit(solution)/shard_map/ppermute | solution.py:360
  18.1 9.8 %collective-permute-start.6 = (f32[516,128]{1,0:T(8,128)S(1)}, f32[516,128]{1,0:T(8,128)S(1)}, u32[]{:S(2)}, u32[]{:S(2)}) collective-permute-start(f32[516,128]{1,0:T(8,128)S(1)} %get-tuple-element.117), channel_id=1, source_target_pairs={{1,0},{2,1},{3,2},{4,3},{5,4},{6,5},{7,6},{9,8},{10,9},{11,10},{12... | collective-permute-start | bytes 792584 | tf_op jit(solution)/shard_map/ppermute | solution.py:375
  22.7 6.4 %collective-permute-start.5 = (f32[516,128]{1,0:T(8,128)S(1)}, f32[516,128]{1,0:T(8,128)S(1)}, u32[]{:S(2)}, u32[]{:S(2)}) collective-permute-start(f32[516,128]{1,0:T(8,128)S(1)} %get-tuple-element.118), channel_id=1, source_target_pairs={{0,1},{1,2},{2,3},{3,4},{4,5},{5,6},{6,7},{8,9},{9,10},{10,11},{11... | collective-permute-start | bytes 792584 | tf_op jit(solution)/shard_map/ppermute | solution.py:374
  25.8 3.9 %copy-start = (f32[4,2,128,128]{3,2,1,0:T(8,128)S(1)}, f32[4,2,128,128]{3,2,1,0:T(8,128)}, u32[]{:S(2)}) copy-start(f32[4,2,128,128]{3,2,1,0:T(8,128)} %refs_2_.17) | copy-start | bytes 1572868
  25.8 3.9 %copy-start.1 = (bf16[4,256,256]{2,1,0:T(8,128)(2,1)S(1)}, bf16[4,256,256]{2,1,0:T(8,128)(2,1)}, u32[]{:S(2)}) copy-start(bf16[4,256,256]{2,1,0:T(8,128)(2,1)} %constant.9.clone.refs_4_.refs_3_) | copy-start | bytes 1572868
  31.4 9.0 %collective-permute-start.9 = (f32[4,128,128]{2,1,0:T(8,128)S(1)}, f32[4,128,128]{2,1,0:T(8,128)S(1)}, u32[]{:S(2)}, u32[]{:S(2)}) collective-permute-start(f32[4,128,128]{2,1,0:T(8,128)S(1)} %get-tuple-element.59), channel_id=1, source_target_pairs={{0,24},{8,0},{16,8},{24,16},{1,25},{9,1},{17,9},{25,17},{2,26},{10... | collective-permute-start | bytes 786440 | tf_op jit(solution)/shard_map/ppermute | solution.py:435
  35.9 10.0 %collective-permute-start.7 = (f32[4,128,128]{2,1,0:T(8,128)S(1)}, f32[4,128,128]{2,1,0:T(8,128)S(1)}, u32[]{:S(2)}, u32[]{:S(2)}) collective-permute-start(f32[4,128,128]{2,1,0:T(8,128)S(1)} %get-tuple-element.56), channel_id=1, source_target_pairs={{0,24},{8,0},{16,8},{24,16},{1,25},{9,1},{17,9},{25,17},{2,26},{10... | collective-permute-start | bytes 786440 | tf_op jit(solution)/shard_map/ppermute | solution.py:435
  40.4 12.4 %collective-permute-start.10 = (f32[4,128,128]{2,1,0:T(8,128)S(1)}, f32[4,128,128]{2,1,0:T(8,128)S(1)}, u32[]{:S(2)}, u32[]{:S(2)}) collective-permute-start(f32[4,128,128]{2,1,0:T(8,128)S(1)} %add.25), channel_id=1, source_target_pairs={{0,24},{8,0},{16,8},{24,16},{1,25},{9,1},{17,9},{25,17},{2,26},{10... | collective-permute-start | bytes 786440 | tf_op jit(solution)/shard_map/ppermute | solution.py:435
  45.9 9.8 %collective-permute-start.8 = (f32[4,128,128]{2,1,0:T(8,128)S(1)}, f32[4,128,128]{2,1,0:T(8,128)S(1)}, u32[]{:S(2)}, u32[]{:S(2)}) collective-permute-start(f32[4,128,128]{2,1,0:T(8,128)S(1)} %add.24), channel_id=1, source_target_pairs={{0,24},{8,0},{16,8},{24,16},{1,25},{9,1},{17,9},{25,17},{2,26},{10... | collective-permute-start | bytes 786440 | tf_op jit(solution)/shard_map/ppermute | solution.py:435
  55.8 16.4 %collective-permute-start.11 = (f32[4,128,128]{2,1,0:T(8,128)S(1)}, f32[4,128,128]{2,1,0:T(8,128)S(1)}, u32[]{:S(2)}, u32[]{:S(2)}) collective-permute-start(f32[4,128,128]{2,1,0:T(8,128)S(1)} %add.26), channel_id=1, source_target_pairs={{0,24},{8,0},{16,8},{24,16},{1,25},{9,1},{17,9},{25,17},{2,26},{10... | collective-permute-start | bytes 786440 | tf_op jit(solution)/shard_map/ppermute | solution.py:435
  58.6 10.5 %collective-permute-start.12 = (f32[4,128,128]{2,1,0:T(8,128)S(1)}, f32[4,128,128]{2,1,0:T(8,128)S(1)}, u32[]{:S(2)}, u32[]{:S(2)}) collective-permute-start(f32[4,128,128]{2,1,0:T(8,128)S(1)} %add.27), channel_id=1, source_target_pairs={{0,24},{8,0},{16,8},{24,16},{1,25},{9,1},{17,9},{25,17},{2,26},{10... | collective-permute-start | bytes 786440 | tf_op jit(solution)/shard_map/ppermute | solution.py:435
  61.8 10.4 %copy-start.4 = (f32[1,1,8,128,128]{4,3,2,1,0:T(8,128)S(1)}, f32[1,1,8,128,128]{4,3,2,1,0:T(8,128)}, u32[]{:S(2)}) copy-start(f32[1,1,8,128,128]{4,3,2,1,0:T(8,128)} %param.12) | copy-start | bytes 1572868
  72.3 10.6 %collective-permute-start.15 = (f32[4,128,128]{2,1,0:T(8,128)S(1)}, f32[4,128,128]{2,1,0:T(8,128)S(1)}, u32[]{:S(2)}, u32[]{:S(2)}) collective-permute-start(f32[4,128,128]{2,1,0:T(8,128)S(1)} %get-tuple-element.103.refs_6_), channel_id=1, source_target_pairs={{0,8},{8,16},{16,24},{24,0},{1,9},{9,17},{17,25},{25,1},{2,10},{10... | collective-permute-start | bytes 786440 | tf_op jit(solution)/shard_map/ppermute | solution.py:454
  72.4 16.2 %collective-permute-start.13 = (f32[4,128,128]{2,1,0:T(8,128)S(1)}, f32[4,128,128]{2,1,0:T(8,128)S(1)}, u32[]{:S(2)}, u32[]{:S(2)}) collective-permute-start(f32[4,128,128]{2,1,0:T(8,128)S(1)} %get-tuple-element.104.refs_9_), channel_id=1, source_target_pairs={{0,8},{8,16},{16,24},{24,0},{1,9},{9,17},{17,25},{25,1},{2,10},{10... | collective-permute-start | bytes 786440 | tf_op jit(solution)/shard_map/ppermute | solution.py:454
  83.0 11.2 %collective-permute-start.17 = (f32[4,128,128]{2,1,0:T(8,128)S(1)}, f32[4,128,128]{2,1,0:T(8,128)S(1)}, u32[]{:S(2)}, u32[]{:S(2)}) collective-permute-start(f32[4,128,128]{2,1,0:T(8,128)S(1)} %collective-permute-done.15.refs_6_), channel_id=1, source_target_pairs={{0,8},{8,16},{16,24},{24,0},{1,9},{9,17},{17,25},{25,1},{2,10},{10... | collective-permute-start | bytes 786440 | tf_op jit(solution)/shard_map/ppermute | solution.py:454
  88.6 11.2 %collective-permute-start.14 = (f32[4,128,128]{2,1,0:T(8,128)S(1)}, f32[4,128,128]{2,1,0:T(8,128)S(1)}, u32[]{:S(2)}, u32[]{:S(2)}) collective-permute-start(f32[4,128,128]{2,1,0:T(8,128)S(1)} %collective-permute-done.13.refs_9_), channel_id=1, source_target_pairs={{0,8},{8,16},{16,24},{24,0},{1,9},{9,17},{17,25},{25,1},{2,10},{10... | collective-permute-start | bytes 786440 | tf_op jit(solution)/shard_map/ppermute | solution.py:454
  94.2 11.2 %collective-permute-start.18 = (f32[4,128,128]{2,1,0:T(8,128)S(1)}, f32[4,128,128]{2,1,0:T(8,128)S(1)}, u32[]{:S(2)}, u32[]{:S(2)}) collective-permute-start(f32[4,128,128]{2,1,0:T(8,128)S(1)} %collective-permute-done.17.refs_6_), channel_id=1, source_target_pairs={{0,8},{8,16},{16,24},{24,0},{1,9},{9,17},{17,25},{25,1},{2,10},{10... | collective-permute-start | bytes 786440 | tf_op jit(solution)/shard_map/ppermute | solution.py:454
  99.8 11.1 %collective-permute-start.16 = (f32[4,128,128]{2,1,0:T(8,128)S(1)}, f32[4,128,128]{2,1,0:T(8,128)S(1)}, u32[]{:S(2)}, u32[]{:S(2)}) collective-permute-start(f32[4,128,128]{2,1,0:T(8,128)S(1)} %collective-permute-done.14.refs_9_), channel_id=1, source_target_pairs={{0,8},{8,16},{16,24},{24,0},{1,9},{9,17},{17,25},{25,1},{2,10},{10... | collective-permute-start | bytes 786440 | tf_op jit(solution)/shard_map/ppermute | solution.py:454
  112.9 8.0 %collective-permute-start.19 = (f32[512,128]{1,0:T(8,128)S(1)}, f32[512,128]{1,0:T(8,128)S(1)}, u32[]{:S(2)}, u32[]{:S(2)}) collective-permute-start(f32[512,128]{1,0:T(8,128)S(1)} %get-tuple-element.97), channel_id=1, source_target_pairs={{0,1},{1,2},{2,3},{3,4},{4,5},{5,6},{6,7},{8,9},{9,10},{10,11},{11... | collective-permute-start | bytes 786440 | tf_op jit(solution)/shard_map/ppermute | solution.py:331
  116.3 8.0 %collective-permute-start.20 = (f32[512,128]{1,0:T(8,128)S(1)}, f32[512,128]{1,0:T(8,128)S(1)}, u32[]{:S(2)}, u32[]{:S(2)}) collective-permute-start(f32[512,128]{1,0:T(8,128)S(1)} %get-tuple-element.98), channel_id=1, source_target_pairs={{1,0},{2,1},{3,2},{4,3},{5,4},{6,5},{7,6},{9,8},{10,9},{11,10},{12... | collective-permute-start | bytes 786440 | tf_op jit(solution)/shard_map/ppermute | solution.py:330
  118.2 8.7 %collective-permute-start.21 = (f32[2,64,384]{2,1,0:T(8,128)S(1)}, f32[2,64,384]{2,1,0:T(8,128)S(1)}, u32[]{:S(2)}, u32[]{:S(2)}) collective-permute-start(f32[2,64,384]{2,1,0:T(8,128)S(1)} %get-tuple-element.99), channel_id=1, source_target_pairs={{0,8},{8,16},{16,24},{1,9},{9,17},{17,25},{2,10},{10,18},{18,26},{... | collective-permute-start | bytes 589832 | tf_op jit(solution)/shard_map/ppermute | solution.py:333
  119.5 7.4 %collective-permute-start.22 = (f32[2,64,384]{2,1,0:T(8,128)S(1)}, f32[2,64,384]{2,1,0:T(8,128)S(1)}, u32[]{:S(2)}, u32[]{:S(2)}) collective-permute-start(f32[2,64,384]{2,1,0:T(8,128)S(1)} %get-tuple-element.100), channel_id=1, source_target_pairs={{8,0},{16,8},{24,16},{9,1},{17,9},{25,17},{10,2},{18,10},{26,18},{... | collective-permute-start | bytes 589832 | tf_op jit(solution)/shard_map/ppermute | solution.py:332
  124.3 2.6 %collective-permute-start.23 = (f32[2,64,128]{2,1,0:T(8,128)S(1)}, f32[2,64,128]{2,1,0:T(8,128)S(1)}, u32[]{:S(2)}, u32[]{:S(2)}) collective-permute-start(f32[2,64,128]{2,1,0:T(8,128)S(1)} %pad_maximum_fusion.2), channel_id=1, source_target_pairs={{0,8},{8,16},{16,24},{1,9},{9,17},{17,25},{2,10},{10,18},{18,26},{... | collective-permute-start | bytes 196616 | tf_op jit(solution)/shard_map/ppermute | solution.py:337
  125.6 5.0 %collective-permute-start.24 = (f32[2,64,128]{2,1,0:T(8,128)S(1)}, f32[2,64,128]{2,1,0:T(8,128)S(1)}, u32[]{:S(2)}, u32[]{:S(2)}) collective-permute-start(f32[2,64,128]{2,1,0:T(8,128)S(1)} %pad_maximum_fusion.3), channel_id=1, source_target_pairs={{8,0},{16,8},{24,16},{9,1},{17,9},{25,17},{10,2},{18,10},{26,18},{... | collective-permute-start | bytes 196616 | tf_op jit(solution)/shard_map/ppermute | solution.py:336

commit v3 on v2

--- a/solution.py
+++ b/solution.py
@@ -69,8 +69,8 @@
     return beam
 
 
-def place(metas, which, slot, size):
-    y, x = metas[which, 2 * slot], metas[which, 2 * slot + 1]
+def place(meta, slot, size):
+    y, x = meta[0, 2 * slot], meta[0, 2 * slot + 1]
     return y, x // size, x % size
 
 
@@ -112,16 +112,19 @@
                 out[ch, t, here, :] = jnp.where(low, parts[t], parts[t + 1])
 
 
-def forward_kernel(parts, *refs):
-    metas, offsets, frame, probe, tables = refs[:5]
-    outs, (x_high, x_low, y_high, y_low) = refs[5:-4], refs[-4:]
+def forward_kernel(parts, adds, *refs):
+    meta, offsets, frame, probe, tables = refs[:5]
+    refs = refs[5:]
+    if adds:
+        arrived, refs = refs[0], refs[1:]
+    outs, (x_high, x_low, y_high, y_low) = refs[:-4], refs[-4:]
     size = probe.shape[-1]
     lane = lanes(size, size)
     for at, (which, start, slots) in enumerate(parts):
         far, wave, power = outs[3 * at : 3 * at + 3]
         for index in range(slots):
             slot = start + index
-            y, tile, shift = place(metas, which, slot, size)
+            y, tile, shift = place(meta, slot, size)
             beam = beam_of(offsets, which, slot)
             back = lax.rem(size - shift, size)
             patch = []
@@ -154,7 +157,16 @@
             for sub in range(2):
                 inside = slice(sub * size, (sub + 1) * size)
                 re, im = result[:size, inside], result[size:, inside]
-                power[slot + sub] = re * re + im * im
+                rows = slice((slot + sub) * size, (slot + sub + 1) * size)
+                own = re * re + im * im
+                power[rows, :] = own + arrived[rows, :] if adds else own
+        if power.shape[0] > slots * size:
+            scans = offsets.shape[0]
+            lane = lanes(power.shape[0] - slots * size, size)
+            row = jnp.zeros(lane.shape, jnp.int32)
+            for index in range(2 * scans + 1):
+                row = jnp.where(lane == index, meta[0, index], row)
+            power[slots * size :, :] = row.astype(F32)
 
 
 def add_patch(total, channel, y, tile, shift, value, lane):
@@ -164,16 +176,15 @@
     total[channel, tile + 1, rows, :] += jnp.where(lane < shift, moved, 0.0)
 
 
-def write_sides(total, side_l, side_r):
-    channels, tiles, rows, size = total.shape
-    half = size // 2
-    low = lanes(rows, size) < half
-    if channels == 1:
-        side_l[...] = total[0, 0]
-        side_r[...] = turn(total[0, tiles - 1])
-    else:
-        side_l[...] = jnp.where(low, total[0, 0], turn(total[1, 0]))
-        side_r[...] = jnp.where(low, turn(total[0, tiles - 1]), total[1, tiles - 1])
+def write_sides(total, weight, side_l, side_r):
+    _, tiles, rows, size = total.shape
+    last, middle = tiles - 1, rows // 2
+    low = lanes(rows, size) < size // 2
+    side_l[:rows, :] = jnp.where(low, total[0, 0], turn(total[1, 0]))
+    side_r[:rows, :] = jnp.where(low, turn(total[0, last]), total[1, last])
+    low = lanes(middle, size) < size // 2
+    side_l[rows:, :] = jnp.where(low, weight[0, 0, :middle, :], turn(weight[0, 0, middle:, :]))
+    side_r[rows:, :] = jnp.where(low, turn(weight[0, last, :middle, :]), weight[0, last, middle:, :])
 
 
 def own_columns(total, channel, rows, low):
@@ -182,19 +193,22 @@
     return [jnp.where(low, turned[t], turned[t + 1]) for t in range(tiles - 1)]
 
 
-def write_rims(total, rim_top, rim_bot):
+def write_rims(total, weight, rim_top, rim_bot):
     channels, _, rows, size = total.shape
     half = size // 2
     low = lanes(half, size) < half
-    for ch in range(channels):
+    for ch in range(channels + 1):
+        source, at = (weight, 0) if ch == channels else (total, ch)
         for start, out in ((0, rim_top), (rows - half, rim_bot)):
-            for t, value in enumerate(own_columns(total, ch, pl.ds(start, half), low)):
+            for t, value in enumerate(own_columns(source, at, pl.ds(start, half), low)):
                 out[ch, :, t * size : (t + 1) * size] = value
 
 
 def backward_kernel(parts, fresh, last, *refs):
-    metas, offsets, probe, tables = refs[:4]
+    meta, offsets, probe, tables = refs[:4]
     inputs, refs = refs[4 : 4 + 3 * len(parts)], refs[4 + 3 * len(parts) :]
+    if last:
+        weight, refs = refs[0], refs[1:]
     if not fresh:
         refs = refs[1:]
     total, refs = refs[0], refs[1:]
@@ -227,7 +241,7 @@
             result = dot3(x_high[rows, :], x_low[rows, :], tables[2], tables[3])
             for sub in range(2):
                 true_slot = start + slot + sub
-                live = (true_slot < metas[which, 2 * scans]).astype(F32)
+                live = (true_slot < meta[0, 2 * scans]).astype(F32)
                 beam = beam_of(offsets, which, true_slot)
                 probe_re, probe_im = probe[beam, 0], probe[beam, 1]
                 inside = slice(sub * size, (sub + 1) * size)
@@ -235,78 +249,74 @@
                 change_im = (result[inside, size:] - wave[slot + sub, 1]) * live
                 grad_re = probe_re * change_re + probe_im * change_im
                 grad_im = probe_re * change_im - probe_im * change_re
-                spot = place(metas, which, true_slot, size)
+                spot = place(meta, true_slot, size)
                 add_patch(total, 0, *spot, grad_re, lane)
                 add_patch(total, 1, *spot, grad_im, lane)
     if last:
-        write_sides(total, side_l, side_r)
-        write_rims(total, rim_top, rim_bot)
-
-
-def weight_kernel(steps, spans, row_count, fresh, *refs):
-    metas, (offsets, probe) = refs[: len(spans)], refs[len(spans) : len(spans) + 2]
-    total = refs[-1]
-    _, tiles, rows, size = total.shape
-    half, scans = size // 2, offsets.shape[0]
-    own_rows, own_columns = rows - 2 * size, (tiles - 2) * size
+        write_sides(total, weight, side_l, side_r)
+        write_rims(total, weight, rim_top, rim_bot)
+
+
+def weight_kernel(*refs):
+    metas, (offsets, probe, total) = refs[:-3], refs[-3:]
+    size = probe.shape[-1]
+    scans = offsets.shape[0]
     lane = lanes(size, size)
-    if fresh:
-        total[...] = jnp.zeros_like(total)
-    else:
-        total[...] = refs[-2][...]
-    for meta, across in zip(metas, spans):
-        for row, down, which in steps:
-
-            def add(slot, carry, meta=meta, across=across, row=row, down=down, which=which):
-                y = meta[row, 2 * slot] + (down * own_rows + half)
-                x = meta[row, 2 * slot + 1] + (across * own_columns + half)
-                near = (y > 0) & (y < rows - size) & (x > 0) & (x < (tiles - 1) * size)
-                below = meta[0, 2 * scans + 1] + down
-                live = (slot < meta[row, 2 * scans]) & (below >= 0) & (below < row_count)
-
-                @pl.when(near & live)
-                def _():
-                    beam = beam_of(offsets, which, slot)
-                    probe_re, probe_im = probe[beam, 0], probe[beam, 1]
-                    value = probe_re * probe_re + probe_im * probe_im
-                    add_patch(total, 0, y, x // size, x % size, value, lane)
-
-                return carry
-
-            lax.fori_loop(0, scans, add, 0)
-
-
-def gathered(total, side_l, side_r, in_top, in_bot, in_ctop, in_cbot, channel, chunk, half):
+    total[...] = jnp.zeros_like(total)
+    for which, meta in enumerate(metas):
+
+        def add(slot, carry, which=which, meta=meta):
+            @pl.when(slot < meta[0, 2 * scans])
+            def _():
+                beam = beam_of(offsets, which, slot)
+                probe_re, probe_im = probe[beam, 0], probe[beam, 1]
+                value = probe_re * probe_re + probe_im * probe_im
+                add_patch(total, 0, *place(meta, slot, size), value, lane)
+
+            return carry
+
+        lax.fori_loop(0, scans, add, 0)
+
+
+def gathered(total, weight, side_l, side_r, in_top, in_bot, in_ctop, in_cbot, channel, chunk, half):
     _, tiles, rows, size = total.shape
     chunks = (rows - size) // half
     low = lanes(half, size) < half
-    ext = pl.ds((chunk + 1) * half, half)
-    values = own_columns(total, channel, ext, low)
-
-    def add_sides(from_l, from_r):
-        from_l = from_l if channel == 0 else turn(from_l)
-        from_r = turn(from_r) if channel == 0 else from_r
+    start = (chunk + 1) * half
+    at, of_upper = pl.ds(start, half), channel == 0
+    if channel == 2:
+        values = own_columns(weight, 0, at, low)
+        of_upper = start < rows // 2
+        at = pl.ds(rows + start % (rows // 2), half)
+    else:
+        values = own_columns(total, channel, at, low)
+
+    def add_sides(from_l, from_r, of_upper):
+        from_l = from_l if of_upper else turn(from_l)
+        from_r = turn(from_r) if of_upper else from_r
         values[0] += jnp.where(low, from_l, 0.0)
         values[-1] += jnp.where(low, 0.0, from_r)
 
-    add_sides(side_l[ext, :], side_r[ext, :])
-    for at, rim, corner in ((0, in_top, in_ctop), (chunks - 1, in_bot, in_cbot)):
-        if chunk == at:
+    add_sides(side_l[at, :], side_r[at, :], of_upper)
+    for where, rim, corner in ((0, in_top, in_ctop), (chunks - 1, in_bot, in_cbot)):
+        if chunk == where:
             for t in range(tiles - 1):
                 values[t] += rim[channel, :, t * size : (t + 1) * size]
-            add_sides(corner[0], corner[1])
+            if channel == 2:
+                values[0] += jnp.where(low, corner[2], 0.0)
+                values[-1] += jnp.where(low, 0.0, corner[2])
+            else:
+                add_sides(corner[0], corner[1], of_upper)
     return values
 
 
 def final_kernel(*refs):
-    obj, weight, out = refs[0], refs[1], refs[-1]
-    grads = refs[2:9]
+    obj, out = refs[0], refs[-1]
+    grads = refs[1:9]
     size = grads[0].shape[-1]
     half = size // 2
-    tiles = obj.shape[2] // size
     for chunk in range(obj.shape[1] // half):
-        wide = pl.ds(size + chunk * half, half)
-        scale = [1.0 / (weight[0, t + 1, wide, :] + DAMPING) for t in range(tiles)]
+        scale = [1.0 / (w + DAMPING) for w in gathered(*grads, 2, chunk, half)]
         rows = slice(chunk * half, (chunk + 1) * half)
         for ch in range(2):
             for t, value in enumerate(gathered(*grads, ch, chunk, half)):
@@ -325,16 +335,21 @@
 
 
 def send_rims(side_l, side_r, rim_top, rim_bot):
-    rows, size = side_l.shape
-    half = size // 2
+    _, half, _ = rim_top.shape
+    size = side_l.shape[1]
+    rows = side_l.shape[0] * 2 // 3
     in_r = lax.ppermute(side_l, "col", line("col", -1))
     in_l = lax.ppermute(side_r, "col", line("col", 1))
     in_bot = lax.ppermute(rim_top, "row", line("row", -1))
     in_top = lax.ppermute(rim_bot, "row", line("row", 1))
-    corner_top = jnp.stack([in_l[:half], in_r[:half]])
-    corner_bot = jnp.stack([in_l[rows - half :], in_r[rows - half :]])
-    in_cbot = lax.ppermute(corner_top, "row", line("row", -1))
-    in_ctop = lax.ppermute(corner_bot, "row", line("row", 1))
+
+    def corner(start, columns):
+        at = rows + start % (rows // 2)
+        weight = jnp.concatenate([x[at : at + half, columns] for x in (in_l, in_r)], axis=1)
+        return jnp.stack([in_l[start : start + half], in_r[start : start + half], weight])
+
+    in_cbot = lax.ppermute(corner(0, slice(0, half)), "row", line("row", -1))
+    in_ctop = lax.ppermute(corner(rows - half, slice(half, size)), "row", line("row", 1))
     return in_l, in_r, in_top, in_bot, in_ctop, in_cbot
 
 
@@ -344,7 +359,6 @@
     half = size // 2
     tile_rows, tile_columns = obj.shape[1:]
     rows, tiles = tile_rows + size, tile_columns // size + 1
-    row_count = lax.axis_size("row")
     tables = dft_tables(size)
 
     def packed(x):
@@ -360,15 +374,11 @@
     top = lax.ppermute(obj[:, tile_rows - half :], "row", line("row", 1))
     bot = lax.ppermute(obj[:, :half], "row", line("row", -1))
 
-    kept = min(row_count, offsets_count + 2)
-    shifts = [k if k <= offsets_count else k - kept for k in range(kept)]
-    metas = [meta] + [lax.ppermute(meta, "row", ring("row", k)) for k in shifts[1:]]
-    metas = jnp.concatenate(metas)
     most = offsets_count - 1
-
-    extra = metas.astype(F32)
+    metas = {0: meta, most: lax.ppermute(meta, "row", ring("row", most))}
+
     edge_l, edge_r = (
-        jnp.concatenate([packed(top[:, :, part]), edge, packed(bot[:, :, part]), extra])
+        jnp.concatenate([packed(top[:, :, part]), edge, packed(bot[:, :, part])])
         for part, edge in ((slice(0, half), edge_l), (slice(tile_columns - half, None), edge_r))
     )
     left = lax.ppermute(edge_r, "col", line("col", 1))
@@ -389,63 +399,47 @@
 
     far, wave, power = {}, {}, {}
 
-    def forward(parts):
+    def forward(which, parts, arrived=None):
         outs = []
-        for _, _, count in parts:
-            outs += [(2 * size, count * size), (count, 2, size, size), (count, size, size)]
+        for start, count in parts:
+            tail = 8 if which and start == 0 else 0
+            outs += [(2 * size, count * size), (count, 2, size, size), (count * size + tail, size)]
+        adds = arrived is not None
         results = call(
-            functools.partial(forward_kernel, parts),
+            functools.partial(forward_kernel, [(which, *part) for part in parts], adds),
             outs,
-            [SMEM, SMEM, VMEM, VMEM, VMEM],
-            (metas, offsets, frame, probe, tables),
+            [SMEM, SMEM, VMEM, VMEM, VMEM] + [VMEM] * adds,
+            (metas[which], offsets, frame, probe, tables) + ((arrived,) if adds else ()),
             flops * len(parts),
             work,
         )
-        for at, (which, start, _) in enumerate(parts):
+        for at, (start, _) in enumerate(parts):
             far[which, start], wave[which, start], power[which, start] = results[3 * at : 3 * at + 3]
 
-    spans = {
-        0: metas,
-        -1: left[rows : rows + kept].astype(jnp.int32),
-        1: right[rows : rows + kept].astype(jnp.int32),
+    forward(most, [halves[0]])
+    forward(most, [halves[1]])
+    forward(0, list(halves))
+    for which in reversed(range(most)):
+        for start, count in halves:
+            arrived = lax.ppermute(power[which + 1, start], "row", ring("row", -1))
+            if which:
+                if start == 0:
+                    metas[which] = arrived[count * size : count * size + 1].astype(jnp.int32)
+                forward(which, [(start, count)], arrived)
+            else:
+                power[0, start] += arrived[: count * size]
+    factors = {
+        start: measured[0, 0, start : start + count]
+        / jnp.sqrt(power[0, start].reshape(count, size, size) + EPSILON)
+        for start, count in halves
     }
-    everything = [(which, down) for down in (-1, 0, 1) for which in range(offsets_count)]
-    pieces = [(0, everything[::2]), (0, everything[1::2]), (-1, everything), (1, everything)]
-    weight = None
-
-    def add_weight(after):
-        nonlocal weight
-        across, chosen = pieces.pop(0)
-        steps = [((which - down) % kept, down, which) for which, down in chosen]
-        span, _ = lax.optimization_barrier((spans[across], after))
-        (weight,) = call(
-            functools.partial(weight_kernel, steps, (across,), row_count, weight is None),
-            [(1, tiles + 1, tile_rows + 2 * size, size)],
-            [SMEM, SMEM, VMEM] + ([] if weight is None else [VMEM]),
-            (span, offsets, probe) + (() if weight is None else (weight,)),
-            flops,
-            aliases={} if weight is None else {3: 0},
-        )
-
-    forward([(most, *halves[0])])
-    forward([(most, *halves[1])])
-    sums = {start: power[most, start] for start, _ in halves}
-    for which in reversed(range(most)):
-        for start, _ in halves:
-            arrived = lax.ppermute(sums[start], "row", ring("row", -1))
-            if which == most - 1 and start == halves[-1][0]:
-                forward([(w, *part) for w in reversed(range(most)) for part in halves])
-            if which < most - 1 and pieces:
-                add_weight(sums[start])
-                arrived, weight = lax.optimization_barrier((arrived, weight))
-            sums[start] = arrived
-        for start, _ in halves:
-            sums[start] = sums[start] + power[which, start]
-    factors = {
-        start: measured[0, 0, start : start + count] / jnp.sqrt(sums[start] + EPSILON) for start, count in halves
-    }
-    while pieces:
-        add_weight(factors[0])
+    (weight,) = call(
+        weight_kernel,
+        [(1, tiles, rows, size)],
+        [SMEM] * (offsets_count + 1) + [VMEM],
+        (*(metas[which] for which in range(offsets_count)), offsets, probe),
+        flops,
+    )
 
     total = None
     for which in range(offsets_count):
@@ -453,6 +447,8 @@
             for start, _ in halves:
                 value = lax.ppermute(factors[start], "row", ring("row", 1))
                 if start == halves[-1][0] and which < most:
+                    if which == 1:
+                        value, weight = lax.optimization_barrier((value, weight))
                     value, total = lax.optimization_barrier((value, total))
                 factors[start] = value
         groups = [[part] for part in halves] if which == most else [list(halves)]
@@ -460,10 +456,11 @@
             fresh, last = total is None, which == most and group[-1] == halves[-1]
             outs = [(2, tiles, rows, size)]
             if last:
-                outs += [(rows, size), (rows, size), (2, half, tile_columns), (2, half, tile_columns)]
-            args = [metas, offsets, probe, tables]
+                outs += [(rows + rows // 2, size)] * 2 + [(3, half, tile_columns)] * 2
+            args = [metas[which], offsets, probe, tables]
             for start, _ in group:
                 args += [far[which, start], wave[which, start], factors[start]]
+            args += [weight] if last else []
             specs = [SMEM, SMEM] + [VMEM] * (len(args) - 2)
             if not fresh:
                 args, specs = args + [total], specs + [VMEM]
@@ -479,7 +476,7 @@
     grad_in = send_rims(*sides)
 
     (new_object,) = call(
-        final_kernel, [obj.shape], [VMEM] * 9, (obj, weight, total, *grad_in), 10**6
+        final_kernel, [obj.shape], [VMEM] * 9, (obj, total, weight, *grad_in), 10**6
     )
     return new_object
 

time: 133 us -> 130 us (0.977)
  starting transfers between devices: 43.6 us -> 54.4 us
  waiting for transfers between devices: 51 us -> 41.5 us
  Pallas kernels: 32.9 us -> 28.9 us
    ppermute x6, waiting for transfers between devices: 29.3 us -> 12.6 us  [on_device(): value = lax.ppermute(factors[start], 'row', ring('row', 1))]
    ppermute x6, starting transfers between devices: 0.79 us -> 11.1 us  [on_device(): value = lax.ppermute(factors[start], 'row', ring('row', 1))]
    ppermute x1, waiting for transfers between devices: 3.42 us -> 7.73 us  [send_rims(): in_r = lax.ppermute(side_l, 'col', line('col', -1))]
    ppermute x11 -> x9, waiting for transfers between devices: 12.5 us -> 16.6 us  [the longest x6 15 us: on_device(): arrived = lax.ppermute(power[which + 1, start], 'row', ring('row', -1))]
    pallas_call x15 -> x16, Pallas kernels: 32.9 us -> 28.9 us  [call(): pl.pallas_call(kernel, out_shape=[s if hasattr(s, 'dtype') else jax.Shape...]
    ppermute x1, starting transfers between devices: 3.41 us -> 7.26 us  [send_rims(): in_l = lax.ppermute(side_r, 'col', line('col', 1))]
    ppermute x1, waiting for transfers between devices: 0.01 us -> 2.55 us  [on_device(): bot = lax.ppermute(obj[:, :half], 'row', line('row', -1))]
    ppermute x1, waiting for transfers between devices: 2.44 us -> 0.01 us  [on_device(): top = lax.ppermute(obj[:, tile_rows - half:], 'row', line('row', 1))]
  transfers between devices with their start and end apart: 25 -> 23, of which waited for: 13 -> 17; matrix products, arithmetic and copies ran while one was open for 1% -> 1% of each run, Pallas kernels for 20% -> 17%
where the time goes in v3:
time: 130 us
  starting transfers between devices  54.4 us (42%)
  waiting for transfers between devices  41.5 us (32%)
  Pallas kernels  28.9 us (22%)
  local copies, waits for them, and re-layouts  3.51 us (3%)
    pallas_call x16, Pallas kernels, call(): pl.pallas_call(kernel, out_shape=[s if hasattr(s, 'dtype') else jax.Shape...  28.9 us
    ppermute x6, waiting for transfers between devices, on_device(): arrived = lax.ppermute(power[which + 1, start], 'row', ring('row', -1))  15 us
    ppermute x6, starting transfers between devices, on_device(): arrived = lax.ppermute(power[which + 1, start], 'row', ring('row', -1))  12.9 us
    ppermute x6, waiting for transfers between devices, on_device(): value = lax.ppermute(factors[start], 'row', ring('row', 1))  12.6 us
    ppermute x6, starting transfers between devices, on_device(): value = lax.ppermute(factors[start], 'row', ring('row', 1))  11.1 us
    ppermute x1, waiting for transfers between devices, send_rims(): in_r = lax.ppermute(side_l, 'col', line('col', -1))  7.73 us
    ppermute x1, starting transfers between devices, send_rims(): in_l = lax.ppermute(side_r, 'col', line('col', 1))  7.26 us
    ppermute x1, starting transfers between devices, on_device(): top = lax.ppermute(obj[:, tile_rows - half:], 'row', line('row', 1))  4.03 us
  transfers between devices with their start and end apart: 23, of which 17 were waited for; matrix products, arithmetic and copies ran while one was open for 1% of the time, Pallas kernels for 17%

profile of v3, /device:TPU:1, one launch (start us, length us, event | category | flops | bytes accessed | tf_op | source)
XLA Modules:
  0.0 129.9 jit_solution(15991731056434766035)
XLA Ops:
  1.1 4.0 %collective-permute-start.1 = (f32[2,64,384]{2,1,0:T(8,128)S(1)}, f32[2,64,384]{2,1,0:T(8,128)S(1)}, u32[]{:S(2)}, u32[]{:S(2)}) collective-permute-start(f32[2,64,384]{2,1,0:T(8,128)S(1)} %get-tuple-element.82), channel_id=1, source_target_pairs={{0,8},{8,16},{16,24},{1,9},{9,17},{17,25},{2,10},{10,18},{18,26},{... | collective-permute-start | bytes 589832 | tf_op jit(solution)/shard_map/ppermute | solution.py:374
  10.0 2.6 %collective-permute-done.2.bot = f32[2,64,384]{2,1,0:T(8,128)S(1)} collective-permute-done((f32[2,64,384]{2,1,0:T(8,128)S(1)}, f32[2,64,384]{2,1,0:T(8,128)S(1)}, u32[]{:S(2)}, u32[]{:S(2)}) %collective-permute-start.2) | collective-permute-done | bytes 196640 | tf_op jit(solution)/shard_map/ppermute | solution.py:375
  12.7 3.7 %collective-permute-start.4 = (f32[512,128]{1,0:T(8,128)S(1)}, f32[512,128]{1,0:T(8,128)S(1)}, u32[]{:S(2)}, u32[]{:S(2)}) collective-permute-start(f32[512,128]{1,0:T(8,128)S(1)} %maximum_maximum_fusion.1), channel_id=1, source_target_pairs={{1,0},{2,1},{3,2},{4,3},{5,4},{6,5},{7,6},{9,8},{10,9},{11,10},{12... | collective-permute-start | bytes 786440 | tf_op jit(solution)/shard_map/ppermute | solution.py:385
  16.5 3.0 %collective-permute-start.3 = (f32[512,128]{1,0:T(8,128)S(1)}, f32[512,128]{1,0:T(8,128)S(1)}, u32[]{:S(2)}, u32[]{:S(2)}) collective-permute-start(f32[512,128]{1,0:T(8,128)S(1)} %maximum_maximum_fusion), channel_id=1, source_target_pairs={{0,1},{1,2},{2,3},{3,4},{4,5},{5,6},{6,7},{8,9},{9,10},{10,11},{11... | collective-permute-start | bytes 786440 | tf_op jit(solution)/shard_map/ppermute | solution.py:384
  23.5 1.7 %shard_map.77 = (f32[256,512]{1,0:T(8,128)S(1)}, f32[4,2,128,128]{3,2,1,0:T(8,128)S(1)}, f32[520,128]{1,0:T(8,128)S(1)}) custom-call(s32[1,128]{1,0:T(1,128)S(1)} %collective-permute-done.refs_0_.refs_3_, s32[8,4]{1,0:T(8,128)S(1)} %copy.25.refs_1_.refs_4_, f32[2,4,512,128]{3,2,1,0:T(8,128)S(1)} %shard_map.74.refs_2_, f32[4,2,128,128]{3,2,1,0:T(8,128)S(1)} %copy-done, ...), custom_call_target="tpu_custom_call" | custom-call | flops 402653184 | bytes 1048576 | tf_op jit(solution)/shard_map/pallas_call | solution.py:23
  28.5 1.9 %collective-permute-start.7 = (f32[512,128]{1,0:T(8,128)S(1)}, f32[512,128]{1,0:T(8,128)S(1)}, u32[]{:S(2)}, u32[]{:S(2)}) collective-permute-start(f32[512,128]{1,0:T(8,128)S(1)} %get-tuple-element.51), channel_id=1, source_target_pairs={{0,24},{8,0},{16,8},{24,16},{1,25},{9,1},{17,9},{25,17},{2,26},{10... | collective-permute-start | bytes 786440 | tf_op jit(solution)/shard_map/ppermute | solution.py:424
  30.4 3.2 %collective-permute-done.5.refs_5_ = f32[520,128]{1,0:T(8,128)S(1)} collective-permute-done((f32[520,128]{1,0:T(8,128)S(1)}, f32[520,128]{1,0:T(8,128)S(1)}, u32[]{:S(2)}, u32[]{:S(2)}) %collective-permute-start.5) | collective-permute-done | bytes 266272 | tf_op jit(solution)/shard_map/ppermute | solution.py:424
  33.6 1.7 %shard_map.78 = (f32[256,512]{1,0:T(8,128)S(1)}, f32[4,2,128,128]{3,2,1,0:T(8,128)S(1)}, f32[520,128]{1,0:T(8,128)S(1)}) custom-call(s32[1,128]{1,0:T(1,128)S(1)} %slice_convert_fusion.1.refs_0_.refs_2_, s32[8,4]{1,0:T(8,128)S(1)} %copy.25.refs_1_.refs_4_, f32[2,4,512,128]{3,2,1,0:T(8,128)S(1)} %shard_map.74.refs_2_, f32[4,2,128,128]{3,2,1,0:T(8,128)S(1)} %copy-done, ...), custom_call_target="tpu_custom_call" | custom-call | flops 402653184 | bytes 1048576 | tf_op jit(solution)/shard_map/pallas_call | solution.py:23
  35.3 2.4 %collective-permute-start.6 = (f32[520,128]{1,0:T(8,128)S(1)}, f32[520,128]{1,0:T(8,128)S(1)}, u32[]{:S(2)}, u32[]{:S(2)}) collective-permute-start(f32[520,128]{1,0:T(8,128)S(1)} %get-tuple-element.50), channel_id=1, source_target_pairs={{0,24},{8,0},{16,8},{24,16},{1,25},{9,1},{17,9},{25,17},{2,26},{10... | collective-permute-start | bytes 798728 | tf_op jit(solution)/shard_map/ppermute | solution.py:424
  40.2 3.2 %collective-permute-start.8 = (f32[512,128]{1,0:T(8,128)S(1)}, f32[512,128]{1,0:T(8,128)S(1)}, u32[]{:S(2)}, u32[]{:S(2)}) collective-permute-start(f32[512,128]{1,0:T(8,128)S(1)} %get-tuple-element.52), channel_id=1, source_target_pairs={{0,24},{8,0},{16,8},{24,16},{1,25},{9,1},{17,9},{25,17},{2,26},{10... | collective-permute-start | bytes 786440 | tf_op jit(solution)/shard_map/ppermute | solution.py:424
  43.9 5.3 %collective-permute-done.8.refs_5_ = f32[512,128]{1,0:T(8,128)S(1)} collective-permute-done((f32[512,128]{1,0:T(8,128)S(1)}, f32[512,128]{1,0:T(8,128)S(1)}, u32[]{:S(2)}, u32[]{:S(2)}) %collective-permute-start.8) | collective-permute-done | bytes 262176 | tf_op jit(solution)/shard_map/ppermute | solution.py:424
  50.9 3.0 %collective-permute-start.9 = (f32[512,128]{1,0:T(8,128)S(1)}, f32[512,128]{1,0:T(8,128)S(1)}, u32[]{:S(2)}, u32[]{:S(2)}) collective-permute-start(f32[512,128]{1,0:T(8,128)S(1)} %get-tuple-element.53), channel_id=1, source_target_pairs={{0,24},{8,0},{16,8},{24,16},{1,25},{9,1},{17,9},{25,17},{2,26},{10... | collective-permute-start | bytes 786440 | tf_op jit(solution)/shard_map/ppermute | solution.py:424
  54.0 1.7 %shard_map.82 = (f32[256,512]{1,0:T(8,128)S(1)}, f32[4,2,128,128]{3,2,1,0:T(8,128)S(1)}, f32[520,128]{1,0:T(8,128)S(1)}) custom-call(s32[1,128]{1,0:T(1,128)S(1)} %slice_convert_fusion.refs_0_.refs_1_, s32[8,4]{1,0:T(8,128)S(1)} %copy.25.refs_1_.refs_4_, f32[2,4,512,128]{3,2,1,0:T(8,128)S(1)} %shard_map.74.refs_2_, f32[4,2,128,128]{3,2,1,0:T(8,128)S(1)} %copy-done, ...), custom_call_target="tpu_custom_call" | custom-call | flops 402653184 | bytes 1048576 | tf_op jit(solution)/shard_map/pallas_call | solution.py:23
  56.3 2.2 %shard_map.76 = (f32[256,512]{1,0:T(8,128)S(1)}, f32[4,2,128,128]{3,2,1,0:T(8,128)S(1)}, f32[512,128]{1,0:T(8,128)S(1)}, f32[256,512]{1,0:T(8,128)S(1)}, f32[4,2...) custom-call(s32[1,128]{1,0:T(1,128)S(1)} %get-tuple-element.43.refs_0_, s32[8,4]{1,0:T(8,128)S(1)} %copy.25.refs_1_.refs_4_, ...), custom_call_target="tpu_custom_call" | custom-call | flops 805306368 | bytes 1048576 | tf_op jit(solution)/shard_map/pallas_call | solution.py:23
  58.6 5.3 %collective-permute-done.11 = f32[520,128]{1,0:T(8,128)S(1)} collective-permute-done((f32[520,128]{1,0:T(8,128)S(1)}, f32[520,128]{1,0:T(8,128)S(1)}, u32[]{:S(2)}, u32[]{:S(2)}) %collective-permute-start.11) | collective-permute-done | bytes 266272 | tf_op jit(solution)/shard_map/ppermute | solution.py:424
  64.0 2.4 %collective-permute-start.13 = (f32[4,128,128]{2,1,0:T(8,128)S(1)}, f32[4,128,128]{2,1,0:T(8,128)S(1)}, u32[]{:S(2)}, u32[]{:S(2)}) collective-permute-start(f32[4,128,128]{2,1,0:T(8,128)S(1)} %get-tuple-element.83.refs_6_), channel_id=1, source_target_pairs={{0,8},{8,16},{16,24},{24,0},{1,9},{9,17},{17,25},{25,1},{2,10},{10... | collective-permute-start | bytes 786440 | tf_op jit(solution)/shard_map/ppermute | solution.py:448
  66.5 3.0 %shard_map.81.refs_7_.refs_2_ = f32[1,4,512,128]{3,2,1,0:T(8,128)S(1)} custom-call(s32[1,128]{1,0:T(1,128)S(1)} %get-tuple-element.43.refs_0_, s32[1,128]{1,0:T(1,128)S(1)} %slice_convert_fusion.refs_0_.refs_1_, s32[1,128]{1,0:T(1,128)S(1)} %slice_convert_fusion.1.refs_0_.refs_2_, s32[1,128]{1,0:T(1,128)S(1)} %collective-permute-done.refs_0_.refs_3_, ...), custom_call_target="tpu_custom_call" | custom-call | flops 402653184 | bytes 1048576 | tf_op jit(solution)/shard_map/pallas_call | solution.py:23
  71.1 2.1 %collective-permute-start.15 = (f32[4,128,128]{2,1,0:T(8,128)S(1)}, f32[4,128,128]{2,1,0:T(8,128)S(1)}, u32[]{:S(2)}, u32[]{:S(2)}) collective-permute-start(f32[4,128,128]{2,1,0:T(8,128)S(1)} %collective-permute-done.13.refs_6_), channel_id=1, source_target_pairs={{0,8},{8,16},{16,24},{24,0},{1,9},{9,17},{17,25},{25,1},{2,10},{10... | collective-permute-start | bytes 786440 | tf_op jit(solution)/shard_map/ppermute | solution.py:448
  73.1 2.4 %shard_map.83.refs_10_ = f32[2,4,512,128]{3,2,1,0:T(8,128)S(1)} custom-call(s32[1,128]{1,0:T(1,128)S(1)} %get-tuple-element.43.refs_0_, s32[8,4]{1,0:T(8,128)S(1)} %copy.25.refs_1_.refs_4_, f32[4,2,128,128]{3,2,1,0:T(8,128)S(1)} %copy-done, bf16[4,256,256]{2,1,0:T(8,128)(2,1)S(1)} %copy-done.1, f32[256,512]{1,0:T(8,128)S(1)} %get-tuple-element.55.refs_4_, ...), custom_call_target="tpu_custom_call" | custom-call | flops 805306368 | bytes 1048576 | tf_op jit(solution)/shard_map/pallas_call | solution.py:23
  76.6 2.2 %collective-permute-start.12 = (f32[4,128,128]{2,1,0:T(8,128)S(1)}, f32[4,128,128]{2,1,0:T(8,128)S(1)}, u32[]{:S(2)}, u32[]{:S(2)}) collective-permute-start(f32[4,128,128]{2,1,0:T(8,128)S(1)} %collective-permute-done.10.refs_9_), channel_id=1, source_target_pairs={{0,8},{8,16},{16,24},{24,0},{1,9},{9,17},{17,25},{25,1},{2,10},{10... | collective-permute-start | bytes 786440 | tf_op jit(solution)/shard_map/ppermute | solution.py:448
  78.8 3.4 %collective-permute-done.15.refs_6_ = f32[4,128,128]{2,1,0:T(8,128)S(1)} collective-permute-done((f32[4,128,128]{2,1,0:T(8,128)S(1)}, f32[4,128,128]{2,1,0:T(8,128)S(1)}, u32[]{:S(2)}, u32[]{:S(2)}) %collective-permute-start.15) | collective-permute-done | bytes 262176 | tf_op jit(solution)/shard_map/ppermute | solution.py:448
  82.2 2.2 %collective-permute-start.16 = (f32[4,128,128]{2,1,0:T(8,128)S(1)}, f32[4,128,128]{2,1,0:T(8,128)S(1)}, u32[]{:S(2)}, u32[]{:S(2)}) collective-permute-start(f32[4,128,128]{2,1,0:T(8,128)S(1)} %collective-permute-done.15.refs_6_), channel_id=1, source_target_pairs={{0,8},{8,16},{16,24},{24,0},{1,9},{9,17},{17,25},{25,1},{2,10},{10... | collective-permute-start | bytes 786440 | tf_op jit(solution)/shard_map/ppermute | solution.py:448
  84.4 2.2 %shard_map.84.refs_10_ = f32[2,4,512,128]{3,2,1,0:T(8,128)S(1)} custom-call(s32[1,128]{1,0:T(1,128)S(1)} %slice_convert_fusion.refs_0_.refs_1_, s32[8,4]{1,0:T(8,128)S(1)} %copy.25.refs_1_.refs_4_, f32[4,2,128,128]{3,2,1,0:T(8,128)S(1)} %copy-done, bf16[4,256,256]{2,1,0:T(8,128)(2,1)S(1)} %copy-done.1, ...), custom_call_target="tpu_custom_call", output_to_operand_aliasing={{}: (10, {})} | custom-call | flops 805306368 | bytes 1048576 | tf_op jit(solution)/shard_map/pallas_call | solution.py:23
  87.8 2.2 %collective-permute-start.14 = (f32[4,128,128]{2,1,0:T(8,128)S(1)}, f32[4,128,128]{2,1,0:T(8,128)S(1)}, u32[]{:S(2)}, u32[]{:S(2)}) collective-permute-start(f32[4,128,128]{2,1,0:T(8,128)S(1)} %collective-permute-done.12.refs_9_), channel_id=1, source_target_pairs={{0,8},{8,16},{16,24},{24,0},{1,9},{9,17},{17,25},{25,1},{2,10},{10... | collective-permute-start | bytes 786440 | tf_op jit(solution)/shard_map/ppermute | solution.py:448
  90.0 2.2 %shard_map.85.refs_7_ = f32[2,4,512,128]{3,2,1,0:T(8,128)S(1)} custom-call(s32[1,128]{1,0:T(1,128)S(1)} %slice_convert_fusion.1.refs_0_.refs_2_, s32[8,4]{1,0:T(8,128)S(1)} %copy.25.refs_1_.refs_4_, f32[4,2,128,128]{3,2,1,0:T(8,128)S(1)} %copy-done, bf16[4,256,256]{2,1,0:T(8,128)(2,1)S(1)} %copy-done.1, ...), custom_call_target="tpu_custom_call", output_to_operand_aliasing={{}: (10, {})} | custom-call | flops 805306368 | bytes 1048576 | tf_op jit(solution)/shard_map/pallas_call | solution.py:23
  95.0 4.0 %collective-permute-done.14.refs_6_ = f32[4,128,128]{2,1,0:T(8,128)S(1)} collective-permute-done((f32[4,128,128]{2,1,0:T(8,128)S(1)}, f32[4,128,128]{2,1,0:T(8,128)S(1)}, u32[]{:S(2)}, u32[]{:S(2)}) %collective-permute-start.14) | collective-permute-done | bytes 262176 | tf_op jit(solution)/shard_map/ppermute | solution.py:448
  99.1 1.9 %shard_map.87 = (f32[2,4,512,128]{3,2,1,0:T(8,128)S(1)}, f32[768,128]{1,0:T(8,128)S(1)}, f32[768,128]{1,0:T(8,128)S(1)}, f32[3,64,384]{2,1,0:T(8,128)S(1)}, f32[3,64,384]{2,1,0:T(8,128)S(1)}) custom-call(s32[1,128]{1,0:T(1,128)S(1)} %collective-permute-done.refs_0_.refs_3_, s32[8,4]{1,0:T(8,128)S(1)} %copy.25.refs_1_.refs_4_, ...), custom_call_target="tpu_custom_call", output_to_operand_aliasing={{0}: (8, {})} | custom-call | flops 402653184 | bytes 1048576 | tf_op jit(solution)/shard_map/pallas_call | solution.py:23
  101.0 7.3 %collective-permute-start.17 = (f32[768,128]{1,0:T(8,128)S(1)}, f32[768,128]{1,0:T(8,128)S(1)}, u32[]{:S(2)}, u32[]{:S(2)}) collective-permute-start(f32[768,128]{1,0:T(8,128)S(1)} %get-tuple-element.77), channel_id=1, source_target_pairs={{0,1},{1,2},{2,3},{3,4},{4,5},{5,6},{6,7},{8,9},{9,10},{10,11},{11... | collective-permute-start | bytes 1179656 | tf_op jit(solution)/shard_map/ppermute | solution.py:342
  108.3 1.9 %collective-permute-start.18 = (f32[768,128]{1,0:T(8,128)S(1)}, f32[768,128]{1,0:T(8,128)S(1)}, u32[]{:S(2)}, u32[]{:S(2)}) collective-permute-start(f32[768,128]{1,0:T(8,128)S(1)} %get-tuple-element.78), channel_id=1, source_target_pairs={{1,0},{2,1},{3,2},{4,3},{5,4},{6,5},{7,6},{9,8},{10,9},{11,10},{12... | collective-permute-start | bytes 1179656 | tf_op jit(solution)/shard_map/ppermute | solution.py:341
  113.0 7.7 %collective-permute-done.18.refs_4_ = f32[768,128]{1,0:T(8,128)S(1)} collective-permute-done((f32[768,128]{1,0:T(8,128)S(1)}, f32[768,128]{1,0:T(8,128)S(1)}, u32[]{:S(2)}, u32[]{:S(2)}) %collective-permute-start.18) | collective-permute-done | bytes 393248 | tf_op jit(solution)/shard_map/ppermute | solution.py:341
  122.4 4.0 %collective-permute-start.21 = (f32[3,64,128]{2,1,0:T(8,128)S(1)}, f32[3,64,128]{2,1,0:T(8,128)S(1)}, u32[]{:S(2)}, u32[]{:S(2)}) collective-permute-start(f32[3,64,128]{2,1,0:T(8,128)S(1)} %pad_maximum_fusion), channel_id=1, source_target_pairs={{0,8},{8,16},{16,24},{1,9},{9,17},{17,25},{2,10},{10,18},{18,26},{... | collective-permute-start | bytes 294920 | tf_op jit(solution)/shard_map/ppermute | solution.py:352
  128.0 1.9 %shard_map.88 = f32[2,384,384]{2,1,0:T(8,128)} custom-call(f32[2,384,384]{2,1,0:T(8,128)S(1)} %copy-done.3, f32[2,4,512,128]{3,2,1,0:T(8,128)S(1)} %get-tuple-element.76.refs_1_, f32[1,4,512,128]{3,2,1,0:T(8,128)S(1)} %shard_map.81.refs_7_.refs_2_, f32[768,128]{1,0:T(8,128)S(1)} %collective-permute-done.17.refs_3_, ...), custom_call_target="tpu_custom_call" | custom-call | flops 1000000 | bytes 1048576 | tf_op jit(solution)/shard_map/pallas_call | solution.py:23
  (62 shorter events, 31.0 us)
Async XLA Ops:
  0.0 20.9 %copy-start.5 = (s32[8,4]{0,1:T(4,128)S(1)}, s32[8,4]{0,1:T(4,128)}, u32[]{:S(2)}) copy-start(s32[8,4]{0,1:T(4,128)} %param.11) | copy-start | bytes 388
  1.1 8.8 %collective-permute-start.1 = (f32[2,64,384]{2,1,0:T(8,128)S(1)}, f32[2,64,384]{2,1,0:T(8,128)S(1)}, u32[]{:S(2)}, u32[]{:S(2)}) collective-permute-start(f32[2,64,384]{2,1,0:T(8,128)S(1)} %get-tuple-element.82), channel_id=1, source_target_pairs={{0,8},{8,16},{16,24},{1,9},{9,17},{17,25},{2,10},{10,18},{18,26},{... | collective-permute-start | bytes 589832 | tf_op jit(solution)/shard_map/ppermute | solution.py:374
  5.1 7.4 %collective-permute-start.2 = (f32[2,64,384]{2,1,0:T(8,128)S(1)}, f32[2,64,384]{2,1,0:T(8,128)S(1)}, u32[]{:S(2)}, u32[]{:S(2)}) collective-permute-start(f32[2,64,384]{2,1,0:T(8,128)S(1)} %get-tuple-element.81), channel_id=1, source_target_pairs={{8,0},{16,8},{24,16},{9,1},{17,9},{25,17},{10,2},{18,10},{26,18},{... | collective-permute-start | bytes 589832 | tf_op jit(solution)/shard_map/ppermute | solution.py:375
  7.8 1.3 copy-start.2
  9.1 13.7 %copy-start.3 = (f32[2,384,384]{2,1,0:T(8,128)S(1)}, f32[2,384,384]{2,1,0:T(8,128)}, u32[]{:S(2)}) copy-start(f32[2,384,384]{2,1,0:T(8,128)} %refs_0_.1) | copy-start | bytes 3538948
  12.7 8.9 %collective-permute-start.4 = (f32[512,128]{1,0:T(8,128)S(1)}, f32[512,128]{1,0:T(8,128)S(1)}, u32[]{:S(2)}, u32[]{:S(2)}) collective-permute-start(f32[512,128]{1,0:T(8,128)S(1)} %maximum_maximum_fusion.1), channel_id=1, source_target_pairs={{1,0},{2,1},{3,2},{4,3},{5,4},{6,5},{7,6},{9,8},{10,9},{11,10},{12... | collective-permute-start | bytes 786440 | tf_op jit(solution)/shard_map/ppermute | solution.py:385
  16.5 6.3 %collective-permute-start.3 = (f32[512,128]{1,0:T(8,128)S(1)}, f32[512,128]{1,0:T(8,128)S(1)}, u32[]{:S(2)}, u32[]{:S(2)}) collective-permute-start(f32[512,128]{1,0:T(8,128)S(1)} %maximum_maximum_fusion), channel_id=1, source_target_pairs={{0,1},{1,2},{2,3},{3,4},{4,5},{5,6},{6,7},{8,9},{9,10},{10,11},{11... | collective-permute-start | bytes 786440 | tf_op jit(solution)/shard_map/ppermute | solution.py:384
  19.5 3.9 %collective-permute-start = (s32[1,128]{1,0:T(1,128)S(1)}, s32[1,128]{1,0:T(1,128)S(1)}, u32[]{:S(2)}, u32[]{:S(2)}) collective-permute-start(s32[1,128]{1,0:T(1,128)S(1)} %get-tuple-element.43.refs_0_), channel_id=1, source_target_pairs={{0,24},{8,0},{16,8},{24,16},{1,25},{9,1},{17,9},{25,17},{2,26},{10... | collective-permute-start | bytes 1544 | tf_op jit(solution)/shard_map/ppermute | solution.py:378
  20.9 2.5 %copy-start = (f32[4,2,128,128]{3,2,1,0:T(8,128)S(1)}, f32[4,2,128,128]{3,2,1,0:T(8,128)}, u32[]{:S(2)}) copy-start(f32[4,2,128,128]{3,2,1,0:T(8,128)} %refs_2_.9) | copy-start | bytes 1572868
  20.9 2.5 %copy-start.1 = (bf16[4,256,256]{2,1,0:T(8,128)(2,1)S(1)}, bf16[4,256,256]{2,1,0:T(8,128)(2,1)}, u32[]{:S(2)}) copy-start(bf16[4,256,256]{2,1,0:T(8,128)(2,1)} %constant.9.clone.refs_4_.refs_3_) | copy-start | bytes 1572868
  25.2 8.5 %collective-permute-start.5 = (f32[520,128]{1,0:T(8,128)S(1)}, f32[520,128]{1,0:T(8,128)S(1)}, u32[]{:S(2)}, u32[]{:S(2)}) collective-permute-start(f32[520,128]{1,0:T(8,128)S(1)} %get-tuple-element.49), channel_id=1, source_target_pairs={{0,24},{8,0},{16,8},{24,16},{1,25},{9,1},{17,9},{25,17},{2,26},{10... | collective-permute-start | bytes 798728 | tf_op jit(solution)/shard_map/ppermute | solution.py:424
  28.5 10.0 %collective-permute-start.7 = (f32[512,128]{1,0:T(8,128)S(1)}, f32[512,128]{1,0:T(8,128)S(1)}, u32[]{:S(2)}, u32[]{:S(2)}) collective-permute-start(f32[512,128]{1,0:T(8,128)S(1)} %get-tuple-element.51), channel_id=1, source_target_pairs={{0,24},{8,0},{16,8},{24,16},{1,25},{9,1},{17,9},{25,17},{2,26},{10... | collective-permute-start | bytes 786440 | tf_op jit(solution)/shard_map/ppermute | solution.py:424
  35.3 8.6 %collective-permute-start.6 = (f32[520,128]{1,0:T(8,128)S(1)}, f32[520,128]{1,0:T(8,128)S(1)}, u32[]{:S(2)}, u32[]{:S(2)}) collective-permute-start(f32[520,128]{1,0:T(8,128)S(1)} %get-tuple-element.50), channel_id=1, source_target_pairs={{0,24},{8,0},{16,8},{24,16},{1,25},{9,1},{17,9},{25,17},{2,26},{10... | collective-permute-start | bytes 798728 | tf_op jit(solution)/shard_map/ppermute | solution.py:424
  40.2 9.0 %collective-permute-start.8 = (f32[512,128]{1,0:T(8,128)S(1)}, f32[512,128]{1,0:T(8,128)S(1)}, u32[]{:S(2)}, u32[]{:S(2)}) collective-permute-start(f32[512,128]{1,0:T(8,128)S(1)} %get-tuple-element.52), channel_id=1, source_target_pairs={{0,24},{8,0},{16,8},{24,16},{1,25},{9,1},{17,9},{25,17},{2,26},{10... | collective-permute-start | bytes 786440 | tf_op jit(solution)/shard_map/ppermute | solution.py:424
  50.9 7.6 %collective-permute-start.9 = (f32[512,128]{1,0:T(8,128)S(1)}, f32[512,128]{1,0:T(8,128)S(1)}, u32[]{:S(2)}, u32[]{:S(2)}) collective-permute-start(f32[512,128]{1,0:T(8,128)S(1)} %get-tuple-element.53), channel_id=1, source_target_pairs={{0,24},{8,0},{16,8},{24,16},{1,25},{9,1},{17,9},{25,17},{2,26},{10... | collective-permute-start | bytes 786440 | tf_op jit(solution)/shard_map/ppermute | solution.py:424
  55.7 8.2 %copy-start.4 = (f32[1,1,8,128,128]{4,3,2,1,0:T(8,128)S(1)}, f32[1,1,8,128,128]{4,3,2,1,0:T(8,128)}, u32[]{:S(2)}) copy-start(f32[1,1,8,128,128]{4,3,2,1,0:T(8,128)} %param.12) | copy-start | bytes 1572868
  55.7 8.2 %collective-permute-start.11 = (f32[520,128]{1,0:T(8,128)S(1)}, f32[520,128]{1,0:T(8,128)S(1)}, u32[]{:S(2)}, u32[]{:S(2)}) collective-permute-start(f32[520,128]{1,0:T(8,128)S(1)} %get-tuple-element.58), channel_id=1, source_target_pairs={{0,24},{8,0},{16,8},{24,16},{1,25},{9,1},{17,9},{25,17},{2,26},{10... | collective-permute-start | bytes 798728 | tf_op jit(solution)/shard_map/ppermute | solution.py:424
  64.0 7.1 %collective-permute-start.13 = (f32[4,128,128]{2,1,0:T(8,128)S(1)}, f32[4,128,128]{2,1,0:T(8,128)S(1)}, u32[]{:S(2)}, u32[]{:S(2)}) collective-permute-start(f32[4,128,128]{2,1,0:T(8,128)S(1)} %get-tuple-element.83.refs_6_), channel_id=1, source_target_pairs={{0,8},{8,16},{16,24},{24,0},{1,9},{9,17},{17,25},{25,1},{2,10},{10... | collective-permute-start | bytes 786440 | tf_op jit(solution)/shard_map/ppermute | solution.py:448
  66.4 10.2 %collective-permute-start.10 = (f32[4,128,128]{2,1,0:T(8,128)S(1)}, f32[4,128,128]{2,1,0:T(8,128)S(1)}, u32[]{:S(2)}, u32[]{:S(2)}) collective-permute-start(f32[4,128,128]{2,1,0:T(8,128)S(1)} %get-tuple-element.84.refs_9_), channel_id=1, source_target_pairs={{0,8},{8,16},{16,24},{24,0},{1,9},{9,17},{17,25},{25,1},{2,10},{10... | collective-permute-start | bytes 786440 | tf_op jit(solution)/shard_map/ppermute | solution.py:448
  71.1 11.1 %collective-permute-start.15 = (f32[4,128,128]{2,1,0:T(8,128)S(1)}, f32[4,128,128]{2,1,0:T(8,128)S(1)}, u32[]{:S(2)}, u32[]{:S(2)}) collective-permute-start(f32[4,128,128]{2,1,0:T(8,128)S(1)} %collective-permute-done.13.refs_6_), channel_id=1, source_target_pairs={{0,8},{8,16},{16,24},{24,0},{1,9},{9,17},{17,25},{25,1},{2,10},{10... | collective-permute-start | bytes 786440 | tf_op jit(solution)/shard_map/ppermute | solution.py:448
  76.6 11.2 %collective-permute-start.12 = (f32[4,128,128]{2,1,0:T(8,128)S(1)}, f32[4,128,128]{2,1,0:T(8,128)S(1)}, u32[]{:S(2)}, u32[]{:S(2)}) collective-permute-start(f32[4,128,128]{2,1,0:T(8,128)S(1)} %collective-permute-done.10.refs_9_), channel_id=1, source_target_pairs={{0,8},{8,16},{16,24},{24,0},{1,9},{9,17},{17,25},{25,1},{2,10},{10... | collective-permute-start | bytes 786440 | tf_op jit(solution)/shard_map/ppermute | solution.py:448
  82.2 11.2 %collective-permute-start.16 = (f32[4,128,128]{2,1,0:T(8,128)S(1)}, f32[4,128,128]{2,1,0:T(8,128)S(1)}, u32[]{:S(2)}, u32[]{:S(2)}) collective-permute-start(f32[4,128,128]{2,1,0:T(8,128)S(1)} %collective-permute-done.15.refs_6_), channel_id=1, source_target_pairs={{0,8},{8,16},{16,24},{24,0},{1,9},{9,17},{17,25},{25,1},{2,10},{10... | collective-permute-start | bytes 786440 | tf_op jit(solution)/shard_map/ppermute | solution.py:448
  87.8 11.2 %collective-permute-start.14 = (f32[4,128,128]{2,1,0:T(8,128)S(1)}, f32[4,128,128]{2,1,0:T(8,128)S(1)}, u32[]{:S(2)}, u32[]{:S(2)}) collective-permute-start(f32[4,128,128]{2,1,0:T(8,128)S(1)} %collective-permute-done.12.refs_9_), channel_id=1, source_target_pairs={{0,8},{8,16},{16,24},{24,0},{1,9},{9,17},{17,25},{25,1},{2,10},{10... | collective-permute-start | bytes 786440 | tf_op jit(solution)/shard_map/ppermute | solution.py:448
  101.0 12.0 %collective-permute-start.17 = (f32[768,128]{1,0:T(8,128)S(1)}, f32[768,128]{1,0:T(8,128)S(1)}, u32[]{:S(2)}, u32[]{:S(2)}) collective-permute-start(f32[768,128]{1,0:T(8,128)S(1)} %get-tuple-element.77), channel_id=1, source_target_pairs={{0,1},{1,2},{2,3},{3,4},{4,5},{5,6},{6,7},{8,9},{9,10},{10,11},{11... | collective-permute-start | bytes 1179656 | tf_op jit(solution)/shard_map/ppermute | solution.py:342
  108.3 12.5 %collective-permute-start.18 = (f32[768,128]{1,0:T(8,128)S(1)}, f32[768,128]{1,0:T(8,128)S(1)}, u32[]{:S(2)}, u32[]{:S(2)}) collective-permute-start(f32[768,128]{1,0:T(8,128)S(1)} %get-tuple-element.78), channel_id=1, source_target_pairs={{1,0},{2,1},{3,2},{4,3},{5,4},{6,5},{7,6},{9,8},{10,9},{11,10},{12... | collective-permute-start | bytes 1179656 | tf_op jit(solution)/shard_map/ppermute | solution.py:341
  110.2 16.2 %collective-permute-start.19 = (f32[3,64,384]{2,1,0:T(8,128)S(1)}, f32[3,64,384]{2,1,0:T(8,128)S(1)}, u32[]{:S(2)}, u32[]{:S(2)}) collective-permute-start(f32[3,64,384]{2,1,0:T(8,128)S(1)} %get-tuple-element.79), channel_id=1, source_target_pairs={{0,8},{8,16},{16,24},{1,9},{9,17},{17,25},{2,10},{10,18},{18,26},{... | collective-permute-start | bytes 884744 | tf_op jit(solution)/shard_map/ppermute | solution.py:344
  111.5 14.9 %collective-permute-start.20 = (f32[3,64,384]{2,1,0:T(8,128)S(1)}, f32[3,64,384]{2,1,0:T(8,128)S(1)}, u32[]{:S(2)}, u32[]{:S(2)}) collective-permute-start(f32[3,64,384]{2,1,0:T(8,128)S(1)} %get-tuple-element.80), channel_id=1, source_target_pairs={{8,0},{16,8},{24,16},{9,1},{17,9},{25,17},{10,2},{18,10},{26,18},{... | collective-permute-start | bytes 884744 | tf_op jit(solution)/shard_map/ppermute | solution.py:343
  121.0 5.4 %collective-permute-start.22 = (f32[3,64,128]{2,1,0:T(8,128)S(1)}, f32[3,64,128]{2,1,0:T(8,128)S(1)}, u32[]{:S(2)}, u32[]{:S(2)}) collective-permute-start(f32[3,64,128]{2,1,0:T(8,128)S(1)} %pad_maximum_fusion.1), channel_id=1, source_target_pairs={{8,0},{16,8},{24,16},{9,1},{17,9},{25,17},{10,2},{18,10},{26,18},{... | collective-permute-start | bytes 294920 | tf_op jit(solution)/shard_map/ppermute | solution.py:351
  122.4 5.6 %collective-permute-start.21 = (f32[3,64,128]{2,1,0:T(8,128)S(1)}, f32[3,64,128]{2,1,0:T(8,128)S(1)}, u32[]{:S(2)}, u32[]{:S(2)}) collective-permute-start(f32[3,64,128]{2,1,0:T(8,128)S(1)} %pad_maximum_fusion), channel_id=1, source_target_pairs={{0,8},{8,16},{16,24},{1,9},{9,17},{17,25},{2,10},{10,18},{18,26},{... | collective-permute-start | bytes 294920 | tf_op jit(solution)/shard_map/ppermute | solution.py:352

commit v4 on v2

--- a/solution.py
+++ b/solution.py
@@ -62,22 +62,24 @@
     return pltpu.roll(x, x.shape[-1] // 2, 1)
 
 
-def beam_of(offsets, which, slot):
+def beam_of(meta, which, slot, scans, beams):
     beam = jnp.int32(0)
-    for index in range(1, offsets.shape[1]):
-        beam = jnp.where(offsets[slot, index] == which, index, beam)
+    for index in range(1, beams):
+        beam = jnp.where(meta[0, 2 * scans + 2 + slot * beams + index] == which, index, beam)
     return beam
 
 
-def place(metas, which, slot, size):
-    y, x = metas[which, 2 * slot], metas[which, 2 * slot + 1]
+def place(meta, slot, size):
+    y, x = meta[0, 2 * slot], meta[0, 2 * slot + 1]
     return y, x // size, x % size
 
 
-def edge_kernel(obj, positions, counts, place_of, edge_l, edge_r, meta):
+def edge_kernel(obj, positions, counts, offsets, place_of, edge_l, edge_r, meta):
     scans = positions.shape[2]
     values = [positions[0, 0, slot, axis] for slot in range(scans) for axis in range(2)]
     values += [counts[0, 0], place_of[0]]
+    values += [offsets[slot, beam] for slot in range(scans) for beam in range(offsets.shape[1])]
+    assert len(values) <= meta.shape[1]
     lane = lax.broadcasted_iota(jnp.int32, meta.shape, 1)
     row = jnp.zeros(meta.shape, jnp.int32)
     for at, value in enumerate(values):
@@ -112,17 +114,20 @@
                 out[ch, t, here, :] = jnp.where(low, parts[t], parts[t + 1])
 
 
-def forward_kernel(parts, *refs):
-    metas, offsets, frame, probe, tables = refs[:5]
-    outs, (x_high, x_low, y_high, y_low) = refs[5:-4], refs[-4:]
+def forward_kernel(parts, scans, adds, *refs):
+    meta, frame, probe, tables = refs[:4]
+    refs = refs[4:]
+    if adds:
+        arrived, refs = refs[0], refs[1:]
+    outs, (x_high, x_low, y_high, y_low) = refs[:-4], refs[-4:]
     size = probe.shape[-1]
     lane = lanes(size, size)
     for at, (which, start, slots) in enumerate(parts):
         far, wave, power = outs[3 * at : 3 * at + 3]
         for index in range(slots):
             slot = start + index
-            y, tile, shift = place(metas, which, slot, size)
-            beam = beam_of(offsets, which, slot)
+            y, tile, shift = place(meta, slot, size)
+            beam = beam_of(meta, which, slot, scans, probe.shape[0])
             back = lax.rem(size - shift, size)
             patch = []
             for ch in range(2):
@@ -154,7 +159,15 @@
             for sub in range(2):
                 inside = slice(sub * size, (sub + 1) * size)
                 re, im = result[:size, inside], result[size:, inside]
-                power[slot + sub] = re * re + im * im
+                rows = slice((slot + sub) * size, (slot + sub + 1) * size)
+                own = re * re + im * im
+                power[rows, :] = own + arrived[rows, :] if adds else own
+        if power.shape[0] > slots * size:
+            lane = lanes(power.shape[0] - slots * size, size)
+            row = jnp.zeros(lane.shape, jnp.int32)
+            for index in range(2 * scans + 2 + scans * probe.shape[0]):
+                row = jnp.where(lane == index, meta[0, index], row)
+            power[slots * size :, :] = row.astype(F32)
 
 
 def add_patch(total, channel, y, tile, shift, value, lane):
@@ -165,15 +178,10 @@
 
 
 def write_sides(total, side_l, side_r):
-    channels, tiles, rows, size = total.shape
-    half = size // 2
-    low = lanes(rows, size) < half
-    if channels == 1:
-        side_l[...] = total[0, 0]
-        side_r[...] = turn(total[0, tiles - 1])
-    else:
-        side_l[...] = jnp.where(low, total[0, 0], turn(total[1, 0]))
-        side_r[...] = jnp.where(low, turn(total[0, tiles - 1]), total[1, tiles - 1])
+    _, tiles, rows, size = total.shape
+    low = lanes(rows, size) < size // 2
+    side_l[...] = jnp.where(low, total[0, 0], turn(total[1, 0]))
+    side_r[...] = jnp.where(low, turn(total[0, tiles - 1]), total[1, tiles - 1])
 
 
 def own_columns(total, channel, rows, low):
@@ -192,9 +200,9 @@
                 out[ch, :, t * size : (t + 1) * size] = value
 
 
-def backward_kernel(parts, fresh, last, *refs):
-    metas, offsets, probe, tables = refs[:4]
-    inputs, refs = refs[4 : 4 + 3 * len(parts)], refs[4 + 3 * len(parts) :]
+def backward_kernel(parts, scans, fresh, last, *refs):
+    meta, probe, tables = refs[:3]
+    inputs, refs = refs[3 : 3 + 3 * len(parts)], refs[3 + 3 * len(parts) :]
     if not fresh:
         refs = refs[1:]
     total, refs = refs[0], refs[1:]
@@ -202,7 +210,6 @@
         (side_l, side_r, rim_top, rim_bot), refs = refs[:4], refs[4:]
     x_high, x_low, y_high, y_low = refs
     size = probe.shape[-1]
-    scans = offsets.shape[0]
     lane = lanes(size, size)
     if fresh:
         total[...] = jnp.zeros_like(total)
@@ -211,7 +218,7 @@
         for slot in range(0, slots, 2):
             for sub in range(2):
                 columns = slice((slot + sub) * size, (slot + sub + 1) * size)
-                scale = factor[slot + sub]
+                scale = factor[(slot + sub) * size : (slot + sub + 1) * size, :]
                 for ch in range(2):
                     into = slice(ch * size, (ch + 1) * size)
                     y_high[into, columns], y_low[into, columns] = split(far[into, columns] * scale)
@@ -227,15 +234,15 @@
             result = dot3(x_high[rows, :], x_low[rows, :], tables[2], tables[3])
             for sub in range(2):
                 true_slot = start + slot + sub
-                live = (true_slot < metas[which, 2 * scans]).astype(F32)
-                beam = beam_of(offsets, which, true_slot)
+                live = (true_slot < meta[0, 2 * scans]).astype(F32)
+                beam = beam_of(meta, which, true_slot, scans, probe.shape[0])
                 probe_re, probe_im = probe[beam, 0], probe[beam, 1]
                 inside = slice(sub * size, (sub + 1) * size)
                 change_re = (result[inside, :size] - wave[slot + sub, 0]) * live
                 change_im = (result[inside, size:] - wave[slot + sub, 1]) * live
                 grad_re = probe_re * change_re + probe_im * change_im
                 grad_im = probe_re * change_im - probe_im * change_re
-                spot = place(metas, which, true_slot, size)
+                spot = place(meta, true_slot, size)
                 add_patch(total, 0, *spot, grad_re, lane)
                 add_patch(total, 1, *spot, grad_im, lane)
     if last:
@@ -243,30 +250,28 @@
         write_rims(total, rim_top, rim_bot)
 
 
-def weight_kernel(steps, spans, row_count, fresh, *refs):
-    metas, (offsets, probe) = refs[: len(spans)], refs[len(spans) : len(spans) + 2]
-    total = refs[-1]
+def weight_kernel(steps, scans, which_tile, row_count, fresh, *refs):
+    metas, probe, total = refs[0], refs[1], refs[-1]
     _, tiles, rows, size = total.shape
-    half, scans = size // 2, offsets.shape[0]
+    half = size // 2
     own_rows, own_columns = rows - 2 * size, (tiles - 2) * size
     lane = lanes(size, size)
     if fresh:
         total[...] = jnp.zeros_like(total)
-    else:
-        total[...] = refs[-2][...]
-    for meta, across in zip(metas, spans):
-        for row, down, which in steps:
-
-            def add(slot, carry, meta=meta, across=across, row=row, down=down, which=which):
-                y = meta[row, 2 * slot] + (down * own_rows + half)
-                x = meta[row, 2 * slot + 1] + (across * own_columns + half)
+    at_row = lax.rem(metas[0, 2 * scans + 1] + which_tile + row_count, row_count)
+    for row, across in enumerate((0, -1, 1)):
+        for down, which in steps:
+
+            def add(slot, carry, row=row, across=across, down=down, which=which):
+                y = metas[row, 2 * slot] + (down * own_rows + half)
+                x = metas[row, 2 * slot + 1] + (across * own_columns + half)
                 near = (y > 0) & (y < rows - size) & (x > 0) & (x < (tiles - 1) * size)
-                below = meta[0, 2 * scans + 1] + down
-                live = (slot < meta[row, 2 * scans]) & (below >= 0) & (below < row_count)
+                below = at_row + down
+                live = (slot < metas[row, 2 * scans]) & (below >= 0) & (below < row_count)
 
                 @pl.when(near & live)
                 def _():
-                    beam = beam_of(offsets, which, slot)
+                    beam = beam_of(metas, which, slot, scans, probe.shape[0])
                     probe_re, probe_im = probe[beam, 0], probe[beam, 1]
                     value = probe_re * probe_re + probe_im * probe_im
                     add_patch(total, 0, y, x // size, x % size, value, lane)
@@ -324,17 +329,21 @@
     return [(i, (i + by) % count) for i in range(count)]
 
 
+def move(x, axis, pairs):
+    return lax.ppermute(x, axis, pairs)
+
+
 def send_rims(side_l, side_r, rim_top, rim_bot):
     rows, size = side_l.shape
     half = size // 2
-    in_r = lax.ppermute(side_l, "col", line("col", -1))
-    in_l = lax.ppermute(side_r, "col", line("col", 1))
-    in_bot = lax.ppermute(rim_top, "row", line("row", -1))
-    in_top = lax.ppermute(rim_bot, "row", line("row", 1))
+    in_r = move(side_l, "col", line("col", -1))
+    in_l = move(side_r, "col", line("col", 1))
+    in_bot = move(rim_top, "row", line("row", -1))
+    in_top = move(rim_bot, "row", line("row", 1))
     corner_top = jnp.stack([in_l[:half], in_r[:half]])
     corner_bot = jnp.stack([in_l[rows - half :], in_r[rows - half :]])
-    in_cbot = lax.ppermute(corner_top, "row", line("row", -1))
-    in_ctop = lax.ppermute(corner_bot, "row", line("row", 1))
+    in_cbot = move(corner_top, "row", line("row", -1))
+    in_ctop = move(corner_bot, "row", line("row", 1))
     return in_l, in_r, in_top, in_bot, in_ctop, in_cbot
 
 
@@ -353,26 +362,23 @@
     edge_l, edge_r, meta = call(
         edge_kernel,
         [(tile_rows, size)] * 2 + [jax.ShapeDtypeStruct((1, size), jnp.int32)],
-        [VMEM, SMEM, SMEM, SMEM],
-        (obj, positions, counts, lax.axis_index("row").astype(jnp.int32).reshape(1)),
+        [VMEM, SMEM, SMEM, SMEM, SMEM],
+        (obj, positions, counts, offsets, lax.axis_index("row").astype(jnp.int32).reshape(1)),
         10**6,
     )
-    top = lax.ppermute(obj[:, tile_rows - half :], "row", line("row", 1))
-    bot = lax.ppermute(obj[:, :half], "row", line("row", -1))
-
-    kept = min(row_count, offsets_count + 2)
-    shifts = [k if k <= offsets_count else k - kept for k in range(kept)]
-    metas = [meta] + [lax.ppermute(meta, "row", ring("row", k)) for k in shifts[1:]]
-    metas = jnp.concatenate(metas)
+    top = move(obj[:, tile_rows - half :], "row", line("row", 1))
+    bot = move(obj[:, :half], "row", line("row", -1))
+
     most = offsets_count - 1
-
-    extra = metas.astype(F32)
+    metas = {0: meta, most: move(meta, "row", ring("row", most))}
+
+    own_meta = jnp.broadcast_to(meta.astype(F32), (8, size))
     edge_l, edge_r = (
-        jnp.concatenate([packed(top[:, :, part]), edge, packed(bot[:, :, part]), extra])
+        jnp.concatenate([packed(top[:, :, part]), edge, packed(bot[:, :, part]), own_meta])
         for part, edge in ((slice(0, half), edge_l), (slice(tile_columns - half, None), edge_r))
     )
-    left = lax.ppermute(edge_r, "col", line("col", 1))
-    right = lax.ppermute(edge_l, "col", line("col", -1))
+    left = move(edge_r, "col", line("col", 1))
+    right = move(edge_l, "col", line("col", -1))
     (frame,) = call(
         frame_kernel, [(2, tiles, rows, size)], [VMEM] * 5, (obj, top, bot, left, right), 10**6
     )
@@ -389,86 +395,95 @@
 
     far, wave, power = {}, {}, {}
 
-    def forward(parts):
+    def forward(which, parts, arrived=None):
         outs = []
-        for _, _, count in parts:
-            outs += [(2 * size, count * size), (count, 2, size, size), (count, size, size)]
+        for start, count in parts:
+            tail = 8 if which and start == 0 else 0
+            outs += [(2 * size, count * size), (count, 2, size, size), (count * size + tail, size)]
+        adds = arrived is not None
         results = call(
-            functools.partial(forward_kernel, parts),
+            functools.partial(forward_kernel, [(which, *part) for part in parts], scans, adds),
             outs,
-            [SMEM, SMEM, VMEM, VMEM, VMEM],
-            (metas, offsets, frame, probe, tables),
+            [SMEM, VMEM, VMEM, VMEM] + [VMEM] * adds,
+            (metas[which], frame, probe, tables) + ((arrived,) if adds else ()),
             flops * len(parts),
             work,
         )
-        for at, (which, start, _) in enumerate(parts):
+        for at, (start, _) in enumerate(parts):
             far[which, start], wave[which, start], power[which, start] = results[3 * at : 3 * at + 3]
 
-    spans = {
-        0: metas,
-        -1: left[rows : rows + kept].astype(jnp.int32),
-        1: right[rows : rows + kept].astype(jnp.int32),
+    forward(most, [halves[0]])
+    forward(most, [halves[1]])
+    forward(0, list(halves))
+    for which in reversed(range(most)):
+        for start, count in halves:
+            arrived = move(power[which + 1, start], "row", ring("row", -1))
+            if which:
+                if start == 0:
+                    metas[which] = arrived[count * size : count * size + 1].astype(jnp.int32)
+                forward(which, [(start, count)], arrived)
+            else:
+                power[0, start] += arrived[: count * size]
+    factors = {
+        start: measured[0, 0, start : start + count].reshape(count * size, size) / jnp.sqrt(power[0, start] + EPSILON)
+        for start, count in halves
     }
-    everything = [(which, down) for down in (-1, 0, 1) for which in range(offsets_count)]
-    pieces = [(0, everything[::2]), (0, everything[1::2]), (-1, everything), (1, everything)]
+    beside = jnp.concatenate([left[rows : rows + 1], right[rows : rows + 1], jnp.zeros((6, size), F32)])
+    factors[0] = jnp.concatenate([factors[0], beside])
+
+    row_count = lax.axis_size("row")
+    kept = min(row_count, offsets_count + 2)
     weight = None
 
-    def add_weight(after):
+    def add_weight(index, shift, beside):
         nonlocal weight
-        across, chosen = pieces.pop(0)
-        steps = [((which - down) % kept, down, which) for which, down in chosen]
-        span, _ = lax.optimization_barrier((spans[across], after))
+        own = metas[shift] if shift in metas else None
+        if own is None:
+            span = move(jnp.concatenate([meta.astype(F32), beside[:2]]), "row", ring("row", shift))
+            span = span.astype(jnp.int32)
+        else:
+            span = jnp.concatenate([own, beside[:2].astype(jnp.int32)])
+        steps = [(d, w) for d in (-1, 0, 1) for w in range(offsets_count) if (w - d) % kept == index]
         (weight,) = call(
-            functools.partial(weight_kernel, steps, (across,), row_count, weight is None),
+            functools.partial(weight_kernel, steps, scans, shift, row_count, weight is None),
             [(1, tiles + 1, tile_rows + 2 * size, size)],
-            [SMEM, SMEM, VMEM] + ([] if weight is None else [VMEM]),
-            (span, offsets, probe) + (() if weight is None else (weight,)),
+            [SMEM, VMEM] + ([] if weight is None else [VMEM]),
+            (span, probe) + (() if weight is None else (weight,)),
             flops,
-            aliases={} if weight is None else {3: 0},
+            aliases={} if weight is None else {2: 0},
         )
 
-    forward([(most, *halves[0])])
-    forward([(most, *halves[1])])
-    sums = {start: power[most, start] for start, _ in halves}
-    for which in reversed(range(most)):
-        for start, _ in halves:
-            arrived = lax.ppermute(sums[start], "row", ring("row", -1))
-            if which == most - 1 and start == halves[-1][0]:
-                forward([(w, *part) for w in reversed(range(most)) for part in halves])
-            if which < most - 1 and pieces:
-                add_weight(sums[start])
-                arrived, weight = lax.optimization_barrier((arrived, weight))
-            sums[start] = arrived
-        for start, _ in halves:
-            sums[start] = sums[start] + power[which, start]
-    factors = {
-        start: measured[0, 0, start : start + count] / jnp.sqrt(sums[start] + EPSILON) for start, count in halves
-    }
-    while pieces:
-        add_weight(factors[0])
+    for index in range(offsets_count, kept):
+        add_weight(index, index if index <= offsets_count else index - kept, beside)
 
     total = None
     for which in range(offsets_count):
         if which:
             for start, _ in halves:
-                value = lax.ppermute(factors[start], "row", ring("row", 1))
-                if start == halves[-1][0] and which < most:
-                    value, total = lax.optimization_barrier((value, total))
+                value = move(factors[start], "row", ring("row", 1))
+                if start == halves[-1][0]:
+                    value, weight = lax.optimization_barrier((value, weight))
+                    if which < most:
+                        value, total = lax.optimization_barrier((value, total))
                 factors[start] = value
+                if start == halves[-1][0]:
+                    add_weight(which, which, factors[0][slots * size :])
+        else:
+            add_weight(0, 0, beside)
         groups = [[part] for part in halves] if which == most else [list(halves)]
         for group in groups:
             fresh, last = total is None, which == most and group[-1] == halves[-1]
             outs = [(2, tiles, rows, size)]
             if last:
-                outs += [(rows, size), (rows, size), (2, half, tile_columns), (2, half, tile_columns)]
-            args = [metas, offsets, probe, tables]
+                outs += [(rows, size)] * 2 + [(2, half, tile_columns)] * 2
+            args = [metas[which], probe, tables]
             for start, _ in group:
                 args += [far[which, start], wave[which, start], factors[start]]
-            specs = [SMEM, SMEM] + [VMEM] * (len(args) - 2)
+            specs = [SMEM] + [VMEM] * (len(args) - 1)
             if not fresh:
                 args, specs = args + [total], specs + [VMEM]
             total, *sides = call(
-                functools.partial(backward_kernel, [(which, *part) for part in group], fresh, last),
+                functools.partial(backward_kernel, [(which, *part) for part in group], scans, fresh, last),
                 outs,
                 specs,
                 args,

time: 133 us -> 131 us (0.985)
  waiting for transfers between devices: 51 us -> 33.4 us
  starting transfers between devices: 43.6 us -> 55 us
  Pallas kernels: 32.9 us -> 35.7 us
    ppermute x25 -> x23, waiting for transfers between devices: 51 us -> 33.4 us  [move(): return lax.ppermute(x, axis, pairs)]
    ppermute x25 -> x23, starting transfers between devices: 43.6 us -> 55 us  [move(): return lax.ppermute(x, axis, pairs)]
    pallas_call x15 -> x19, Pallas kernels: 32.9 us -> 35.7 us  [call(): pl.pallas_call(kernel, out_shape=[s if hasattr(s, 'dtype') else jax.Shape...]
    unnamed x14 -> x12, local copies, waits for them, and re-layouts: 2.13 us -> 2.8 us
  transfers between devices with their start and end apart: 25 -> 23, of which waited for: 13 -> 12; matrix products, arithmetic and copies ran while one was open for 1% -> 2% of each run, Pallas kernels for 20% -> 21%
where the time goes in v4:
time: 131 us; the launch traced here: 130 us
  starting transfers between devices  55 us (42%)
  Pallas kernels  35.7 us (27%)
  waiting for transfers between devices  33.4 us (25%)
  local copies, waits for them, and re-layouts  4.14 us (3%)
    ppermute x23, starting transfers between devices, move(): return lax.ppermute(x, axis, pairs)  55 us
    pallas_call x19, Pallas kernels, call(): pl.pallas_call(kernel, out_shape=[s if hasattr(s, 'dtype') else jax.Shape...  35.7 us
    ppermute x23, waiting for transfers between devices, move(): return lax.ppermute(x, axis, pairs)  33.4 us
    unnamed x12, local copies, waits for them, and re-layouts  2.8 us
  transfers between devices with their start and end apart: 23, of which 12 were waited for; matrix products, arithmetic and copies ran while one was open for 2% of the time, Pallas kernels for 21%

profile of v4, /device:TPU:1, one launch (start us, length us, event | category | flops | bytes accessed | tf_op | source)
XLA Modules:
  0.0 129.8 jit_solution(4617942554390717458)
XLA Ops:
  1.1 4.0 %collective-permute-start.1 = (f32[2,64,384]{2,1,0:T(8,128)S(1)}, f32[2,64,384]{2,1,0:T(8,128)S(1)}, u32[]{:S(2)}, u32[]{:S(2)}) collective-permute-start(f32[2,64,384]{2,1,0:T(8,128)S(1)} %get-tuple-element.89), channel_id=1, source_target_pairs={{0,8},{8,16},{16,24},{1,9},{9,17},{17,25},{2,10},{10,18},{18,26},{... | collective-permute-start | bytes 589832 | tf_op jit(solution)/shard_map/ppermute | solution.py:333
  12.7 4.8 %collective-permute-start.3 = (f32[520,128]{1,0:T(8,128)S(1)}, f32[520,128]{1,0:T(8,128)S(1)}, u32[]{:S(2)}, u32[]{:S(2)}) collective-permute-start(f32[520,128]{1,0:T(8,128)S(1)} %get-tuple-element.105), channel_id=1, source_target_pairs={{0,1},{1,2},{2,3},{3,4},{4,5},{5,6},{6,7},{8,9},{9,10},{10,11},{11... | collective-permute-start | bytes 798728 | tf_op jit(solution)/shard_map/ppermute | solution.py:333
  17.5 2.1 %collective-permute-start.4 = (f32[520,128]{1,0:T(8,128)S(1)}, f32[520,128]{1,0:T(8,128)S(1)}, u32[]{:S(2)}, u32[]{:S(2)}) collective-permute-start(f32[520,128]{1,0:T(8,128)S(1)} %get-tuple-element.106), channel_id=1, source_target_pairs={{1,0},{2,1},{3,2},{4,3},{5,4},{6,5},{7,6},{9,8},{10,9},{11,10},{12... | collective-permute-start | bytes 798728 | tf_op jit(solution)/shard_map/ppermute | solution.py:333
  19.6 1.9 %collective-permute-start = (s32[1,128]{1,0:T(1,128)S(1)}, s32[1,128]{1,0:T(1,128)S(1)}, u32[]{:S(2)}, u32[]{:S(2)}) collective-permute-start(s32[1,128]{1,0:T(1,128)S(1)} %get-tuple-element.47.refs_0_), channel_id=1, source_target_pairs={{0,24},{8,0},{16,8},{24,16},{1,25},{9,1},{17,9},{25,17},{2,26},{10... | collective-permute-start | bytes 1544 | tf_op jit(solution)/shard_map/ppermute | solution.py:333
  21.5 3.9 %collective-permute-done.4.right = f32[520,128]{1,0:T(8,128)S(1)} collective-permute-done((f32[520,128]{1,0:T(8,128)S(1)}, f32[520,128]{1,0:T(8,128)S(1)}, u32[]{:S(2)}, u32[]{:S(2)}) %collective-permute-start.4) | collective-permute-done | bytes 266272 | tf_op jit(solution)/shard_map/ppermute | solution.py:333
  27.7 1.9 %collective-permute-start.5 = (f32[520,128]{1,0:T(8,128)S(1)}, f32[520,128]{1,0:T(8,128)S(1)}, u32[]{:S(2)}, u32[]{:S(2)}) collective-permute-start(f32[520,128]{1,0:T(8,128)S(1)} %get-tuple-element.51), channel_id=1, source_target_pairs={{0,24},{8,0},{16,8},{24,16},{1,25},{9,1},{17,9},{25,17},{2,26},{10... | collective-permute-start | bytes 798728 | tf_op jit(solution)/shard_map/ppermute | solution.py:333
  32.9 2.9 %collective-permute-done.5.refs_4_ = f32[520,128]{1,0:T(8,128)S(1)} collective-permute-done((f32[520,128]{1,0:T(8,128)S(1)}, f32[520,128]{1,0:T(8,128)S(1)}, u32[]{:S(2)}, u32[]{:S(2)}) %collective-permute-start.5) | collective-permute-done | bytes 266272 | tf_op jit(solution)/shard_map/ppermute | solution.py:333
  37.4 3.9 %collective-permute-start.6 = (f32[520,128]{1,0:T(8,128)S(1)}, f32[520,128]{1,0:T(8,128)S(1)}, u32[]{:S(2)}, u32[]{:S(2)}) collective-permute-start(f32[520,128]{1,0:T(8,128)S(1)} %get-tuple-element.52), channel_id=1, source_target_pairs={{0,24},{8,0},{16,8},{24,16},{1,25},{9,1},{17,9},{25,17},{2,26},{10... | collective-permute-start | bytes 798728 | tf_op jit(solution)/shard_map/ppermute | solution.py:333
  42.9 2.7 %collective-permute-start.12 = (f32[512,128]{1,0:T(8,128)S(1)}, f32[512,128]{1,0:T(8,128)S(1)}, u32[]{:S(2)}, u32[]{:S(2)}) collective-permute-start(f32[512,128]{1,0:T(8,128)S(1)} %get-tuple-element.56), channel_id=1, source_target_pairs={{0,24},{8,0},{16,8},{24,16},{1,25},{9,1},{17,9},{25,17},{2,26},{10... | collective-permute-start | bytes 786440 | tf_op jit(solution)/shard_map/ppermute | solution.py:333
  46.7 3.6 %collective-permute-done.12.refs_4_ = f32[512,128]{1,0:T(8,128)S(1)} collective-permute-done((f32[512,128]{1,0:T(8,128)S(1)}, f32[512,128]{1,0:T(8,128)S(1)}, u32[]{:S(2)}, u32[]{:S(2)}) %collective-permute-start.12) | collective-permute-done | bytes 262176 | tf_op jit(solution)/shard_map/ppermute | solution.py:333
  51.9 3.8 %collective-permute-start.13 = (f32[512,128]{1,0:T(8,128)S(1)}, f32[512,128]{1,0:T(8,128)S(1)}, u32[]{:S(2)}, u32[]{:S(2)}) collective-permute-start(f32[512,128]{1,0:T(8,128)S(1)} %get-tuple-element.57), channel_id=1, source_target_pairs={{0,24},{8,0},{16,8},{24,16},{1,25},{9,1},{17,9},{25,17},{2,26},{10... | collective-permute-start | bytes 786440 | tf_op jit(solution)/shard_map/ppermute | solution.py:333
  57.4 2.1 %shard_map.75 = (f32[256,512]{1,0:T(8,128)S(1)}, f32[4,2,128,128]{3,2,1,0:T(8,128)S(1)}, f32[512,128]{1,0:T(8,128)S(1)}, f32[256,512]{1,0:T(8,128)S(1)}, f32[4,2...) custom-call(s32[1,128]{1,0:T(1,128)S(1)} %get-tuple-element.47.refs_0_, f32[2,4,512,128]{3,2,1,0:T(8,128)S(1)} %shard_map.74.refs_1_, ...), custom_call_target="tpu_custom_call" | custom-call | flops 805306368 | bytes 1048576 | tf_op jit(solution)/shard_map/pallas_call | solution.py:23
  59.6 2.2 %collective-permute-done.13 = f32[512,128]{1,0:T(8,128)S(1)} collective-permute-done((f32[512,128]{1,0:T(8,128)S(1)}, f32[512,128]{1,0:T(8,128)S(1)}, u32[]{:S(2)}, u32[]{:S(2)}) %collective-permute-start.13) | collective-permute-done | bytes 262176 | tf_op jit(solution)/shard_map/ppermute | solution.py:333
  61.9 5.6 %collective-permute-done.7 = f32[520,128]{1,0:T(8,128)S(1)} collective-permute-done((f32[520,128]{1,0:T(8,128)S(1)}, f32[520,128]{1,0:T(8,128)S(1)}, u32[]{:S(2)}, u32[]{:S(2)}) %collective-permute-start.7) | collective-permute-done | bytes 266272 | tf_op jit(solution)/shard_map/ppermute | solution.py:333
  67.8 2.5 %shard_map.82.refs_2_ = f32[1,5,640,128]{3,2,1,0:T(8,128)S(1)} custom-call(s32[3,128]{1,0:T(4,128)S(1)} %pad_add_fusion.1.refs_0_, f32[4,2,128,128]{3,2,1,0:T(8,128)S(1)} %copy-done), custom_call_target="tpu_custom_call" | custom-call | flops 402653184 | bytes 1048576 | tf_op jit(solution)/shard_map/pallas_call | solution.py:23
  70.4 2.3 %shard_map.83.refs_9_ = f32[2,4,512,128]{3,2,1,0:T(8,128)S(1)} custom-call(s32[1,128]{1,0:T(1,128)S(1)} %get-tuple-element.47.refs_0_, f32[4,2,128,128]{3,2,1,0:T(8,128)S(1)} %copy-done, bf16[4,256,256]{2,1,0:T(8,128)(2,1)S(1)} %copy-done.1, f32[256,512]{1,0:T(8,128)S(1)} %get-tuple-element.59.refs_3_, f32[4,2,128,128]{3,2,1,0:T(8,128)S(1)} %get-tuple-element.60.refs_4_, ...), custom_call_target="tpu_custom_call" | custom-call | flops 805306368 | bytes 1048576 | tf_op jit(solution)/shard_map/pallas_call | solution.py:23
  73.4 2.0 %collective-permute-start.15 = (f32[512,128]{1,0:T(8,128)S(1)}, f32[512,128]{1,0:T(8,128)S(1)}, u32[]{:S(2)}, u32[]{:S(2)}) collective-permute-start(f32[512,128]{1,0:T(8,128)S(1)} %collective-permute-done.14.refs_8_), channel_id=1, source_target_pairs={{0,8},{8,16},{16,24},{24,0},{1,9},{9,17},{17,25},{25,1},{2,10},{10... | collective-permute-start | bytes 786440 | tf_op jit(solution)/shard_map/ppermute | solution.py:333
  75.4 3.5 %collective-permute-done.8.refs_5_ = f32[520,128]{1,0:T(8,128)S(1)} collective-permute-done((f32[520,128]{1,0:T(8,128)S(1)}, f32[520,128]{1,0:T(8,128)S(1)}, u32[]{:S(2)}, u32[]{:S(2)}) %collective-permute-start.8) | collective-permute-done | bytes 266272 | tf_op jit(solution)/shard_map/ppermute | solution.py:333
  78.9 2.2 %collective-permute-start.9 = (f32[520,128]{1,0:T(8,128)S(1)}, f32[520,128]{1,0:T(8,128)S(1)}, u32[]{:S(2)}, u32[]{:S(2)}) collective-permute-start(f32[520,128]{1,0:T(8,128)S(1)} %collective-permute-done.8.refs_5_), channel_id=1, source_target_pairs={{0,8},{8,16},{16,24},{24,0},{1,9},{9,17},{17,25},{25,1},{2,10},{10... | collective-permute-start | bytes 798728 | tf_op jit(solution)/shard_map/ppermute | solution.py:333
  81.1 2.8 %shard_map.84.refs_2_ = f32[1,5,640,128]{3,2,1,0:T(8,128)S(1)} custom-call(s32[3,128]{1,0:T(4,128)S(1)} %pad_add_fusion.2.refs_0_, f32[4,2,128,128]{3,2,1,0:T(8,128)S(1)} %copy-done, f32[1,5,640,128]{3,2,1,0:T(8,128)S(1)} %shard_map.82.refs_2_), custom_call_target="tpu_custom_call", output_to_operand_aliasing={{}: (2, {})} | custom-call | flops 402653184 | bytes 1048576 | tf_op jit(solution)/shard_map/pallas_call | solution.py:23
  83.9 2.1 %shard_map.85.refs_9_ = f32[2,4,512,128]{3,2,1,0:T(8,128)S(1)} custom-call(s32[1,128]{1,0:T(1,128)S(1)} %slice_convert_fusion.3.refs_0_, f32[4,2,128,128]{3,2,1,0:T(8,128)S(1)} %copy-done, bf16[4,256,256]{2,1,0:T(8,128)(2,1)S(1)} %copy-done.1, f32[256,512]{1,0:T(8,128)S(1)} %get-tuple-element.66.refs_3_, ...), custom_call_target="tpu_custom_call", output_to_operand_aliasing={{}: (9, {})} | custom-call | flops 805306368 | bytes 1048576 | tf_op jit(solution)/shard_map/pallas_call | solution.py:23
  86.7 3.5 %collective-permute-done.9.refs_5_ = f32[520,128]{1,0:T(8,128)S(1)} collective-permute-done((f32[520,128]{1,0:T(8,128)S(1)}, f32[520,128]{1,0:T(8,128)S(1)}, u32[]{:S(2)}, u32[]{:S(2)}) %collective-permute-start.9) | collective-permute-done | bytes 266272 | tf_op jit(solution)/shard_map/ppermute | solution.py:333
  90.2 2.2 %collective-permute-start.10 = (f32[520,128]{1,0:T(8,128)S(1)}, f32[520,128]{1,0:T(8,128)S(1)}, u32[]{:S(2)}, u32[]{:S(2)}) collective-permute-start(f32[520,128]{1,0:T(8,128)S(1)} %collective-permute-done.9.refs_5_), channel_id=1, source_target_pairs={{0,8},{8,16},{16,24},{24,0},{1,9},{9,17},{17,25},{25,1},{2,10},{10... | collective-permute-start | bytes 798728 | tf_op jit(solution)/shard_map/ppermute | solution.py:333
  92.4 2.9 %shard_map.86.refs_2_ = f32[1,5,640,128]{3,2,1,0:T(8,128)S(1)} custom-call(s32[3,128]{1,0:T(4,128)S(1)} %pad_add_fusion.3.refs_0_, f32[4,2,128,128]{3,2,1,0:T(8,128)S(1)} %copy-done, f32[1,5,640,128]{3,2,1,0:T(8,128)S(1)} %shard_map.84.refs_2_), custom_call_target="tpu_custom_call", output_to_operand_aliasing={{}: (2, {})} | custom-call | flops 402653184 | bytes 1048576 | tf_op jit(solution)/shard_map/pallas_call | solution.py:23
  95.3 2.1 %shard_map.88.refs_6_ = f32[2,4,512,128]{3,2,1,0:T(8,128)S(1)} custom-call(s32[1,128]{1,0:T(1,128)S(1)} %slice_convert_fusion.4.refs_0_, f32[4,2,128,128]{3,2,1,0:T(8,128)S(1)} %copy-done, bf16[4,256,256]{2,1,0:T(8,128)(2,1)S(1)} %copy-done.1, f32[256,512]{1,0:T(8,128)S(1)} %get-tuple-element.79.refs_3_, ...), custom_call_target="tpu_custom_call", output_to_operand_aliasing={{}: (9, {})} | custom-call | flops 805306368 | bytes 1048576 | tf_op jit(solution)/shard_map/pallas_call | solution.py:23
  97.4 3.7 %collective-permute-done.10.refs_5_ = f32[520,128]{1,0:T(8,128)S(1)} collective-permute-done((f32[520,128]{1,0:T(8,128)S(1)}, f32[520,128]{1,0:T(8,128)S(1)}, u32[]{:S(2)}, u32[]{:S(2)}) %collective-permute-start.10) | collective-permute-done | bytes 266272 | tf_op jit(solution)/shard_map/ppermute | solution.py:333
  102.7 1.9 %shard_map.90 = (f32[2,4,512,128]{3,2,1,0:T(8,128)S(1)}, f32[512,128]{1,0:T(8,128)S(1)}, f32[512,128]{1,0:T(8,128)S(1)}, f32[2,64,384]{2,1,0:T(8,128)S(1)}, f32[2,64,384]{2,1,0:T(8,128)S(1)}) custom-call(s32[1,128]{1,0:T(1,128)S(1)} %collective-permute-done.refs_0_, f32[4,2,128,128]{3,2,1,0:T(8,128)S(1)} %copy-done, ...), custom_call_target="tpu_custom_call", output_to_operand_aliasing={{0}: (6, {})} | custom-call | flops 402653184 | bytes 1048576 | tf_op jit(solution)/shard_map/pallas_call | solution.py:23
  104.5 7.8 %collective-permute-start.17 = (f32[512,128]{1,0:T(8,128)S(1)}, f32[512,128]{1,0:T(8,128)S(1)}, u32[]{:S(2)}, u32[]{:S(2)}) collective-permute-start(f32[512,128]{1,0:T(8,128)S(1)} %get-tuple-element.85), channel_id=1, source_target_pairs={{0,1},{1,2},{2,3},{3,4},{4,5},{5,6},{6,7},{8,9},{9,10},{10,11},{11... | collective-permute-start | bytes 786440 | tf_op jit(solution)/shard_map/ppermute | solution.py:333
  112.4 1.9 %collective-permute-start.18 = (f32[512,128]{1,0:T(8,128)S(1)}, f32[512,128]{1,0:T(8,128)S(1)}, u32[]{:S(2)}, u32[]{:S(2)}) collective-permute-start(f32[512,128]{1,0:T(8,128)S(1)} %get-tuple-element.86), channel_id=1, source_target_pairs={{1,0},{2,1},{3,2},{4,3},{5,4},{6,5},{7,6},{9,8},{10,9},{11,10},{12... | collective-permute-start | bytes 786440 | tf_op jit(solution)/shard_map/ppermute | solution.py:333
  114.3 3.5 %collective-permute-start.19 = (f32[2,64,384]{2,1,0:T(8,128)S(1)}, f32[2,64,384]{2,1,0:T(8,128)S(1)}, u32[]{:S(2)}, u32[]{:S(2)}) collective-permute-start(f32[2,64,384]{2,1,0:T(8,128)S(1)} %get-tuple-element.87), channel_id=1, source_target_pairs={{0,8},{8,16},{16,24},{1,9},{9,17},{17,25},{2,10},{10,18},{18,26},{... | collective-permute-start | bytes 589832 | tf_op jit(solution)/shard_map/ppermute | solution.py:333
  121.4 4.1 %collective-permute-start.21 = (f32[2,64,128]{2,1,0:T(8,128)S(1)}, f32[2,64,128]{2,1,0:T(8,128)S(1)}, u32[]{:S(2)}, u32[]{:S(2)}) collective-permute-start(f32[2,64,128]{2,1,0:T(8,128)S(1)} %pad_maximum_fusion.2), channel_id=1, source_target_pairs={{0,8},{8,16},{16,24},{1,9},{9,17},{17,25},{2,10},{10,18},{18,26},{... | collective-permute-start | bytes 196616 | tf_op jit(solution)/shard_map/ppermute | solution.py:333
  125.5 2.6 %shard_map.87.refs_1_ = f32[1,5,640,128]{3,2,1,0:T(8,128)S(1)} custom-call(s32[3,128]{1,0:T(4,128)S(1)} %pad_add_fusion.refs_0_, f32[4,2,128,128]{3,2,1,0:T(8,128)S(1)} %copy-done, f32[1,5,640,128]{3,2,1,0:T(8,128)S(1)} %shard_map.86.refs_2_), custom_call_target="tpu_custom_call", output_to_operand_aliasing={{}: (2, {})} | custom-call | flops 402653184 | bytes 1048576 | tf_op jit(solution)/shard_map/pallas_call | solution.py:23
  (73 shorter events, 29.8 us)
Async XLA Ops:
  1.1 9.6 %collective-permute-start.1 = (f32[2,64,384]{2,1,0:T(8,128)S(1)}, f32[2,64,384]{2,1,0:T(8,128)S(1)}, u32[]{:S(2)}, u32[]{:S(2)}) collective-permute-start(f32[2,64,384]{2,1,0:T(8,128)S(1)} %get-tuple-element.89), channel_id=1, source_target_pairs={{0,8},{8,16},{16,24},{1,9},{9,17},{17,25},{2,10},{10,18},{18,26},{... | collective-permute-start | bytes 589832 | tf_op jit(solution)/shard_map/ppermute | solution.py:333
  5.1 7.4 %collective-permute-start.2 = (f32[2,64,384]{2,1,0:T(8,128)S(1)}, f32[2,64,384]{2,1,0:T(8,128)S(1)}, u32[]{:S(2)}, u32[]{:S(2)}) collective-permute-start(f32[2,64,384]{2,1,0:T(8,128)S(1)} %get-tuple-element.90), channel_id=1, source_target_pairs={{8,0},{16,8},{24,16},{9,1},{17,9},{25,17},{10,2},{18,10},{26,18},{... | collective-permute-start | bytes 589832 | tf_op jit(solution)/shard_map/ppermute | solution.py:333
  8.6 1.3 copy-start.2
  12.7 8.8 %collective-permute-start.3 = (f32[520,128]{1,0:T(8,128)S(1)}, f32[520,128]{1,0:T(8,128)S(1)}, u32[]{:S(2)}, u32[]{:S(2)}) collective-permute-start(f32[520,128]{1,0:T(8,128)S(1)} %get-tuple-element.105), channel_id=1, source_target_pairs={{0,1},{1,2},{2,3},{3,4},{4,5},{5,6},{6,7},{8,9},{9,10},{10,11},{11... | collective-permute-start | bytes 798728 | tf_op jit(solution)/shard_map/ppermute | solution.py:333
  17.5 8.5 %copy-start = (f32[4,2,128,128]{3,2,1,0:T(8,128)S(1)}, f32[4,2,128,128]{3,2,1,0:T(8,128)}, u32[]{:S(2)}) copy-start(f32[4,2,128,128]{3,2,1,0:T(8,128)} %refs_1_.17) | copy-start | bytes 1572868
  17.5 8.5 %copy-start.1 = (bf16[4,256,256]{2,1,0:T(8,128)(2,1)S(1)}, bf16[4,256,256]{2,1,0:T(8,128)(2,1)}, u32[]{:S(2)}) copy-start(bf16[4,256,256]{2,1,0:T(8,128)(2,1)} %constant.11.clone.refs_3_.refs_2_) | copy-start | bytes 1572868
  17.5 7.9 %collective-permute-start.4 = (f32[520,128]{1,0:T(8,128)S(1)}, f32[520,128]{1,0:T(8,128)S(1)}, u32[]{:S(2)}, u32[]{:S(2)}) collective-permute-start(f32[520,128]{1,0:T(8,128)S(1)} %get-tuple-element.106), channel_id=1, source_target_pairs={{1,0},{2,1},{3,2},{4,3},{5,4},{6,5},{7,6},{9,8},{10,9},{11,10},{12... | collective-permute-start | bytes 798728 | tf_op jit(solution)/shard_map/ppermute | solution.py:333
  19.6 6.4 %collective-permute-start = (s32[1,128]{1,0:T(1,128)S(1)}, s32[1,128]{1,0:T(1,128)S(1)}, u32[]{:S(2)}, u32[]{:S(2)}) collective-permute-start(s32[1,128]{1,0:T(1,128)S(1)} %get-tuple-element.47.refs_0_), channel_id=1, source_target_pairs={{0,24},{8,0},{16,8},{24,16},{1,25},{9,1},{17,9},{25,17},{2,26},{10... | collective-permute-start | bytes 1544 | tf_op jit(solution)/shard_map/ppermute | solution.py:333
  27.7 8.1 %collective-permute-start.5 = (f32[520,128]{1,0:T(8,128)S(1)}, f32[520,128]{1,0:T(8,128)S(1)}, u32[]{:S(2)}, u32[]{:S(2)}) collective-permute-start(f32[520,128]{1,0:T(8,128)S(1)} %get-tuple-element.51), channel_id=1, source_target_pairs={{0,24},{8,0},{16,8},{24,16},{1,25},{9,1},{17,9},{25,17},{2,26},{10... | collective-permute-start | bytes 798728 | tf_op jit(solution)/shard_map/ppermute | solution.py:333
  31.2 10.1 %collective-permute-start.11 = (f32[512,128]{1,0:T(8,128)S(1)}, f32[512,128]{1,0:T(8,128)S(1)}, u32[]{:S(2)}, u32[]{:S(2)}) collective-permute-start(f32[512,128]{1,0:T(8,128)S(1)} %get-tuple-element.55), channel_id=1, source_target_pairs={{0,24},{8,0},{16,8},{24,16},{1,25},{9,1},{17,9},{25,17},{2,26},{10... | collective-permute-start | bytes 786440 | tf_op jit(solution)/shard_map/ppermute | solution.py:333
  37.4 9.2 %collective-permute-start.6 = (f32[520,128]{1,0:T(8,128)S(1)}, f32[520,128]{1,0:T(8,128)S(1)}, u32[]{:S(2)}, u32[]{:S(2)}) collective-permute-start(f32[520,128]{1,0:T(8,128)S(1)} %get-tuple-element.52), channel_id=1, source_target_pairs={{0,24},{8,0},{16,8},{24,16},{1,25},{9,1},{17,9},{25,17},{2,26},{10... | collective-permute-start | bytes 798728 | tf_op jit(solution)/shard_map/ppermute | solution.py:333
  42.9 7.3 %collective-permute-start.12 = (f32[512,128]{1,0:T(8,128)S(1)}, f32[512,128]{1,0:T(8,128)S(1)}, u32[]{:S(2)}, u32[]{:S(2)}) collective-permute-start(f32[512,128]{1,0:T(8,128)S(1)} %get-tuple-element.56), channel_id=1, source_target_pairs={{0,24},{8,0},{16,8},{24,16},{1,25},{9,1},{17,9},{25,17},{2,26},{10... | collective-permute-start | bytes 786440 | tf_op jit(solution)/shard_map/ppermute | solution.py:333
  46.7 9.0 %copy-start.4 = (f32[1,1,8,128,128]{4,3,2,1,0:T(8,128)S(1)}, f32[1,1,8,128,128]{4,3,2,1,0:T(8,128)}, u32[]{:S(2)}) copy-start(f32[1,1,8,128,128]{4,3,2,1,0:T(8,128)} %param.12) | copy-start | bytes 1572868
  51.9 9.9 %collective-permute-start.13 = (f32[512,128]{1,0:T(8,128)S(1)}, f32[512,128]{1,0:T(8,128)S(1)}, u32[]{:S(2)}, u32[]{:S(2)}) collective-permute-start(f32[512,128]{1,0:T(8,128)S(1)} %get-tuple-element.57), channel_id=1, source_target_pairs={{0,24},{8,0},{16,8},{24,16},{1,25},{9,1},{17,9},{25,17},{2,26},{10... | collective-permute-start | bytes 786440 | tf_op jit(solution)/shard_map/ppermute | solution.py:333
  57.3 10.2 %collective-permute-start.7 = (f32[520,128]{1,0:T(8,128)S(1)}, f32[520,128]{1,0:T(8,128)S(1)}, u32[]{:S(2)}, u32[]{:S(2)}) collective-permute-start(f32[520,128]{1,0:T(8,128)S(1)} %get-tuple-element.53), channel_id=1, source_target_pairs={{0,24},{8,0},{16,8},{24,16},{1,25},{9,1},{17,9},{25,17},{2,26},{10... | collective-permute-start | bytes 798728 | tf_op jit(solution)/shard_map/ppermute | solution.py:333
  61.8 11.5 %collective-permute-start.14 = (f32[512,128]{1,0:T(8,128)S(1)}, f32[512,128]{1,0:T(8,128)S(1)}, u32[]{:S(2)}, u32[]{:S(2)}) collective-permute-start(f32[512,128]{1,0:T(8,128)S(1)} %bitcast_multiply_fusion.refs_8_), channel_id=1, source_target_pairs={{0,8},{8,16},{16,24},{24,0},{1,9},{9,17},{17,25},{25,1},{2,10},{10... | collective-permute-start | bytes 786440 | tf_op jit(solution)/shard_map/ppermute | solution.py:333
  67.7 11.1 %collective-permute-start.8 = (f32[520,128]{1,0:T(8,128)S(1)}, f32[520,128]{1,0:T(8,128)S(1)}, u32[]{:S(2)}, u32[]{:S(2)}) collective-permute-start(f32[520,128]{1,0:T(8,128)S(1)} %maximum_maximum_fusion.refs_5_), channel_id=1, source_target_pairs={{0,8},{8,16},{16,24},{24,0},{1,9},{9,17},{17,25},{25,1},{2,10},{10... | collective-permute-start | bytes 798728 | tf_op jit(solution)/shard_map/ppermute | solution.py:333
  73.4 12.6 %collective-permute-start.15 = (f32[512,128]{1,0:T(8,128)S(1)}, f32[512,128]{1,0:T(8,128)S(1)}, u32[]{:S(2)}, u32[]{:S(2)}) collective-permute-start(f32[512,128]{1,0:T(8,128)S(1)} %collective-permute-done.14.refs_8_), channel_id=1, source_target_pairs={{0,8},{8,16},{16,24},{24,0},{1,9},{9,17},{17,25},{25,1},{2,10},{10... | collective-permute-start | bytes 786440 | tf_op jit(solution)/shard_map/ppermute | solution.py:333
  78.9 11.3 %collective-permute-start.9 = (f32[520,128]{1,0:T(8,128)S(1)}, f32[520,128]{1,0:T(8,128)S(1)}, u32[]{:S(2)}, u32[]{:S(2)}) collective-permute-start(f32[520,128]{1,0:T(8,128)S(1)} %collective-permute-done.8.refs_5_), channel_id=1, source_target_pairs={{0,8},{8,16},{16,24},{24,0},{1,9},{9,17},{17,25},{25,1},{2,10},{10... | collective-permute-start | bytes 798728 | tf_op jit(solution)/shard_map/ppermute | solution.py:333
  86.0 11.4 %collective-permute-start.16 = (f32[512,128]{1,0:T(8,128)S(1)}, f32[512,128]{1,0:T(8,128)S(1)}, u32[]{:S(2)}, u32[]{:S(2)}) collective-permute-start(f32[512,128]{1,0:T(8,128)S(1)} %collective-permute-done.15.refs_8_), channel_id=1, source_target_pairs={{0,8},{8,16},{16,24},{24,0},{1,9},{9,17},{17,25},{25,1},{2,10},{10... | collective-permute-start | bytes 786440 | tf_op jit(solution)/shard_map/ppermute | solution.py:333
  90.2 10.9 %collective-permute-start.10 = (f32[520,128]{1,0:T(8,128)S(1)}, f32[520,128]{1,0:T(8,128)S(1)}, u32[]{:S(2)}, u32[]{:S(2)}) collective-permute-start(f32[520,128]{1,0:T(8,128)S(1)} %collective-permute-done.9.refs_5_), channel_id=1, source_target_pairs={{0,8},{8,16},{16,24},{24,0},{1,9},{9,17},{17,25},{25,1},{2,10},{10... | collective-permute-start | bytes 798728 | tf_op jit(solution)/shard_map/ppermute | solution.py:333
  104.5 14.5 %collective-permute-start.17 = (f32[512,128]{1,0:T(8,128)S(1)}, f32[512,128]{1,0:T(8,128)S(1)}, u32[]{:S(2)}, u32[]{:S(2)}) collective-permute-start(f32[512,128]{1,0:T(8,128)S(1)} %get-tuple-element.85), channel_id=1, source_target_pairs={{0,1},{1,2},{2,3},{3,4},{4,5},{5,6},{6,7},{8,9},{9,10},{10,11},{11... | collective-permute-start | bytes 786440 | tf_op jit(solution)/shard_map/ppermute | solution.py:333
  112.4 7.7 %collective-permute-start.18 = (f32[512,128]{1,0:T(8,128)S(1)}, f32[512,128]{1,0:T(8,128)S(1)}, u32[]{:S(2)}, u32[]{:S(2)}) collective-permute-start(f32[512,128]{1,0:T(8,128)S(1)} %get-tuple-element.86), channel_id=1, source_target_pairs={{1,0},{2,1},{3,2},{4,3},{5,4},{6,5},{7,6},{9,8},{10,9},{11,10},{12... | collective-permute-start | bytes 786440 | tf_op jit(solution)/shard_map/ppermute | solution.py:333
  114.3 13.8 %collective-permute-start.19 = (f32[2,64,384]{2,1,0:T(8,128)S(1)}, f32[2,64,384]{2,1,0:T(8,128)S(1)}, u32[]{:S(2)}, u32[]{:S(2)}) collective-permute-start(f32[2,64,384]{2,1,0:T(8,128)S(1)} %get-tuple-element.87), channel_id=1, source_target_pairs={{0,8},{8,16},{16,24},{1,9},{9,17},{17,25},{2,10},{10,18},{18,26},{... | collective-permute-start | bytes 589832 | tf_op jit(solution)/shard_map/ppermute | solution.py:333
  117.8 10.4 %collective-permute-start.20 = (f32[2,64,384]{2,1,0:T(8,128)S(1)}, f32[2,64,384]{2,1,0:T(8,128)S(1)}, u32[]{:S(2)}, u32[]{:S(2)}) collective-permute-start(f32[2,64,384]{2,1,0:T(8,128)S(1)} %get-tuple-element.88), channel_id=1, source_target_pairs={{8,0},{16,8},{24,16},{9,1},{17,9},{25,17},{10,2},{18,10},{26,18},{... | collective-permute-start | bytes 589832 | tf_op jit(solution)/shard_map/ppermute | solution.py:333
  120.1 8.1 %collective-permute-start.22 = (f32[2,64,128]{2,1,0:T(8,128)S(1)}, f32[2,64,128]{2,1,0:T(8,128)S(1)}, u32[]{:S(2)}, u32[]{:S(2)}) collective-permute-start(f32[2,64,128]{2,1,0:T(8,128)S(1)} %pad_maximum_fusion.3), channel_id=1, source_target_pairs={{8,0},{16,8},{24,16},{9,1},{17,9},{25,17},{10,2},{18,10},{26,18},{... | collective-permute-start | bytes 196616 | tf_op jit(solution)/shard_map/ppermute | solution.py:333
  121.4 6.8 %collective-permute-start.21 = (f32[2,64,128]{2,1,0:T(8,128)S(1)}, f32[2,64,128]{2,1,0:T(8,128)S(1)}, u32[]{:S(2)}, u32[]{:S(2)}) collective-permute-start(f32[2,64,128]{2,1,0:T(8,128)S(1)} %pad_maximum_fusion.2), channel_id=1, source_target_pairs={{0,8},{8,16},{16,24},{1,9},{9,17},{17,25},{2,10},{10,18},{18,26},{... | collective-permute-start | bytes 196616 | tf_op jit(solution)/shard_map/ppermute | solution.py:333
  125.5 2.7 %copy-start.3 = (f32[2,384,384]{2,1,0:T(8,128)S(1)}, f32[2,384,384]{2,1,0:T(8,128)}, u32[]{:S(2)}) copy-start(f32[2,384,384]{2,1,0:T(8,128)} %refs_0_.1) | copy-start | bytes 3538948

commit v5 on v4

--- a/solution.py
+++ b/solution.py
@@ -170,6 +170,15 @@
             power[slots * size :, :] = row.astype(F32)
 
 
+def factor_kernel(arrived, own, measured, *refs):
+    out = refs[-1]
+    count = own.shape[0]
+    total = own[...] + arrived[:count, :]
+    out[:count, :] = measured[...] / jnp.sqrt(total + EPSILON)
+    if len(refs) > 1:
+        out[count:, :] = refs[0][...]
+
+
 def add_patch(total, channel, y, tile, shift, value, lane):
     moved = pltpu.roll(value, shift, 1)
     rows = pl.ds(y, value.shape[0])
@@ -379,9 +388,7 @@
     )
     left = move(edge_r, "col", line("col", 1))
     right = move(edge_l, "col", line("col", -1))
-    (frame,) = call(
-        frame_kernel, [(2, tiles, rows, size)], [VMEM] * 5, (obj, top, bot, left, right), 10**6
-    )
+    (frame,) = call(frame_kernel, [(2, tiles, rows, size)], [VMEM] * 5, (obj, top, bot, left, right), 10**6)
 
     slots = scans // 2
     halves = ((0, slots), (slots, scans - slots))
@@ -423,13 +430,14 @@
                     metas[which] = arrived[count * size : count * size + 1].astype(jnp.int32)
                 forward(which, [(start, count)], arrived)
             else:
-                power[0, start] += arrived[: count * size]
-    factors = {
-        start: measured[0, 0, start : start + count].reshape(count * size, size) / jnp.sqrt(power[0, start] + EPSILON)
-        for start, count in halves
-    }
+                power[1, start] = arrived
     beside = jnp.concatenate([left[rows : rows + 1], right[rows : rows + 1], jnp.zeros((6, size), F32)])
-    factors[0] = jnp.concatenate([factors[0], beside])
+    factors = {}
+    for start, count in halves:
+        args = [power[1, start], power[0, start], measured[0, 0, start : start + count].reshape(-1, size)]
+        args += [beside] if start == 0 else []
+        height = count * size + (beside.shape[0] if start == 0 else 0)
+        (factors[start],) = call(factor_kernel, [(height, size)], [VMEM] * len(args), args, 10**6)
 
     row_count = lax.axis_size("row")
     kept = min(row_count, offsets_count + 2)
@@ -461,13 +469,10 @@
         if which:
             for start, _ in halves:
                 value = move(factors[start], "row", ring("row", 1))
-                if start == halves[-1][0]:
-                    value, weight = lax.optimization_barrier((value, weight))
-                    if which < most:
-                        value, total = lax.optimization_barrier((value, total))
+                if start == 0 and which < most:
+                    value, total = lax.optimization_barrier((value, total))
                 factors[start] = value
-                if start == halves[-1][0]:
-                    add_weight(which, which, factors[0][slots * size :])
+            add_weight(which, which, factors[0][slots * size :])
         else:
             add_weight(0, 0, beside)
         groups = [[part] for part in halves] if which == most else [list(halves)]
@@ -493,9 +498,7 @@
             )
     grad_in = send_rims(*sides)
 
-    (new_object,) = call(
-        final_kernel, [obj.shape], [VMEM] * 9, (obj, weight, total, *grad_in), 10**6
-    )
+    (new_object,) = call(final_kernel, [obj.shape], [VMEM] * 9, (obj, weight, total, *grad_in), 10**6)
     return new_object
 
 

time: 131 us -> 130 us (level)
  starting transfers between devices: 55 us -> 50.9 us
  waiting for transfers between devices: 33.4 us -> 37.2 us
    ppermute x23, starting transfers between devices: 55 us -> 50.9 us  [move(): return lax.ppermute(x, axis, pairs)]
    ppermute x23, waiting for transfers between devices: 33.4 us -> 37.2 us  [move(): return lax.ppermute(x, axis, pairs)]
    pallas_call x19 -> x21, Pallas kernels: 35.7 us -> 36 us  [call(): pl.pallas_call(kernel, out_shape=[s if hasattr(s, 'dtype') else jax.Shape...]
  transfers between devices with their start and end apart: 23 -> 23, of which waited for: 12 -> 12; matrix products, arithmetic and copies ran while one was open for 2% -> 1% of each run, Pallas kernels for 21% -> 24%
where the time goes in v5:
time: 130 us; the launch traced here: 129 us
  starting transfers between devices  50.9 us (39%)
  waiting for transfers between devices  37.2 us (29%)
  Pallas kernels  36 us (28%)
  local copies, waits for them, and re-layouts  4.15 us (3%)
    ppermute x23, starting transfers between devices, move(): return lax.ppermute(x, axis, pairs)  50.9 us
    ppermute x23, waiting for transfers between devices, move(): return lax.ppermute(x, axis, pairs)  37.2 us
    pallas_call x21, Pallas kernels, call(): pl.pallas_call(kernel, out_shape=[s if hasattr(s, 'dtype') else jax.Shape...  36 us
    unnamed x12, local copies, waits for them, and re-layouts  2.81 us
  transfers between devices with their start and end apart: 23, of which 12 were waited for; matrix products, arithmetic and copies ran while one was open for 1% of the time, Pallas kernels for 24%

profile of v5, /device:TPU:1, one launch (start us, length us, event | category | flops | bytes accessed | tf_op | source)
XLA Modules:
  0.0 129.5 jit_solution(5318564197074213251)
XLA Ops:
  1.1 4.0 %collective-permute-start.1 = (f32[2,64,384]{2,1,0:T(8,128)S(1)}, f32[2,64,384]{2,1,0:T(8,128)S(1)}, u32[]{:S(2)}, u32[]{:S(2)}) collective-permute-start(f32[2,64,384]{2,1,0:T(8,128)S(1)} %get-tuple-element.78), channel_id=1, source_target_pairs={{0,8},{8,16},{16,24},{1,9},{9,17},{17,25},{2,10},{10,18},{18,26},{... | collective-permute-start | bytes 589832 | tf_op jit(solution)/shard_map/ppermute | solution.py:342
  10.7 1.8 %collective-permute-done.2.bot = f32[2,64,384]{2,1,0:T(8,128)S(1)} collective-permute-done((f32[2,64,384]{2,1,0:T(8,128)S(1)}, f32[2,64,384]{2,1,0:T(8,128)S(1)}, u32[]{:S(2)}, u32[]{:S(2)}) %collective-permute-start.2) | collective-permute-done | bytes 196640 | tf_op jit(solution)/shard_map/ppermute | solution.py:342
  12.8 4.8 %collective-permute-start.3 = (f32[520,128]{1,0:T(8,128)S(1)}, f32[520,128]{1,0:T(8,128)S(1)}, u32[]{:S(2)}, u32[]{:S(2)}) collective-permute-start(f32[520,128]{1,0:T(8,128)S(1)} %get-tuple-element.94), channel_id=1, source_target_pairs={{0,1},{1,2},{2,3},{3,4},{4,5},{5,6},{6,7},{8,9},{9,10},{10,11},{11... | collective-permute-start | bytes 798728 | tf_op jit(solution)/shard_map/ppermute | solution.py:342
  17.6 2.1 %collective-permute-start.4 = (f32[520,128]{1,0:T(8,128)S(1)}, f32[520,128]{1,0:T(8,128)S(1)}, u32[]{:S(2)}, u32[]{:S(2)}) collective-permute-start(f32[520,128]{1,0:T(8,128)S(1)} %get-tuple-element.93), channel_id=1, source_target_pairs={{1,0},{2,1},{3,2},{4,3},{5,4},{6,5},{7,6},{9,8},{10,9},{11,10},{12... | collective-permute-start | bytes 798728 | tf_op jit(solution)/shard_map/ppermute | solution.py:342
  19.7 1.8 %collective-permute-start = (s32[1,128]{1,0:T(1,128)S(1)}, s32[1,128]{1,0:T(1,128)S(1)}, u32[]{:S(2)}, u32[]{:S(2)}) collective-permute-start(s32[1,128]{1,0:T(1,128)S(1)} %get-tuple-element.41.refs_0_), channel_id=1, source_target_pairs={{0,24},{8,0},{16,8},{24,16},{1,25},{9,1},{17,9},{25,17},{2,26},{10... | collective-permute-start | bytes 1544 | tf_op jit(solution)/shard_map/ppermute | solution.py:342
  21.5 4.0 %collective-permute-done.4.right = f32[520,128]{1,0:T(8,128)S(1)} collective-permute-done((f32[520,128]{1,0:T(8,128)S(1)}, f32[520,128]{1,0:T(8,128)S(1)}, u32[]{:S(2)}, u32[]{:S(2)}) %collective-permute-start.4) | collective-permute-done | bytes 266272 | tf_op jit(solution)/shard_map/ppermute | solution.py:342
  27.8 1.8 %collective-permute-start.5 = (f32[520,128]{1,0:T(8,128)S(1)}, f32[520,128]{1,0:T(8,128)S(1)}, u32[]{:S(2)}, u32[]{:S(2)}) collective-permute-start(f32[520,128]{1,0:T(8,128)S(1)} %get-tuple-element.44), channel_id=1, source_target_pairs={{0,24},{8,0},{16,8},{24,16},{1,25},{9,1},{17,9},{25,17},{2,26},{10... | collective-permute-start | bytes 798728 | tf_op jit(solution)/shard_map/ppermute | solution.py:342
  31.3 1.8 %collective-permute-start.9 = (f32[512,128]{1,0:T(8,128)S(1)}, f32[512,128]{1,0:T(8,128)S(1)}, u32[]{:S(2)}, u32[]{:S(2)}) collective-permute-start(f32[512,128]{1,0:T(8,128)S(1)} %get-tuple-element.52), channel_id=1, source_target_pairs={{0,24},{8,0},{16,8},{24,16},{1,25},{9,1},{17,9},{25,17},{2,26},{10... | collective-permute-start | bytes 786440 | tf_op jit(solution)/shard_map/ppermute | solution.py:342
  33.1 2.7 %collective-permute-done.5.refs_4_ = f32[520,128]{1,0:T(8,128)S(1)} collective-permute-done((f32[520,128]{1,0:T(8,128)S(1)}, f32[520,128]{1,0:T(8,128)S(1)}, u32[]{:S(2)}, u32[]{:S(2)}) %collective-permute-start.5) | collective-permute-done | bytes 266272 | tf_op jit(solution)/shard_map/ppermute | solution.py:342
  37.4 3.9 %collective-permute-start.6 = (f32[520,128]{1,0:T(8,128)S(1)}, f32[520,128]{1,0:T(8,128)S(1)}, u32[]{:S(2)}, u32[]{:S(2)}) collective-permute-start(f32[520,128]{1,0:T(8,128)S(1)} %get-tuple-element.45), channel_id=1, source_target_pairs={{0,24},{8,0},{16,8},{24,16},{1,25},{9,1},{17,9},{25,17},{2,26},{10... | collective-permute-start | bytes 798728 | tf_op jit(solution)/shard_map/ppermute | solution.py:342
  41.4 1.6 %shard_map.81 = (f32[256,512]{1,0:T(8,128)S(1)}, f32[4,2,128,128]{3,2,1,0:T(8,128)S(1)}, f32[512,128]{1,0:T(8,128)S(1)}) custom-call(s32[1,128]{1,0:T(1,128)S(1)} %slice_convert_fusion.4.refs_0_, f32[2,4,512,128]{3,2,1,0:T(8,128)S(1)} %shard_map.74.refs_1_, f32[4,2,128,128]{3,2,1,0:T(8,128)S(1)} %copy-done, bf16[4,256,256]{2,1,0:T(8,128)(2,1)S(1)} %copy-done.1, ...), custom_call_target="tpu_custom_call" | custom-call | flops 402653184 | bytes 1048576 | tf_op jit(solution)/shard_map/pallas_call | solution.py:23
  43.0 2.6 %collective-permute-start.10 = (f32[512,128]{1,0:T(8,128)S(1)}, f32[512,128]{1,0:T(8,128)S(1)}, u32[]{:S(2)}, u32[]{:S(2)}) collective-permute-start(f32[512,128]{1,0:T(8,128)S(1)} %get-tuple-element.53), channel_id=1, source_target_pairs={{0,24},{8,0},{16,8},{24,16},{1,25},{9,1},{17,9},{25,17},{2,26},{10... | collective-permute-start | bytes 786440 | tf_op jit(solution)/shard_map/ppermute | solution.py:342
  48.3 4.1 %collective-permute-start.7 = (f32[520,128]{1,0:T(8,128)S(1)}, f32[520,128]{1,0:T(8,128)S(1)}, u32[]{:S(2)}, u32[]{:S(2)}) collective-permute-start(f32[520,128]{1,0:T(8,128)S(1)} %get-tuple-element.46), channel_id=1, source_target_pairs={{0,24},{8,0},{16,8},{24,16},{1,25},{9,1},{17,9},{25,17},{2,26},{10... | collective-permute-start | bytes 798728 | tf_op jit(solution)/shard_map/ppermute | solution.py:342
  54.0 3.9 %collective-permute-start.11 = (f32[512,128]{1,0:T(8,128)S(1)}, f32[512,128]{1,0:T(8,128)S(1)}, u32[]{:S(2)}, u32[]{:S(2)}) collective-permute-start(f32[512,128]{1,0:T(8,128)S(1)} %get-tuple-element.54), channel_id=1, source_target_pairs={{0,24},{8,0},{16,8},{24,16},{1,25},{9,1},{17,9},{25,17},{2,26},{10... | collective-permute-start | bytes 786440 | tf_op jit(solution)/shard_map/ppermute | solution.py:342
  57.9 2.1 %shard_map.78 = (f32[256,512]{1,0:T(8,128)S(1)}, f32[4,2,128,128]{3,2,1,0:T(8,128)S(1)}, f32[512,128]{1,0:T(8,128)S(1)}, f32[256,512]{1,0:T(8,128)S(1)}, f32[4,2...) custom-call(s32[1,128]{1,0:T(1,128)S(1)} %get-tuple-element.41.refs_0_, f32[2,4,512,128]{3,2,1,0:T(8,128)S(1)} %shard_map.74.refs_1_, ...), custom_call_target="tpu_custom_call" | custom-call | flops 805306368 | bytes 1048576 | tf_op jit(solution)/shard_map/pallas_call | solution.py:23
  60.1 2.2 %collective-permute-done.11.arrived = f32[512,128]{1,0:T(8,128)S(1)} collective-permute-done((f32[512,128]{1,0:T(8,128)S(1)}, f32[512,128]{1,0:T(8,128)S(1)}, u32[]{:S(2)}, u32[]{:S(2)}) %collective-permute-start.11) | collective-permute-done | bytes 262176 | tf_op jit(solution)/shard_map/ppermute | solution.py:342
  63.3 2.5 %shard_map.86.refs_2_ = f32[1,5,640,128]{3,2,1,0:T(8,128)S(1)} custom-call(s32[3,128]{1,0:T(4,128)S(1)} %pad_add_fusion.3.refs_0_, f32[4,2,128,128]{3,2,1,0:T(8,128)S(1)} %copy-done), custom_call_target="tpu_custom_call" | custom-call | flops 402653184 | bytes 1048576 | tf_op jit(solution)/shard_map/pallas_call | solution.py:23
  65.9 2.3 %shard_map.84.refs_9_ = f32[2,4,512,128]{3,2,1,0:T(8,128)S(1)} custom-call(s32[1,128]{1,0:T(1,128)S(1)} %get-tuple-element.41.refs_0_, f32[4,2,128,128]{3,2,1,0:T(8,128)S(1)} %copy-done, bf16[4,256,256]{2,1,0:T(8,128)(2,1)S(1)} %copy-done.1, f32[256,512]{1,0:T(8,128)S(1)} %get-tuple-element.48.refs_3_, f32[4,2,128,128]{3,2,1,0:T(8,128)S(1)} %get-tuple-element.49.refs_4_, ...), custom_call_target="tpu_custom_call" | custom-call | flops 805306368 | bytes 1048576 | tf_op jit(solution)/shard_map/pallas_call | solution.py:23
  68.1 4.9 %collective-permute-done.13.refs_8_ = f32[512,128]{1,0:T(8,128)S(1)} collective-permute-done((f32[512,128]{1,0:T(8,128)S(1)}, f32[512,128]{1,0:T(8,128)S(1)}, u32[]{:S(2)}, u32[]{:S(2)}) %collective-permute-start.13) | collective-permute-done | bytes 262176 | tf_op jit(solution)/shard_map/ppermute | solution.py:342
  73.1 5.7 %collective-permute-done.8.refs_5_ = f32[520,128]{1,0:T(8,128)S(1)} collective-permute-done((f32[520,128]{1,0:T(8,128)S(1)}, f32[520,128]{1,0:T(8,128)S(1)}, u32[]{:S(2)}, u32[]{:S(2)}) %collective-permute-start.8) | collective-permute-done | bytes 266272 | tf_op jit(solution)/shard_map/ppermute | solution.py:342
  78.8 2.8 %shard_map.87.refs_2_ = f32[1,5,640,128]{3,2,1,0:T(8,128)S(1)} custom-call(s32[3,128]{1,0:T(4,128)S(1)} %pad_add_fusion.2.refs_0_, f32[4,2,128,128]{3,2,1,0:T(8,128)S(1)} %copy-done, f32[1,5,640,128]{3,2,1,0:T(8,128)S(1)} %shard_map.86.refs_2_), custom_call_target="tpu_custom_call", output_to_operand_aliasing={{}: (2, {})} | custom-call | flops 402653184 | bytes 1048576 | tf_op jit(solution)/shard_map/pallas_call | solution.py:23
  81.6 2.1 %shard_map.85.refs_9_ = f32[2,4,512,128]{3,2,1,0:T(8,128)S(1)} custom-call(s32[1,128]{1,0:T(1,128)S(1)} %slice_convert_fusion.3.refs_0_, f32[4,2,128,128]{3,2,1,0:T(8,128)S(1)} %copy-done, bf16[4,256,256]{2,1,0:T(8,128)(2,1)S(1)} %copy-done.1, f32[256,512]{1,0:T(8,128)S(1)} %get-tuple-element.57.refs_3_, ...), custom_call_target="tpu_custom_call", output_to_operand_aliasing={{}: (9, {})} | custom-call | flops 805306368 | bytes 1048576 | tf_op jit(solution)/shard_map/pallas_call | solution.py:23
  84.4 5.7 %collective-permute-done.12.refs_5_ = f32[520,128]{1,0:T(8,128)S(1)} collective-permute-done((f32[520,128]{1,0:T(8,128)S(1)}, f32[520,128]{1,0:T(8,128)S(1)}, u32[]{:S(2)}, u32[]{:S(2)}) %collective-permute-start.12) | collective-permute-done | bytes 266272 | tf_op jit(solution)/shard_map/ppermute | solution.py:342
  90.1 2.1 %shard_map.90.refs_6_ = f32[2,4,512,128]{3,2,1,0:T(8,128)S(1)} custom-call(s32[1,128]{1,0:T(1,128)S(1)} %slice_convert_fusion.4.refs_0_, f32[4,2,128,128]{3,2,1,0:T(8,128)S(1)} %copy-done, bf16[4,256,256]{2,1,0:T(8,128)(2,1)S(1)} %copy-done.1, f32[256,512]{1,0:T(8,128)S(1)} %get-tuple-element.67.refs_3_, ...), custom_call_target="tpu_custom_call", output_to_operand_aliasing={{}: (9, {})} | custom-call | flops 805306368 | bytes 1048576 | tf_op jit(solution)/shard_map/pallas_call | solution.py:23
  92.2 6.7 %collective-permute-done.14.refs_5_ = f32[520,128]{1,0:T(8,128)S(1)} collective-permute-done((f32[520,128]{1,0:T(8,128)S(1)}, f32[520,128]{1,0:T(8,128)S(1)}, u32[]{:S(2)}, u32[]{:S(2)}) %collective-permute-start.14) | collective-permute-done | bytes 266272 | tf_op jit(solution)/shard_map/ppermute | solution.py:342
  100.5 1.9 %shard_map.92 = (f32[2,4,512,128]{3,2,1,0:T(8,128)S(1)}, f32[512,128]{1,0:T(8,128)S(1)}, f32[512,128]{1,0:T(8,128)S(1)}, f32[2,64,384]{2,1,0:T(8,128)S(1)}, f32[2,64,384]{2,1,0:T(8,128)S(1)}) custom-call(s32[1,128]{1,0:T(1,128)S(1)} %collective-permute-done.refs_0_, f32[4,2,128,128]{3,2,1,0:T(8,128)S(1)} %copy-done, ...), custom_call_target="tpu_custom_call", output_to_operand_aliasing={{0}: (6, {})} | custom-call | flops 402653184 | bytes 1048576 | tf_op jit(solution)/shard_map/pallas_call | solution.py:23
  102.3 1.9 %collective-permute-start.18 = (f32[512,128]{1,0:T(8,128)S(1)}, f32[512,128]{1,0:T(8,128)S(1)}, u32[]{:S(2)}, u32[]{:S(2)}) collective-permute-start(f32[512,128]{1,0:T(8,128)S(1)} %get-tuple-element.74), channel_id=1, source_target_pairs={{1,0},{2,1},{3,2},{4,3},{5,4},{6,5},{7,6},{9,8},{10,9},{11,10},{12... | collective-permute-start | bytes 786440 | tf_op jit(solution)/shard_map/ppermute | solution.py:342
  104.3 2.9 %shard_map.88.refs_2_ = f32[1,5,640,128]{3,2,1,0:T(8,128)S(1)} custom-call(s32[3,128]{1,0:T(4,128)S(1)} %pad_add_fusion.1.refs_0_, f32[4,2,128,128]{3,2,1,0:T(8,128)S(1)} %copy-done, f32[1,5,640,128]{3,2,1,0:T(8,128)S(1)} %shard_map.87.refs_2_), custom_call_target="tpu_custom_call", output_to_operand_aliasing={{}: (2, {})} | custom-call | flops 402653184 | bytes 1048576 | tf_op jit(solution)/shard_map/pallas_call | solution.py:23
  107.1 9.0 %collective-permute-start.17 = (f32[512,128]{1,0:T(8,128)S(1)}, f32[512,128]{1,0:T(8,128)S(1)}, u32[]{:S(2)}, u32[]{:S(2)}) collective-permute-start(f32[512,128]{1,0:T(8,128)S(1)} %get-tuple-element.73), channel_id=1, source_target_pairs={{0,1},{1,2},{2,3},{3,4},{4,5},{5,6},{6,7},{8,9},{9,10},{10,11},{11... | collective-permute-start | bytes 786440 | tf_op jit(solution)/shard_map/ppermute | solution.py:342
  119.4 3.4 %collective-permute-start.21 = (f32[2,64,128]{2,1,0:T(8,128)S(1)}, f32[2,64,128]{2,1,0:T(8,128)S(1)}, u32[]{:S(2)}, u32[]{:S(2)}) collective-permute-start(f32[2,64,128]{2,1,0:T(8,128)S(1)} %pad_maximum_fusion.2), channel_id=1, source_target_pairs={{0,8},{8,16},{16,24},{1,9},{9,17},{17,25},{2,10},{10,18},{18,26},{... | collective-permute-start | bytes 196616 | tf_op jit(solution)/shard_map/ppermute | solution.py:342
  124.1 2.6 %shard_map.89.refs_1_ = f32[1,5,640,128]{3,2,1,0:T(8,128)S(1)} custom-call(s32[3,128]{1,0:T(4,128)S(1)} %pad_add_fusion.refs_0_, f32[4,2,128,128]{3,2,1,0:T(8,128)S(1)} %copy-done, f32[1,5,640,128]{3,2,1,0:T(8,128)S(1)} %shard_map.88.refs_2_), custom_call_target="tpu_custom_call", output_to_operand_aliasing={{}: (2, {})} | custom-call | flops 402653184 | bytes 1048576 | tf_op jit(solution)/shard_map/pallas_call | solution.py:23
  127.8 1.6 %shard_map.93 = f32[2,384,384]{2,1,0:T(8,128)} custom-call(f32[2,384,384]{2,1,0:T(8,128)S(1)} %copy-done.3, f32[1,5,640,128]{3,2,1,0:T(8,128)S(1)} %shard_map.89.refs_1_, f32[2,4,512,128]{3,2,1,0:T(8,128)S(1)} %get-tuple-element.72.refs_2_, f32[512,128]{1,0:T(8,128)S(1)} %collective-permute-done.17.refs_3_, f32[512,128]{1,0:T(8,128)S(1)} %collective-permute-done.18.refs_4_, ...), custom_call_target="tpu_custom_call" | custom-call | flops 1000000 | bytes 1048576 | tf_op jit(solution)/shard_map/pallas_call | solution.py:23
  (73 shorter events, 25.1 us)
Async XLA Ops:
  1.1 11.5 %collective-permute-start.1 = (f32[2,64,384]{2,1,0:T(8,128)S(1)}, f32[2,64,384]{2,1,0:T(8,128)S(1)}, u32[]{:S(2)}, u32[]{:S(2)}) collective-permute-start(f32[2,64,384]{2,1,0:T(8,128)S(1)} %get-tuple-element.78), channel_id=1, source_target_pairs={{0,8},{8,16},{16,24},{1,9},{9,17},{17,25},{2,10},{10,18},{18,26},{... | collective-permute-start | bytes 589832 | tf_op jit(solution)/shard_map/ppermute | solution.py:342
  5.1 7.4 %collective-permute-start.2 = (f32[2,64,384]{2,1,0:T(8,128)S(1)}, f32[2,64,384]{2,1,0:T(8,128)S(1)}, u32[]{:S(2)}, u32[]{:S(2)}) collective-permute-start(f32[2,64,384]{2,1,0:T(8,128)S(1)} %get-tuple-element.77), channel_id=1, source_target_pairs={{8,0},{16,8},{24,16},{9,1},{17,9},{25,17},{10,2},{18,10},{26,18},{... | collective-permute-start | bytes 589832 | tf_op jit(solution)/shard_map/ppermute | solution.py:342
  8.6 1.3 copy-start.2
  12.8 8.7 %collective-permute-start.3 = (f32[520,128]{1,0:T(8,128)S(1)}, f32[520,128]{1,0:T(8,128)S(1)}, u32[]{:S(2)}, u32[]{:S(2)}) collective-permute-start(f32[520,128]{1,0:T(8,128)S(1)} %get-tuple-element.94), channel_id=1, source_target_pairs={{0,1},{1,2},{2,3},{3,4},{4,5},{5,6},{6,7},{8,9},{9,10},{10,11},{11... | collective-permute-start | bytes 798728 | tf_op jit(solution)/shard_map/ppermute | solution.py:342
  17.6 8.5 %copy-start = (f32[4,2,128,128]{3,2,1,0:T(8,128)S(1)}, f32[4,2,128,128]{3,2,1,0:T(8,128)}, u32[]{:S(2)}) copy-start(f32[4,2,128,128]{3,2,1,0:T(8,128)} %refs_1_.17) | copy-start | bytes 1572868
  17.6 8.5 %copy-start.1 = (bf16[4,256,256]{2,1,0:T(8,128)(2,1)S(1)}, bf16[4,256,256]{2,1,0:T(8,128)(2,1)}, u32[]{:S(2)}) copy-start(bf16[4,256,256]{2,1,0:T(8,128)(2,1)} %constant.9.clone.refs_3_.refs_2_) | copy-start | bytes 1572868
  17.6 7.9 %collective-permute-start.4 = (f32[520,128]{1,0:T(8,128)S(1)}, f32[520,128]{1,0:T(8,128)S(1)}, u32[]{:S(2)}, u32[]{:S(2)}) collective-permute-start(f32[520,128]{1,0:T(8,128)S(1)} %get-tuple-element.93), channel_id=1, source_target_pairs={{1,0},{2,1},{3,2},{4,3},{5,4},{6,5},{7,6},{9,8},{10,9},{11,10},{12... | collective-permute-start | bytes 798728 | tf_op jit(solution)/shard_map/ppermute | solution.py:342
  19.7 6.4 %collective-permute-start = (s32[1,128]{1,0:T(1,128)S(1)}, s32[1,128]{1,0:T(1,128)S(1)}, u32[]{:S(2)}, u32[]{:S(2)}) collective-permute-start(s32[1,128]{1,0:T(1,128)S(1)} %get-tuple-element.41.refs_0_), channel_id=1, source_target_pairs={{0,24},{8,0},{16,8},{24,16},{1,25},{9,1},{17,9},{25,17},{2,26},{10... | collective-permute-start | bytes 1544 | tf_op jit(solution)/shard_map/ppermute | solution.py:342
  27.8 8.0 %collective-permute-start.5 = (f32[520,128]{1,0:T(8,128)S(1)}, f32[520,128]{1,0:T(8,128)S(1)}, u32[]{:S(2)}, u32[]{:S(2)}) collective-permute-start(f32[520,128]{1,0:T(8,128)S(1)} %get-tuple-element.44), channel_id=1, source_target_pairs={{0,24},{8,0},{16,8},{24,16},{1,25},{9,1},{17,9},{25,17},{2,26},{10... | collective-permute-start | bytes 798728 | tf_op jit(solution)/shard_map/ppermute | solution.py:342
  31.3 10.1 %collective-permute-start.9 = (f32[512,128]{1,0:T(8,128)S(1)}, f32[512,128]{1,0:T(8,128)S(1)}, u32[]{:S(2)}, u32[]{:S(2)}) collective-permute-start(f32[512,128]{1,0:T(8,128)S(1)} %get-tuple-element.52), channel_id=1, source_target_pairs={{0,24},{8,0},{16,8},{24,16},{1,25},{9,1},{17,9},{25,17},{2,26},{10... | collective-permute-start | bytes 786440 | tf_op jit(solution)/shard_map/ppermute | solution.py:342
  35.8 5.6 %copy-start.4 = (f32[1,1,8,128,128]{4,3,2,1,0:T(8,128)S(1)}, f32[1,1,8,128,128]{4,3,2,1,0:T(8,128)}, u32[]{:S(2)}) copy-start(f32[1,1,8,128,128]{4,3,2,1,0:T(8,128)} %param.12) | copy-start | bytes 1572868
  37.4 9.3 %collective-permute-start.6 = (f32[520,128]{1,0:T(8,128)S(1)}, f32[520,128]{1,0:T(8,128)S(1)}, u32[]{:S(2)}, u32[]{:S(2)}) collective-permute-start(f32[520,128]{1,0:T(8,128)S(1)} %get-tuple-element.45), channel_id=1, source_target_pairs={{0,24},{8,0},{16,8},{24,16},{1,25},{9,1},{17,9},{25,17},{2,26},{10... | collective-permute-start | bytes 798728 | tf_op jit(solution)/shard_map/ppermute | solution.py:342
  43.0 9.4 %collective-permute-start.10 = (f32[512,128]{1,0:T(8,128)S(1)}, f32[512,128]{1,0:T(8,128)S(1)}, u32[]{:S(2)}, u32[]{:S(2)}) collective-permute-start(f32[512,128]{1,0:T(8,128)S(1)} %get-tuple-element.53), channel_id=1, source_target_pairs={{0,24},{8,0},{16,8},{24,16},{1,25},{9,1},{17,9},{25,17},{2,26},{10... | collective-permute-start | bytes 786440 | tf_op jit(solution)/shard_map/ppermute | solution.py:342
  48.3 14.2 %collective-permute-start.7 = (f32[520,128]{1,0:T(8,128)S(1)}, f32[520,128]{1,0:T(8,128)S(1)}, u32[]{:S(2)}, u32[]{:S(2)}) collective-permute-start(f32[520,128]{1,0:T(8,128)S(1)} %get-tuple-element.46), channel_id=1, source_target_pairs={{0,24},{8,0},{16,8},{24,16},{1,25},{9,1},{17,9},{25,17},{2,26},{10... | collective-permute-start | bytes 798728 | tf_op jit(solution)/shard_map/ppermute | solution.py:342
  54.0 8.3 %collective-permute-start.11 = (f32[512,128]{1,0:T(8,128)S(1)}, f32[512,128]{1,0:T(8,128)S(1)}, u32[]{:S(2)}, u32[]{:S(2)}) collective-permute-start(f32[512,128]{1,0:T(8,128)S(1)} %get-tuple-element.54), channel_id=1, source_target_pairs={{0,24},{8,0},{16,8},{24,16},{1,25},{9,1},{17,9},{25,17},{2,26},{10... | collective-permute-start | bytes 786440 | tf_op jit(solution)/shard_map/ppermute | solution.py:342
  62.4 10.6 %collective-permute-start.13 = (f32[512,128]{1,0:T(8,128)S(1)}, f32[512,128]{1,0:T(8,128)S(1)}, u32[]{:S(2)}, u32[]{:S(2)}) collective-permute-start(f32[512,128]{1,0:T(8,128)S(1)} %shard_map.83.refs_8_), channel_id=1, source_target_pairs={{0,8},{8,16},{16,24},{24,0},{1,9},{9,17},{17,25},{25,1},{2,10},{10... | collective-permute-start | bytes 786440 | tf_op jit(solution)/shard_map/ppermute | solution.py:342
  62.6 16.1 %collective-permute-start.8 = (f32[520,128]{1,0:T(8,128)S(1)}, f32[520,128]{1,0:T(8,128)S(1)}, u32[]{:S(2)}, u32[]{:S(2)}) collective-permute-start(f32[520,128]{1,0:T(8,128)S(1)} %shard_map.79.refs_5_), channel_id=1, source_target_pairs={{0,8},{8,16},{16,24},{24,0},{1,9},{9,17},{17,25},{25,1},{2,10},{10... | collective-permute-start | bytes 798728 | tf_op jit(solution)/shard_map/ppermute | solution.py:342
  73.0 11.3 %collective-permute-start.15 = (f32[512,128]{1,0:T(8,128)S(1)}, f32[512,128]{1,0:T(8,128)S(1)}, u32[]{:S(2)}, u32[]{:S(2)}) collective-permute-start(f32[512,128]{1,0:T(8,128)S(1)} %collective-permute-done.13.refs_8_), channel_id=1, source_target_pairs={{0,8},{8,16},{16,24},{24,0},{1,9},{9,17},{17,25},{25,1},{2,10},{10... | collective-permute-start | bytes 786440 | tf_op jit(solution)/shard_map/ppermute | solution.py:342
  78.8 11.3 %collective-permute-start.12 = (f32[520,128]{1,0:T(8,128)S(1)}, f32[520,128]{1,0:T(8,128)S(1)}, u32[]{:S(2)}, u32[]{:S(2)}) collective-permute-start(f32[520,128]{1,0:T(8,128)S(1)} %collective-permute-done.8.refs_5_), channel_id=1, source_target_pairs={{0,8},{8,16},{16,24},{24,0},{1,9},{9,17},{17,25},{25,1},{2,10},{10... | collective-permute-start | bytes 798728 | tf_op jit(solution)/shard_map/ppermute | solution.py:342
  84.4 16.1 %collective-permute-start.16 = (f32[512,128]{1,0:T(8,128)S(1)}, f32[512,128]{1,0:T(8,128)S(1)}, u32[]{:S(2)}, u32[]{:S(2)}) collective-permute-start(f32[512,128]{1,0:T(8,128)S(1)} %collective-permute-done.15.refs_8_), channel_id=1, source_target_pairs={{0,8},{8,16},{16,24},{24,0},{1,9},{9,17},{17,25},{25,1},{2,10},{10... | collective-permute-start | bytes 786440 | tf_op jit(solution)/shard_map/ppermute | solution.py:342
  90.1 8.8 %collective-permute-start.14 = (f32[520,128]{1,0:T(8,128)S(1)}, f32[520,128]{1,0:T(8,128)S(1)}, u32[]{:S(2)}, u32[]{:S(2)}) collective-permute-start(f32[520,128]{1,0:T(8,128)S(1)} %collective-permute-done.12.refs_5_), channel_id=1, source_target_pairs={{0,8},{8,16},{16,24},{24,0},{1,9},{9,17},{17,25},{25,1},{2,10},{10... | collective-permute-start | bytes 798728 | tf_op jit(solution)/shard_map/ppermute | solution.py:342
  102.3 16.4 %collective-permute-start.18 = (f32[512,128]{1,0:T(8,128)S(1)}, f32[512,128]{1,0:T(8,128)S(1)}, u32[]{:S(2)}, u32[]{:S(2)}) collective-permute-start(f32[512,128]{1,0:T(8,128)S(1)} %get-tuple-element.74), channel_id=1, source_target_pairs={{1,0},{2,1},{3,2},{4,3},{5,4},{6,5},{7,6},{9,8},{10,9},{11,10},{12... | collective-permute-start | bytes 786440 | tf_op jit(solution)/shard_map/ppermute | solution.py:342
  107.1 12.3 %collective-permute-start.17 = (f32[512,128]{1,0:T(8,128)S(1)}, f32[512,128]{1,0:T(8,128)S(1)}, u32[]{:S(2)}, u32[]{:S(2)}) collective-permute-start(f32[512,128]{1,0:T(8,128)S(1)} %get-tuple-element.73), channel_id=1, source_target_pairs={{0,1},{1,2},{2,3},{3,4},{4,5},{5,6},{6,7},{8,9},{9,10},{10,11},{11... | collective-permute-start | bytes 786440 | tf_op jit(solution)/shard_map/ppermute | solution.py:342
  116.1 10.7 %collective-permute-start.19 = (f32[2,64,384]{2,1,0:T(8,128)S(1)}, f32[2,64,384]{2,1,0:T(8,128)S(1)}, u32[]{:S(2)}, u32[]{:S(2)}) collective-permute-start(f32[2,64,384]{2,1,0:T(8,128)S(1)} %get-tuple-element.75), channel_id=1, source_target_pairs={{0,8},{8,16},{16,24},{1,9},{9,17},{17,25},{2,10},{10,18},{18,26},{... | collective-permute-start | bytes 589832 | tf_op jit(solution)/shard_map/ppermute | solution.py:342
  117.4 9.4 %collective-permute-start.20 = (f32[2,64,384]{2,1,0:T(8,128)S(1)}, f32[2,64,384]{2,1,0:T(8,128)S(1)}, u32[]{:S(2)}, u32[]{:S(2)}) collective-permute-start(f32[2,64,384]{2,1,0:T(8,128)S(1)} %get-tuple-element.76), channel_id=1, source_target_pairs={{8,0},{16,8},{24,16},{9,1},{17,9},{25,17},{10,2},{18,10},{26,18},{... | collective-permute-start | bytes 589832 | tf_op jit(solution)/shard_map/ppermute | solution.py:342
  119.4 7.4 %collective-permute-start.21 = (f32[2,64,128]{2,1,0:T(8,128)S(1)}, f32[2,64,128]{2,1,0:T(8,128)S(1)}, u32[]{:S(2)}, u32[]{:S(2)}) collective-permute-start(f32[2,64,128]{2,1,0:T(8,128)S(1)} %pad_maximum_fusion.2), channel_id=1, source_target_pairs={{0,8},{8,16},{16,24},{1,9},{9,17},{17,25},{2,10},{10,18},{18,26},{... | collective-permute-start | bytes 196616 | tf_op jit(solution)/shard_map/ppermute | solution.py:342
  122.8 5.0 %collective-permute-start.22 = (f32[2,64,128]{2,1,0:T(8,128)S(1)}, f32[2,64,128]{2,1,0:T(8,128)S(1)}, u32[]{:S(2)}, u32[]{:S(2)}) collective-permute-start(f32[2,64,128]{2,1,0:T(8,128)S(1)} %pad_maximum_fusion.3), channel_id=1, source_target_pairs={{8,0},{16,8},{24,16},{9,1},{17,9},{25,17},{10,2},{18,10},{26,18},{... | collective-permute-start | bytes 196616 | tf_op jit(solution)/shard_map/ppermute | solution.py:342
  124.1 3.7 %copy-start.3 = (f32[2,384,384]{2,1,0:T(8,128)S(1)}, f32[2,384,384]{2,1,0:T(8,128)}, u32[]{:S(2)}) copy-start(f32[2,384,384]{2,1,0:T(8,128)} %refs_0_.1) | copy-start | bytes 3538948

commit v6 on v5

--- a/solution.py
+++ b/solution.py
@@ -65,7 +65,7 @@
 def beam_of(meta, which, slot, scans, beams):
     beam = jnp.int32(0)
     for index in range(1, beams):
-        beam = jnp.where(meta[0, 2 * scans + 2 + slot * beams + index] == which, index, beam)
+        beam = jnp.where(meta[0, 2 * scans + 3 + slot * beams + index] == which, index, beam)
     return beam
 
 
@@ -77,7 +77,7 @@
 def edge_kernel(obj, positions, counts, offsets, place_of, edge_l, edge_r, meta):
     scans = positions.shape[2]
     values = [positions[0, 0, slot, axis] for slot in range(scans) for axis in range(2)]
-    values += [counts[0, 0], place_of[0]]
+    values += [counts[0, 0], place_of[0], place_of[1]]
     values += [offsets[slot, beam] for slot in range(scans) for beam in range(offsets.shape[1])]
     assert len(values) <= meta.shape[1]
     lane = lax.broadcasted_iota(jnp.int32, meta.shape, 1)
@@ -165,7 +165,7 @@
         if power.shape[0] > slots * size:
             lane = lanes(power.shape[0] - slots * size, size)
             row = jnp.zeros(lane.shape, jnp.int32)
-            for index in range(2 * scans + 2 + scans * probe.shape[0]):
+            for index in range(2 * scans + 3 + scans * probe.shape[0]):
                 row = jnp.where(lane == index, meta[0, index], row)
             power[slots * size :, :] = row.astype(F32)
 
@@ -186,11 +186,13 @@
     total[channel, tile + 1, rows, :] += jnp.where(lane < shift, moved, 0.0)
 
 
-def write_sides(total, side_l, side_r):
+def write_sides(total, odd, side_1, side_2):
     _, tiles, rows, size = total.shape
     low = lanes(rows, size) < size // 2
-    side_l[...] = jnp.where(low, total[0, 0], turn(total[1, 0]))
-    side_r[...] = jnp.where(low, turn(total[0, tiles - 1]), total[1, tiles - 1])
+    left = jnp.where(low, total[0, 0], turn(total[1, 0]))
+    right = jnp.where(low, turn(total[0, tiles - 1]), total[1, tiles - 1])
+    side_1[...] = jnp.where(odd == 1, left, right)
+    side_2[...] = jnp.where(odd == 1, right, left)
 
 
 def own_columns(total, channel, rows, low):
@@ -199,24 +201,27 @@
     return [jnp.where(low, turned[t], turned[t + 1]) for t in range(tiles - 1)]
 
 
-def write_rims(total, rim_top, rim_bot):
+def write_rims(total, odd, rim_1, rim_2):
     channels, _, rows, size = total.shape
     half = size // 2
     low = lanes(half, size) < half
     for ch in range(channels):
-        for start, out in ((0, rim_top), (rows - half, rim_bot)):
-            for t, value in enumerate(own_columns(total, ch, pl.ds(start, half), low)):
-                out[ch, :, t * size : (t + 1) * size] = value
-
-
-def backward_kernel(parts, scans, fresh, last, *refs):
+        tops = own_columns(total, ch, pl.ds(0, half), low)
+        bottoms = own_columns(total, ch, pl.ds(rows - half, half), low)
+        for t, (top, bottom) in enumerate(zip(tops, bottoms)):
+            columns = slice(t * size, (t + 1) * size)
+            rim_1[ch, :, columns] = jnp.where(odd == 1, top, bottom)
+            rim_2[ch, :, columns] = jnp.where(odd == 1, bottom, top)
+
+
+def backward_kernel(parts, scans, row_count, fresh, last, *refs):
     meta, probe, tables = refs[:3]
     inputs, refs = refs[3 : 3 + 3 * len(parts)], refs[3 + 3 * len(parts) :]
     if not fresh:
         refs = refs[1:]
     total, refs = refs[0], refs[1:]
     if last:
-        (side_l, side_r, rim_top, rim_bot), refs = refs[:4], refs[4:]
+        (side_1, side_2, rim_1, rim_2), refs = refs[:4], refs[4:]
     x_high, x_low, y_high, y_low = refs
     size = probe.shape[-1]
     lane = lanes(size, size)
@@ -255,8 +260,10 @@
                 add_patch(total, 0, *spot, grad_re, lane)
                 add_patch(total, 1, *spot, grad_im, lane)
     if last:
-        write_sides(total, side_l, side_r)
-        write_rims(total, rim_top, rim_bot)
+        odd = lax.rem(meta[0, 2 * scans + 2], 2)
+        write_sides(total, odd, side_1, side_2)
+        odd = lax.rem(lax.rem(meta[0, 2 * scans + 1] + parts[0][0], row_count), 2)
+        write_rims(total, odd, rim_1, rim_2)
 
 
 def weight_kernel(steps, scans, which_tile, row_count, fresh, *refs):
@@ -328,9 +335,9 @@
                 out[ch, rows, columns] = obj[ch, rows, columns] + value * scale[t]
 
 
-def line(axis, by):
-    count = lax.axis_size(axis)
-    return [(i, i + by) for i in range(count) if 0 <= i + by < count]
+def swap(axis, first):
+    lower = range(first, lax.axis_size(axis) - 1, 2)
+    return [(i, i + 1) for i in lower] + [(i + 1, i) for i in lower]
 
 
 def ring(axis, by):
@@ -342,17 +349,21 @@
     return lax.ppermute(x, axis, pairs)
 
 
-def send_rims(side_l, side_r, rim_top, rim_bot):
-    rows, size = side_l.shape
+def send_rims(side_1, side_2, rim_1, rim_2, odd_row, odd_col):
+    rows, size = side_1.shape
     half = size // 2
-    in_r = move(side_l, "col", line("col", -1))
-    in_l = move(side_r, "col", line("col", 1))
-    in_bot = move(rim_top, "row", line("row", -1))
-    in_top = move(rim_bot, "row", line("row", 1))
-    corner_top = jnp.stack([in_l[:half], in_r[:half]])
-    corner_bot = jnp.stack([in_l[rows - half :], in_r[rows - half :]])
-    in_cbot = move(corner_top, "row", line("row", -1))
-    in_ctop = move(corner_bot, "row", line("row", 1))
+    in_2 = move(side_2, "col", swap("col", 1))
+    in_1 = move(side_1, "col", swap("col", 0))
+    rim_1 = move(rim_1, "row", swap("row", 0))
+    rim_2 = move(rim_2, "row", swap("row", 1))
+    in_l, in_r = jnp.where(odd_col, in_1, in_2), jnp.where(odd_col, in_2, in_1)
+    tops = jnp.where(odd_col, jnp.stack([in_1[:half], in_2[:half]]), jnp.stack([in_2[:half], in_1[:half]]))
+    low = rows - half
+    bottoms = jnp.where(odd_col, jnp.stack([in_1[low:], in_2[low:]]), jnp.stack([in_2[low:], in_1[low:]]))
+    corner_1 = move(jnp.where(odd_row, tops, bottoms), "row", swap("row", 0))
+    corner_2 = move(jnp.where(odd_row, bottoms, tops), "row", swap("row", 1))
+    in_top, in_bot = jnp.where(odd_row, rim_1, rim_2), jnp.where(odd_row, rim_2, rim_1)
+    in_ctop, in_cbot = jnp.where(odd_row, corner_1, corner_2), jnp.where(odd_row, corner_2, corner_1)
     return in_l, in_r, in_top, in_bot, in_ctop, in_cbot
 
 
@@ -368,15 +379,21 @@
     def packed(x):
         return jnp.concatenate([x[0], x[1]], axis=1)
 
+    at_row, at_col = lax.axis_index("row").astype(jnp.int32), lax.axis_index("col").astype(jnp.int32)
+    odd_row, odd_col = lax.rem(at_row, 2) == 1, lax.rem(at_col, 2) == 1
+    ends = jnp.where(odd_row, 0, tile_rows - half), jnp.where(odd_row, tile_rows - half, 0)
+    rows_1, rows_2 = (
+        move(lax.dynamic_slice_in_dim(obj, ends[i], half, axis=1), "row", swap("row", i))
+        for i in range(2)
+    )
+    top, bot = jnp.where(odd_row, rows_1, rows_2), jnp.where(odd_row, rows_2, rows_1)
     edge_l, edge_r, meta = call(
         edge_kernel,
         [(tile_rows, size)] * 2 + [jax.ShapeDtypeStruct((1, size), jnp.int32)],
         [VMEM, SMEM, SMEM, SMEM, SMEM],
-        (obj, positions, counts, offsets, lax.axis_index("row").astype(jnp.int32).reshape(1)),
+        (obj, positions, counts, offsets, jnp.stack([at_row, at_col])),
         10**6,
     )
-    top = move(obj[:, tile_rows - half :], "row", line("row", 1))
-    bot = move(obj[:, :half], "row", line("row", -1))
 
     most = offsets_count - 1
     metas = {0: meta, most: move(meta, "row", ring("row", most))}
@@ -386,8 +403,9 @@
         jnp.concatenate([packed(top[:, :, part]), edge, packed(bot[:, :, part]), own_meta])
         for part, edge in ((slice(0, half), edge_l), (slice(tile_columns - half, None), edge_r))
     )
-    left = move(edge_r, "col", line("col", 1))
-    right = move(edge_l, "col", line("col", -1))
+    columns_2 = move(jnp.where(odd_col, edge_r, edge_l), "col", swap("col", 1))
+    columns_1 = move(jnp.where(odd_col, edge_l, edge_r), "col", swap("col", 0))
+    left, right = jnp.where(odd_col, columns_1, columns_2), jnp.where(odd_col, columns_2, columns_1)
     (frame,) = call(frame_kernel, [(2, tiles, rows, size)], [VMEM] * 5, (obj, top, bot, left, right), 10**6)
 
     slots = scans // 2
@@ -488,7 +506,7 @@
             if not fresh:
                 args, specs = args + [total], specs + [VMEM]
             total, *sides = call(
-                functools.partial(backward_kernel, [(which, *part) for part in group], scans, fresh, last),
+                functools.partial(backward_kernel, [(which, *part) for part in group], scans, row_count, fresh, last),
                 outs,
                 specs,
                 args,
@@ -496,7 +514,7 @@
                 work,
                 {} if fresh else {len(args) - 1: 0},
             )
-    grad_in = send_rims(*sides)
+    grad_in = send_rims(*sides, odd_row, odd_col)
 
     (new_object,) = call(final_kernel, [obj.shape], [VMEM] * 9, (obj, weight, total, *grad_in), 10**6)
     return new_object

time: 130 us -> 123 us (0.946)
  the two profiles are of different devices: /device:TPU:1 before, /device:TPU:0 now
where the time goes in v6:
time: 123 us
  starting transfers between devices  44.5 us (36%)
  waiting for transfers between devices  36.8 us (30%)
  Pallas kernels  35.7 us (29%)
  local copies, waits for them, and re-layouts  4.08 us (3%)
    ppermute x23, starting transfers between devices, move(): return lax.ppermute(x, axis, pairs)  44.5 us
    ppermute x23, waiting for transfers between devices, move(): return lax.ppermute(x, axis, pairs)  36.8 us
    pallas_call x21, Pallas kernels, call(): pl.pallas_call(kernel, out_shape=[s if hasattr(s, 'dtype') else jax.Shape...  35.7 us
    unnamed x12, local copies, waits for them, and re-layouts  2.8 us
  transfers between devices with their start and end apart: 23, of which 13 were waited for; matrix products, arithmetic and copies ran while one was open for 2% of the time, Pallas kernels for 25%

profile of v6, /device:TPU:0, one launch (start us, length us, event | category | flops | bytes accessed | tf_op | source)
XLA Modules:
  0.0 122.8 jit_solution(6347340507478477371)
XLA Ops:
  1.7 5.9 %collective-permute-start.1 = (f32[2,64,384]{2,1,0:T(8,128)S(1)}, f32[2,64,384]{2,1,0:T(8,128)S(1)}, u32[]{:S(2)}, u32[]{:S(2)}) collective-permute-start(f32[2,64,384]{2,1,0:T(8,128)S(1)} %get-tuple-element.78), channel_id=1, source_target_pairs={{0,8},{16,24},{8,0},{24,16},{1,9},{17,25},{9,1},{25,17},{2,10},{18... | collective-permute-start | bytes 589832 | tf_op jit(solution)/shard_map/ppermute | solution.py:349
  13.3 2.9 %collective-permute-start.3 = (f32[520,128]{1,0:T(8,128)S(1)}, f32[520,128]{1,0:T(8,128)S(1)}, u32[]{:S(2)}, u32[]{:S(2)}) collective-permute-start(f32[520,128]{1,0:T(8,128)S(1)} %broadcast_select_fusion.3), channel_id=1, source_target_pairs={{0,1},{2,3},{4,5},{6,7},{1,0},{3,2},{5,4},{7,6},{8,9},{10,11},{12,... | collective-permute-start | bytes 798728 | tf_op jit(solution)/shard_map/ppermute | solution.py:349
  19.8 1.6 %shard_map.75 = (f32[256,512]{1,0:T(8,128)S(1)}, f32[4,2,128,128]{3,2,1,0:T(8,128)S(1)}, f32[520,128]{1,0:T(8,128)S(1)}) custom-call(s32[1,128]{1,0:T(1,128)S(1)} %collective-permute-done.refs_0_, f32[2,4,512,128]{3,2,1,0:T(8,128)S(1)} %shard_map.74.refs_1_, f32[4,2,128,128]{3,2,1,0:T(8,128)S(1)} %copy-done, bf16[4,256,256]{2,1,0:T(8,128)(2,1)S(1)} %copy-done.1), custom_call_target="tpu_custom_call" | custom-call | flops 402653184 | bytes 1048576 | tf_op jit(solution)/shard_map/pallas_call | solution.py:23
  21.5 3.2 %collective-permute-start.5 = (f32[520,128]{1,0:T(8,128)S(1)}, f32[520,128]{1,0:T(8,128)S(1)}, u32[]{:S(2)}, u32[]{:S(2)}) collective-permute-start(f32[520,128]{1,0:T(8,128)S(1)} %get-tuple-element.44), channel_id=1, source_target_pairs={{0,24},{8,0},{16,8},{24,16},{1,25},{9,1},{17,9},{25,17},{2,26},{10... | collective-permute-start | bytes 798728 | tf_op jit(solution)/shard_map/ppermute | solution.py:349
  26.4 4.1 %collective-permute-done.5.refs_4_ = f32[520,128]{1,0:T(8,128)S(1)} collective-permute-done((f32[520,128]{1,0:T(8,128)S(1)}, f32[520,128]{1,0:T(8,128)S(1)}, u32[]{:S(2)}, u32[]{:S(2)}) %collective-permute-start.5) | collective-permute-done | bytes 266272 | tf_op jit(solution)/shard_map/ppermute | solution.py:349
  32.2 4.3 %collective-permute-start.6 = (f32[520,128]{1,0:T(8,128)S(1)}, f32[520,128]{1,0:T(8,128)S(1)}, u32[]{:S(2)}, u32[]{:S(2)}) collective-permute-start(f32[520,128]{1,0:T(8,128)S(1)} %get-tuple-element.45), channel_id=1, source_target_pairs={{0,24},{8,0},{16,8},{24,16},{1,25},{9,1},{17,9},{25,17},{2,26},{10... | collective-permute-start | bytes 798728 | tf_op jit(solution)/shard_map/ppermute | solution.py:349
  36.6 1.6 %shard_map.81 = (f32[256,512]{1,0:T(8,128)S(1)}, f32[4,2,128,128]{3,2,1,0:T(8,128)S(1)}, f32[512,128]{1,0:T(8,128)S(1)}) custom-call(s32[1,128]{1,0:T(1,128)S(1)} %slice_convert_fusion.4.refs_0_, f32[2,4,512,128]{3,2,1,0:T(8,128)S(1)} %shard_map.74.refs_1_, f32[4,2,128,128]{3,2,1,0:T(8,128)S(1)} %copy-done, bf16[4,256,256]{2,1,0:T(8,128)(2,1)S(1)} %copy-done.1, ...), custom_call_target="tpu_custom_call" | custom-call | flops 402653184 | bytes 1048576 | tf_op jit(solution)/shard_map/pallas_call | solution.py:23
  38.2 3.9 %collective-permute-start.10 = (f32[512,128]{1,0:T(8,128)S(1)}, f32[512,128]{1,0:T(8,128)S(1)}, u32[]{:S(2)}, u32[]{:S(2)}) collective-permute-start(f32[512,128]{1,0:T(8,128)S(1)} %get-tuple-element.53), channel_id=1, source_target_pairs={{0,24},{8,0},{16,8},{24,16},{1,25},{9,1},{17,9},{25,17},{2,26},{10... | collective-permute-start | bytes 786440 | tf_op jit(solution)/shard_map/ppermute | solution.py:349
  44.0 4.3 %collective-permute-start.7 = (f32[520,128]{1,0:T(8,128)S(1)}, f32[520,128]{1,0:T(8,128)S(1)}, u32[]{:S(2)}, u32[]{:S(2)}) collective-permute-start(f32[520,128]{1,0:T(8,128)S(1)} %get-tuple-element.46), channel_id=1, source_target_pairs={{0,24},{8,0},{16,8},{24,16},{1,25},{9,1},{17,9},{25,17},{2,26},{10... | collective-permute-start | bytes 798728 | tf_op jit(solution)/shard_map/ppermute | solution.py:349
  48.8 1.6 %shard_map.82 = (f32[256,512]{1,0:T(8,128)S(1)}, f32[4,2,128,128]{3,2,1,0:T(8,128)S(1)}, f32[512,128]{1,0:T(8,128)S(1)}) custom-call(s32[1,128]{1,0:T(1,128)S(1)} %slice_convert_fusion.3.refs_0_, f32[2,4,512,128]{3,2,1,0:T(8,128)S(1)} %shard_map.74.refs_1_, f32[4,2,128,128]{3,2,1,0:T(8,128)S(1)} %copy-done, bf16[4,256,256]{2,1,0:T(8,128)(2,1)S(1)} %copy-done.1, ...), custom_call_target="tpu_custom_call" | custom-call | flops 402653184 | bytes 1048576 | tf_op jit(solution)/shard_map/pallas_call | solution.py:23
  50.5 4.3 %collective-permute-start.11 = (f32[512,128]{1,0:T(8,128)S(1)}, f32[512,128]{1,0:T(8,128)S(1)}, u32[]{:S(2)}, u32[]{:S(2)}) collective-permute-start(f32[512,128]{1,0:T(8,128)S(1)} %get-tuple-element.54), channel_id=1, source_target_pairs={{0,24},{8,0},{16,8},{24,16},{1,25},{9,1},{17,9},{25,17},{2,26},{10... | collective-permute-start | bytes 786440 | tf_op jit(solution)/shard_map/ppermute | solution.py:349
  54.8 2.1 %shard_map.78 = (f32[256,512]{1,0:T(8,128)S(1)}, f32[4,2,128,128]{3,2,1,0:T(8,128)S(1)}, f32[512,128]{1,0:T(8,128)S(1)}, f32[256,512]{1,0:T(8,128)S(1)}, f32[4,2...) custom-call(s32[1,128]{1,0:T(1,128)S(1)} %get-tuple-element.41.refs_0_, f32[2,4,512,128]{3,2,1,0:T(8,128)S(1)} %shard_map.74.refs_1_, ...), custom_call_target="tpu_custom_call" | custom-call | flops 805306368 | bytes 1048576 | tf_op jit(solution)/shard_map/pallas_call | solution.py:23
  57.0 3.8 %collective-permute-done.11.arrived = f32[512,128]{1,0:T(8,128)S(1)} collective-permute-done((f32[512,128]{1,0:T(8,128)S(1)}, f32[512,128]{1,0:T(8,128)S(1)}, u32[]{:S(2)}, u32[]{:S(2)}) %collective-permute-start.11) | collective-permute-done | bytes 262176 | tf_op jit(solution)/shard_map/ppermute | solution.py:349
  61.0 1.8 %collective-permute-start.8 = (f32[520,128]{1,0:T(8,128)S(1)}, f32[520,128]{1,0:T(8,128)S(1)}, u32[]{:S(2)}, u32[]{:S(2)}) collective-permute-start(f32[520,128]{1,0:T(8,128)S(1)} %shard_map.79.refs_5_), channel_id=1, source_target_pairs={{0,8},{8,16},{16,24},{24,0},{1,9},{9,17},{17,25},{25,1},{2,10},{10... | collective-permute-start | bytes 798728 | tf_op jit(solution)/shard_map/ppermute | solution.py:349
  62.9 2.6 %shard_map.86.refs_2_ = f32[1,5,640,128]{3,2,1,0:T(8,128)S(1)} custom-call(s32[3,128]{1,0:T(4,128)S(1)} %pad_add_fusion.3.refs_0_, f32[4,2,128,128]{3,2,1,0:T(8,128)S(1)} %copy-done), custom_call_target="tpu_custom_call" | custom-call | flops 402653184 | bytes 1048576 | tf_op jit(solution)/shard_map/pallas_call | solution.py:23
  65.5 2.3 %shard_map.84.refs_9_ = f32[2,4,512,128]{3,2,1,0:T(8,128)S(1)} custom-call(s32[1,128]{1,0:T(1,128)S(1)} %get-tuple-element.41.refs_0_, f32[4,2,128,128]{3,2,1,0:T(8,128)S(1)} %copy-done, bf16[4,256,256]{2,1,0:T(8,128)(2,1)S(1)} %copy-done.1, f32[256,512]{1,0:T(8,128)S(1)} %get-tuple-element.48.refs_3_, f32[4,2,128,128]{3,2,1,0:T(8,128)S(1)} %get-tuple-element.49.refs_4_, ...), custom_call_target="tpu_custom_call" | custom-call | flops 805306368 | bytes 1048576 | tf_op jit(solution)/shard_map/pallas_call | solution.py:23
  67.8 4.6 %collective-permute-done.13.refs_8_ = f32[512,128]{1,0:T(8,128)S(1)} collective-permute-done((f32[512,128]{1,0:T(8,128)S(1)}, f32[512,128]{1,0:T(8,128)S(1)}, u32[]{:S(2)}, u32[]{:S(2)}) %collective-permute-start.13) | collective-permute-done | bytes 262176 | tf_op jit(solution)/shard_map/ppermute | solution.py:349
  72.3 5.7 %collective-permute-done.8.refs_5_ = f32[520,128]{1,0:T(8,128)S(1)} collective-permute-done((f32[520,128]{1,0:T(8,128)S(1)}, f32[520,128]{1,0:T(8,128)S(1)}, u32[]{:S(2)}, u32[]{:S(2)}) %collective-permute-start.8) | collective-permute-done | bytes 266272 | tf_op jit(solution)/shard_map/ppermute | solution.py:349
  78.1 2.9 %shard_map.87.refs_2_ = f32[1,5,640,128]{3,2,1,0:T(8,128)S(1)} custom-call(s32[3,128]{1,0:T(4,128)S(1)} %pad_add_fusion.2.refs_0_, f32[4,2,128,128]{3,2,1,0:T(8,128)S(1)} %copy-done, f32[1,5,640,128]{3,2,1,0:T(8,128)S(1)} %shard_map.86.refs_2_), custom_call_target="tpu_custom_call", output_to_operand_aliasing={{}: (2, {})} | custom-call | flops 402653184 | bytes 1048576 | tf_op jit(solution)/shard_map/pallas_call | solution.py:23
  81.0 2.2 %shard_map.85.refs_9_ = f32[2,4,512,128]{3,2,1,0:T(8,128)S(1)} custom-call(s32[1,128]{1,0:T(1,128)S(1)} %slice_convert_fusion.3.refs_0_, f32[4,2,128,128]{3,2,1,0:T(8,128)S(1)} %copy-done, bf16[4,256,256]{2,1,0:T(8,128)(2,1)S(1)} %copy-done.1, f32[256,512]{1,0:T(8,128)S(1)} %get-tuple-element.57.refs_3_, ...), custom_call_target="tpu_custom_call", output_to_operand_aliasing={{}: (9, {})} | custom-call | flops 805306368 | bytes 1048576 | tf_op jit(solution)/shard_map/pallas_call | solution.py:23
  83.7 5.7 %collective-permute-done.12.refs_5_ = f32[520,128]{1,0:T(8,128)S(1)} collective-permute-done((f32[520,128]{1,0:T(8,128)S(1)}, f32[520,128]{1,0:T(8,128)S(1)}, u32[]{:S(2)}, u32[]{:S(2)}) %collective-permute-start.12) | collective-permute-done | bytes 266272 | tf_op jit(solution)/shard_map/ppermute | solution.py:349
  89.4 2.4 %shard_map.88.refs_2_ = f32[1,5,640,128]{3,2,1,0:T(8,128)S(1)} custom-call(s32[3,128]{1,0:T(4,128)S(1)} %pad_add_fusion.1.refs_0_, f32[4,2,128,128]{3,2,1,0:T(8,128)S(1)} %copy-done, f32[1,5,640,128]{3,2,1,0:T(8,128)S(1)} %shard_map.87.refs_2_), custom_call_target="tpu_custom_call", output_to_operand_aliasing={{}: (2, {})} | custom-call | flops 402653184 | bytes 1048576 | tf_op jit(solution)/shard_map/pallas_call | solution.py:23
  91.8 2.1 %shard_map.90.refs_6_ = f32[2,4,512,128]{3,2,1,0:T(8,128)S(1)} custom-call(s32[1,128]{1,0:T(1,128)S(1)} %slice_convert_fusion.4.refs_0_, f32[4,2,128,128]{3,2,1,0:T(8,128)S(1)} %copy-done, bf16[4,256,256]{2,1,0:T(8,128)(2,1)S(1)} %copy-done.1, f32[256,512]{1,0:T(8,128)S(1)} %get-tuple-element.67.refs_3_, ...), custom_call_target="tpu_custom_call", output_to_operand_aliasing={{}: (9, {})} | custom-call | flops 805306368 | bytes 1048576 | tf_op jit(solution)/shard_map/pallas_call | solution.py:23
  93.9 5.5 %collective-permute-done.14.refs_5_ = f32[520,128]{1,0:T(8,128)S(1)} collective-permute-done((f32[520,128]{1,0:T(8,128)S(1)}, f32[520,128]{1,0:T(8,128)S(1)}, u32[]{:S(2)}, u32[]{:S(2)}) %collective-permute-start.14) | collective-permute-done | bytes 266272 | tf_op jit(solution)/shard_map/ppermute | solution.py:349
  100.9 1.9 %shard_map.92 = (f32[2,4,512,128]{3,2,1,0:T(8,128)S(1)}, f32[512,128]{1,0:T(8,128)S(1)}, f32[512,128]{1,0:T(8,128)S(1)}, f32[2,64,384]{2,1,0:T(8,128)S(1)}, f32[2,64,384]{2,1,0:T(8,128)S(1)}) custom-call(s32[1,128]{1,0:T(1,128)S(1)} %collective-permute-done.refs_0_, f32[4,2,128,128]{3,2,1,0:T(8,128)S(1)} %copy-done, ...), custom_call_target="tpu_custom_call", output_to_operand_aliasing={{0}: (6, {})} | custom-call | flops 402653184 | bytes 1048576 | tf_op jit(solution)/shard_map/pallas_call | solution.py:23
  103.5 2.9 %collective-permute-start.17 = (f32[512,128]{1,0:T(8,128)S(1)}, f32[512,128]{1,0:T(8,128)S(1)}, u32[]{:S(2)}, u32[]{:S(2)}) collective-permute-start(f32[512,128]{1,0:T(8,128)S(1)} %get-tuple-element.73), channel_id=1, source_target_pairs={{0,1},{2,3},{4,5},{6,7},{1,0},{3,2},{5,4},{7,6},{8,9},{10,11},{12,... | collective-permute-start | bytes 786440 | tf_op jit(solution)/shard_map/ppermute | solution.py:349
  107.0 1.9 %collective-permute-start.19 = (f32[2,64,384]{2,1,0:T(8,128)S(1)}, f32[2,64,384]{2,1,0:T(8,128)S(1)}, u32[]{:S(2)}, u32[]{:S(2)}) collective-permute-start(f32[2,64,384]{2,1,0:T(8,128)S(1)} %get-tuple-element.75), channel_id=1, source_target_pairs={{0,8},{16,24},{8,0},{24,16},{1,9},{17,25},{9,1},{25,17},{2,10},{18... | collective-permute-start | bytes 589832 | tf_op jit(solution)/shard_map/ppermute | solution.py:349
  108.9 2.7 %shard_map.89.refs_1_ = f32[1,5,640,128]{3,2,1,0:T(8,128)S(1)} custom-call(s32[3,128]{1,0:T(4,128)S(1)} %pad_add_fusion.refs_0_, f32[4,2,128,128]{3,2,1,0:T(8,128)S(1)} %copy-done, f32[1,5,640,128]{3,2,1,0:T(8,128)S(1)} %shard_map.88.refs_2_), custom_call_target="tpu_custom_call", output_to_operand_aliasing={{}: (2, {})} | custom-call | flops 402653184 | bytes 1048576 | tf_op jit(solution)/shard_map/pallas_call | solution.py:23
  111.7 2.3 %collective-permute-done.19 = f32[2,64,384]{2,1,0:T(8,128)S(1)} collective-permute-done((f32[2,64,384]{2,1,0:T(8,128)S(1)}, f32[2,64,384]{2,1,0:T(8,128)S(1)}, u32[]{:S(2)}, u32[]{:S(2)}) %collective-permute-start.19) | collective-permute-done | bytes 196640 | tf_op jit(solution)/shard_map/ppermute | solution.py:349
  114.7 4.2 %collective-permute-start.21 = (f32[2,64,128]{2,1,0:T(8,128)S(1)}, f32[2,64,128]{2,1,0:T(8,128)S(1)}, u32[]{:S(2)}, u32[]{:S(2)}) collective-permute-start(f32[2,64,128]{2,1,0:T(8,128)S(1)} %get-tuple-element.104), channel_id=1, source_target_pairs={{0,8},{16,24},{8,0},{24,16},{1,9},{17,25},{9,1},{25,17},{2,10},{18... | collective-permute-start | bytes 196616 | tf_op jit(solution)/shard_map/ppermute | solution.py:349
  118.9 2.2 %collective-permute-done.21 = f32[2,64,128]{2,1,0:T(8,128)S(1)} collective-permute-done((f32[2,64,128]{2,1,0:T(8,128)S(1)}, f32[2,64,128]{2,1,0:T(8,128)S(1)}, u32[]{:S(2)}, u32[]{:S(2)}) %collective-permute-start.21) | collective-permute-done | bytes 65568 | tf_op jit(solution)/shard_map/ppermute | solution.py:349
  121.2 1.6 %shard_map.93 = f32[2,384,384]{2,1,0:T(8,128)} custom-call(f32[2,384,384]{2,1,0:T(8,128)S(1)} %copy-done.3, f32[1,5,640,128]{3,2,1,0:T(8,128)S(1)} %shard_map.89.refs_1_, f32[2,4,512,128]{3,2,1,0:T(8,128)S(1)} %get-tuple-element.72.refs_2_, f32[512,128]{1,0:T(8,128)S(1)} %get-tuple-element.82.refs_3_, f32[512,128]{1,0:T(8,128)S(1)} %get-tuple-element.81.refs_4_, ...), custom_call_target="tpu_custom_call" | custom-call | flops 1000000 | bytes 1048576 | tf_op jit(solution)/shard_map/pallas_call | solution.py:23
  (78 shorter events, 20.7 us)
Async XLA Ops:
  1.1 11.0 %collective-permute-start.2 = (f32[2,64,384]{2,1,0:T(8,128)S(1)}, f32[2,64,384]{2,1,0:T(8,128)S(1)}, u32[]{:S(2)}, u32[]{:S(2)}) collective-permute-start(f32[2,64,384]{2,1,0:T(8,128)S(1)} %get-tuple-element.77), channel_id=1, source_target_pairs={{8,16},{16,8},{9,17},{17,9},{10,18},{18,10},{11,19},{19,11},{12,20... | collective-permute-start | bytes 589832 | tf_op jit(solution)/shard_map/ppermute | solution.py:349
  1.7 10.6 %collective-permute-start.1 = (f32[2,64,384]{2,1,0:T(8,128)S(1)}, f32[2,64,384]{2,1,0:T(8,128)S(1)}, u32[]{:S(2)}, u32[]{:S(2)}) collective-permute-start(f32[2,64,384]{2,1,0:T(8,128)S(1)} %get-tuple-element.78), channel_id=1, source_target_pairs={{0,8},{16,24},{8,0},{24,16},{1,9},{17,25},{9,1},{25,17},{2,10},{18... | collective-permute-start | bytes 589832 | tf_op jit(solution)/shard_map/ppermute | solution.py:349
  9.9 1.3 %copy-start.2 = (f32[2,384,384]{2,1,0:T(8,128)S(1)}, f32[2,384,384]{2,1,0:T(8,128)}, u32[]{:S(2)}) copy-start(f32[2,384,384]{2,1,0:T(8,128)} %refs_0_.1) | copy-start | bytes 3538948
  12.7 4.9 %collective-permute-start.4 = (f32[520,128]{1,0:T(8,128)S(1)}, f32[520,128]{1,0:T(8,128)S(1)}, u32[]{:S(2)}, u32[]{:S(2)}) collective-permute-start(f32[520,128]{1,0:T(8,128)S(1)} %broadcast_select_fusion.2), channel_id=1, source_target_pairs={{1,2},{3,4},{5,6},{2,1},{4,3},{6,5},{9,10},{11,12},{13,14},{10,9},... | collective-permute-start | bytes 798728 | tf_op jit(solution)/shard_map/ppermute | solution.py:349
  13.3 4.3 %collective-permute-start.3 = (f32[520,128]{1,0:T(8,128)S(1)}, f32[520,128]{1,0:T(8,128)S(1)}, u32[]{:S(2)}, u32[]{:S(2)}) collective-permute-start(f32[520,128]{1,0:T(8,128)S(1)} %broadcast_select_fusion.3), channel_id=1, source_target_pairs={{0,1},{2,3},{4,5},{6,7},{1,0},{3,2},{5,4},{7,6},{8,9},{10,11},{12,... | collective-permute-start | bytes 798728 | tf_op jit(solution)/shard_map/ppermute | solution.py:349
  16.2 3.6 %collective-permute-start = (s32[1,128]{1,0:T(1,128)S(1)}, s32[1,128]{1,0:T(1,128)S(1)}, u32[]{:S(2)}, u32[]{:S(2)}) collective-permute-start(s32[1,128]{1,0:T(1,128)S(1)} %get-tuple-element.41.refs_0_), channel_id=1, source_target_pairs={{0,24},{8,0},{16,8},{24,16},{1,25},{9,1},{17,9},{25,17},{2,26},{10... | collective-permute-start | bytes 1544 | tf_op jit(solution)/shard_map/ppermute | solution.py:349
  17.7 2.1 %copy-start = (f32[4,2,128,128]{3,2,1,0:T(8,128)S(1)}, f32[4,2,128,128]{3,2,1,0:T(8,128)}, u32[]{:S(2)}) copy-start(f32[4,2,128,128]{3,2,1,0:T(8,128)} %refs_1_.17) | copy-start | bytes 1572868
  17.7 2.1 %copy-start.1 = (bf16[4,256,256]{2,1,0:T(8,128)(2,1)S(1)}, bf16[4,256,256]{2,1,0:T(8,128)(2,1)}, u32[]{:S(2)}) copy-start(bf16[4,256,256]{2,1,0:T(8,128)(2,1)} %constant.26.clone.refs_3_.refs_2_) | copy-start | bytes 1572868
  21.5 9.1 %collective-permute-start.5 = (f32[520,128]{1,0:T(8,128)S(1)}, f32[520,128]{1,0:T(8,128)S(1)}, u32[]{:S(2)}, u32[]{:S(2)}) collective-permute-start(f32[520,128]{1,0:T(8,128)S(1)} %get-tuple-element.44), channel_id=1, source_target_pairs={{0,24},{8,0},{16,8},{24,16},{1,25},{9,1},{17,9},{25,17},{2,26},{10... | collective-permute-start | bytes 798728 | tf_op jit(solution)/shard_map/ppermute | solution.py:349
  26.4 10.2 %collective-permute-start.9 = (f32[512,128]{1,0:T(8,128)S(1)}, f32[512,128]{1,0:T(8,128)S(1)}, u32[]{:S(2)}, u32[]{:S(2)}) collective-permute-start(f32[512,128]{1,0:T(8,128)S(1)} %get-tuple-element.52), channel_id=1, source_target_pairs={{0,24},{8,0},{16,8},{24,16},{1,25},{9,1},{17,9},{25,17},{2,26},{10... | collective-permute-start | bytes 786440 | tf_op jit(solution)/shard_map/ppermute | solution.py:349
  30.5 6.0 %copy-start.4 = (f32[1,1,8,128,128]{4,3,2,1,0:T(8,128)S(1)}, f32[1,1,8,128,128]{4,3,2,1,0:T(8,128)}, u32[]{:S(2)}) copy-start(f32[1,1,8,128,128]{4,3,2,1,0:T(8,128)} %param.12) | copy-start | bytes 1572868
  32.2 10.2 %collective-permute-start.6 = (f32[520,128]{1,0:T(8,128)S(1)}, f32[520,128]{1,0:T(8,128)S(1)}, u32[]{:S(2)}, u32[]{:S(2)}) collective-permute-start(f32[520,128]{1,0:T(8,128)S(1)} %get-tuple-element.45), channel_id=1, source_target_pairs={{0,24},{8,0},{16,8},{24,16},{1,25},{9,1},{17,9},{25,17},{2,26},{10... | collective-permute-start | bytes 798728 | tf_op jit(solution)/shard_map/ppermute | solution.py:349
  38.2 10.6 %collective-permute-start.10 = (f32[512,128]{1,0:T(8,128)S(1)}, f32[512,128]{1,0:T(8,128)S(1)}, u32[]{:S(2)}, u32[]{:S(2)}) collective-permute-start(f32[512,128]{1,0:T(8,128)S(1)} %get-tuple-element.53), channel_id=1, source_target_pairs={{0,24},{8,0},{16,8},{24,16},{1,25},{9,1},{17,9},{25,17},{2,26},{10... | collective-permute-start | bytes 786440 | tf_op jit(solution)/shard_map/ppermute | solution.py:349
  44.0 16.9 %collective-permute-start.7 = (f32[520,128]{1,0:T(8,128)S(1)}, f32[520,128]{1,0:T(8,128)S(1)}, u32[]{:S(2)}, u32[]{:S(2)}) collective-permute-start(f32[520,128]{1,0:T(8,128)S(1)} %get-tuple-element.46), channel_id=1, source_target_pairs={{0,24},{8,0},{16,8},{24,16},{1,25},{9,1},{17,9},{25,17},{2,26},{10... | collective-permute-start | bytes 798728 | tf_op jit(solution)/shard_map/ppermute | solution.py:349
  50.5 10.3 %collective-permute-start.11 = (f32[512,128]{1,0:T(8,128)S(1)}, f32[512,128]{1,0:T(8,128)S(1)}, u32[]{:S(2)}, u32[]{:S(2)}) collective-permute-start(f32[512,128]{1,0:T(8,128)S(1)} %get-tuple-element.54), channel_id=1, source_target_pairs={{0,24},{8,0},{16,8},{24,16},{1,25},{9,1},{17,9},{25,17},{2,26},{10... | collective-permute-start | bytes 786440 | tf_op jit(solution)/shard_map/ppermute | solution.py:349
  60.9 11.5 %collective-permute-start.13 = (f32[512,128]{1,0:T(8,128)S(1)}, f32[512,128]{1,0:T(8,128)S(1)}, u32[]{:S(2)}, u32[]{:S(2)}) collective-permute-start(f32[512,128]{1,0:T(8,128)S(1)} %shard_map.83.refs_8_), channel_id=1, source_target_pairs={{0,8},{8,16},{16,24},{24,0},{1,9},{9,17},{17,25},{25,1},{2,10},{10... | collective-permute-start | bytes 786440 | tf_op jit(solution)/shard_map/ppermute | solution.py:349
  61.0 17.0 %collective-permute-start.8 = (f32[520,128]{1,0:T(8,128)S(1)}, f32[520,128]{1,0:T(8,128)S(1)}, u32[]{:S(2)}, u32[]{:S(2)}) collective-permute-start(f32[520,128]{1,0:T(8,128)S(1)} %shard_map.79.refs_5_), channel_id=1, source_target_pairs={{0,8},{8,16},{16,24},{24,0},{1,9},{9,17},{17,25},{25,1},{2,10},{10... | collective-permute-start | bytes 798728 | tf_op jit(solution)/shard_map/ppermute | solution.py:349
  72.3 11.3 %collective-permute-start.15 = (f32[512,128]{1,0:T(8,128)S(1)}, f32[512,128]{1,0:T(8,128)S(1)}, u32[]{:S(2)}, u32[]{:S(2)}) collective-permute-start(f32[512,128]{1,0:T(8,128)S(1)} %collective-permute-done.13.refs_8_), channel_id=1, source_target_pairs={{0,8},{8,16},{16,24},{24,0},{1,9},{9,17},{17,25},{25,1},{2,10},{10... | collective-permute-start | bytes 786440 | tf_op jit(solution)/shard_map/ppermute | solution.py:349
  78.1 11.3 %collective-permute-start.12 = (f32[520,128]{1,0:T(8,128)S(1)}, f32[520,128]{1,0:T(8,128)S(1)}, u32[]{:S(2)}, u32[]{:S(2)}) collective-permute-start(f32[520,128]{1,0:T(8,128)S(1)} %collective-permute-done.8.refs_5_), channel_id=1, source_target_pairs={{0,8},{8,16},{16,24},{24,0},{1,9},{9,17},{17,25},{25,1},{2,10},{10... | collective-permute-start | bytes 798728 | tf_op jit(solution)/shard_map/ppermute | solution.py:349
  83.7 17.2 %collective-permute-start.16 = (f32[512,128]{1,0:T(8,128)S(1)}, f32[512,128]{1,0:T(8,128)S(1)}, u32[]{:S(2)}, u32[]{:S(2)}) collective-permute-start(f32[512,128]{1,0:T(8,128)S(1)} %collective-permute-done.15.refs_8_), channel_id=1, source_target_pairs={{0,8},{8,16},{16,24},{24,0},{1,9},{9,17},{17,25},{25,1},{2,10},{10... | collective-permute-start | bytes 786440 | tf_op jit(solution)/shard_map/ppermute | solution.py:349
  89.4 10.0 %collective-permute-start.14 = (f32[520,128]{1,0:T(8,128)S(1)}, f32[520,128]{1,0:T(8,128)S(1)}, u32[]{:S(2)}, u32[]{:S(2)}) collective-permute-start(f32[520,128]{1,0:T(8,128)S(1)} %collective-permute-done.12.refs_5_), channel_id=1, source_target_pairs={{0,8},{8,16},{16,24},{24,0},{1,9},{9,17},{17,25},{25,1},{2,10},{10... | collective-permute-start | bytes 798728 | tf_op jit(solution)/shard_map/ppermute | solution.py:349
  102.8 11.2 %collective-permute-start.18 = (f32[512,128]{1,0:T(8,128)S(1)}, f32[512,128]{1,0:T(8,128)S(1)}, u32[]{:S(2)}, u32[]{:S(2)}) collective-permute-start(f32[512,128]{1,0:T(8,128)S(1)} %get-tuple-element.74), channel_id=1, source_target_pairs={{1,2},{3,4},{5,6},{2,1},{4,3},{6,5},{9,10},{11,12},{13,14},{10,9},... | collective-permute-start | bytes 786440 | tf_op jit(solution)/shard_map/ppermute | solution.py:349
  103.5 10.5 %collective-permute-start.17 = (f32[512,128]{1,0:T(8,128)S(1)}, f32[512,128]{1,0:T(8,128)S(1)}, u32[]{:S(2)}, u32[]{:S(2)}) collective-permute-start(f32[512,128]{1,0:T(8,128)S(1)} %get-tuple-element.73), channel_id=1, source_target_pairs={{0,1},{2,3},{4,5},{6,7},{1,0},{3,2},{5,4},{7,6},{8,9},{10,11},{12,... | collective-permute-start | bytes 786440 | tf_op jit(solution)/shard_map/ppermute | solution.py:349
  106.3 5.3 %collective-permute-start.20 = (f32[2,64,384]{2,1,0:T(8,128)S(1)}, f32[2,64,384]{2,1,0:T(8,128)S(1)}, u32[]{:S(2)}, u32[]{:S(2)}) collective-permute-start(f32[2,64,384]{2,1,0:T(8,128)S(1)} %get-tuple-element.76), channel_id=1, source_target_pairs={{8,16},{16,8},{9,17},{17,9},{10,18},{18,10},{11,19},{19,11},{12,20... | collective-permute-start | bytes 589832 | tf_op jit(solution)/shard_map/ppermute | solution.py:349
  107.0 6.9 %collective-permute-start.19 = (f32[2,64,384]{2,1,0:T(8,128)S(1)}, f32[2,64,384]{2,1,0:T(8,128)S(1)}, u32[]{:S(2)}, u32[]{:S(2)}) collective-permute-start(f32[2,64,384]{2,1,0:T(8,128)S(1)} %get-tuple-element.75), channel_id=1, source_target_pairs={{0,8},{16,24},{8,0},{24,16},{1,9},{17,25},{9,1},{25,17},{2,10},{18... | collective-permute-start | bytes 589832 | tf_op jit(solution)/shard_map/ppermute | solution.py:349
  111.6 9.5 %copy-start.3 = (f32[2,384,384]{2,1,0:T(8,128)S(1)}, f32[2,384,384]{2,1,0:T(8,128)}, u32[]{:S(2)}) copy-start(f32[2,384,384]{2,1,0:T(8,128)} %refs_0_.1) | copy-start | bytes 3538948
  114.0 4.9 %collective-permute-start.22 = (f32[2,64,128]{2,1,0:T(8,128)S(1)}, f32[2,64,128]{2,1,0:T(8,128)S(1)}, u32[]{:S(2)}, u32[]{:S(2)}) collective-permute-start(f32[2,64,128]{2,1,0:T(8,128)S(1)} %get-tuple-element.103), channel_id=1, source_target_pairs={{8,16},{16,8},{9,17},{17,9},{10,18},{18,10},{11,19},{19,11},{12,20... | collective-permute-start | bytes 196616 | tf_op jit(solution)/shard_map/ppermute | solution.py:349
  114.7 6.4 %collective-permute-start.21 = (f32[2,64,128]{2,1,0:T(8,128)S(1)}, f32[2,64,128]{2,1,0:T(8,128)S(1)}, u32[]{:S(2)}, u32[]{:S(2)}) collective-permute-start(f32[2,64,128]{2,1,0:T(8,128)S(1)} %get-tuple-element.104), channel_id=1, source_target_pairs={{0,8},{16,24},{8,0},{24,16},{1,9},{17,25},{9,1},{25,17},{2,10},{18... | collective-permute-start | bytes 196616 | tf_op jit(solution)/shard_map/ppermute | solution.py:349

commit v7 on v6

--- a/solution.py
+++ b/solution.py
@@ -75,10 +75,10 @@
 
 
 def edge_kernel(obj, positions, counts, offsets, place_of, edge_l, edge_r, meta):
-    scans = positions.shape[2]
-    values = [positions[0, 0, slot, axis] for slot in range(scans) for axis in range(2)]
+    scans = positions.shape[1]
+    values = [positions[axis, slot] for slot in range(scans) for axis in range(2)]
     values += [counts[0, 0], place_of[0], place_of[1]]
-    values += [offsets[slot, beam] for slot in range(scans) for beam in range(offsets.shape[1])]
+    values += [offsets[beam, slot] for slot in range(scans) for beam in range(offsets.shape[0])]
     assert len(values) <= meta.shape[1]
     lane = lax.broadcasted_iota(jnp.int32, meta.shape, 1)
     row = jnp.zeros(meta.shape, jnp.int32)
@@ -382,6 +382,8 @@
     at_row, at_col = lax.axis_index("row").astype(jnp.int32), lax.axis_index("col").astype(jnp.int32)
     odd_row, odd_col = lax.rem(at_row, 2) == 1, lax.rem(at_col, 2) == 1
     ends = jnp.where(odd_row, 0, tile_rows - half), jnp.where(odd_row, tile_rows - half, 0)
+    here = jnp.stack([at_row, at_col])
+    ends, here, odd_row, odd_col = lax.optimization_barrier((ends, here, odd_row, odd_col))
     rows_1, rows_2 = (
         move(lax.dynamic_slice_in_dim(obj, ends[i], half, axis=1), "row", swap("row", i))
         for i in range(2)
@@ -391,7 +393,7 @@
         edge_kernel,
         [(tile_rows, size)] * 2 + [jax.ShapeDtypeStruct((1, size), jnp.int32)],
         [VMEM, SMEM, SMEM, SMEM, SMEM],
-        (obj, positions, counts, offsets, jnp.stack([at_row, at_col])),
+        (obj, positions[0, 0].T, counts, offsets.T, here),
         10**6,
     )
 

time: 123 us -> 123 us (level)
    unnamed x12 -> x14, local copies, waits for them, and re-layouts: 2.8 us -> 2.65 us
  transfers between devices with their start and end apart: 23 -> 23, of which waited for: 13 -> 13; matrix products, arithmetic and copies ran while one was open for 2% -> 0% of each run, Pallas kernels for 25% -> 25%
where the time goes in v7:
time: 123 us
  starting transfers between devices  44.3 us (36%)
  waiting for transfers between devices  37.3 us (30%)
  Pallas kernels  35.6 us (29%)
  local copies, waits for them, and re-layouts  3.95 us (3%)
    ppermute x23, starting transfers between devices, move(): return lax.ppermute(x, axis, pairs)  44.3 us
    ppermute x23, waiting for transfers between devices, move(): return lax.ppermute(x, axis, pairs)  37.3 us
    pallas_call x21, Pallas kernels, call(): pl.pallas_call(kernel, out_shape=[s if hasattr(s, 'dtype') else jax.Shape...  35.6 us
    unnamed x14, local copies, waits for them, and re-layouts  2.65 us
  transfers between devices with their start and end apart: 23, of which 13 were waited for; matrix products, arithmetic and copies ran while one was open for 0% of the time, Pallas kernels for 25%

profile of v7, /device:TPU:0, one launch (start us, length us, event | category | flops | bytes accessed | tf_op | source)
XLA Modules:
  0.0 122.9 jit_solution(14469116951549144043)
XLA Ops:
  1.8 5.9 %collective-permute-start.1 = (f32[2,64,384]{2,1,0:T(8,128)S(1)}, f32[2,64,384]{2,1,0:T(8,128)S(1)}, u32[]{:S(2)}, u32[]{:S(2)}) collective-permute-start(f32[2,64,384]{2,1,0:T(8,128)S(1)} %get-tuple-element.88), channel_id=1, source_target_pairs={{0,8},{16,24},{8,0},{24,16},{1,9},{17,25},{9,1},{25,17},{2,10},{18... | collective-permute-start | bytes 589832 | tf_op jit(solution)/shard_map/ppermute | solution.py:349
  13.4 2.9 %collective-permute-start.3 = (f32[520,128]{1,0:T(8,128)S(1)}, f32[520,128]{1,0:T(8,128)S(1)}, u32[]{:S(2)}, u32[]{:S(2)}) collective-permute-start(f32[520,128]{1,0:T(8,128)S(1)} %broadcast_select_fusion.3), channel_id=1, source_target_pairs={{0,1},{2,3},{4,5},{6,7},{1,0},{3,2},{5,4},{7,6},{8,9},{10,11},{12,... | collective-permute-start | bytes 798728 | tf_op jit(solution)/shard_map/ppermute | solution.py:349
  19.9 1.6 %shard_map.75 = (f32[256,512]{1,0:T(8,128)S(1)}, f32[4,2,128,128]{3,2,1,0:T(8,128)S(1)}, f32[520,128]{1,0:T(8,128)S(1)}) custom-call(s32[1,128]{1,0:T(1,128)S(1)} %collective-permute-done.refs_0_, f32[2,4,512,128]{3,2,1,0:T(8,128)S(1)} %shard_map.74.refs_1_, f32[4,2,128,128]{3,2,1,0:T(8,128)S(1)} %copy-done, bf16[4,256,256]{2,1,0:T(8,128)(2,1)S(1)} %copy-done.1), custom_call_target="tpu_custom_call" | custom-call | flops 402653184 | bytes 1048576 | tf_op jit(solution)/shard_map/pallas_call | solution.py:23
  21.6 3.2 %collective-permute-start.5 = (f32[520,128]{1,0:T(8,128)S(1)}, f32[520,128]{1,0:T(8,128)S(1)}, u32[]{:S(2)}, u32[]{:S(2)}) collective-permute-start(f32[520,128]{1,0:T(8,128)S(1)} %get-tuple-element.54), channel_id=1, source_target_pairs={{0,24},{8,0},{16,8},{24,16},{1,25},{9,1},{17,9},{25,17},{2,26},{10... | collective-permute-start | bytes 798728 | tf_op jit(solution)/shard_map/ppermute | solution.py:349
  26.5 4.1 %collective-permute-done.5.refs_4_ = f32[520,128]{1,0:T(8,128)S(1)} collective-permute-done((f32[520,128]{1,0:T(8,128)S(1)}, f32[520,128]{1,0:T(8,128)S(1)}, u32[]{:S(2)}, u32[]{:S(2)}) %collective-permute-start.5) | collective-permute-done | bytes 266272 | tf_op jit(solution)/shard_map/ppermute | solution.py:349
  32.3 4.3 %collective-permute-start.6 = (f32[520,128]{1,0:T(8,128)S(1)}, f32[520,128]{1,0:T(8,128)S(1)}, u32[]{:S(2)}, u32[]{:S(2)}) collective-permute-start(f32[520,128]{1,0:T(8,128)S(1)} %get-tuple-element.55), channel_id=1, source_target_pairs={{0,24},{8,0},{16,8},{24,16},{1,25},{9,1},{17,9},{25,17},{2,26},{10... | collective-permute-start | bytes 798728 | tf_op jit(solution)/shard_map/ppermute | solution.py:349
  36.7 1.6 %shard_map.81 = (f32[256,512]{1,0:T(8,128)S(1)}, f32[4,2,128,128]{3,2,1,0:T(8,128)S(1)}, f32[512,128]{1,0:T(8,128)S(1)}) custom-call(s32[1,128]{1,0:T(1,128)S(1)} %slice_convert_fusion.4.refs_0_, f32[2,4,512,128]{3,2,1,0:T(8,128)S(1)} %shard_map.74.refs_1_, f32[4,2,128,128]{3,2,1,0:T(8,128)S(1)} %copy-done, bf16[4,256,256]{2,1,0:T(8,128)(2,1)S(1)} %copy-done.1, ...), custom_call_target="tpu_custom_call" | custom-call | flops 402653184 | bytes 1048576 | tf_op jit(solution)/shard_map/pallas_call | solution.py:23
  38.3 3.9 %collective-permute-start.10 = (f32[512,128]{1,0:T(8,128)S(1)}, f32[512,128]{1,0:T(8,128)S(1)}, u32[]{:S(2)}, u32[]{:S(2)}) collective-permute-start(f32[512,128]{1,0:T(8,128)S(1)} %get-tuple-element.63), channel_id=1, source_target_pairs={{0,24},{8,0},{16,8},{24,16},{1,25},{9,1},{17,9},{25,17},{2,26},{10... | collective-permute-start | bytes 786440 | tf_op jit(solution)/shard_map/ppermute | solution.py:349
  44.1 4.3 %collective-permute-start.7 = (f32[520,128]{1,0:T(8,128)S(1)}, f32[520,128]{1,0:T(8,128)S(1)}, u32[]{:S(2)}, u32[]{:S(2)}) collective-permute-start(f32[520,128]{1,0:T(8,128)S(1)} %get-tuple-element.56), channel_id=1, source_target_pairs={{0,24},{8,0},{16,8},{24,16},{1,25},{9,1},{17,9},{25,17},{2,26},{10... | collective-permute-start | bytes 798728 | tf_op jit(solution)/shard_map/ppermute | solution.py:349
  48.9 1.6 %shard_map.82 = (f32[256,512]{1,0:T(8,128)S(1)}, f32[4,2,128,128]{3,2,1,0:T(8,128)S(1)}, f32[512,128]{1,0:T(8,128)S(1)}) custom-call(s32[1,128]{1,0:T(1,128)S(1)} %slice_convert_fusion.3.refs_0_, f32[2,4,512,128]{3,2,1,0:T(8,128)S(1)} %shard_map.74.refs_1_, f32[4,2,128,128]{3,2,1,0:T(8,128)S(1)} %copy-done, bf16[4,256,256]{2,1,0:T(8,128)(2,1)S(1)} %copy-done.1, ...), custom_call_target="tpu_custom_call" | custom-call | flops 402653184 | bytes 1048576 | tf_op jit(solution)/shard_map/pallas_call | solution.py:23
  50.6 4.3 %collective-permute-start.11 = (f32[512,128]{1,0:T(8,128)S(1)}, f32[512,128]{1,0:T(8,128)S(1)}, u32[]{:S(2)}, u32[]{:S(2)}) collective-permute-start(f32[512,128]{1,0:T(8,128)S(1)} %get-tuple-element.64), channel_id=1, source_target_pairs={{0,24},{8,0},{16,8},{24,16},{1,25},{9,1},{17,9},{25,17},{2,26},{10... | collective-permute-start | bytes 786440 | tf_op jit(solution)/shard_map/ppermute | solution.py:349
  54.9 2.1 %shard_map.78 = (f32[256,512]{1,0:T(8,128)S(1)}, f32[4,2,128,128]{3,2,1,0:T(8,128)S(1)}, f32[512,128]{1,0:T(8,128)S(1)}, f32[256,512]{1,0:T(8,128)S(1)}, f32[4,2...) custom-call(s32[1,128]{1,0:T(1,128)S(1)} %get-tuple-element.47.refs_0_, f32[2,4,512,128]{3,2,1,0:T(8,128)S(1)} %shard_map.74.refs_1_, ...), custom_call_target="tpu_custom_call" | custom-call | flops 805306368 | bytes 1048576 | tf_op jit(solution)/shard_map/pallas_call | solution.py:23
  57.1 3.8 %collective-permute-done.11.arrived = f32[512,128]{1,0:T(8,128)S(1)} collective-permute-done((f32[512,128]{1,0:T(8,128)S(1)}, f32[512,128]{1,0:T(8,128)S(1)}, u32[]{:S(2)}, u32[]{:S(2)}) %collective-permute-start.11) | collective-permute-done | bytes 262176 | tf_op jit(solution)/shard_map/ppermute | solution.py:349
  61.1 1.8 %collective-permute-start.8 = (f32[520,128]{1,0:T(8,128)S(1)}, f32[520,128]{1,0:T(8,128)S(1)}, u32[]{:S(2)}, u32[]{:S(2)}) collective-permute-start(f32[520,128]{1,0:T(8,128)S(1)} %shard_map.79.refs_5_), channel_id=1, source_target_pairs={{0,8},{8,16},{16,24},{24,0},{1,9},{9,17},{17,25},{25,1},{2,10},{10... | collective-permute-start | bytes 798728 | tf_op jit(solution)/shard_map/ppermute | solution.py:349
  63.0 2.6 %shard_map.86.refs_2_ = f32[1,5,640,128]{3,2,1,0:T(8,128)S(1)} custom-call(s32[3,128]{1,0:T(4,128)S(1)} %pad_add_fusion.3.refs_0_, f32[4,2,128,128]{3,2,1,0:T(8,128)S(1)} %copy-done), custom_call_target="tpu_custom_call" | custom-call | flops 402653184 | bytes 1048576 | tf_op jit(solution)/shard_map/pallas_call | solution.py:23
  65.6 2.3 %shard_map.84.refs_9_ = f32[2,4,512,128]{3,2,1,0:T(8,128)S(1)} custom-call(s32[1,128]{1,0:T(1,128)S(1)} %get-tuple-element.47.refs_0_, f32[4,2,128,128]{3,2,1,0:T(8,128)S(1)} %copy-done, bf16[4,256,256]{2,1,0:T(8,128)(2,1)S(1)} %copy-done.1, f32[256,512]{1,0:T(8,128)S(1)} %get-tuple-element.58.refs_3_, f32[4,2,128,128]{3,2,1,0:T(8,128)S(1)} %get-tuple-element.59.refs_4_, ...), custom_call_target="tpu_custom_call" | custom-call | flops 805306368 | bytes 1048576 | tf_op jit(solution)/shard_map/pallas_call | solution.py:23
  67.9 4.6 %collective-permute-done.13.refs_8_ = f32[512,128]{1,0:T(8,128)S(1)} collective-permute-done((f32[512,128]{1,0:T(8,128)S(1)}, f32[512,128]{1,0:T(8,128)S(1)}, u32[]{:S(2)}, u32[]{:S(2)}) %collective-permute-start.13) | collective-permute-done | bytes 262176 | tf_op jit(solution)/shard_map/ppermute | solution.py:349
  72.4 5.7 %collective-permute-done.8.refs_5_ = f32[520,128]{1,0:T(8,128)S(1)} collective-permute-done((f32[520,128]{1,0:T(8,128)S(1)}, f32[520,128]{1,0:T(8,128)S(1)}, u32[]{:S(2)}, u32[]{:S(2)}) %collective-permute-start.8) | collective-permute-done | bytes 266272 | tf_op jit(solution)/shard_map/ppermute | solution.py:349
  78.2 2.9 %shard_map.87.refs_2_ = f32[1,5,640,128]{3,2,1,0:T(8,128)S(1)} custom-call(s32[3,128]{1,0:T(4,128)S(1)} %pad_add_fusion.2.refs_0_, f32[4,2,128,128]{3,2,1,0:T(8,128)S(1)} %copy-done, f32[1,5,640,128]{3,2,1,0:T(8,128)S(1)} %shard_map.86.refs_2_), custom_call_target="tpu_custom_call", output_to_operand_aliasing={{}: (2, {})} | custom-call | flops 402653184 | bytes 1048576 | tf_op jit(solution)/shard_map/pallas_call | solution.py:23
  81.0 2.2 %shard_map.85.refs_9_ = f32[2,4,512,128]{3,2,1,0:T(8,128)S(1)} custom-call(s32[1,128]{1,0:T(1,128)S(1)} %slice_convert_fusion.3.refs_0_, f32[4,2,128,128]{3,2,1,0:T(8,128)S(1)} %copy-done, bf16[4,256,256]{2,1,0:T(8,128)(2,1)S(1)} %copy-done.1, f32[256,512]{1,0:T(8,128)S(1)} %get-tuple-element.67.refs_3_, ...), custom_call_target="tpu_custom_call", output_to_operand_aliasing={{}: (9, {})} | custom-call | flops 805306368 | bytes 1048576 | tf_op jit(solution)/shard_map/pallas_call | solution.py:23
  83.8 5.7 %collective-permute-done.12.refs_5_ = f32[520,128]{1,0:T(8,128)S(1)} collective-permute-done((f32[520,128]{1,0:T(8,128)S(1)}, f32[520,128]{1,0:T(8,128)S(1)}, u32[]{:S(2)}, u32[]{:S(2)}) %collective-permute-start.12) | collective-permute-done | bytes 266272 | tf_op jit(solution)/shard_map/ppermute | solution.py:349
  89.5 2.4 %shard_map.88.refs_2_ = f32[1,5,640,128]{3,2,1,0:T(8,128)S(1)} custom-call(s32[3,128]{1,0:T(4,128)S(1)} %pad_add_fusion.1.refs_0_, f32[4,2,128,128]{3,2,1,0:T(8,128)S(1)} %copy-done, f32[1,5,640,128]{3,2,1,0:T(8,128)S(1)} %shard_map.87.refs_2_), custom_call_target="tpu_custom_call", output_to_operand_aliasing={{}: (2, {})} | custom-call | flops 402653184 | bytes 1048576 | tf_op jit(solution)/shard_map/pallas_call | solution.py:23
  91.8 2.1 %shard_map.90.refs_6_ = f32[2,4,512,128]{3,2,1,0:T(8,128)S(1)} custom-call(s32[1,128]{1,0:T(1,128)S(1)} %slice_convert_fusion.4.refs_0_, f32[4,2,128,128]{3,2,1,0:T(8,128)S(1)} %copy-done, bf16[4,256,256]{2,1,0:T(8,128)(2,1)S(1)} %copy-done.1, f32[256,512]{1,0:T(8,128)S(1)} %get-tuple-element.77.refs_3_, ...), custom_call_target="tpu_custom_call", output_to_operand_aliasing={{}: (9, {})} | custom-call | flops 805306368 | bytes 1048576 | tf_op jit(solution)/shard_map/pallas_call | solution.py:23
  94.0 5.5 %collective-permute-done.14.refs_5_ = f32[520,128]{1,0:T(8,128)S(1)} collective-permute-done((f32[520,128]{1,0:T(8,128)S(1)}, f32[520,128]{1,0:T(8,128)S(1)}, u32[]{:S(2)}, u32[]{:S(2)}) %collective-permute-start.14) | collective-permute-done | bytes 266272 | tf_op jit(solution)/shard_map/ppermute | solution.py:349
  101.0 1.9 %shard_map.92 = (f32[2,4,512,128]{3,2,1,0:T(8,128)S(1)}, f32[512,128]{1,0:T(8,128)S(1)}, f32[512,128]{1,0:T(8,128)S(1)}, f32[2,64,384]{2,1,0:T(8,128)S(1)}, f32[2,64,384]{2,1,0:T(8,128)S(1)}) custom-call(s32[1,128]{1,0:T(1,128)S(1)} %collective-permute-done.refs_0_, f32[4,2,128,128]{3,2,1,0:T(8,128)S(1)} %copy-done, ...), custom_call_target="tpu_custom_call", output_to_operand_aliasing={{0}: (6, {})} | custom-call | flops 402653184 | bytes 1048576 | tf_op jit(solution)/shard_map/pallas_call | solution.py:23
  103.6 3.4 %collective-permute-start.17 = (f32[512,128]{1,0:T(8,128)S(1)}, f32[512,128]{1,0:T(8,128)S(1)}, u32[]{:S(2)}, u32[]{:S(2)}) collective-permute-start(f32[512,128]{1,0:T(8,128)S(1)} %get-tuple-element.83), channel_id=1, source_target_pairs={{0,1},{2,3},{4,5},{6,7},{1,0},{3,2},{5,4},{7,6},{8,9},{10,11},{12,... | collective-permute-start | bytes 786440 | tf_op jit(solution)/shard_map/ppermute | solution.py:349
  107.7 1.7 %collective-permute-start.19 = (f32[2,64,384]{2,1,0:T(8,128)S(1)}, f32[2,64,384]{2,1,0:T(8,128)S(1)}, u32[]{:S(2)}, u32[]{:S(2)}) collective-permute-start(f32[2,64,384]{2,1,0:T(8,128)S(1)} %get-tuple-element.85), channel_id=1, source_target_pairs={{0,8},{16,24},{8,0},{24,16},{1,9},{17,25},{9,1},{25,17},{2,10},{18... | collective-permute-start | bytes 589832 | tf_op jit(solution)/shard_map/ppermute | solution.py:349
  109.4 2.7 %shard_map.89.refs_1_ = f32[1,5,640,128]{3,2,1,0:T(8,128)S(1)} custom-call(s32[3,128]{1,0:T(4,128)S(1)} %pad_add_fusion.refs_0_, f32[4,2,128,128]{3,2,1,0:T(8,128)S(1)} %copy-done, f32[1,5,640,128]{3,2,1,0:T(8,128)S(1)} %shard_map.88.refs_2_), custom_call_target="tpu_custom_call", output_to_operand_aliasing={{}: (2, {})} | custom-call | flops 402653184 | bytes 1048576 | tf_op jit(solution)/shard_map/pallas_call | solution.py:23
  112.1 2.5 %collective-permute-done.19 = f32[2,64,384]{2,1,0:T(8,128)S(1)} collective-permute-done((f32[2,64,384]{2,1,0:T(8,128)S(1)}, f32[2,64,384]{2,1,0:T(8,128)S(1)}, u32[]{:S(2)}, u32[]{:S(2)}) %collective-permute-start.19) | collective-permute-done | bytes 196640 | tf_op jit(solution)/shard_map/ppermute | solution.py:349
  115.4 3.6 %collective-permute-start.21 = (f32[2,64,128]{2,1,0:T(8,128)S(1)}, f32[2,64,128]{2,1,0:T(8,128)S(1)}, u32[]{:S(2)}, u32[]{:S(2)}) collective-permute-start(f32[2,64,128]{2,1,0:T(8,128)S(1)} %get-tuple-element.114), channel_id=1, source_target_pairs={{0,8},{16,24},{8,0},{24,16},{1,9},{17,25},{9,1},{25,17},{2,10},{18... | collective-permute-start | bytes 196616 | tf_op jit(solution)/shard_map/ppermute | solution.py:349
  119.0 2.2 %collective-permute-done.21 = f32[2,64,128]{2,1,0:T(8,128)S(1)} collective-permute-done((f32[2,64,128]{2,1,0:T(8,128)S(1)}, f32[2,64,128]{2,1,0:T(8,128)S(1)}, u32[]{:S(2)}, u32[]{:S(2)}) %collective-permute-start.21) | collective-permute-done | bytes 65568 | tf_op jit(solution)/shard_map/ppermute | solution.py:349
  121.3 1.6 %shard_map.93 = f32[2,384,384]{2,1,0:T(8,128)} custom-call(f32[2,384,384]{2,1,0:T(8,128)S(1)} %copy-done.3, f32[1,5,640,128]{3,2,1,0:T(8,128)S(1)} %shard_map.89.refs_1_, f32[2,4,512,128]{3,2,1,0:T(8,128)S(1)} %get-tuple-element.82.refs_2_, f32[512,128]{1,0:T(8,128)S(1)} %get-tuple-element.92.refs_3_, f32[512,128]{1,0:T(8,128)S(1)} %get-tuple-element.91.refs_4_, ...), custom_call_target="tpu_custom_call" | custom-call | flops 1000000 | bytes 1048576 | tf_op jit(solution)/shard_map/pallas_call | solution.py:23
  (80 shorter events, 20.8 us)
Async XLA Ops:
  1.1 10.7 %collective-permute-start.2 = (f32[2,64,384]{2,1,0:T(8,128)S(1)}, f32[2,64,384]{2,1,0:T(8,128)S(1)}, u32[]{:S(2)}, u32[]{:S(2)}) collective-permute-start(f32[2,64,384]{2,1,0:T(8,128)S(1)} %get-tuple-element.87), channel_id=1, source_target_pairs={{8,16},{16,8},{9,17},{17,9},{10,18},{18,10},{11,19},{19,11},{12,20... | collective-permute-start | bytes 589832 | tf_op jit(solution)/shard_map/ppermute | solution.py:349
  1.8 10.6 %collective-permute-start.1 = (f32[2,64,384]{2,1,0:T(8,128)S(1)}, f32[2,64,384]{2,1,0:T(8,128)S(1)}, u32[]{:S(2)}, u32[]{:S(2)}) collective-permute-start(f32[2,64,384]{2,1,0:T(8,128)S(1)} %get-tuple-element.88), channel_id=1, source_target_pairs={{0,8},{16,24},{8,0},{24,16},{1,9},{17,25},{9,1},{25,17},{2,10},{18... | collective-permute-start | bytes 589832 | tf_op jit(solution)/shard_map/ppermute | solution.py:349
  8.4 1.3 %copy-start.2 = (f32[2,384,384]{2,1,0:T(8,128)S(1)}, f32[2,384,384]{2,1,0:T(8,128)}, u32[]{:S(2)}) copy-start(f32[2,384,384]{2,1,0:T(8,128)} %refs_0_.1) | copy-start | bytes 3538948
  9.7 0.7 copy-start.4
  10.4 0.7 copy-start.5
  12.8 4.9 %collective-permute-start.4 = (f32[520,128]{1,0:T(8,128)S(1)}, f32[520,128]{1,0:T(8,128)S(1)}, u32[]{:S(2)}, u32[]{:S(2)}) collective-permute-start(f32[520,128]{1,0:T(8,128)S(1)} %broadcast_select_fusion.2), channel_id=1, source_target_pairs={{1,2},{3,4},{5,6},{2,1},{4,3},{6,5},{9,10},{11,12},{13,14},{10,9},... | collective-permute-start | bytes 798728 | tf_op jit(solution)/shard_map/ppermute | solution.py:349
  13.4 4.3 %collective-permute-start.3 = (f32[520,128]{1,0:T(8,128)S(1)}, f32[520,128]{1,0:T(8,128)S(1)}, u32[]{:S(2)}, u32[]{:S(2)}) collective-permute-start(f32[520,128]{1,0:T(8,128)S(1)} %broadcast_select_fusion.3), channel_id=1, source_target_pairs={{0,1},{2,3},{4,5},{6,7},{1,0},{3,2},{5,4},{7,6},{8,9},{10,11},{12,... | collective-permute-start | bytes 798728 | tf_op jit(solution)/shard_map/ppermute | solution.py:349
  16.3 3.6 %collective-permute-start = (s32[1,128]{1,0:T(1,128)S(1)}, s32[1,128]{1,0:T(1,128)S(1)}, u32[]{:S(2)}, u32[]{:S(2)}) collective-permute-start(s32[1,128]{1,0:T(1,128)S(1)} %get-tuple-element.47.refs_0_), channel_id=1, source_target_pairs={{0,24},{8,0},{16,8},{24,16},{1,25},{9,1},{17,9},{25,17},{2,26},{10... | collective-permute-start | bytes 1544 | tf_op jit(solution)/shard_map/ppermute | solution.py:349
  17.8 2.2 %copy-start = (f32[4,2,128,128]{3,2,1,0:T(8,128)S(1)}, f32[4,2,128,128]{3,2,1,0:T(8,128)}, u32[]{:S(2)}) copy-start(f32[4,2,128,128]{3,2,1,0:T(8,128)} %refs_1_.17) | copy-start | bytes 1572868
  17.8 2.1 %copy-start.1 = (bf16[4,256,256]{2,1,0:T(8,128)(2,1)S(1)}, bf16[4,256,256]{2,1,0:T(8,128)(2,1)}, u32[]{:S(2)}) copy-start(bf16[4,256,256]{2,1,0:T(8,128)(2,1)} %constant.25.clone.refs_3_.refs_2_) | copy-start | bytes 1572868
  21.6 9.1 %collective-permute-start.5 = (f32[520,128]{1,0:T(8,128)S(1)}, f32[520,128]{1,0:T(8,128)S(1)}, u32[]{:S(2)}, u32[]{:S(2)}) collective-permute-start(f32[520,128]{1,0:T(8,128)S(1)} %get-tuple-element.54), channel_id=1, source_target_pairs={{0,24},{8,0},{16,8},{24,16},{1,25},{9,1},{17,9},{25,17},{2,26},{10... | collective-permute-start | bytes 798728 | tf_op jit(solution)/shard_map/ppermute | solution.py:349
  26.5 10.2 %collective-permute-start.9 = (f32[512,128]{1,0:T(8,128)S(1)}, f32[512,128]{1,0:T(8,128)S(1)}, u32[]{:S(2)}, u32[]{:S(2)}) collective-permute-start(f32[512,128]{1,0:T(8,128)S(1)} %get-tuple-element.62), channel_id=1, source_target_pairs={{0,24},{8,0},{16,8},{24,16},{1,25},{9,1},{17,9},{25,17},{2,26},{10... | collective-permute-start | bytes 786440 | tf_op jit(solution)/shard_map/ppermute | solution.py:349
  30.6 6.0 %copy-start.6 = (f32[1,1,8,128,128]{4,3,2,1,0:T(8,128)S(1)}, f32[1,1,8,128,128]{4,3,2,1,0:T(8,128)}, u32[]{:S(2)}) copy-start(f32[1,1,8,128,128]{4,3,2,1,0:T(8,128)} %param.12) | copy-start | bytes 1572868
  32.3 10.2 %collective-permute-start.6 = (f32[520,128]{1,0:T(8,128)S(1)}, f32[520,128]{1,0:T(8,128)S(1)}, u32[]{:S(2)}, u32[]{:S(2)}) collective-permute-start(f32[520,128]{1,0:T(8,128)S(1)} %get-tuple-element.55), channel_id=1, source_target_pairs={{0,24},{8,0},{16,8},{24,16},{1,25},{9,1},{17,9},{25,17},{2,26},{10... | collective-permute-start | bytes 798728 | tf_op jit(solution)/shard_map/ppermute | solution.py:349
  38.3 10.6 %collective-permute-start.10 = (f32[512,128]{1,0:T(8,128)S(1)}, f32[512,128]{1,0:T(8,128)S(1)}, u32[]{:S(2)}, u32[]{:S(2)}) collective-permute-start(f32[512,128]{1,0:T(8,128)S(1)} %get-tuple-element.63), channel_id=1, source_target_pairs={{0,24},{8,0},{16,8},{24,16},{1,25},{9,1},{17,9},{25,17},{2,26},{10... | collective-permute-start | bytes 786440 | tf_op jit(solution)/shard_map/ppermute | solution.py:349
  44.1 16.9 %collective-permute-start.7 = (f32[520,128]{1,0:T(8,128)S(1)}, f32[520,128]{1,0:T(8,128)S(1)}, u32[]{:S(2)}, u32[]{:S(2)}) collective-permute-start(f32[520,128]{1,0:T(8,128)S(1)} %get-tuple-element.56), channel_id=1, source_target_pairs={{0,24},{8,0},{16,8},{24,16},{1,25},{9,1},{17,9},{25,17},{2,26},{10... | collective-permute-start | bytes 798728 | tf_op jit(solution)/shard_map/ppermute | solution.py:349
  50.6 10.3 %collective-permute-start.11 = (f32[512,128]{1,0:T(8,128)S(1)}, f32[512,128]{1,0:T(8,128)S(1)}, u32[]{:S(2)}, u32[]{:S(2)}) collective-permute-start(f32[512,128]{1,0:T(8,128)S(1)} %get-tuple-element.64), channel_id=1, source_target_pairs={{0,24},{8,0},{16,8},{24,16},{1,25},{9,1},{17,9},{25,17},{2,26},{10... | collective-permute-start | bytes 786440 | tf_op jit(solution)/shard_map/ppermute | solution.py:349
  61.0 11.5 %collective-permute-start.13 = (f32[512,128]{1,0:T(8,128)S(1)}, f32[512,128]{1,0:T(8,128)S(1)}, u32[]{:S(2)}, u32[]{:S(2)}) collective-permute-start(f32[512,128]{1,0:T(8,128)S(1)} %shard_map.83.refs_8_), channel_id=1, source_target_pairs={{0,8},{8,16},{16,24},{24,0},{1,9},{9,17},{17,25},{25,1},{2,10},{10... | collective-permute-start | bytes 786440 | tf_op jit(solution)/shard_map/ppermute | solution.py:349
  61.1 17.0 %collective-permute-start.8 = (f32[520,128]{1,0:T(8,128)S(1)}, f32[520,128]{1,0:T(8,128)S(1)}, u32[]{:S(2)}, u32[]{:S(2)}) collective-permute-start(f32[520,128]{1,0:T(8,128)S(1)} %shard_map.79.refs_5_), channel_id=1, source_target_pairs={{0,8},{8,16},{16,24},{24,0},{1,9},{9,17},{17,25},{25,1},{2,10},{10... | collective-permute-start | bytes 798728 | tf_op jit(solution)/shard_map/ppermute | solution.py:349
  72.4 11.3 %collective-permute-start.15 = (f32[512,128]{1,0:T(8,128)S(1)}, f32[512,128]{1,0:T(8,128)S(1)}, u32[]{:S(2)}, u32[]{:S(2)}) collective-permute-start(f32[512,128]{1,0:T(8,128)S(1)} %collective-permute-done.13.refs_8_), channel_id=1, source_target_pairs={{0,8},{8,16},{16,24},{24,0},{1,9},{9,17},{17,25},{25,1},{2,10},{10... | collective-permute-start | bytes 786440 | tf_op jit(solution)/shard_map/ppermute | solution.py:349
  78.1 11.3 %collective-permute-start.12 = (f32[520,128]{1,0:T(8,128)S(1)}, f32[520,128]{1,0:T(8,128)S(1)}, u32[]{:S(2)}, u32[]{:S(2)}) collective-permute-start(f32[520,128]{1,0:T(8,128)S(1)} %collective-permute-done.8.refs_5_), channel_id=1, source_target_pairs={{0,8},{8,16},{16,24},{24,0},{1,9},{9,17},{17,25},{25,1},{2,10},{10... | collective-permute-start | bytes 798728 | tf_op jit(solution)/shard_map/ppermute | solution.py:349
  83.8 17.2 %collective-permute-start.16 = (f32[512,128]{1,0:T(8,128)S(1)}, f32[512,128]{1,0:T(8,128)S(1)}, u32[]{:S(2)}, u32[]{:S(2)}) collective-permute-start(f32[512,128]{1,0:T(8,128)S(1)} %collective-permute-done.15.refs_8_), channel_id=1, source_target_pairs={{0,8},{8,16},{16,24},{24,0},{1,9},{9,17},{17,25},{25,1},{2,10},{10... | collective-permute-start | bytes 786440 | tf_op jit(solution)/shard_map/ppermute | solution.py:349
  89.5 10.0 %collective-permute-start.14 = (f32[520,128]{1,0:T(8,128)S(1)}, f32[520,128]{1,0:T(8,128)S(1)}, u32[]{:S(2)}, u32[]{:S(2)}) collective-permute-start(f32[520,128]{1,0:T(8,128)S(1)} %collective-permute-done.12.refs_5_), channel_id=1, source_target_pairs={{0,8},{8,16},{16,24},{24,0},{1,9},{9,17},{17,25},{25,1},{2,10},{10... | collective-permute-start | bytes 798728 | tf_op jit(solution)/shard_map/ppermute | solution.py:349
  102.9 11.7 %collective-permute-start.18 = (f32[512,128]{1,0:T(8,128)S(1)}, f32[512,128]{1,0:T(8,128)S(1)}, u32[]{:S(2)}, u32[]{:S(2)}) collective-permute-start(f32[512,128]{1,0:T(8,128)S(1)} %get-tuple-element.84), channel_id=1, source_target_pairs={{1,2},{3,4},{5,6},{2,1},{4,3},{6,5},{9,10},{11,12},{13,14},{10,9},... | collective-permute-start | bytes 786440 | tf_op jit(solution)/shard_map/ppermute | solution.py:349
  103.6 11.0 %collective-permute-start.17 = (f32[512,128]{1,0:T(8,128)S(1)}, f32[512,128]{1,0:T(8,128)S(1)}, u32[]{:S(2)}, u32[]{:S(2)}) collective-permute-start(f32[512,128]{1,0:T(8,128)S(1)} %get-tuple-element.83), channel_id=1, source_target_pairs={{0,1},{2,3},{4,5},{6,7},{1,0},{3,2},{5,4},{7,6},{8,9},{10,11},{12,... | collective-permute-start | bytes 786440 | tf_op jit(solution)/shard_map/ppermute | solution.py:349
  107.0 5.1 %collective-permute-start.20 = (f32[2,64,384]{2,1,0:T(8,128)S(1)}, f32[2,64,384]{2,1,0:T(8,128)S(1)}, u32[]{:S(2)}, u32[]{:S(2)}) collective-permute-start(f32[2,64,384]{2,1,0:T(8,128)S(1)} %get-tuple-element.86), channel_id=1, source_target_pairs={{8,16},{16,8},{9,17},{17,9},{10,18},{18,10},{11,19},{19,11},{12,20... | collective-permute-start | bytes 589832 | tf_op jit(solution)/shard_map/ppermute | solution.py:349
  107.7 6.9 %collective-permute-start.19 = (f32[2,64,384]{2,1,0:T(8,128)S(1)}, f32[2,64,384]{2,1,0:T(8,128)S(1)}, u32[]{:S(2)}, u32[]{:S(2)}) collective-permute-start(f32[2,64,384]{2,1,0:T(8,128)S(1)} %get-tuple-element.85), channel_id=1, source_target_pairs={{0,8},{16,24},{8,0},{24,16},{1,9},{17,25},{9,1},{25,17},{2,10},{18... | collective-permute-start | bytes 589832 | tf_op jit(solution)/shard_map/ppermute | solution.py:349
  112.1 9.2 %copy-start.3 = (f32[2,384,384]{2,1,0:T(8,128)S(1)}, f32[2,384,384]{2,1,0:T(8,128)}, u32[]{:S(2)}) copy-start(f32[2,384,384]{2,1,0:T(8,128)} %refs_0_.1) | copy-start | bytes 3538948
  114.7 4.3 %collective-permute-start.22 = (f32[2,64,128]{2,1,0:T(8,128)S(1)}, f32[2,64,128]{2,1,0:T(8,128)S(1)}, u32[]{:S(2)}, u32[]{:S(2)}) collective-permute-start(f32[2,64,128]{2,1,0:T(8,128)S(1)} %get-tuple-element.113), channel_id=1, source_target_pairs={{8,16},{16,8},{9,17},{17,9},{10,18},{18,10},{11,19},{19,11},{12,20... | collective-permute-start | bytes 196616 | tf_op jit(solution)/shard_map/ppermute | solution.py:349
  115.4 5.9 %collective-permute-start.21 = (f32[2,64,128]{2,1,0:T(8,128)S(1)}, f32[2,64,128]{2,1,0:T(8,128)S(1)}, u32[]{:S(2)}, u32[]{:S(2)}) collective-permute-start(f32[2,64,128]{2,1,0:T(8,128)S(1)} %get-tuple-element.114), channel_id=1, source_target_pairs={{0,8},{16,24},{8,0},{24,16},{1,9},{17,25},{9,1},{25,17},{2,10},{18... | collective-permute-start | bytes 196616 | tf_op jit(solution)/shard_map/ppermute | solution.py:349

commit v8 on v6

--- a/solution.py
+++ b/solution.py
@@ -186,13 +186,17 @@
     total[channel, tile + 1, rows, :] += jnp.where(lane < shift, moved, 0.0)
 
 
-def write_sides(total, odd, side_1, side_2):
+def write_sides(total, odd, side_1, side_2, ends_2):
     _, tiles, rows, size = total.shape
     low = lanes(rows, size) < size // 2
     left = jnp.where(low, total[0, 0], turn(total[1, 0]))
     right = jnp.where(low, turn(total[0, tiles - 1]), total[1, tiles - 1])
     side_1[...] = jnp.where(odd == 1, left, right)
-    side_2[...] = jnp.where(odd == 1, right, left)
+    second = jnp.where(odd == 1, right, left)
+    half = size // 2
+    side_2[...] = second[half : rows - half, :]
+    ends_2[:half, :] = second[:half, :]
+    ends_2[half:, :] = second[rows - half :, :]
 
 
 def own_columns(total, channel, rows, low):
@@ -221,7 +225,7 @@
         refs = refs[1:]
     total, refs = refs[0], refs[1:]
     if last:
-        (side_1, side_2, rim_1, rim_2), refs = refs[:4], refs[4:]
+        (side_1, side_2, ends_2, rim_1, rim_2), refs = refs[:5], refs[5:]
     x_high, x_low, y_high, y_low = refs
     size = probe.shape[-1]
     lane = lanes(size, size)
@@ -261,7 +265,7 @@
                 add_patch(total, 1, *spot, grad_im, lane)
     if last:
         odd = lax.rem(meta[0, 2 * scans + 2], 2)
-        write_sides(total, odd, side_1, side_2)
+        write_sides(total, odd, side_1, side_2, ends_2)
         odd = lax.rem(lax.rem(meta[0, 2 * scans + 1] + parts[0][0], row_count), 2)
         write_rims(total, odd, rim_1, rim_2)
 
@@ -301,8 +305,7 @@
     _, tiles, rows, size = total.shape
     chunks = (rows - size) // half
     low = lanes(half, size) < half
-    ext = pl.ds((chunk + 1) * half, half)
-    values = own_columns(total, channel, ext, low)
+    values = own_columns(total, channel, pl.ds((chunk + 1) * half, half), low)
 
     def add_sides(from_l, from_r):
         from_l = from_l if channel == 0 else turn(from_l)
@@ -310,7 +313,8 @@
         values[0] += jnp.where(low, from_l, 0.0)
         values[-1] += jnp.where(low, 0.0, from_r)
 
-    add_sides(side_l[ext, :], side_r[ext, :])
+    own = pl.ds(chunk * half, half)
+    add_sides(side_l[own, :], side_r[own, :])
     for at, rim, corner in ((0, in_top, in_ctop), (chunks - 1, in_bot, in_cbot)):
         if chunk == at:
             for t in range(tiles - 1):
@@ -349,17 +353,21 @@
     return lax.ppermute(x, axis, pairs)
 
 
-def send_rims(side_1, side_2, rim_1, rim_2, odd_row, odd_col):
+def send_rims(side_1, side_2, ends_2, rim_1, rim_2, odd_row, odd_col):
     rows, size = side_1.shape
     half = size // 2
+    ends_2 = move(ends_2, "col", swap("col", 1))
+    in_1 = move(side_1, "col", swap("col", 0))
     in_2 = move(side_2, "col", swap("col", 1))
-    in_1 = move(side_1, "col", swap("col", 0))
     rim_1 = move(rim_1, "row", swap("row", 0))
     rim_2 = move(rim_2, "row", swap("row", 1))
+
+    def both(of_1, of_2):
+        return jnp.where(odd_col, jnp.stack([of_1, of_2]), jnp.stack([of_2, of_1]))
+
+    tops, bottoms = both(in_1[:half], ends_2[:half]), both(in_1[rows - half :], ends_2[half:])
+    in_1 = in_1[half : rows - half]
     in_l, in_r = jnp.where(odd_col, in_1, in_2), jnp.where(odd_col, in_2, in_1)
-    tops = jnp.where(odd_col, jnp.stack([in_1[:half], in_2[:half]]), jnp.stack([in_2[:half], in_1[:half]]))
-    low = rows - half
-    bottoms = jnp.where(odd_col, jnp.stack([in_1[low:], in_2[low:]]), jnp.stack([in_2[low:], in_1[low:]]))
     corner_1 = move(jnp.where(odd_row, tops, bottoms), "row", swap("row", 0))
     corner_2 = move(jnp.where(odd_row, bottoms, tops), "row", swap("row", 1))
     in_top, in_bot = jnp.where(odd_row, rim_1, rim_2), jnp.where(odd_row, rim_2, rim_1)
@@ -498,7 +506,7 @@
             fresh, last = total is None, which == most and group[-1] == halves[-1]
             outs = [(2, tiles, rows, size)]
             if last:
-                outs += [(rows, size)] * 2 + [(2, half, tile_columns)] * 2
+                outs += [(rows, size), (tile_rows, size), (size, size)] + [(2, half, tile_columns)] * 2
             args = [metas[which], probe, tables]
             for start, _ in group:
                 args += [far[which, start], wave[which, start], factors[start]]

time: 123 us -> 123 us (level)
  the two profiles are of different devices: /device:TPU:0 before, /device:TPU:1 now
where the time goes in v8:
time: 123 us; the launch traced here: 122 us
  starting transfers between devices  44.5 us (36%)
  Pallas kernels  36 us (29%)
  waiting for transfers between devices  35.3 us (29%)
  local copies, waits for them, and re-layouts  4.64 us (4%)
    ppermute x24, starting transfers between devices, move(): return lax.ppermute(x, axis, pairs)  44.5 us
    pallas_call x21, Pallas kernels, call(): pl.pallas_call(kernel, out_shape=[s if hasattr(s, 'dtype') else jax.Shape...  36 us
    ppermute x24, waiting for transfers between devices, move(): return lax.ppermute(x, axis, pairs)  35.3 us
    unnamed x12, local copies, waits for them, and re-layouts  3.35 us
  transfers between devices with their start and end apart: 24, of which 10 were waited for; matrix products, arithmetic and copies ran while one was open for 2% of the time, Pallas kernels for 25%

profile of v8, /device:TPU:1, one launch (start us, length us, event | category | flops | bytes accessed | tf_op | source)
XLA Modules:
  0.0 122.0 jit_solution(1655708064676151498)
XLA Ops:
  1.7 4.7 %collective-permute-start.1 = (f32[2,64,384]{2,1,0:T(8,128)S(1)}, f32[2,64,384]{2,1,0:T(8,128)S(1)}, u32[]{:S(2)}, u32[]{:S(2)}) collective-permute-start(f32[2,64,384]{2,1,0:T(8,128)S(1)} %get-tuple-element.80), channel_id=1, source_target_pairs={{0,8},{16,24},{8,0},{24,16},{1,9},{17,25},{9,1},{25,17},{2,10},{18... | collective-permute-start | bytes 589832 | tf_op jit(solution)/shard_map/ppermute | solution.py:353
  11.2 4.5 %collective-permute-start.4 = (f32[520,128]{1,0:T(8,128)S(1)}, f32[520,128]{1,0:T(8,128)S(1)}, u32[]{:S(2)}, u32[]{:S(2)}) collective-permute-start(f32[520,128]{1,0:T(8,128)S(1)} %broadcast_select_fusion.2), channel_id=1, source_target_pairs={{1,2},{3,4},{5,6},{2,1},{4,3},{6,5},{9,10},{11,12},{13,14},{10,9},... | collective-permute-start | bytes 798728 | tf_op jit(solution)/shard_map/ppermute | solution.py:353
  16.9 4.8 %collective-permute-done.4 = f32[520,128]{1,0:T(8,128)S(1)} collective-permute-done((f32[520,128]{1,0:T(8,128)S(1)}, f32[520,128]{1,0:T(8,128)S(1)}, u32[]{:S(2)}, u32[]{:S(2)}) %collective-permute-start.4) | collective-permute-done | bytes 266272 | tf_op jit(solution)/shard_map/ppermute | solution.py:353
  23.0 1.6 %shard_map.75 = (f32[256,512]{1,0:T(8,128)S(1)}, f32[4,2,128,128]{3,2,1,0:T(8,128)S(1)}, f32[520,128]{1,0:T(8,128)S(1)}) custom-call(s32[1,128]{1,0:T(1,128)S(1)} %collective-permute-done.refs_0_, f32[2,4,512,128]{3,2,1,0:T(8,128)S(1)} %shard_map.74.refs_1_, f32[4,2,128,128]{3,2,1,0:T(8,128)S(1)} %copy-done, bf16[4,256,256]{2,1,0:T(8,128)(2,1)S(1)} %copy-done.1), custom_call_target="tpu_custom_call" | custom-call | flops 402653184 | bytes 1048576 | tf_op jit(solution)/shard_map/pallas_call | solution.py:23
  29.0 3.0 %collective-permute-done.5.refs_4_ = f32[520,128]{1,0:T(8,128)S(1)} collective-permute-done((f32[520,128]{1,0:T(8,128)S(1)}, f32[520,128]{1,0:T(8,128)S(1)}, u32[]{:S(2)}, u32[]{:S(2)}) %collective-permute-start.5) | collective-permute-done | bytes 266272 | tf_op jit(solution)/shard_map/ppermute | solution.py:353
  32.0 1.6 %shard_map.76 = (f32[256,512]{1,0:T(8,128)S(1)}, f32[4,2,128,128]{3,2,1,0:T(8,128)S(1)}, f32[520,128]{1,0:T(8,128)S(1)}) custom-call(s32[1,128]{1,0:T(1,128)S(1)} %slice_convert_fusion.4.refs_0_, f32[2,4,512,128]{3,2,1,0:T(8,128)S(1)} %shard_map.74.refs_1_, f32[4,2,128,128]{3,2,1,0:T(8,128)S(1)} %copy-done, bf16[4,256,256]{2,1,0:T(8,128)(2,1)S(1)} %copy-done.1, ...), custom_call_target="tpu_custom_call" | custom-call | flops 402653184 | bytes 1048576 | tf_op jit(solution)/shard_map/pallas_call | solution.py:23
  33.6 4.1 %collective-permute-start.6 = (f32[520,128]{1,0:T(8,128)S(1)}, f32[520,128]{1,0:T(8,128)S(1)}, u32[]{:S(2)}, u32[]{:S(2)}) collective-permute-start(f32[520,128]{1,0:T(8,128)S(1)} %get-tuple-element.46), channel_id=1, source_target_pairs={{0,24},{8,0},{16,8},{24,16},{1,25},{9,1},{17,9},{25,17},{2,26},{10... | collective-permute-start | bytes 798728 | tf_op jit(solution)/shard_map/ppermute | solution.py:353
  37.7 1.6 %shard_map.81 = (f32[256,512]{1,0:T(8,128)S(1)}, f32[4,2,128,128]{3,2,1,0:T(8,128)S(1)}, f32[512,128]{1,0:T(8,128)S(1)}) custom-call(s32[1,128]{1,0:T(1,128)S(1)} %slice_convert_fusion.4.refs_0_, f32[2,4,512,128]{3,2,1,0:T(8,128)S(1)} %shard_map.74.refs_1_, f32[4,2,128,128]{3,2,1,0:T(8,128)S(1)} %copy-done, bf16[4,256,256]{2,1,0:T(8,128)(2,1)S(1)} %copy-done.1, ...), custom_call_target="tpu_custom_call" | custom-call | flops 402653184 | bytes 1048576 | tf_op jit(solution)/shard_map/pallas_call | solution.py:23
  39.3 2.7 %collective-permute-start.10 = (f32[512,128]{1,0:T(8,128)S(1)}, f32[512,128]{1,0:T(8,128)S(1)}, u32[]{:S(2)}, u32[]{:S(2)}) collective-permute-start(f32[512,128]{1,0:T(8,128)S(1)} %get-tuple-element.54), channel_id=1, source_target_pairs={{0,24},{8,0},{16,8},{24,16},{1,25},{9,1},{17,9},{25,17},{2,26},{10... | collective-permute-start | bytes 786440 | tf_op jit(solution)/shard_map/ppermute | solution.py:353
  42.9 1.6 %shard_map.77 = (f32[256,512]{1,0:T(8,128)S(1)}, f32[4,2,128,128]{3,2,1,0:T(8,128)S(1)}, f32[520,128]{1,0:T(8,128)S(1)}) custom-call(s32[1,128]{1,0:T(1,128)S(1)} %slice_convert_fusion.3.refs_0_, f32[2,4,512,128]{3,2,1,0:T(8,128)S(1)} %shard_map.74.refs_1_, f32[4,2,128,128]{3,2,1,0:T(8,128)S(1)} %copy-done, bf16[4,256,256]{2,1,0:T(8,128)(2,1)S(1)} %copy-done.1, ...), custom_call_target="tpu_custom_call" | custom-call | flops 402653184 | bytes 1048576 | tf_op jit(solution)/shard_map/pallas_call | solution.py:23
  44.6 4.1 %collective-permute-start.7 = (f32[520,128]{1,0:T(8,128)S(1)}, f32[520,128]{1,0:T(8,128)S(1)}, u32[]{:S(2)}, u32[]{:S(2)}) collective-permute-start(f32[520,128]{1,0:T(8,128)S(1)} %get-tuple-element.47), channel_id=1, source_target_pairs={{0,24},{8,0},{16,8},{24,16},{1,25},{9,1},{17,9},{25,17},{2,26},{10... | collective-permute-start | bytes 798728 | tf_op jit(solution)/shard_map/ppermute | solution.py:353
  48.7 1.6 %shard_map.82 = (f32[256,512]{1,0:T(8,128)S(1)}, f32[4,2,128,128]{3,2,1,0:T(8,128)S(1)}, f32[512,128]{1,0:T(8,128)S(1)}) custom-call(s32[1,128]{1,0:T(1,128)S(1)} %slice_convert_fusion.3.refs_0_, f32[2,4,512,128]{3,2,1,0:T(8,128)S(1)} %shard_map.74.refs_1_, f32[4,2,128,128]{3,2,1,0:T(8,128)S(1)} %copy-done, bf16[4,256,256]{2,1,0:T(8,128)(2,1)S(1)} %copy-done.1, ...), custom_call_target="tpu_custom_call" | custom-call | flops 402653184 | bytes 1048576 | tf_op jit(solution)/shard_map/pallas_call | solution.py:23
  50.4 3.8 %collective-permute-start.11 = (f32[512,128]{1,0:T(8,128)S(1)}, f32[512,128]{1,0:T(8,128)S(1)}, u32[]{:S(2)}, u32[]{:S(2)}) collective-permute-start(f32[512,128]{1,0:T(8,128)S(1)} %get-tuple-element.55), channel_id=1, source_target_pairs={{0,24},{8,0},{16,8},{24,16},{1,25},{9,1},{17,9},{25,17},{2,26},{10... | collective-permute-start | bytes 786440 | tf_op jit(solution)/shard_map/ppermute | solution.py:353
  54.1 2.1 %shard_map.78 = (f32[256,512]{1,0:T(8,128)S(1)}, f32[4,2,128,128]{3,2,1,0:T(8,128)S(1)}, f32[512,128]{1,0:T(8,128)S(1)}, f32[256,512]{1,0:T(8,128)S(1)}, f32[4,2...) custom-call(s32[1,128]{1,0:T(1,128)S(1)} %get-tuple-element.42.refs_0_, f32[2,4,512,128]{3,2,1,0:T(8,128)S(1)} %shard_map.74.refs_1_, ...), custom_call_target="tpu_custom_call" | custom-call | flops 805306368 | bytes 1048576 | tf_op jit(solution)/shard_map/pallas_call | solution.py:23
  56.3 3.3 %collective-permute-done.11.arrived = f32[512,128]{1,0:T(8,128)S(1)} collective-permute-done((f32[512,128]{1,0:T(8,128)S(1)}, f32[512,128]{1,0:T(8,128)S(1)}, u32[]{:S(2)}, u32[]{:S(2)}) %collective-permute-start.11) | collective-permute-done | bytes 262176 | tf_op jit(solution)/shard_map/ppermute | solution.py:353
  61.4 2.5 %shard_map.86.refs_2_ = f32[1,5,640,128]{3,2,1,0:T(8,128)S(1)} custom-call(s32[3,128]{1,0:T(4,128)S(1)} %pad_add_fusion.3.refs_0_, f32[4,2,128,128]{3,2,1,0:T(8,128)S(1)} %copy-done), custom_call_target="tpu_custom_call" | custom-call | flops 402653184 | bytes 1048576 | tf_op jit(solution)/shard_map/pallas_call | solution.py:23
  63.9 2.3 %shard_map.84.refs_9_ = f32[2,4,512,128]{3,2,1,0:T(8,128)S(1)} custom-call(s32[1,128]{1,0:T(1,128)S(1)} %get-tuple-element.42.refs_0_, f32[4,2,128,128]{3,2,1,0:T(8,128)S(1)} %copy-done, bf16[4,256,256]{2,1,0:T(8,128)(2,1)S(1)} %copy-done.1, f32[256,512]{1,0:T(8,128)S(1)} %get-tuple-element.49.refs_3_, f32[4,2,128,128]{3,2,1,0:T(8,128)S(1)} %get-tuple-element.50.refs_4_, ...), custom_call_target="tpu_custom_call" | custom-call | flops 805306368 | bytes 1048576 | tf_op jit(solution)/shard_map/pallas_call | solution.py:23
  66.2 3.1 %collective-permute-done.13.refs_8_ = f32[512,128]{1,0:T(8,128)S(1)} collective-permute-done((f32[512,128]{1,0:T(8,128)S(1)}, f32[512,128]{1,0:T(8,128)S(1)}, u32[]{:S(2)}, u32[]{:S(2)}) %collective-permute-start.13) | collective-permute-done | bytes 262176 | tf_op jit(solution)/shard_map/ppermute | solution.py:353
  69.6 5.4 %collective-permute-done.8.refs_5_ = f32[520,128]{1,0:T(8,128)S(1)} collective-permute-done((f32[520,128]{1,0:T(8,128)S(1)}, f32[520,128]{1,0:T(8,128)S(1)}, u32[]{:S(2)}, u32[]{:S(2)}) %collective-permute-start.8) | collective-permute-done | bytes 266272 | tf_op jit(solution)/shard_map/ppermute | solution.py:353
  75.0 2.8 %shard_map.87.refs_2_ = f32[1,5,640,128]{3,2,1,0:T(8,128)S(1)} custom-call(s32[3,128]{1,0:T(4,128)S(1)} %pad_add_fusion.2.refs_0_, f32[4,2,128,128]{3,2,1,0:T(8,128)S(1)} %copy-done, f32[1,5,640,128]{3,2,1,0:T(8,128)S(1)} %shard_map.86.refs_2_), custom_call_target="tpu_custom_call", output_to_operand_aliasing={{}: (2, {})} | custom-call | flops 402653184 | bytes 1048576 | tf_op jit(solution)/shard_map/pallas_call | solution.py:23
  77.8 2.1 %shard_map.85.refs_9_ = f32[2,4,512,128]{3,2,1,0:T(8,128)S(1)} custom-call(s32[1,128]{1,0:T(1,128)S(1)} %slice_convert_fusion.3.refs_0_, f32[4,2,128,128]{3,2,1,0:T(8,128)S(1)} %copy-done, bf16[4,256,256]{2,1,0:T(8,128)(2,1)S(1)} %copy-done.1, f32[256,512]{1,0:T(8,128)S(1)} %get-tuple-element.58.refs_3_, ...), custom_call_target="tpu_custom_call", output_to_operand_aliasing={{}: (9, {})} | custom-call | flops 805306368 | bytes 1048576 | tf_op jit(solution)/shard_map/pallas_call | solution.py:23
  80.6 5.7 %collective-permute-done.12.refs_5_ = f32[520,128]{1,0:T(8,128)S(1)} collective-permute-done((f32[520,128]{1,0:T(8,128)S(1)}, f32[520,128]{1,0:T(8,128)S(1)}, u32[]{:S(2)}, u32[]{:S(2)}) %collective-permute-start.12) | collective-permute-done | bytes 266272 | tf_op jit(solution)/shard_map/ppermute | solution.py:353
  86.4 2.9 %shard_map.88.refs_2_ = f32[1,5,640,128]{3,2,1,0:T(8,128)S(1)} custom-call(s32[3,128]{1,0:T(4,128)S(1)} %pad_add_fusion.1.refs_0_, f32[4,2,128,128]{3,2,1,0:T(8,128)S(1)} %copy-done, f32[1,5,640,128]{3,2,1,0:T(8,128)S(1)} %shard_map.87.refs_2_), custom_call_target="tpu_custom_call", output_to_operand_aliasing={{}: (2, {})} | custom-call | flops 402653184 | bytes 1048576 | tf_op jit(solution)/shard_map/pallas_call | solution.py:23
  89.2 2.1 %shard_map.90.refs_6_ = f32[2,4,512,128]{3,2,1,0:T(8,128)S(1)} custom-call(s32[1,128]{1,0:T(1,128)S(1)} %slice_convert_fusion.4.refs_0_, f32[4,2,128,128]{3,2,1,0:T(8,128)S(1)} %copy-done, bf16[4,256,256]{2,1,0:T(8,128)(2,1)S(1)} %copy-done.1, f32[256,512]{1,0:T(8,128)S(1)} %get-tuple-element.68.refs_3_, ...), custom_call_target="tpu_custom_call", output_to_operand_aliasing={{}: (9, {})} | custom-call | flops 805306368 | bytes 1048576 | tf_op jit(solution)/shard_map/pallas_call | solution.py:23
  91.4 6.3 %collective-permute-done.14.refs_5_ = f32[520,128]{1,0:T(8,128)S(1)} collective-permute-done((f32[520,128]{1,0:T(8,128)S(1)}, f32[520,128]{1,0:T(8,128)S(1)}, u32[]{:S(2)}, u32[]{:S(2)}) %collective-permute-start.14) | collective-permute-done | bytes 266272 | tf_op jit(solution)/shard_map/ppermute | solution.py:353
  99.2 1.9 %shard_map.92 = (f32[2,4,512,128]{3,2,1,0:T(8,128)S(1)}, f32[512,128]{1,0:T(8,128)S(1)}, f32[384,128]{1,0:T(8,128)S(1)}, f32[128,128]{1,0:T(8,128)S(1)}, f32[2,6...) custom-call(s32[1,128]{1,0:T(1,128)S(1)} %collective-permute-done.refs_0_, ...), custom_call_target="tpu_custom_call", output_to_operand_aliasing={{0}: (6, {})} | custom-call | flops 402653184 | bytes 1048576 | tf_op jit(solution)/shard_map/pallas_call | solution.py:23
  101.1 4.7 %collective-permute-start.18 = (f32[384,128]{1,0:T(8,128)S(1)}, f32[384,128]{1,0:T(8,128)S(1)}, u32[]{:S(2)}, u32[]{:S(2)}) collective-permute-start(f32[384,128]{1,0:T(8,128)S(1)} %get-tuple-element.75), channel_id=1, source_target_pairs={{1,2},{3,4},{5,6},{2,1},{4,3},{6,5},{9,10},{11,12},{13,14},{10,9},... | collective-permute-start | bytes 589832 | tf_op jit(solution)/shard_map/ppermute | solution.py:353
  107.9 5.1 %collective-permute-start.21 = (f32[128,128]{1,0:T(8,128)S(1)}, f32[128,128]{1,0:T(8,128)S(1)}, u32[]{:S(2)}, u32[]{:S(2)}) collective-permute-start(f32[128,128]{1,0:T(8,128)S(1)} %get-tuple-element.78), channel_id=1, source_target_pairs={{1,2},{3,4},{5,6},{2,1},{4,3},{6,5},{9,10},{11,12},{13,14},{10,9},... | collective-permute-start | bytes 196616 | tf_op jit(solution)/shard_map/ppermute | solution.py:353
  113.0 2.6 %shard_map.89.refs_1_ = f32[1,5,640,128]{3,2,1,0:T(8,128)S(1)} custom-call(s32[3,128]{1,0:T(4,128)S(1)} %pad_add_fusion.refs_0_, f32[4,2,128,128]{3,2,1,0:T(8,128)S(1)} %copy-done, f32[1,5,640,128]{3,2,1,0:T(8,128)S(1)} %shard_map.88.refs_2_), custom_call_target="tpu_custom_call", output_to_operand_aliasing={{}: (2, {})} | custom-call | flops 402653184 | bytes 1048576 | tf_op jit(solution)/shard_map/pallas_call | solution.py:23
  116.6 1.7 %collective-permute-start.22 = (f32[2,64,128]{2,1,0:T(8,128)S(1)}, f32[2,64,128]{2,1,0:T(8,128)S(1)}, u32[]{:S(2)}, u32[]{:S(2)}) collective-permute-start(f32[2,64,128]{2,1,0:T(8,128)S(1)} %get-tuple-element.104), channel_id=1, source_target_pairs={{0,8},{16,24},{8,0},{24,16},{1,9},{17,25},{9,1},{25,17},{2,10},{18... | collective-permute-start | bytes 196616 | tf_op jit(solution)/shard_map/ppermute | solution.py:353
  118.3 2.1 %collective-permute-done.22 = f32[2,64,128]{2,1,0:T(8,128)S(1)} collective-permute-done((f32[2,64,128]{2,1,0:T(8,128)S(1)}, f32[2,64,128]{2,1,0:T(8,128)S(1)}, u32[]{:S(2)}, u32[]{:S(2)}) %collective-permute-start.22) | collective-permute-done | bytes 65568 | tf_op jit(solution)/shard_map/ppermute | solution.py:353
  120.4 1.6 %shard_map.93 = f32[2,384,384]{2,1,0:T(8,128)} custom-call(f32[2,384,384]{2,1,0:T(8,128)S(1)} %copy-done.3, f32[1,5,640,128]{3,2,1,0:T(8,128)S(1)} %shard_map.89.refs_1_, f32[2,4,512,128]{3,2,1,0:T(8,128)S(1)} %get-tuple-element.73.refs_2_, f32[384,128]{1,0:T(8,128)S(1)} %get-tuple-element.86.refs_3_, f32[384,128]{1,0:T(8,128)S(1)} %get-tuple-element.85.refs_4_, ...), custom_call_target="tpu_custom_call" | custom-call | flops 1000000 | bytes 1048576 | tf_op jit(solution)/shard_map/pallas_call | solution.py:23
  (80 shorter events, 20.8 us)
Async XLA Ops:
  1.1 9.8 %collective-permute-start.2 = (f32[2,64,384]{2,1,0:T(8,128)S(1)}, f32[2,64,384]{2,1,0:T(8,128)S(1)}, u32[]{:S(2)}, u32[]{:S(2)}) collective-permute-start(f32[2,64,384]{2,1,0:T(8,128)S(1)} %get-tuple-element.79), channel_id=1, source_target_pairs={{8,16},{16,8},{9,17},{17,9},{10,18},{18,10},{11,19},{19,11},{12,20... | collective-permute-start | bytes 589832 | tf_op jit(solution)/shard_map/ppermute | solution.py:353
  1.7 9.1 %collective-permute-start.1 = (f32[2,64,384]{2,1,0:T(8,128)S(1)}, f32[2,64,384]{2,1,0:T(8,128)S(1)}, u32[]{:S(2)}, u32[]{:S(2)}) collective-permute-start(f32[2,64,384]{2,1,0:T(8,128)S(1)} %get-tuple-element.80), channel_id=1, source_target_pairs={{0,8},{16,24},{8,0},{24,16},{1,9},{17,25},{9,1},{25,17},{2,10},{18... | collective-permute-start | bytes 589832 | tf_op jit(solution)/shard_map/ppermute | solution.py:353
  8.7 1.3 %copy-start.2 = (f32[2,384,384]{2,1,0:T(8,128)S(1)}, f32[2,384,384]{2,1,0:T(8,128)}, u32[]{:S(2)}) copy-start(f32[2,384,384]{2,1,0:T(8,128)} %refs_0_.1) | copy-start | bytes 3538948
  11.2 10.5 %collective-permute-start.4 = (f32[520,128]{1,0:T(8,128)S(1)}, f32[520,128]{1,0:T(8,128)S(1)}, u32[]{:S(2)}, u32[]{:S(2)}) collective-permute-start(f32[520,128]{1,0:T(8,128)S(1)} %broadcast_select_fusion.2), channel_id=1, source_target_pairs={{1,2},{3,4},{5,6},{2,1},{4,3},{6,5},{9,10},{11,12},{13,14},{10,9},... | collective-permute-start | bytes 798728 | tf_op jit(solution)/shard_map/ppermute | solution.py:353
  15.7 6.0 %collective-permute-start.3 = (f32[520,128]{1,0:T(8,128)S(1)}, f32[520,128]{1,0:T(8,128)S(1)}, u32[]{:S(2)}, u32[]{:S(2)}) collective-permute-start(f32[520,128]{1,0:T(8,128)S(1)} %broadcast_select_fusion.3), channel_id=1, source_target_pairs={{0,1},{2,3},{4,5},{6,7},{1,0},{3,2},{5,4},{7,6},{8,9},{10,11},{12,... | collective-permute-start | bytes 798728 | tf_op jit(solution)/shard_map/ppermute | solution.py:353
  15.8 6.7 %collective-permute-start = (s32[1,128]{1,0:T(1,128)S(1)}, s32[1,128]{1,0:T(1,128)S(1)}, u32[]{:S(2)}, u32[]{:S(2)}) collective-permute-start(s32[1,128]{1,0:T(1,128)S(1)} %get-tuple-element.42.refs_0_), channel_id=1, source_target_pairs={{0,24},{8,0},{16,8},{24,16},{1,25},{9,1},{17,9},{25,17},{2,26},{10... | collective-permute-start | bytes 1544 | tf_op jit(solution)/shard_map/ppermute | solution.py:353
  21.8 1.0 copy-start
  21.8 1.2 copy-start.1
  24.6 7.3 %collective-permute-start.5 = (f32[520,128]{1,0:T(8,128)S(1)}, f32[520,128]{1,0:T(8,128)S(1)}, u32[]{:S(2)}, u32[]{:S(2)}) collective-permute-start(f32[520,128]{1,0:T(8,128)S(1)} %get-tuple-element.45), channel_id=1, source_target_pairs={{0,24},{8,0},{16,8},{24,16},{1,25},{9,1},{17,9},{25,17},{2,26},{10... | collective-permute-start | bytes 798728 | tf_op jit(solution)/shard_map/ppermute | solution.py:353
  27.5 10.2 %collective-permute-start.9 = (f32[512,128]{1,0:T(8,128)S(1)}, f32[512,128]{1,0:T(8,128)S(1)}, u32[]{:S(2)}, u32[]{:S(2)}) collective-permute-start(f32[512,128]{1,0:T(8,128)S(1)} %get-tuple-element.53), channel_id=1, source_target_pairs={{0,24},{8,0},{16,8},{24,16},{1,25},{9,1},{17,9},{25,17},{2,26},{10... | collective-permute-start | bytes 786440 | tf_op jit(solution)/shard_map/ppermute | solution.py:353
  32.0 5.7 %copy-start.4 = (f32[1,1,8,128,128]{4,3,2,1,0:T(8,128)S(1)}, f32[1,1,8,128,128]{4,3,2,1,0:T(8,128)}, u32[]{:S(2)}) copy-start(f32[1,1,8,128,128]{4,3,2,1,0:T(8,128)} %param.12) | copy-start | bytes 1572868
  33.6 9.3 %collective-permute-start.6 = (f32[520,128]{1,0:T(8,128)S(1)}, f32[520,128]{1,0:T(8,128)S(1)}, u32[]{:S(2)}, u32[]{:S(2)}) collective-permute-start(f32[520,128]{1,0:T(8,128)S(1)} %get-tuple-element.46), channel_id=1, source_target_pairs={{0,24},{8,0},{16,8},{24,16},{1,25},{9,1},{17,9},{25,17},{2,26},{10... | collective-permute-start | bytes 798728 | tf_op jit(solution)/shard_map/ppermute | solution.py:353
  39.3 9.4 %collective-permute-start.10 = (f32[512,128]{1,0:T(8,128)S(1)}, f32[512,128]{1,0:T(8,128)S(1)}, u32[]{:S(2)}, u32[]{:S(2)}) collective-permute-start(f32[512,128]{1,0:T(8,128)S(1)} %get-tuple-element.54), channel_id=1, source_target_pairs={{0,24},{8,0},{16,8},{24,16},{1,25},{9,1},{17,9},{25,17},{2,26},{10... | collective-permute-start | bytes 786440 | tf_op jit(solution)/shard_map/ppermute | solution.py:353
  44.6 15.4 %collective-permute-start.7 = (f32[520,128]{1,0:T(8,128)S(1)}, f32[520,128]{1,0:T(8,128)S(1)}, u32[]{:S(2)}, u32[]{:S(2)}) collective-permute-start(f32[520,128]{1,0:T(8,128)S(1)} %get-tuple-element.47), channel_id=1, source_target_pairs={{0,24},{8,0},{16,8},{24,16},{1,25},{9,1},{17,9},{25,17},{2,26},{10... | collective-permute-start | bytes 798728 | tf_op jit(solution)/shard_map/ppermute | solution.py:353
  50.4 9.3 %collective-permute-start.11 = (f32[512,128]{1,0:T(8,128)S(1)}, f32[512,128]{1,0:T(8,128)S(1)}, u32[]{:S(2)}, u32[]{:S(2)}) collective-permute-start(f32[512,128]{1,0:T(8,128)S(1)} %get-tuple-element.55), channel_id=1, source_target_pairs={{0,24},{8,0},{16,8},{24,16},{1,25},{9,1},{17,9},{25,17},{2,26},{10... | collective-permute-start | bytes 786440 | tf_op jit(solution)/shard_map/ppermute | solution.py:353
  59.7 9.6 %collective-permute-start.13 = (f32[512,128]{1,0:T(8,128)S(1)}, f32[512,128]{1,0:T(8,128)S(1)}, u32[]{:S(2)}, u32[]{:S(2)}) collective-permute-start(f32[512,128]{1,0:T(8,128)S(1)} %shard_map.83.refs_8_), channel_id=1, source_target_pairs={{0,8},{8,16},{16,24},{24,0},{1,9},{9,17},{17,25},{25,1},{2,10},{10... | collective-permute-start | bytes 786440 | tf_op jit(solution)/shard_map/ppermute | solution.py:353
  60.1 14.9 %collective-permute-start.8 = (f32[520,128]{1,0:T(8,128)S(1)}, f32[520,128]{1,0:T(8,128)S(1)}, u32[]{:S(2)}, u32[]{:S(2)}) collective-permute-start(f32[520,128]{1,0:T(8,128)S(1)} %shard_map.79.refs_5_), channel_id=1, source_target_pairs={{0,8},{8,16},{16,24},{24,0},{1,9},{9,17},{17,25},{25,1},{2,10},{10... | collective-permute-start | bytes 798728 | tf_op jit(solution)/shard_map/ppermute | solution.py:353
  69.3 11.3 %collective-permute-start.15 = (f32[512,128]{1,0:T(8,128)S(1)}, f32[512,128]{1,0:T(8,128)S(1)}, u32[]{:S(2)}, u32[]{:S(2)}) collective-permute-start(f32[512,128]{1,0:T(8,128)S(1)} %collective-permute-done.13.refs_8_), channel_id=1, source_target_pairs={{0,8},{8,16},{16,24},{24,0},{1,9},{9,17},{17,25},{25,1},{2,10},{10... | collective-permute-start | bytes 786440 | tf_op jit(solution)/shard_map/ppermute | solution.py:353
  75.0 11.3 %collective-permute-start.12 = (f32[520,128]{1,0:T(8,128)S(1)}, f32[520,128]{1,0:T(8,128)S(1)}, u32[]{:S(2)}, u32[]{:S(2)}) collective-permute-start(f32[520,128]{1,0:T(8,128)S(1)} %collective-permute-done.8.refs_5_), channel_id=1, source_target_pairs={{0,8},{8,16},{16,24},{24,0},{1,9},{9,17},{17,25},{25,1},{2,10},{10... | collective-permute-start | bytes 798728 | tf_op jit(solution)/shard_map/ppermute | solution.py:353
  80.6 18.6 %collective-permute-start.16 = (f32[512,128]{1,0:T(8,128)S(1)}, f32[512,128]{1,0:T(8,128)S(1)}, u32[]{:S(2)}, u32[]{:S(2)}) collective-permute-start(f32[512,128]{1,0:T(8,128)S(1)} %collective-permute-done.15.refs_8_), channel_id=1, source_target_pairs={{0,8},{8,16},{16,24},{24,0},{1,9},{9,17},{17,25},{25,1},{2,10},{10... | collective-permute-start | bytes 786440 | tf_op jit(solution)/shard_map/ppermute | solution.py:353
  86.3 11.3 %collective-permute-start.14 = (f32[520,128]{1,0:T(8,128)S(1)}, f32[520,128]{1,0:T(8,128)S(1)}, u32[]{:S(2)}, u32[]{:S(2)}) collective-permute-start(f32[520,128]{1,0:T(8,128)S(1)} %collective-permute-done.12.refs_5_), channel_id=1, source_target_pairs={{0,8},{8,16},{16,24},{24,0},{1,9},{9,17},{17,25},{25,1},{2,10},{10... | collective-permute-start | bytes 798728 | tf_op jit(solution)/shard_map/ppermute | solution.py:353
  101.1 17.1 %collective-permute-start.18 = (f32[384,128]{1,0:T(8,128)S(1)}, f32[384,128]{1,0:T(8,128)S(1)}, u32[]{:S(2)}, u32[]{:S(2)}) collective-permute-start(f32[384,128]{1,0:T(8,128)S(1)} %get-tuple-element.75), channel_id=1, source_target_pairs={{1,2},{3,4},{5,6},{2,1},{4,3},{6,5},{9,10},{11,12},{13,14},{10,9},... | collective-permute-start | bytes 589832 | tf_op jit(solution)/shard_map/ppermute | solution.py:353
  105.8 9.9 %collective-permute-start.17 = (f32[512,128]{1,0:T(8,128)S(1)}, f32[512,128]{1,0:T(8,128)S(1)}, u32[]{:S(2)}, u32[]{:S(2)}) collective-permute-start(f32[512,128]{1,0:T(8,128)S(1)} %get-tuple-element.74), channel_id=1, source_target_pairs={{0,1},{2,3},{4,5},{6,7},{1,0},{3,2},{5,4},{7,6},{8,9},{10,11},{12,... | collective-permute-start | bytes 786440 | tf_op jit(solution)/shard_map/ppermute | solution.py:353
  105.9 9.8 %collective-permute-start.20 = (f32[2,64,384]{2,1,0:T(8,128)S(1)}, f32[2,64,384]{2,1,0:T(8,128)S(1)}, u32[]{:S(2)}, u32[]{:S(2)}) collective-permute-start(f32[2,64,384]{2,1,0:T(8,128)S(1)} %get-tuple-element.77), channel_id=1, source_target_pairs={{8,16},{16,8},{9,17},{17,9},{10,18},{18,10},{11,19},{19,11},{12,20... | collective-permute-start | bytes 589832 | tf_op jit(solution)/shard_map/ppermute | solution.py:353
  106.5 9.1 %collective-permute-start.19 = (f32[2,64,384]{2,1,0:T(8,128)S(1)}, f32[2,64,384]{2,1,0:T(8,128)S(1)}, u32[]{:S(2)}, u32[]{:S(2)}) collective-permute-start(f32[2,64,384]{2,1,0:T(8,128)S(1)} %get-tuple-element.76), channel_id=1, source_target_pairs={{0,8},{16,24},{8,0},{24,16},{1,9},{17,25},{9,1},{25,17},{2,10},{18... | collective-permute-start | bytes 589832 | tf_op jit(solution)/shard_map/ppermute | solution.py:353
  107.9 7.7 %collective-permute-start.21 = (f32[128,128]{1,0:T(8,128)S(1)}, f32[128,128]{1,0:T(8,128)S(1)}, u32[]{:S(2)}, u32[]{:S(2)}) collective-permute-start(f32[128,128]{1,0:T(8,128)S(1)} %get-tuple-element.78), channel_id=1, source_target_pairs={{1,2},{3,4},{5,6},{2,1},{4,3},{6,5},{9,10},{11,12},{13,14},{10,9},... | collective-permute-start | bytes 196616 | tf_op jit(solution)/shard_map/ppermute | solution.py:353
  115.6 4.8 %copy-start.3 = (f32[2,384,384]{2,1,0:T(8,128)S(1)}, f32[2,384,384]{2,1,0:T(8,128)}, u32[]{:S(2)}) copy-start(f32[2,384,384]{2,1,0:T(8,128)} %refs_0_.1) | copy-start | bytes 3538948
  115.8 2.5 %collective-permute-start.23 = (f32[2,64,128]{2,1,0:T(8,128)S(1)}, f32[2,64,128]{2,1,0:T(8,128)S(1)}, u32[]{:S(2)}, u32[]{:S(2)}) collective-permute-start(f32[2,64,128]{2,1,0:T(8,128)S(1)} %get-tuple-element.103), channel_id=1, source_target_pairs={{8,16},{16,8},{9,17},{17,9},{10,18},{18,10},{11,19},{19,11},{12,20... | collective-permute-start | bytes 196616 | tf_op jit(solution)/shard_map/ppermute | solution.py:353
  116.6 3.8 %collective-permute-start.22 = (f32[2,64,128]{2,1,0:T(8,128)S(1)}, f32[2,64,128]{2,1,0:T(8,128)S(1)}, u32[]{:S(2)}, u32[]{:S(2)}) collective-permute-start(f32[2,64,128]{2,1,0:T(8,128)S(1)} %get-tuple-element.104), channel_id=1, source_target_pairs={{0,8},{16,24},{8,0},{24,16},{1,9},{17,25},{9,1},{25,17},{2,10},{18... | collective-permute-start | bytes 196616 | tf_op jit(solution)/shard_map/ppermute | solution.py:353

commit v9 on v8

--- a/solution.py
+++ b/solution.py
@@ -74,11 +74,11 @@
     return y, x // size, x % size
 
 
-def edge_kernel(obj, positions, counts, offsets, place_of, edge_l, edge_r, meta):
-    scans = positions.shape[2]
-    values = [positions[0, 0, slot, axis] for slot in range(scans) for axis in range(2)]
-    values += [counts[0, 0], place_of[0], place_of[1]]
-    values += [offsets[slot, beam] for slot in range(scans) for beam in range(offsets.shape[1])]
+def edge_kernel(obj, joined, edge_l, edge_r, meta):
+    beams, scans = joined.shape[0] - 3, joined.shape[1]
+    values = [joined[axis, slot] for slot in range(scans) for axis in range(2)]
+    values += [joined[2 + beams, at] for at in range(3)]
+    values += [joined[2 + beam, slot] for slot in range(scans) for beam in range(beams)]
     assert len(values) <= meta.shape[1]
     lane = lax.broadcasted_iota(jnp.int32, meta.shape, 1)
     row = jnp.zeros(meta.shape, jnp.int32)
@@ -301,42 +301,49 @@
             lax.fori_loop(0, scans, add, 0)
 
 
-def gathered(total, side_l, side_r, in_top, in_bot, in_ctop, in_cbot, channel, chunk, half):
-    _, tiles, rows, size = total.shape
-    chunks = (rows - size) // half
+def inner_kernel(obj, weight, total, base, scale):
+    _, tiles, _, size = total.shape
+    half = size // 2
     low = lanes(half, size) < half
-    values = own_columns(total, channel, pl.ds((chunk + 1) * half, half), low)
-
-    def add_sides(from_l, from_r):
-        from_l = from_l if channel == 0 else turn(from_l)
-        from_r = turn(from_r) if channel == 0 else from_r
-        values[0] += jnp.where(low, from_l, 0.0)
-        values[-1] += jnp.where(low, 0.0, from_r)
-
-    own = pl.ds(chunk * half, half)
-    add_sides(side_l[own, :], side_r[own, :])
-    for at, rim, corner in ((0, in_top, in_ctop), (chunks - 1, in_bot, in_cbot)):
-        if chunk == at:
-            for t in range(tiles - 1):
-                values[t] += rim[channel, :, t * size : (t + 1) * size]
-            add_sides(corner[0], corner[1])
-    return values
-
-
-def final_kernel(*refs):
-    obj, weight, out = refs[0], refs[1], refs[-1]
-    grads = refs[2:9]
-    size = grads[0].shape[-1]
-    half = size // 2
-    tiles = obj.shape[2] // size
     for chunk in range(obj.shape[1] // half):
-        wide = pl.ds(size + chunk * half, half)
-        scale = [1.0 / (weight[0, t + 1, wide, :] + DAMPING) for t in range(tiles)]
-        rows = slice(chunk * half, (chunk + 1) * half)
+        own = slice(chunk * half, (chunk + 1) * half)
+        for t in range(tiles - 1):
+            columns = slice(t * size, (t + 1) * size)
+            scale[own, columns] = 1.0 / (weight[0, t + 1, pl.ds(size + chunk * half, half), :] + DAMPING)
         for ch in range(2):
-            for t, value in enumerate(gathered(*grads, ch, chunk, half)):
+            for t, value in enumerate(own_columns(total, ch, pl.ds((chunk + 1) * half, half), low)):
                 columns = slice(t * size, (t + 1) * size)
-                out[ch, rows, columns] = obj[ch, rows, columns] + value * scale[t]
+                base[ch, own, columns] = obj[ch, own, columns] + value * scale[own, columns]
+
+
+def final_kernel(base, scale, side_l, side_r, in_top, in_bot, in_ctop, in_cbot, out):
+    _, rows, columns = base.shape
+    size = side_l.shape[1]
+    half, tiles, chunks = size // 2, columns // size, rows // (size // 2)
+    low = lanes(half, size) < half
+    for chunk in range(chunks):
+        own = slice(chunk * half, (chunk + 1) * half)
+        for channel in range(2):
+
+            def sides(from_l, from_r, channel=channel):
+                from_l = from_l if channel == 0 else turn(from_l)
+                from_r = turn(from_r) if channel == 0 else from_r
+                return jnp.where(low, from_l, 0.0), jnp.where(low, 0.0, from_r)
+
+            added = {}
+            for where, rim, corner in ((0, in_top, in_ctop), (chunks - 1, in_bot, in_cbot)):
+                if chunk == where:
+                    for t in range(tiles):
+                        value = rim[channel, :, t * size : (t + 1) * size]
+                        added[t] = added[t] + value if t in added else value
+                    for t, value in zip((0, tiles - 1), sides(corner[0], corner[1])):
+                        added[t] = added[t] + value
+            for t, value in zip((0, tiles - 1), sides(side_l[own, :], side_r[own, :])):
+                added[t] = added[t] + value if t in added else value
+            for t in range(tiles):
+                at = slice(t * size, (t + 1) * size)
+                value = base[channel, own, at]
+                out[channel, own, at] = value + added[t] * scale[own, at] if t in added else value
 
 
 def swap(axis, first):
@@ -390,16 +397,19 @@
     at_row, at_col = lax.axis_index("row").astype(jnp.int32), lax.axis_index("col").astype(jnp.int32)
     odd_row, odd_col = lax.rem(at_row, 2) == 1, lax.rem(at_col, 2) == 1
     ends = jnp.where(odd_row, 0, tile_rows - half), jnp.where(odd_row, tile_rows - half, 0)
-    rows_1, rows_2 = (
-        move(lax.dynamic_slice_in_dim(obj, ends[i], half, axis=1), "row", swap("row", i))
-        for i in range(2)
-    )
+    which = lax.broadcasted_iota(jnp.int32, (1, scans), 1)
+    places = jnp.where(which == 0, counts[0, 0], jnp.where(which == 1, at_row, at_col))
+    joined = jnp.concatenate([positions[0, 0].T, offsets.T, places])
+    first = lax.dynamic_slice_in_dim(obj, ends[0], half, axis=1)
+    rows_1 = move(first, "row", swap("row", 0))
+    later, _ = lax.optimization_barrier((obj, first))
+    rows_2 = move(lax.dynamic_slice_in_dim(later, ends[1], half, axis=1), "row", swap("row", 1))
     top, bot = jnp.where(odd_row, rows_1, rows_2), jnp.where(odd_row, rows_2, rows_1)
     edge_l, edge_r, meta = call(
         edge_kernel,
         [(tile_rows, size)] * 2 + [jax.ShapeDtypeStruct((1, size), jnp.int32)],
-        [VMEM, SMEM, SMEM, SMEM, SMEM],
-        (obj, positions, counts, offsets, jnp.stack([at_row, at_col])),
+        [VMEM, SMEM],
+        (obj, joined),
         10**6,
     )
 
@@ -524,7 +534,8 @@
             )
     grad_in = send_rims(*sides, odd_row, odd_col)
 
-    (new_object,) = call(final_kernel, [obj.shape], [VMEM] * 9, (obj, weight, total, *grad_in), 10**6)
+    base, scale = call(inner_kernel, [obj.shape, obj.shape[1:]], [VMEM] * 3, (obj, weight, total), 10**6)
+    (new_object,) = call(final_kernel, [obj.shape], [VMEM] * 8, (base, scale, *grad_in), 10**6)
     return new_object
 
 

time: 123 us -> 124 us (level); the launches traced: 122 us -> 121 us
  waiting for transfers between devices: 35.3 us -> 33.6 us
    ppermute x24, waiting for transfers between devices: 35.3 us -> 33.6 us  [move(): return lax.ppermute(x, axis, pairs)]
    unnamed x12 -> x10, local copies, waits for them, and re-layouts: 3.35 us -> 1.84 us
    pallas_call x21 -> x22, Pallas kernels: 36 us -> 36 us  [call(): pl.pallas_call(kernel, out_shape=[s if hasattr(s, 'dtype') else jax.Shape...]
  transfers between devices with their start and end apart: 24 -> 24, of which waited for: 10 -> 12; matrix products, arithmetic and copies ran while one was open for 2% -> 2% of each run, Pallas kernels for 25% -> 26%
where the time goes in v9:
time: 124 us; the launch traced here: 121 us
  starting transfers between devices  45.2 us (36%)
  Pallas kernels  36 us (29%)
  waiting for transfers between devices  33.6 us (27%)
  local copies, waits for them, and re-layouts  3.95 us (3%)
  other arithmetic  1.26 us (1%)
    ppermute x24, starting transfers between devices, move(): return lax.ppermute(x, axis, pairs)  45.2 us
    pallas_call x22, Pallas kernels, call(): pl.pallas_call(kernel, out_shape=[s if hasattr(s, 'dtype') else jax.Shape...  36 us
    ppermute x24, waiting for transfers between devices, move(): return lax.ppermute(x, axis, pairs)  33.6 us
  transfers between devices with their start and end apart: 24, of which 12 were waited for; matrix products, arithmetic and copies ran while one was open for 2% of the time, Pallas kernels for 26%

profile of v9, /device:TPU:1, one launch (start us, length us, event | category | flops | bytes accessed | tf_op | source)
XLA Modules:
  0.0 121.1 jit_solution(8776463107488861329)
XLA Ops:
  0.9 2.2 %collective-permute-start.1 = (f32[2,64,384]{2,1,0:T(8,128)S(1)}, f32[2,64,384]{2,1,0:T(8,128)S(1)}, u32[]{:S(2)}, u32[]{:S(2)}) collective-permute-start(f32[2,64,384]{2,1,0:T(8,128)S(1)} %constant_dynamic-slice_fusion.1), channel_id=1, source_target_pairs={{0,8},{16,24},{8,0},{24,16},{1,9},{17,25},{9,1},{25,17},{2,10},{18... | collective-permute-start | bytes 589832 | tf_op jit(solution)/shard_map/ppermute | solution.py:360
  8.6 4.1 %collective-permute-start.4 = (f32[520,128]{1,0:T(8,128)S(1)}, f32[520,128]{1,0:T(8,128)S(1)}, u32[]{:S(2)}, u32[]{:S(2)}) collective-permute-start(f32[520,128]{1,0:T(8,128)S(1)} %broadcast_select_fusion.2), channel_id=1, source_target_pairs={{1,2},{3,4},{5,6},{2,1},{4,3},{6,5},{9,10},{11,12},{13,14},{10,9},... | collective-permute-start | bytes 798728 | tf_op jit(solution)/shard_map/ppermute | solution.py:360
  12.8 3.4 %collective-permute-start = (s32[1,128]{1,0:T(1,128)S(1)}, s32[1,128]{1,0:T(1,128)S(1)}, u32[]{:S(2)}, u32[]{:S(2)}) collective-permute-start(s32[1,128]{1,0:T(1,128)S(1)} %get-tuple-element.45.refs_0_), channel_id=1, source_target_pairs={{0,24},{8,0},{16,8},{24,16},{1,25},{9,1},{17,9},{25,17},{2,26},{10... | collective-permute-start | bytes 1544 | tf_op jit(solution)/shard_map/ppermute | solution.py:360
  16.1 2.6 %collective-permute-done.4 = f32[520,128]{1,0:T(8,128)S(1)} collective-permute-done((f32[520,128]{1,0:T(8,128)S(1)}, f32[520,128]{1,0:T(8,128)S(1)}, u32[]{:S(2)}, u32[]{:S(2)}) %collective-permute-start.4) | collective-permute-done | bytes 266272 | tf_op jit(solution)/shard_map/ppermute | solution.py:360
  21.6 3.4 %collective-permute-start.5 = (f32[520,128]{1,0:T(8,128)S(1)}, f32[520,128]{1,0:T(8,128)S(1)}, u32[]{:S(2)}, u32[]{:S(2)}) collective-permute-start(f32[520,128]{1,0:T(8,128)S(1)} %get-tuple-element.49), channel_id=1, source_target_pairs={{0,24},{8,0},{16,8},{24,16},{1,25},{9,1},{17,9},{25,17},{2,26},{10... | collective-permute-start | bytes 798728 | tf_op jit(solution)/shard_map/ppermute | solution.py:360
  26.7 4.4 %collective-permute-start.9 = (f32[512,128]{1,0:T(8,128)S(1)}, f32[512,128]{1,0:T(8,128)S(1)}, u32[]{:S(2)}, u32[]{:S(2)}) collective-permute-start(f32[512,128]{1,0:T(8,128)S(1)} %get-tuple-element.57), channel_id=1, source_target_pairs={{0,24},{8,0},{16,8},{24,16},{1,25},{9,1},{17,9},{25,17},{2,26},{10... | collective-permute-start | bytes 786440 | tf_op jit(solution)/shard_map/ppermute | solution.py:360
  31.1 1.7 %collective-permute-done.5.refs_4_ = f32[520,128]{1,0:T(8,128)S(1)} collective-permute-done((f32[520,128]{1,0:T(8,128)S(1)}, f32[520,128]{1,0:T(8,128)S(1)}, u32[]{:S(2)}, u32[]{:S(2)}) %collective-permute-start.5) | collective-permute-done | bytes 266272 | tf_op jit(solution)/shard_map/ppermute | solution.py:360
  34.4 2.8 %collective-permute-start.6 = (f32[520,128]{1,0:T(8,128)S(1)}, f32[520,128]{1,0:T(8,128)S(1)}, u32[]{:S(2)}, u32[]{:S(2)}) collective-permute-start(f32[520,128]{1,0:T(8,128)S(1)} %get-tuple-element.50), channel_id=1, source_target_pairs={{0,24},{8,0},{16,8},{24,16},{1,25},{9,1},{17,9},{25,17},{2,26},{10... | collective-permute-start | bytes 798728 | tf_op jit(solution)/shard_map/ppermute | solution.py:360
  37.7 1.6 %shard_map.81 = (f32[256,512]{1,0:T(8,128)S(1)}, f32[4,2,128,128]{3,2,1,0:T(8,128)S(1)}, f32[512,128]{1,0:T(8,128)S(1)}) custom-call(s32[1,128]{1,0:T(1,128)S(1)} %slice_convert_fusion.4.refs_0_, f32[2,4,512,128]{3,2,1,0:T(8,128)S(1)} %shard_map.74.refs_1_, f32[4,2,128,128]{3,2,1,0:T(8,128)S(1)} %copy-done, bf16[4,256,256]{2,1,0:T(8,128)(2,1)S(1)} %copy-done.1, ...), custom_call_target="tpu_custom_call" | custom-call | flops 402653184 | bytes 1048576 | tf_op jit(solution)/shard_map/pallas_call | solution.py:23
  39.3 2.5 %collective-permute-start.10 = (f32[512,128]{1,0:T(8,128)S(1)}, f32[512,128]{1,0:T(8,128)S(1)}, u32[]{:S(2)}, u32[]{:S(2)}) collective-permute-start(f32[512,128]{1,0:T(8,128)S(1)} %get-tuple-element.58), channel_id=1, source_target_pairs={{0,24},{8,0},{16,8},{24,16},{1,25},{9,1},{17,9},{25,17},{2,26},{10... | collective-permute-start | bytes 786440 | tf_op jit(solution)/shard_map/ppermute | solution.py:360
  45.1 4.1 %collective-permute-start.7 = (f32[520,128]{1,0:T(8,128)S(1)}, f32[520,128]{1,0:T(8,128)S(1)}, u32[]{:S(2)}, u32[]{:S(2)}) collective-permute-start(f32[520,128]{1,0:T(8,128)S(1)} %get-tuple-element.51), channel_id=1, source_target_pairs={{0,24},{8,0},{16,8},{24,16},{1,25},{9,1},{17,9},{25,17},{2,26},{10... | collective-permute-start | bytes 798728 | tf_op jit(solution)/shard_map/ppermute | solution.py:360
  49.1 1.6 %shard_map.82 = (f32[256,512]{1,0:T(8,128)S(1)}, f32[4,2,128,128]{3,2,1,0:T(8,128)S(1)}, f32[512,128]{1,0:T(8,128)S(1)}) custom-call(s32[1,128]{1,0:T(1,128)S(1)} %slice_convert_fusion.3.refs_0_, f32[2,4,512,128]{3,2,1,0:T(8,128)S(1)} %shard_map.74.refs_1_, f32[4,2,128,128]{3,2,1,0:T(8,128)S(1)} %copy-done, bf16[4,256,256]{2,1,0:T(8,128)(2,1)S(1)} %copy-done.1, ...), custom_call_target="tpu_custom_call" | custom-call | flops 402653184 | bytes 1048576 | tf_op jit(solution)/shard_map/pallas_call | solution.py:23
  50.8 3.5 %collective-permute-start.11 = (f32[512,128]{1,0:T(8,128)S(1)}, f32[512,128]{1,0:T(8,128)S(1)}, u32[]{:S(2)}, u32[]{:S(2)}) collective-permute-start(f32[512,128]{1,0:T(8,128)S(1)} %get-tuple-element.59), channel_id=1, source_target_pairs={{0,24},{8,0},{16,8},{24,16},{1,25},{9,1},{17,9},{25,17},{2,26},{10... | collective-permute-start | bytes 786440 | tf_op jit(solution)/shard_map/ppermute | solution.py:360
  54.3 2.1 %shard_map.78 = (f32[256,512]{1,0:T(8,128)S(1)}, f32[4,2,128,128]{3,2,1,0:T(8,128)S(1)}, f32[512,128]{1,0:T(8,128)S(1)}, f32[256,512]{1,0:T(8,128)S(1)}, f32[4,2...) custom-call(s32[1,128]{1,0:T(1,128)S(1)} %get-tuple-element.45.refs_0_, f32[2,4,512,128]{3,2,1,0:T(8,128)S(1)} %shard_map.74.refs_1_, ...), custom_call_target="tpu_custom_call" | custom-call | flops 805306368 | bytes 1048576 | tf_op jit(solution)/shard_map/pallas_call | solution.py:23
  56.4 4.1 %collective-permute-done.11.arrived = f32[512,128]{1,0:T(8,128)S(1)} collective-permute-done((f32[512,128]{1,0:T(8,128)S(1)}, f32[512,128]{1,0:T(8,128)S(1)}, u32[]{:S(2)}, u32[]{:S(2)}) %collective-permute-start.11) | collective-permute-done | bytes 262176 | tf_op jit(solution)/shard_map/ppermute | solution.py:360
  60.9 1.7 %collective-permute-start.8 = (f32[520,128]{1,0:T(8,128)S(1)}, f32[520,128]{1,0:T(8,128)S(1)}, u32[]{:S(2)}, u32[]{:S(2)}) collective-permute-start(f32[520,128]{1,0:T(8,128)S(1)} %shard_map.79.refs_5_), channel_id=1, source_target_pairs={{0,8},{8,16},{16,24},{24,0},{1,9},{9,17},{17,25},{25,1},{2,10},{10... | collective-permute-start | bytes 798728 | tf_op jit(solution)/shard_map/ppermute | solution.py:360
  62.6 2.5 %shard_map.86.refs_2_ = f32[1,5,640,128]{3,2,1,0:T(8,128)S(1)} custom-call(s32[3,128]{1,0:T(4,128)S(1)} %pad_add_fusion.4.refs_0_, f32[4,2,128,128]{3,2,1,0:T(8,128)S(1)} %copy-done), custom_call_target="tpu_custom_call" | custom-call | flops 402653184 | bytes 1048576 | tf_op jit(solution)/shard_map/pallas_call | solution.py:23
  65.2 2.3 %shard_map.84.refs_9_ = f32[2,4,512,128]{3,2,1,0:T(8,128)S(1)} custom-call(s32[1,128]{1,0:T(1,128)S(1)} %get-tuple-element.45.refs_0_, f32[4,2,128,128]{3,2,1,0:T(8,128)S(1)} %copy-done, bf16[4,256,256]{2,1,0:T(8,128)(2,1)S(1)} %copy-done.1, f32[256,512]{1,0:T(8,128)S(1)} %get-tuple-element.53.refs_3_, f32[4,2,128,128]{3,2,1,0:T(8,128)S(1)} %get-tuple-element.54.refs_4_, ...), custom_call_target="tpu_custom_call" | custom-call | flops 805306368 | bytes 1048576 | tf_op jit(solution)/shard_map/pallas_call | solution.py:23
  67.4 3.2 %collective-permute-done.13.refs_8_ = f32[512,128]{1,0:T(8,128)S(1)} collective-permute-done((f32[512,128]{1,0:T(8,128)S(1)}, f32[512,128]{1,0:T(8,128)S(1)}, u32[]{:S(2)}, u32[]{:S(2)}) %collective-permute-start.13) | collective-permute-done | bytes 262176 | tf_op jit(solution)/shard_map/ppermute | solution.py:360
  70.6 5.7 %collective-permute-done.8.refs_5_ = f32[520,128]{1,0:T(8,128)S(1)} collective-permute-done((f32[520,128]{1,0:T(8,128)S(1)}, f32[520,128]{1,0:T(8,128)S(1)}, u32[]{:S(2)}, u32[]{:S(2)}) %collective-permute-start.8) | collective-permute-done | bytes 266272 | tf_op jit(solution)/shard_map/ppermute | solution.py:360
  76.4 2.8 %shard_map.87.refs_2_ = f32[1,5,640,128]{3,2,1,0:T(8,128)S(1)} custom-call(s32[3,128]{1,0:T(4,128)S(1)} %pad_add_fusion.3.refs_0_, f32[4,2,128,128]{3,2,1,0:T(8,128)S(1)} %copy-done, f32[1,5,640,128]{3,2,1,0:T(8,128)S(1)} %shard_map.86.refs_2_), custom_call_target="tpu_custom_call", output_to_operand_aliasing={{}: (2, {})} | custom-call | flops 402653184 | bytes 1048576 | tf_op jit(solution)/shard_map/pallas_call | solution.py:23
  79.2 2.1 %shard_map.85.refs_9_ = f32[2,4,512,128]{3,2,1,0:T(8,128)S(1)} custom-call(s32[1,128]{1,0:T(1,128)S(1)} %slice_convert_fusion.3.refs_0_, f32[4,2,128,128]{3,2,1,0:T(8,128)S(1)} %copy-done, bf16[4,256,256]{2,1,0:T(8,128)(2,1)S(1)} %copy-done.1, f32[256,512]{1,0:T(8,128)S(1)} %get-tuple-element.62.refs_3_, ...), custom_call_target="tpu_custom_call", output_to_operand_aliasing={{}: (9, {})} | custom-call | flops 805306368 | bytes 1048576 | tf_op jit(solution)/shard_map/pallas_call | solution.py:23
  82.0 5.7 %collective-permute-done.12.refs_5_ = f32[520,128]{1,0:T(8,128)S(1)} collective-permute-done((f32[520,128]{1,0:T(8,128)S(1)}, f32[520,128]{1,0:T(8,128)S(1)}, u32[]{:S(2)}, u32[]{:S(2)}) %collective-permute-start.12) | collective-permute-done | bytes 266272 | tf_op jit(solution)/shard_map/ppermute | solution.py:360
  87.7 2.9 %shard_map.88.refs_2_ = f32[1,5,640,128]{3,2,1,0:T(8,128)S(1)} custom-call(s32[3,128]{1,0:T(4,128)S(1)} %pad_add_fusion.2.refs_0_, f32[4,2,128,128]{3,2,1,0:T(8,128)S(1)} %copy-done, f32[1,5,640,128]{3,2,1,0:T(8,128)S(1)} %shard_map.87.refs_2_), custom_call_target="tpu_custom_call", output_to_operand_aliasing={{}: (2, {})} | custom-call | flops 402653184 | bytes 1048576 | tf_op jit(solution)/shard_map/pallas_call | solution.py:23
  90.6 2.1 %shard_map.90.refs_6_ = f32[2,4,512,128]{3,2,1,0:T(8,128)S(1)} custom-call(s32[1,128]{1,0:T(1,128)S(1)} %slice_convert_fusion.4.refs_0_, f32[4,2,128,128]{3,2,1,0:T(8,128)S(1)} %copy-done, bf16[4,256,256]{2,1,0:T(8,128)(2,1)S(1)} %copy-done.1, f32[256,512]{1,0:T(8,128)S(1)} %get-tuple-element.72.refs_3_, ...), custom_call_target="tpu_custom_call", output_to_operand_aliasing={{}: (9, {})} | custom-call | flops 805306368 | bytes 1048576 | tf_op jit(solution)/shard_map/pallas_call | solution.py:23
  92.7 6.3 %collective-permute-done.14.refs_5_ = f32[520,128]{1,0:T(8,128)S(1)} collective-permute-done((f32[520,128]{1,0:T(8,128)S(1)}, f32[520,128]{1,0:T(8,128)S(1)}, u32[]{:S(2)}, u32[]{:S(2)}) %collective-permute-start.14) | collective-permute-done | bytes 266272 | tf_op jit(solution)/shard_map/ppermute | solution.py:360
  100.5 1.9 %shard_map.92 = (f32[2,4,512,128]{3,2,1,0:T(8,128)S(1)}, f32[512,128]{1,0:T(8,128)S(1)}, f32[384,128]{1,0:T(8,128)S(1)}, f32[128,128]{1,0:T(8,128)S(1)}, f32[2,6...) custom-call(s32[1,128]{1,0:T(1,128)S(1)} %collective-permute-done.refs_0_, ...), custom_call_target="tpu_custom_call", output_to_operand_aliasing={{0}: (6, {})} | custom-call | flops 402653184 | bytes 1048576 | tf_op jit(solution)/shard_map/pallas_call | solution.py:23
  102.4 3.8 %collective-permute-start.18 = (f32[384,128]{1,0:T(8,128)S(1)}, f32[384,128]{1,0:T(8,128)S(1)}, u32[]{:S(2)}, u32[]{:S(2)}) collective-permute-start(f32[384,128]{1,0:T(8,128)S(1)} %get-tuple-element.81), channel_id=1, source_target_pairs={{1,2},{3,4},{5,6},{2,1},{4,3},{6,5},{9,10},{11,12},{13,14},{10,9},... | collective-permute-start | bytes 589832 | tf_op jit(solution)/shard_map/ppermute | solution.py:360
  107.0 2.7 %collective-permute-start.19 = (f32[2,64,384]{2,1,0:T(8,128)S(1)}, f32[2,64,384]{2,1,0:T(8,128)S(1)}, u32[]{:S(2)}, u32[]{:S(2)}) collective-permute-start(f32[2,64,384]{2,1,0:T(8,128)S(1)} %get-tuple-element.82), channel_id=1, source_target_pairs={{0,8},{16,24},{8,0},{24,16},{1,9},{17,25},{9,1},{25,17},{2,10},{18... | collective-permute-start | bytes 589832 | tf_op jit(solution)/shard_map/ppermute | solution.py:360
  109.7 2.5 %collective-permute-start.21 = (f32[128,128]{1,0:T(8,128)S(1)}, f32[128,128]{1,0:T(8,128)S(1)}, u32[]{:S(2)}, u32[]{:S(2)}) collective-permute-start(f32[128,128]{1,0:T(8,128)S(1)} %get-tuple-element.84), channel_id=1, source_target_pairs={{1,2},{3,4},{5,6},{2,1},{4,3},{6,5},{9,10},{11,12},{13,14},{10,9},... | collective-permute-start | bytes 196616 | tf_op jit(solution)/shard_map/ppermute | solution.py:360
  112.2 2.6 %shard_map.89.weight = f32[1,5,640,128]{3,2,1,0:T(8,128)S(1)} custom-call(s32[3,128]{1,0:T(4,128)S(1)} %pad_add_fusion.1.refs_0_, f32[4,2,128,128]{3,2,1,0:T(8,128)S(1)} %copy-done, f32[1,5,640,128]{3,2,1,0:T(8,128)S(1)} %shard_map.88.refs_2_), custom_call_target="tpu_custom_call", output_to_operand_aliasing={{}: (2, {})} | custom-call | flops 402653184 | bytes 1048576 | tf_op jit(solution)/shard_map/pallas_call | solution.py:23
  116.2 1.9 %collective-permute-start.22 = (f32[2,64,128]{2,1,0:T(8,128)S(1)}, f32[2,64,128]{2,1,0:T(8,128)S(1)}, u32[]{:S(2)}, u32[]{:S(2)}) collective-permute-start(f32[2,64,128]{2,1,0:T(8,128)S(1)} %get-tuple-element.108), channel_id=1, source_target_pairs={{0,8},{16,24},{8,0},{24,16},{1,9},{17,25},{9,1},{25,17},{2,10},{18... | collective-permute-start | bytes 196616 | tf_op jit(solution)/shard_map/ppermute | solution.py:360
  (81 shorter events, 23.3 us)
Async XLA Ops:
  0.9 7.2 %collective-permute-start.1 = (f32[2,64,384]{2,1,0:T(8,128)S(1)}, f32[2,64,384]{2,1,0:T(8,128)S(1)}, u32[]{:S(2)}, u32[]{:S(2)}) collective-permute-start(f32[2,64,384]{2,1,0:T(8,128)S(1)} %constant_dynamic-slice_fusion.1), channel_id=1, source_target_pairs={{0,8},{16,24},{8,0},{24,16},{1,9},{17,25},{9,1},{25,17},{2,10},{18... | collective-permute-start | bytes 589832 | tf_op jit(solution)/shard_map/ppermute | solution.py:360
  4.1 4.1 %collective-permute-start.2 = (f32[2,64,384]{2,1,0:T(8,128)S(1)}, f32[2,64,384]{2,1,0:T(8,128)S(1)}, u32[]{:S(2)}, u32[]{:S(2)}) collective-permute-start(f32[2,64,384]{2,1,0:T(8,128)S(1)} %constant_dynamic-slice_fusion), channel_id=1, source_target_pairs={{8,16},{16,8},{9,17},{17,9},{10,18},{18,10},{11,19},{19,11},{12,20... | collective-permute-start | bytes 589832 | tf_op jit(solution)/shard_map/ppermute | solution.py:360
  6.1 1.3 %copy-start.2 = (f32[2,384,384]{2,1,0:T(8,128)S(1)}, f32[2,384,384]{2,1,0:T(8,128)}, u32[]{:S(2)}) copy-start(f32[2,384,384]{2,1,0:T(8,128)} %obj.5) | copy-start | bytes 3538948
  8.2 10.6 %copy-start.3 = (f32[2,384,384]{2,1,0:T(8,128)S(1)}, f32[2,384,384]{2,1,0:T(8,128)}, u32[]{:S(2)}) copy-start(f32[2,384,384]{2,1,0:T(8,128)} %obj.5) | copy-start | bytes 3538948
  8.6 10.1 %collective-permute-start.4 = (f32[520,128]{1,0:T(8,128)S(1)}, f32[520,128]{1,0:T(8,128)S(1)}, u32[]{:S(2)}, u32[]{:S(2)}) collective-permute-start(f32[520,128]{1,0:T(8,128)S(1)} %broadcast_select_fusion.2), channel_id=1, source_target_pairs={{1,2},{3,4},{5,6},{2,1},{4,3},{6,5},{9,10},{11,12},{13,14},{10,9},... | collective-permute-start | bytes 798728 | tf_op jit(solution)/shard_map/ppermute | solution.py:360
  12.7 6.0 %collective-permute-start.3 = (f32[520,128]{1,0:T(8,128)S(1)}, f32[520,128]{1,0:T(8,128)S(1)}, u32[]{:S(2)}, u32[]{:S(2)}) collective-permute-start(f32[520,128]{1,0:T(8,128)S(1)} %broadcast_select_fusion.3), channel_id=1, source_target_pairs={{0,1},{2,3},{4,5},{6,7},{1,0},{3,2},{5,4},{7,6},{8,9},{10,11},{12,... | collective-permute-start | bytes 798728 | tf_op jit(solution)/shard_map/ppermute | solution.py:360
  12.8 6.7 %collective-permute-start = (s32[1,128]{1,0:T(1,128)S(1)}, s32[1,128]{1,0:T(1,128)S(1)}, u32[]{:S(2)}, u32[]{:S(2)}) collective-permute-start(s32[1,128]{1,0:T(1,128)S(1)} %get-tuple-element.45.refs_0_), channel_id=1, source_target_pairs={{0,24},{8,0},{16,8},{24,16},{1,25},{9,1},{17,9},{25,17},{2,26},{10... | collective-permute-start | bytes 1544 | tf_op jit(solution)/shard_map/ppermute | solution.py:360
  18.8 1.0 copy-start
  18.8 1.2 copy-start.1
  21.6 11.1 %collective-permute-start.5 = (f32[520,128]{1,0:T(8,128)S(1)}, f32[520,128]{1,0:T(8,128)S(1)}, u32[]{:S(2)}, u32[]{:S(2)}) collective-permute-start(f32[520,128]{1,0:T(8,128)S(1)} %get-tuple-element.49), channel_id=1, source_target_pairs={{0,24},{8,0},{16,8},{24,16},{1,25},{9,1},{17,9},{25,17},{2,26},{10... | collective-permute-start | bytes 798728 | tf_op jit(solution)/shard_map/ppermute | solution.py:360
  26.7 10.9 %collective-permute-start.9 = (f32[512,128]{1,0:T(8,128)S(1)}, f32[512,128]{1,0:T(8,128)S(1)}, u32[]{:S(2)}, u32[]{:S(2)}) collective-permute-start(f32[512,128]{1,0:T(8,128)S(1)} %get-tuple-element.57), channel_id=1, source_target_pairs={{0,24},{8,0},{16,8},{24,16},{1,25},{9,1},{17,9},{25,17},{2,26},{10... | collective-permute-start | bytes 786440 | tf_op jit(solution)/shard_map/ppermute | solution.py:360
  32.7 4.5 %copy-start.4 = (f32[1,1,8,128,128]{4,3,2,1,0:T(8,128)S(1)}, f32[1,1,8,128,128]{4,3,2,1,0:T(8,128)}, u32[]{:S(2)}) copy-start(f32[1,1,8,128,128]{4,3,2,1,0:T(8,128)} %param.12) | copy-start | bytes 1572868
  34.4 9.0 %collective-permute-start.6 = (f32[520,128]{1,0:T(8,128)S(1)}, f32[520,128]{1,0:T(8,128)S(1)}, u32[]{:S(2)}, u32[]{:S(2)}) collective-permute-start(f32[520,128]{1,0:T(8,128)S(1)} %get-tuple-element.50), channel_id=1, source_target_pairs={{0,24},{8,0},{16,8},{24,16},{1,25},{9,1},{17,9},{25,17},{2,26},{10... | collective-permute-start | bytes 798728 | tf_op jit(solution)/shard_map/ppermute | solution.py:360
  39.3 9.8 %collective-permute-start.10 = (f32[512,128]{1,0:T(8,128)S(1)}, f32[512,128]{1,0:T(8,128)S(1)}, u32[]{:S(2)}, u32[]{:S(2)}) collective-permute-start(f32[512,128]{1,0:T(8,128)S(1)} %get-tuple-element.58), channel_id=1, source_target_pairs={{0,24},{8,0},{16,8},{24,16},{1,25},{9,1},{17,9},{25,17},{2,26},{10... | collective-permute-start | bytes 786440 | tf_op jit(solution)/shard_map/ppermute | solution.py:360
  45.1 15.7 %collective-permute-start.7 = (f32[520,128]{1,0:T(8,128)S(1)}, f32[520,128]{1,0:T(8,128)S(1)}, u32[]{:S(2)}, u32[]{:S(2)}) collective-permute-start(f32[520,128]{1,0:T(8,128)S(1)} %get-tuple-element.51), channel_id=1, source_target_pairs={{0,24},{8,0},{16,8},{24,16},{1,25},{9,1},{17,9},{25,17},{2,26},{10... | collective-permute-start | bytes 798728 | tf_op jit(solution)/shard_map/ppermute | solution.py:360
  50.8 9.8 %collective-permute-start.11 = (f32[512,128]{1,0:T(8,128)S(1)}, f32[512,128]{1,0:T(8,128)S(1)}, u32[]{:S(2)}, u32[]{:S(2)}) collective-permute-start(f32[512,128]{1,0:T(8,128)S(1)} %get-tuple-element.59), channel_id=1, source_target_pairs={{0,24},{8,0},{16,8},{24,16},{1,25},{9,1},{17,9},{25,17},{2,26},{10... | collective-permute-start | bytes 786440 | tf_op jit(solution)/shard_map/ppermute | solution.py:360
  60.7 10.0 %collective-permute-start.13 = (f32[512,128]{1,0:T(8,128)S(1)}, f32[512,128]{1,0:T(8,128)S(1)}, u32[]{:S(2)}, u32[]{:S(2)}) collective-permute-start(f32[512,128]{1,0:T(8,128)S(1)} %shard_map.83.refs_8_), channel_id=1, source_target_pairs={{0,8},{8,16},{16,24},{24,0},{1,9},{9,17},{17,25},{25,1},{2,10},{10... | collective-permute-start | bytes 786440 | tf_op jit(solution)/shard_map/ppermute | solution.py:360
  60.9 15.4 %collective-permute-start.8 = (f32[520,128]{1,0:T(8,128)S(1)}, f32[520,128]{1,0:T(8,128)S(1)}, u32[]{:S(2)}, u32[]{:S(2)}) collective-permute-start(f32[520,128]{1,0:T(8,128)S(1)} %shard_map.79.refs_5_), channel_id=1, source_target_pairs={{0,8},{8,16},{16,24},{24,0},{1,9},{9,17},{17,25},{25,1},{2,10},{10... | collective-permute-start | bytes 798728 | tf_op jit(solution)/shard_map/ppermute | solution.py:360
  70.6 11.3 %collective-permute-start.15 = (f32[512,128]{1,0:T(8,128)S(1)}, f32[512,128]{1,0:T(8,128)S(1)}, u32[]{:S(2)}, u32[]{:S(2)}) collective-permute-start(f32[512,128]{1,0:T(8,128)S(1)} %collective-permute-done.13.refs_8_), channel_id=1, source_target_pairs={{0,8},{8,16},{16,24},{24,0},{1,9},{9,17},{17,25},{25,1},{2,10},{10... | collective-permute-start | bytes 786440 | tf_op jit(solution)/shard_map/ppermute | solution.py:360
  76.3 11.3 %collective-permute-start.12 = (f32[520,128]{1,0:T(8,128)S(1)}, f32[520,128]{1,0:T(8,128)S(1)}, u32[]{:S(2)}, u32[]{:S(2)}) collective-permute-start(f32[520,128]{1,0:T(8,128)S(1)} %collective-permute-done.8.refs_5_), channel_id=1, source_target_pairs={{0,8},{8,16},{16,24},{24,0},{1,9},{9,17},{17,25},{25,1},{2,10},{10... | collective-permute-start | bytes 798728 | tf_op jit(solution)/shard_map/ppermute | solution.py:360
  82.0 18.6 %collective-permute-start.16 = (f32[512,128]{1,0:T(8,128)S(1)}, f32[512,128]{1,0:T(8,128)S(1)}, u32[]{:S(2)}, u32[]{:S(2)}) collective-permute-start(f32[512,128]{1,0:T(8,128)S(1)} %collective-permute-done.15.refs_8_), channel_id=1, source_target_pairs={{0,8},{8,16},{16,24},{24,0},{1,9},{9,17},{17,25},{25,1},{2,10},{10... | collective-permute-start | bytes 786440 | tf_op jit(solution)/shard_map/ppermute | solution.py:360
  87.7 11.3 %collective-permute-start.14 = (f32[520,128]{1,0:T(8,128)S(1)}, f32[520,128]{1,0:T(8,128)S(1)}, u32[]{:S(2)}, u32[]{:S(2)}) collective-permute-start(f32[520,128]{1,0:T(8,128)S(1)} %collective-permute-done.12.refs_5_), channel_id=1, source_target_pairs={{0,8},{8,16},{16,24},{24,0},{1,9},{9,17},{17,25},{25,1},{2,10},{10... | collective-permute-start | bytes 798728 | tf_op jit(solution)/shard_map/ppermute | solution.py:360
  102.4 15.7 %collective-permute-start.18 = (f32[384,128]{1,0:T(8,128)S(1)}, f32[384,128]{1,0:T(8,128)S(1)}, u32[]{:S(2)}, u32[]{:S(2)}) collective-permute-start(f32[384,128]{1,0:T(8,128)S(1)} %get-tuple-element.81), channel_id=1, source_target_pairs={{1,2},{3,4},{5,6},{2,1},{4,3},{6,5},{9,10},{11,12},{13,14},{10,9},... | collective-permute-start | bytes 589832 | tf_op jit(solution)/shard_map/ppermute | solution.py:360
  106.3 9.2 %collective-permute-start.17 = (f32[512,128]{1,0:T(8,128)S(1)}, f32[512,128]{1,0:T(8,128)S(1)}, u32[]{:S(2)}, u32[]{:S(2)}) collective-permute-start(f32[512,128]{1,0:T(8,128)S(1)} %get-tuple-element.80), channel_id=1, source_target_pairs={{0,1},{2,3},{4,5},{6,7},{1,0},{3,2},{5,4},{7,6},{8,9},{10,11},{12,... | collective-permute-start | bytes 786440 | tf_op jit(solution)/shard_map/ppermute | solution.py:360
  106.4 9.1 %collective-permute-start.20 = (f32[2,64,384]{2,1,0:T(8,128)S(1)}, f32[2,64,384]{2,1,0:T(8,128)S(1)}, u32[]{:S(2)}, u32[]{:S(2)}) collective-permute-start(f32[2,64,384]{2,1,0:T(8,128)S(1)} %get-tuple-element.83), channel_id=1, source_target_pairs={{8,16},{16,8},{9,17},{17,9},{10,18},{18,10},{11,19},{19,11},{12,20... | collective-permute-start | bytes 589832 | tf_op jit(solution)/shard_map/ppermute | solution.py:360
  107.0 8.4 %collective-permute-start.19 = (f32[2,64,384]{2,1,0:T(8,128)S(1)}, f32[2,64,384]{2,1,0:T(8,128)S(1)}, u32[]{:S(2)}, u32[]{:S(2)}) collective-permute-start(f32[2,64,384]{2,1,0:T(8,128)S(1)} %get-tuple-element.82), channel_id=1, source_target_pairs={{0,8},{16,24},{8,0},{24,16},{1,9},{17,25},{9,1},{25,17},{2,10},{18... | collective-permute-start | bytes 589832 | tf_op jit(solution)/shard_map/ppermute | solution.py:360
  109.7 5.7 %collective-permute-start.21 = (f32[128,128]{1,0:T(8,128)S(1)}, f32[128,128]{1,0:T(8,128)S(1)}, u32[]{:S(2)}, u32[]{:S(2)}) collective-permute-start(f32[128,128]{1,0:T(8,128)S(1)} %get-tuple-element.84), channel_id=1, source_target_pairs={{1,2},{3,4},{5,6},{2,1},{4,3},{6,5},{9,10},{11,12},{13,14},{10,9},... | collective-permute-start | bytes 196616 | tf_op jit(solution)/shard_map/ppermute | solution.py:360
  115.6 2.6 %collective-permute-start.23 = (f32[2,64,128]{2,1,0:T(8,128)S(1)}, f32[2,64,128]{2,1,0:T(8,128)S(1)}, u32[]{:S(2)}, u32[]{:S(2)}) collective-permute-start(f32[2,64,128]{2,1,0:T(8,128)S(1)} %get-tuple-element.107), channel_id=1, source_target_pairs={{8,16},{16,8},{9,17},{17,9},{10,18},{18,10},{11,19},{19,11},{12,20... | collective-permute-start | bytes 196616 | tf_op jit(solution)/shard_map/ppermute | solution.py:360
  116.2 3.6 %collective-permute-start.22 = (f32[2,64,128]{2,1,0:T(8,128)S(1)}, f32[2,64,128]{2,1,0:T(8,128)S(1)}, u32[]{:S(2)}, u32[]{:S(2)}) collective-permute-start(f32[2,64,128]{2,1,0:T(8,128)S(1)} %get-tuple-element.108), channel_id=1, source_target_pairs={{0,8},{16,24},{8,0},{24,16},{1,9},{17,25},{9,1},{25,17},{2,10},{18... | collective-permute-start | bytes 196616 | tf_op jit(solution)/shard_map/ppermute | solution.py:360

commit v10 on v9

--- a/solution.py
+++ b/solution.py
@@ -400,10 +400,10 @@
     which = lax.broadcasted_iota(jnp.int32, (1, scans), 1)
     places = jnp.where(which == 0, counts[0, 0], jnp.where(which == 1, at_row, at_col))
     joined = jnp.concatenate([positions[0, 0].T, offsets.T, places])
-    first = lax.dynamic_slice_in_dim(obj, ends[0], half, axis=1)
-    rows_1 = move(first, "row", swap("row", 0))
-    later, _ = lax.optimization_barrier((obj, first))
-    rows_2 = move(lax.dynamic_slice_in_dim(later, ends[1], half, axis=1), "row", swap("row", 1))
+    rows_1, rows_2 = (
+        move(lax.dynamic_slice_in_dim(obj, ends[i], half, axis=1), "row", swap("row", i))
+        for i in range(2)
+    )
     top, bot = jnp.where(odd_row, rows_1, rows_2), jnp.where(odd_row, rows_2, rows_1)
     edge_l, edge_r, meta = call(
         edge_kernel,

time: 124 us -> 123 us (level); the launches traced: 121 us -> 122 us
  waiting for transfers between devices: 33.6 us -> 36.3 us
    ppermute x24, waiting for transfers between devices: 33.6 us -> 36.3 us  [move(): return lax.ppermute(x, axis, pairs)]
  transfers between devices with their start and end apart: 24 -> 24, of which waited for: 12 -> 11; matrix products, arithmetic and copies ran while one was open for 2% -> 1% of each run, Pallas kernels for 26% -> 26%
where the time goes in v10:
time: 123 us; the launch traced here: 122 us
  starting transfers between devices  44.7 us (36%)
  waiting for transfers between devices  36.3 us (30%)
  Pallas kernels  36 us (29%)
  local copies, waits for them, and re-layouts  3.12 us (3%)
  other arithmetic  1.26 us (1%)
    ppermute x24, starting transfers between devices, move(): return lax.ppermute(x, axis, pairs)  44.7 us
    ppermute x24, waiting for transfers between devices, move(): return lax.ppermute(x, axis, pairs)  36.3 us
    pallas_call x22, Pallas kernels, call(): pl.pallas_call(kernel, out_shape=[s if hasattr(s, 'dtype') else jax.Shape...  36 us
  transfers between devices with their start and end apart: 24, of which 11 were waited for; matrix products, arithmetic and copies ran while one was open for 1% of the time, Pallas kernels for 26%

profile of v10, /device:TPU:1, one launch (start us, length us, event | category | flops | bytes accessed | tf_op | source)
XLA Modules:
  0.0 122.5 jit_solution(11793155005405048749)
XLA Ops:
  1.7 4.7 %collective-permute-start.1 = (f32[2,64,384]{2,1,0:T(8,128)S(1)}, f32[2,64,384]{2,1,0:T(8,128)S(1)}, u32[]{:S(2)}, u32[]{:S(2)}) collective-permute-start(f32[2,64,384]{2,1,0:T(8,128)S(1)} %get-tuple-element.84), channel_id=1, source_target_pairs={{0,8},{16,24},{8,0},{24,16},{1,9},{17,25},{9,1},{25,17},{2,10},{18... | collective-permute-start | bytes 589832 | tf_op jit(solution)/shard_map/ppermute | solution.py:360
  11.1 4.7 %collective-permute-start.4 = (f32[520,128]{1,0:T(8,128)S(1)}, f32[520,128]{1,0:T(8,128)S(1)}, u32[]{:S(2)}, u32[]{:S(2)}) collective-permute-start(f32[520,128]{1,0:T(8,128)S(1)} %broadcast_select_fusion.2), channel_id=1, source_target_pairs={{1,2},{3,4},{5,6},{2,1},{4,3},{6,5},{9,10},{11,12},{13,14},{10,9},... | collective-permute-start | bytes 798728 | tf_op jit(solution)/shard_map/ppermute | solution.py:360
  17.0 4.8 %collective-permute-done.4 = f32[520,128]{1,0:T(8,128)S(1)} collective-permute-done((f32[520,128]{1,0:T(8,128)S(1)}, f32[520,128]{1,0:T(8,128)S(1)}, u32[]{:S(2)}, u32[]{:S(2)}) %collective-permute-start.4) | collective-permute-done | bytes 266272 | tf_op jit(solution)/shard_map/ppermute | solution.py:360
  23.1 1.6 %shard_map.75 = (f32[256,512]{1,0:T(8,128)S(1)}, f32[4,2,128,128]{3,2,1,0:T(8,128)S(1)}, f32[520,128]{1,0:T(8,128)S(1)}) custom-call(s32[1,128]{1,0:T(1,128)S(1)} %collective-permute-done.refs_0_, f32[2,4,512,128]{3,2,1,0:T(8,128)S(1)} %shard_map.74.refs_1_, f32[4,2,128,128]{3,2,1,0:T(8,128)S(1)} %copy-done, bf16[4,256,256]{2,1,0:T(8,128)(2,1)S(1)} %copy-done.1), custom_call_target="tpu_custom_call" | custom-call | flops 402653184 | bytes 1048576 | tf_op jit(solution)/shard_map/pallas_call | solution.py:23
  26.0 1.6 %shard_map.80 = (f32[256,512]{1,0:T(8,128)S(1)}, f32[4,2,128,128]{3,2,1,0:T(8,128)S(1)}, f32[512,128]{1,0:T(8,128)S(1)}) custom-call(s32[1,128]{1,0:T(1,128)S(1)} %collective-permute-done.refs_0_, f32[2,4,512,128]{3,2,1,0:T(8,128)S(1)} %shard_map.74.refs_1_, f32[4,2,128,128]{3,2,1,0:T(8,128)S(1)} %copy-done, bf16[4,256,256]{2,1,0:T(8,128)(2,1)S(1)} %copy-done.1), custom_call_target="tpu_custom_call" | custom-call | flops 402653184 | bytes 1048576 | tf_op jit(solution)/shard_map/pallas_call | solution.py:23
  29.1 3.0 %collective-permute-done.5.refs_4_ = f32[520,128]{1,0:T(8,128)S(1)} collective-permute-done((f32[520,128]{1,0:T(8,128)S(1)}, f32[520,128]{1,0:T(8,128)S(1)}, u32[]{:S(2)}, u32[]{:S(2)}) %collective-permute-start.5) | collective-permute-done | bytes 266272 | tf_op jit(solution)/shard_map/ppermute | solution.py:360
  32.1 1.6 %shard_map.76 = (f32[256,512]{1,0:T(8,128)S(1)}, f32[4,2,128,128]{3,2,1,0:T(8,128)S(1)}, f32[520,128]{1,0:T(8,128)S(1)}) custom-call(s32[1,128]{1,0:T(1,128)S(1)} %slice_convert_fusion.4.refs_0_, f32[2,4,512,128]{3,2,1,0:T(8,128)S(1)} %shard_map.74.refs_1_, f32[4,2,128,128]{3,2,1,0:T(8,128)S(1)} %copy-done, bf16[4,256,256]{2,1,0:T(8,128)(2,1)S(1)} %copy-done.1, ...), custom_call_target="tpu_custom_call" | custom-call | flops 402653184 | bytes 1048576 | tf_op jit(solution)/shard_map/pallas_call | solution.py:23
  33.8 4.1 %collective-permute-start.6 = (f32[520,128]{1,0:T(8,128)S(1)}, f32[520,128]{1,0:T(8,128)S(1)}, u32[]{:S(2)}, u32[]{:S(2)}) collective-permute-start(f32[520,128]{1,0:T(8,128)S(1)} %get-tuple-element.48), channel_id=1, source_target_pairs={{0,24},{8,0},{16,8},{24,16},{1,25},{9,1},{17,9},{25,17},{2,26},{10... | collective-permute-start | bytes 798728 | tf_op jit(solution)/shard_map/ppermute | solution.py:360
  37.9 1.6 %shard_map.81 = (f32[256,512]{1,0:T(8,128)S(1)}, f32[4,2,128,128]{3,2,1,0:T(8,128)S(1)}, f32[512,128]{1,0:T(8,128)S(1)}) custom-call(s32[1,128]{1,0:T(1,128)S(1)} %slice_convert_fusion.4.refs_0_, f32[2,4,512,128]{3,2,1,0:T(8,128)S(1)} %shard_map.74.refs_1_, f32[4,2,128,128]{3,2,1,0:T(8,128)S(1)} %copy-done, bf16[4,256,256]{2,1,0:T(8,128)(2,1)S(1)} %copy-done.1, ...), custom_call_target="tpu_custom_call" | custom-call | flops 402653184 | bytes 1048576 | tf_op jit(solution)/shard_map/pallas_call | solution.py:23
  39.5 2.7 %collective-permute-start.10 = (f32[512,128]{1,0:T(8,128)S(1)}, f32[512,128]{1,0:T(8,128)S(1)}, u32[]{:S(2)}, u32[]{:S(2)}) collective-permute-start(f32[512,128]{1,0:T(8,128)S(1)} %get-tuple-element.56), channel_id=1, source_target_pairs={{0,24},{8,0},{16,8},{24,16},{1,25},{9,1},{17,9},{25,17},{2,26},{10... | collective-permute-start | bytes 786440 | tf_op jit(solution)/shard_map/ppermute | solution.py:360
  43.1 1.6 %shard_map.77 = (f32[256,512]{1,0:T(8,128)S(1)}, f32[4,2,128,128]{3,2,1,0:T(8,128)S(1)}, f32[520,128]{1,0:T(8,128)S(1)}) custom-call(s32[1,128]{1,0:T(1,128)S(1)} %slice_convert_fusion.3.refs_0_, f32[2,4,512,128]{3,2,1,0:T(8,128)S(1)} %shard_map.74.refs_1_, f32[4,2,128,128]{3,2,1,0:T(8,128)S(1)} %copy-done, bf16[4,256,256]{2,1,0:T(8,128)(2,1)S(1)} %copy-done.1, ...), custom_call_target="tpu_custom_call" | custom-call | flops 402653184 | bytes 1048576 | tf_op jit(solution)/shard_map/pallas_call | solution.py:23
  44.7 4.1 %collective-permute-start.7 = (f32[520,128]{1,0:T(8,128)S(1)}, f32[520,128]{1,0:T(8,128)S(1)}, u32[]{:S(2)}, u32[]{:S(2)}) collective-permute-start(f32[520,128]{1,0:T(8,128)S(1)} %get-tuple-element.49), channel_id=1, source_target_pairs={{0,24},{8,0},{16,8},{24,16},{1,25},{9,1},{17,9},{25,17},{2,26},{10... | collective-permute-start | bytes 798728 | tf_op jit(solution)/shard_map/ppermute | solution.py:360
  48.8 1.6 %shard_map.82 = (f32[256,512]{1,0:T(8,128)S(1)}, f32[4,2,128,128]{3,2,1,0:T(8,128)S(1)}, f32[512,128]{1,0:T(8,128)S(1)}) custom-call(s32[1,128]{1,0:T(1,128)S(1)} %slice_convert_fusion.3.refs_0_, f32[2,4,512,128]{3,2,1,0:T(8,128)S(1)} %shard_map.74.refs_1_, f32[4,2,128,128]{3,2,1,0:T(8,128)S(1)} %copy-done, bf16[4,256,256]{2,1,0:T(8,128)(2,1)S(1)} %copy-done.1, ...), custom_call_target="tpu_custom_call" | custom-call | flops 402653184 | bytes 1048576 | tf_op jit(solution)/shard_map/pallas_call | solution.py:23
  50.5 3.8 %collective-permute-start.11 = (f32[512,128]{1,0:T(8,128)S(1)}, f32[512,128]{1,0:T(8,128)S(1)}, u32[]{:S(2)}, u32[]{:S(2)}) collective-permute-start(f32[512,128]{1,0:T(8,128)S(1)} %get-tuple-element.57), channel_id=1, source_target_pairs={{0,24},{8,0},{16,8},{24,16},{1,25},{9,1},{17,9},{25,17},{2,26},{10... | collective-permute-start | bytes 786440 | tf_op jit(solution)/shard_map/ppermute | solution.py:360
  54.3 2.1 %shard_map.78 = (f32[256,512]{1,0:T(8,128)S(1)}, f32[4,2,128,128]{3,2,1,0:T(8,128)S(1)}, f32[512,128]{1,0:T(8,128)S(1)}, f32[256,512]{1,0:T(8,128)S(1)}, f32[4,2...) custom-call(s32[1,128]{1,0:T(1,128)S(1)} %get-tuple-element.44.refs_0_, f32[2,4,512,128]{3,2,1,0:T(8,128)S(1)} %shard_map.74.refs_1_, ...), custom_call_target="tpu_custom_call" | custom-call | flops 805306368 | bytes 1048576 | tf_op jit(solution)/shard_map/pallas_call | solution.py:23
  56.5 3.2 %collective-permute-done.11.arrived = f32[512,128]{1,0:T(8,128)S(1)} collective-permute-done((f32[512,128]{1,0:T(8,128)S(1)}, f32[512,128]{1,0:T(8,128)S(1)}, u32[]{:S(2)}, u32[]{:S(2)}) %collective-permute-start.11) | collective-permute-done | bytes 262176 | tf_op jit(solution)/shard_map/ppermute | solution.py:360
  61.5 2.5 %shard_map.86.refs_2_ = f32[1,5,640,128]{3,2,1,0:T(8,128)S(1)} custom-call(s32[3,128]{1,0:T(4,128)S(1)} %pad_add_fusion.4.refs_0_, f32[4,2,128,128]{3,2,1,0:T(8,128)S(1)} %copy-done), custom_call_target="tpu_custom_call" | custom-call | flops 402653184 | bytes 1048576 | tf_op jit(solution)/shard_map/pallas_call | solution.py:23
  64.0 2.3 %shard_map.84.refs_9_ = f32[2,4,512,128]{3,2,1,0:T(8,128)S(1)} custom-call(s32[1,128]{1,0:T(1,128)S(1)} %get-tuple-element.44.refs_0_, f32[4,2,128,128]{3,2,1,0:T(8,128)S(1)} %copy-done, bf16[4,256,256]{2,1,0:T(8,128)(2,1)S(1)} %copy-done.1, f32[256,512]{1,0:T(8,128)S(1)} %get-tuple-element.51.refs_3_, f32[4,2,128,128]{3,2,1,0:T(8,128)S(1)} %get-tuple-element.52.refs_4_, ...), custom_call_target="tpu_custom_call" | custom-call | flops 805306368 | bytes 1048576 | tf_op jit(solution)/shard_map/pallas_call | solution.py:23
  66.3 3.1 %collective-permute-done.13.refs_8_ = f32[512,128]{1,0:T(8,128)S(1)} collective-permute-done((f32[512,128]{1,0:T(8,128)S(1)}, f32[512,128]{1,0:T(8,128)S(1)}, u32[]{:S(2)}, u32[]{:S(2)}) %collective-permute-start.13) | collective-permute-done | bytes 262176 | tf_op jit(solution)/shard_map/ppermute | solution.py:360
  69.7 5.4 %collective-permute-done.8.refs_5_ = f32[520,128]{1,0:T(8,128)S(1)} collective-permute-done((f32[520,128]{1,0:T(8,128)S(1)}, f32[520,128]{1,0:T(8,128)S(1)}, u32[]{:S(2)}, u32[]{:S(2)}) %collective-permute-start.8) | collective-permute-done | bytes 266272 | tf_op jit(solution)/shard_map/ppermute | solution.py:360
  75.1 2.8 %shard_map.87.refs_2_ = f32[1,5,640,128]{3,2,1,0:T(8,128)S(1)} custom-call(s32[3,128]{1,0:T(4,128)S(1)} %pad_add_fusion.3.refs_0_, f32[4,2,128,128]{3,2,1,0:T(8,128)S(1)} %copy-done, f32[1,5,640,128]{3,2,1,0:T(8,128)S(1)} %shard_map.86.refs_2_), custom_call_target="tpu_custom_call", output_to_operand_aliasing={{}: (2, {})} | custom-call | flops 402653184 | bytes 1048576 | tf_op jit(solution)/shard_map/pallas_call | solution.py:23
  77.9 2.1 %shard_map.85.refs_9_ = f32[2,4,512,128]{3,2,1,0:T(8,128)S(1)} custom-call(s32[1,128]{1,0:T(1,128)S(1)} %slice_convert_fusion.3.refs_0_, f32[4,2,128,128]{3,2,1,0:T(8,128)S(1)} %copy-done, bf16[4,256,256]{2,1,0:T(8,128)(2,1)S(1)} %copy-done.1, f32[256,512]{1,0:T(8,128)S(1)} %get-tuple-element.60.refs_3_, ...), custom_call_target="tpu_custom_call", output_to_operand_aliasing={{}: (9, {})} | custom-call | flops 805306368 | bytes 1048576 | tf_op jit(solution)/shard_map/pallas_call | solution.py:23
  80.7 5.7 %collective-permute-done.12.refs_5_ = f32[520,128]{1,0:T(8,128)S(1)} collective-permute-done((f32[520,128]{1,0:T(8,128)S(1)}, f32[520,128]{1,0:T(8,128)S(1)}, u32[]{:S(2)}, u32[]{:S(2)}) %collective-permute-start.12) | collective-permute-done | bytes 266272 | tf_op jit(solution)/shard_map/ppermute | solution.py:360
  86.4 2.9 %shard_map.88.refs_2_ = f32[1,5,640,128]{3,2,1,0:T(8,128)S(1)} custom-call(s32[3,128]{1,0:T(4,128)S(1)} %pad_add_fusion.2.refs_0_, f32[4,2,128,128]{3,2,1,0:T(8,128)S(1)} %copy-done, f32[1,5,640,128]{3,2,1,0:T(8,128)S(1)} %shard_map.87.refs_2_), custom_call_target="tpu_custom_call", output_to_operand_aliasing={{}: (2, {})} | custom-call | flops 402653184 | bytes 1048576 | tf_op jit(solution)/shard_map/pallas_call | solution.py:23
  89.3 2.1 %shard_map.90.refs_6_ = f32[2,4,512,128]{3,2,1,0:T(8,128)S(1)} custom-call(s32[1,128]{1,0:T(1,128)S(1)} %slice_convert_fusion.4.refs_0_, f32[4,2,128,128]{3,2,1,0:T(8,128)S(1)} %copy-done, bf16[4,256,256]{2,1,0:T(8,128)(2,1)S(1)} %copy-done.1, f32[256,512]{1,0:T(8,128)S(1)} %get-tuple-element.70.refs_3_, ...), custom_call_target="tpu_custom_call", output_to_operand_aliasing={{}: (9, {})} | custom-call | flops 805306368 | bytes 1048576 | tf_op jit(solution)/shard_map/pallas_call | solution.py:23
  91.5 6.3 %collective-permute-done.14.refs_5_ = f32[520,128]{1,0:T(8,128)S(1)} collective-permute-done((f32[520,128]{1,0:T(8,128)S(1)}, f32[520,128]{1,0:T(8,128)S(1)}, u32[]{:S(2)}, u32[]{:S(2)}) %collective-permute-start.14) | collective-permute-done | bytes 266272 | tf_op jit(solution)/shard_map/ppermute | solution.py:360
  99.3 1.9 %shard_map.92 = (f32[2,4,512,128]{3,2,1,0:T(8,128)S(1)}, f32[512,128]{1,0:T(8,128)S(1)}, f32[384,128]{1,0:T(8,128)S(1)}, f32[128,128]{1,0:T(8,128)S(1)}, f32[2,6...) custom-call(s32[1,128]{1,0:T(1,128)S(1)} %collective-permute-done.refs_0_, ...), custom_call_target="tpu_custom_call", output_to_operand_aliasing={{0}: (6, {})} | custom-call | flops 402653184 | bytes 1048576 | tf_op jit(solution)/shard_map/pallas_call | solution.py:23
  101.2 5.3 %collective-permute-start.18 = (f32[384,128]{1,0:T(8,128)S(1)}, f32[384,128]{1,0:T(8,128)S(1)}, u32[]{:S(2)}, u32[]{:S(2)}) collective-permute-start(f32[384,128]{1,0:T(8,128)S(1)} %get-tuple-element.79), channel_id=1, source_target_pairs={{1,2},{3,4},{5,6},{2,1},{4,3},{6,5},{9,10},{11,12},{13,14},{10,9},... | collective-permute-start | bytes 589832 | tf_op jit(solution)/shard_map/ppermute | solution.py:360
  108.4 4.7 %collective-permute-start.21 = (f32[128,128]{1,0:T(8,128)S(1)}, f32[128,128]{1,0:T(8,128)S(1)}, u32[]{:S(2)}, u32[]{:S(2)}) collective-permute-start(f32[128,128]{1,0:T(8,128)S(1)} %get-tuple-element.82), channel_id=1, source_target_pairs={{1,2},{3,4},{5,6},{2,1},{4,3},{6,5},{9,10},{11,12},{13,14},{10,9},... | collective-permute-start | bytes 196616 | tf_op jit(solution)/shard_map/ppermute | solution.py:360
  113.1 2.6 %shard_map.89.weight = f32[1,5,640,128]{3,2,1,0:T(8,128)S(1)} custom-call(s32[3,128]{1,0:T(4,128)S(1)} %pad_add_fusion.1.refs_0_, f32[4,2,128,128]{3,2,1,0:T(8,128)S(1)} %copy-done, f32[1,5,640,128]{3,2,1,0:T(8,128)S(1)} %shard_map.88.refs_2_), custom_call_target="tpu_custom_call", output_to_operand_aliasing={{}: (2, {})} | custom-call | flops 402653184 | bytes 1048576 | tf_op jit(solution)/shard_map/pallas_call | solution.py:23
  117.1 1.7 %collective-permute-start.22 = (f32[2,64,128]{2,1,0:T(8,128)S(1)}, f32[2,64,128]{2,1,0:T(8,128)S(1)}, u32[]{:S(2)}, u32[]{:S(2)}) collective-permute-start(f32[2,64,128]{2,1,0:T(8,128)S(1)} %get-tuple-element.108), channel_id=1, source_target_pairs={{0,8},{16,24},{8,0},{24,16},{1,9},{17,25},{9,1},{25,17},{2,10},{18... | collective-permute-start | bytes 196616 | tf_op jit(solution)/shard_map/ppermute | solution.py:360
  118.8 2.4 %collective-permute-done.22 = f32[2,64,128]{2,1,0:T(8,128)S(1)} collective-permute-done((f32[2,64,128]{2,1,0:T(8,128)S(1)}, f32[2,64,128]{2,1,0:T(8,128)S(1)}, u32[]{:S(2)}, u32[]{:S(2)}) %collective-permute-start.22) | collective-permute-done | bytes 65568 | tf_op jit(solution)/shard_map/ppermute | solution.py:360
  (80 shorter events, 20.5 us)
Async XLA Ops:
  1.1 8.8 %collective-permute-start.2 = (f32[2,64,384]{2,1,0:T(8,128)S(1)}, f32[2,64,384]{2,1,0:T(8,128)S(1)}, u32[]{:S(2)}, u32[]{:S(2)}) collective-permute-start(f32[2,64,384]{2,1,0:T(8,128)S(1)} %get-tuple-element.83), channel_id=1, source_target_pairs={{8,16},{16,8},{9,17},{17,9},{10,18},{18,10},{11,19},{19,11},{12,20... | collective-permute-start | bytes 589832 | tf_op jit(solution)/shard_map/ppermute | solution.py:360
  1.7 9.0 %collective-permute-start.1 = (f32[2,64,384]{2,1,0:T(8,128)S(1)}, f32[2,64,384]{2,1,0:T(8,128)S(1)}, u32[]{:S(2)}, u32[]{:S(2)}) collective-permute-start(f32[2,64,384]{2,1,0:T(8,128)S(1)} %get-tuple-element.84), channel_id=1, source_target_pairs={{0,8},{16,24},{8,0},{24,16},{1,9},{17,25},{9,1},{25,17},{2,10},{18... | collective-permute-start | bytes 589832 | tf_op jit(solution)/shard_map/ppermute | solution.py:360
  7.8 1.3 %copy-start.2 = (f32[2,384,384]{2,1,0:T(8,128)S(1)}, f32[2,384,384]{2,1,0:T(8,128)}, u32[]{:S(2)}) copy-start(f32[2,384,384]{2,1,0:T(8,128)} %obj.5) | copy-start | bytes 3538948
  10.8 11.1 %copy-start.3 = (f32[2,384,384]{2,1,0:T(8,128)S(1)}, f32[2,384,384]{2,1,0:T(8,128)}, u32[]{:S(2)}) copy-start(f32[2,384,384]{2,1,0:T(8,128)} %obj.5) | copy-start | bytes 3538948
  11.1 10.7 %collective-permute-start.4 = (f32[520,128]{1,0:T(8,128)S(1)}, f32[520,128]{1,0:T(8,128)S(1)}, u32[]{:S(2)}, u32[]{:S(2)}) collective-permute-start(f32[520,128]{1,0:T(8,128)S(1)} %broadcast_select_fusion.2), channel_id=1, source_target_pairs={{1,2},{3,4},{5,6},{2,1},{4,3},{6,5},{9,10},{11,12},{13,14},{10,9},... | collective-permute-start | bytes 798728 | tf_op jit(solution)/shard_map/ppermute | solution.py:360
  15.8 6.0 %collective-permute-start.3 = (f32[520,128]{1,0:T(8,128)S(1)}, f32[520,128]{1,0:T(8,128)S(1)}, u32[]{:S(2)}, u32[]{:S(2)}) collective-permute-start(f32[520,128]{1,0:T(8,128)S(1)} %broadcast_select_fusion.3), channel_id=1, source_target_pairs={{0,1},{2,3},{4,5},{6,7},{1,0},{3,2},{5,4},{7,6},{8,9},{10,11},{12,... | collective-permute-start | bytes 798728 | tf_op jit(solution)/shard_map/ppermute | solution.py:360
  15.9 6.7 %collective-permute-start = (s32[1,128]{1,0:T(1,128)S(1)}, s32[1,128]{1,0:T(1,128)S(1)}, u32[]{:S(2)}, u32[]{:S(2)}) collective-permute-start(s32[1,128]{1,0:T(1,128)S(1)} %get-tuple-element.44.refs_0_), channel_id=1, source_target_pairs={{0,24},{8,0},{16,8},{24,16},{1,25},{9,1},{17,9},{25,17},{2,26},{10... | collective-permute-start | bytes 1544 | tf_op jit(solution)/shard_map/ppermute | solution.py:360
  21.9 1.0 copy-start
  21.9 1.2 copy-start.1
  24.8 7.3 %collective-permute-start.5 = (f32[520,128]{1,0:T(8,128)S(1)}, f32[520,128]{1,0:T(8,128)S(1)}, u32[]{:S(2)}, u32[]{:S(2)}) collective-permute-start(f32[520,128]{1,0:T(8,128)S(1)} %get-tuple-element.47), channel_id=1, source_target_pairs={{0,24},{8,0},{16,8},{24,16},{1,25},{9,1},{17,9},{25,17},{2,26},{10... | collective-permute-start | bytes 798728 | tf_op jit(solution)/shard_map/ppermute | solution.py:360
  27.6 10.2 %collective-permute-start.9 = (f32[512,128]{1,0:T(8,128)S(1)}, f32[512,128]{1,0:T(8,128)S(1)}, u32[]{:S(2)}, u32[]{:S(2)}) collective-permute-start(f32[512,128]{1,0:T(8,128)S(1)} %get-tuple-element.55), channel_id=1, source_target_pairs={{0,24},{8,0},{16,8},{24,16},{1,25},{9,1},{17,9},{25,17},{2,26},{10... | collective-permute-start | bytes 786440 | tf_op jit(solution)/shard_map/ppermute | solution.py:360
  32.1 5.7 %copy-start.4 = (f32[1,1,8,128,128]{4,3,2,1,0:T(8,128)S(1)}, f32[1,1,8,128,128]{4,3,2,1,0:T(8,128)}, u32[]{:S(2)}) copy-start(f32[1,1,8,128,128]{4,3,2,1,0:T(8,128)} %param.12) | copy-start | bytes 1572868
  33.8 9.3 %collective-permute-start.6 = (f32[520,128]{1,0:T(8,128)S(1)}, f32[520,128]{1,0:T(8,128)S(1)}, u32[]{:S(2)}, u32[]{:S(2)}) collective-permute-start(f32[520,128]{1,0:T(8,128)S(1)} %get-tuple-element.48), channel_id=1, source_target_pairs={{0,24},{8,0},{16,8},{24,16},{1,25},{9,1},{17,9},{25,17},{2,26},{10... | collective-permute-start | bytes 798728 | tf_op jit(solution)/shard_map/ppermute | solution.py:360
  39.5 9.4 %collective-permute-start.10 = (f32[512,128]{1,0:T(8,128)S(1)}, f32[512,128]{1,0:T(8,128)S(1)}, u32[]{:S(2)}, u32[]{:S(2)}) collective-permute-start(f32[512,128]{1,0:T(8,128)S(1)} %get-tuple-element.56), channel_id=1, source_target_pairs={{0,24},{8,0},{16,8},{24,16},{1,25},{9,1},{17,9},{25,17},{2,26},{10... | collective-permute-start | bytes 786440 | tf_op jit(solution)/shard_map/ppermute | solution.py:360
  44.7 15.4 %collective-permute-start.7 = (f32[520,128]{1,0:T(8,128)S(1)}, f32[520,128]{1,0:T(8,128)S(1)}, u32[]{:S(2)}, u32[]{:S(2)}) collective-permute-start(f32[520,128]{1,0:T(8,128)S(1)} %get-tuple-element.49), channel_id=1, source_target_pairs={{0,24},{8,0},{16,8},{24,16},{1,25},{9,1},{17,9},{25,17},{2,26},{10... | collective-permute-start | bytes 798728 | tf_op jit(solution)/shard_map/ppermute | solution.py:360
  50.5 9.2 %collective-permute-start.11 = (f32[512,128]{1,0:T(8,128)S(1)}, f32[512,128]{1,0:T(8,128)S(1)}, u32[]{:S(2)}, u32[]{:S(2)}) collective-permute-start(f32[512,128]{1,0:T(8,128)S(1)} %get-tuple-element.57), channel_id=1, source_target_pairs={{0,24},{8,0},{16,8},{24,16},{1,25},{9,1},{17,9},{25,17},{2,26},{10... | collective-permute-start | bytes 786440 | tf_op jit(solution)/shard_map/ppermute | solution.py:360
  59.8 9.6 %collective-permute-start.13 = (f32[512,128]{1,0:T(8,128)S(1)}, f32[512,128]{1,0:T(8,128)S(1)}, u32[]{:S(2)}, u32[]{:S(2)}) collective-permute-start(f32[512,128]{1,0:T(8,128)S(1)} %shard_map.83.refs_8_), channel_id=1, source_target_pairs={{0,8},{8,16},{16,24},{24,0},{1,9},{9,17},{17,25},{25,1},{2,10},{10... | collective-permute-start | bytes 786440 | tf_op jit(solution)/shard_map/ppermute | solution.py:360
  60.2 14.8 %collective-permute-start.8 = (f32[520,128]{1,0:T(8,128)S(1)}, f32[520,128]{1,0:T(8,128)S(1)}, u32[]{:S(2)}, u32[]{:S(2)}) collective-permute-start(f32[520,128]{1,0:T(8,128)S(1)} %shard_map.79.refs_5_), channel_id=1, source_target_pairs={{0,8},{8,16},{16,24},{24,0},{1,9},{9,17},{17,25},{25,1},{2,10},{10... | collective-permute-start | bytes 798728 | tf_op jit(solution)/shard_map/ppermute | solution.py:360
  69.4 11.3 %collective-permute-start.15 = (f32[512,128]{1,0:T(8,128)S(1)}, f32[512,128]{1,0:T(8,128)S(1)}, u32[]{:S(2)}, u32[]{:S(2)}) collective-permute-start(f32[512,128]{1,0:T(8,128)S(1)} %collective-permute-done.13.refs_8_), channel_id=1, source_target_pairs={{0,8},{8,16},{16,24},{24,0},{1,9},{9,17},{17,25},{25,1},{2,10},{10... | collective-permute-start | bytes 786440 | tf_op jit(solution)/shard_map/ppermute | solution.py:360
  75.1 11.3 %collective-permute-start.12 = (f32[520,128]{1,0:T(8,128)S(1)}, f32[520,128]{1,0:T(8,128)S(1)}, u32[]{:S(2)}, u32[]{:S(2)}) collective-permute-start(f32[520,128]{1,0:T(8,128)S(1)} %collective-permute-done.8.refs_5_), channel_id=1, source_target_pairs={{0,8},{8,16},{16,24},{24,0},{1,9},{9,17},{17,25},{25,1},{2,10},{10... | collective-permute-start | bytes 798728 | tf_op jit(solution)/shard_map/ppermute | solution.py:360
  80.7 18.6 %collective-permute-start.16 = (f32[512,128]{1,0:T(8,128)S(1)}, f32[512,128]{1,0:T(8,128)S(1)}, u32[]{:S(2)}, u32[]{:S(2)}) collective-permute-start(f32[512,128]{1,0:T(8,128)S(1)} %collective-permute-done.15.refs_8_), channel_id=1, source_target_pairs={{0,8},{8,16},{16,24},{24,0},{1,9},{9,17},{17,25},{25,1},{2,10},{10... | collective-permute-start | bytes 786440 | tf_op jit(solution)/shard_map/ppermute | solution.py:360
  86.4 11.3 %collective-permute-start.14 = (f32[520,128]{1,0:T(8,128)S(1)}, f32[520,128]{1,0:T(8,128)S(1)}, u32[]{:S(2)}, u32[]{:S(2)}) collective-permute-start(f32[520,128]{1,0:T(8,128)S(1)} %collective-permute-done.12.refs_5_), channel_id=1, source_target_pairs={{0,8},{8,16},{16,24},{24,0},{1,9},{9,17},{17,25},{25,1},{2,10},{10... | collective-permute-start | bytes 798728 | tf_op jit(solution)/shard_map/ppermute | solution.py:360
  101.2 17.6 %collective-permute-start.18 = (f32[384,128]{1,0:T(8,128)S(1)}, f32[384,128]{1,0:T(8,128)S(1)}, u32[]{:S(2)}, u32[]{:S(2)}) collective-permute-start(f32[384,128]{1,0:T(8,128)S(1)} %get-tuple-element.79), channel_id=1, source_target_pairs={{1,2},{3,4},{5,6},{2,1},{4,3},{6,5},{9,10},{11,12},{13,14},{10,9},... | collective-permute-start | bytes 589832 | tf_op jit(solution)/shard_map/ppermute | solution.py:360
  106.5 9.8 %collective-permute-start.17 = (f32[512,128]{1,0:T(8,128)S(1)}, f32[512,128]{1,0:T(8,128)S(1)}, u32[]{:S(2)}, u32[]{:S(2)}) collective-permute-start(f32[512,128]{1,0:T(8,128)S(1)} %get-tuple-element.78), channel_id=1, source_target_pairs={{0,1},{2,3},{4,5},{6,7},{1,0},{3,2},{5,4},{7,6},{8,9},{10,11},{12,... | collective-permute-start | bytes 786440 | tf_op jit(solution)/shard_map/ppermute | solution.py:360
  106.6 9.7 %collective-permute-start.20 = (f32[2,64,384]{2,1,0:T(8,128)S(1)}, f32[2,64,384]{2,1,0:T(8,128)S(1)}, u32[]{:S(2)}, u32[]{:S(2)}) collective-permute-start(f32[2,64,384]{2,1,0:T(8,128)S(1)} %get-tuple-element.81), channel_id=1, source_target_pairs={{8,16},{16,8},{9,17},{17,9},{10,18},{18,10},{11,19},{19,11},{12,20... | collective-permute-start | bytes 589832 | tf_op jit(solution)/shard_map/ppermute | solution.py:360
  107.3 9.0 %collective-permute-start.19 = (f32[2,64,384]{2,1,0:T(8,128)S(1)}, f32[2,64,384]{2,1,0:T(8,128)S(1)}, u32[]{:S(2)}, u32[]{:S(2)}) collective-permute-start(f32[2,64,384]{2,1,0:T(8,128)S(1)} %get-tuple-element.80), channel_id=1, source_target_pairs={{0,8},{16,24},{8,0},{24,16},{1,9},{17,25},{9,1},{25,17},{2,10},{18... | collective-permute-start | bytes 589832 | tf_op jit(solution)/shard_map/ppermute | solution.py:360
  108.4 7.9 %collective-permute-start.21 = (f32[128,128]{1,0:T(8,128)S(1)}, f32[128,128]{1,0:T(8,128)S(1)}, u32[]{:S(2)}, u32[]{:S(2)}) collective-permute-start(f32[128,128]{1,0:T(8,128)S(1)} %get-tuple-element.82), channel_id=1, source_target_pairs={{1,2},{3,4},{5,6},{2,1},{4,3},{6,5},{9,10},{11,12},{13,14},{10,9},... | collective-permute-start | bytes 196616 | tf_op jit(solution)/shard_map/ppermute | solution.py:360
  116.4 2.4 %collective-permute-start.23 = (f32[2,64,128]{2,1,0:T(8,128)S(1)}, f32[2,64,128]{2,1,0:T(8,128)S(1)}, u32[]{:S(2)}, u32[]{:S(2)}) collective-permute-start(f32[2,64,128]{2,1,0:T(8,128)S(1)} %get-tuple-element.107), channel_id=1, source_target_pairs={{8,16},{16,8},{9,17},{17,9},{10,18},{18,10},{11,19},{19,11},{12,20... | collective-permute-start | bytes 196616 | tf_op jit(solution)/shard_map/ppermute | solution.py:360
  117.1 4.1 %collective-permute-start.22 = (f32[2,64,128]{2,1,0:T(8,128)S(1)}, f32[2,64,128]{2,1,0:T(8,128)S(1)}, u32[]{:S(2)}, u32[]{:S(2)}) collective-permute-start(f32[2,64,128]{2,1,0:T(8,128)S(1)} %get-tuple-element.108), channel_id=1, source_target_pairs={{0,8},{16,24},{8,0},{24,16},{1,9},{17,25},{9,1},{25,17},{2,10},{18... | collective-permute-start | bytes 196616 | tf_op jit(solution)/shard_map/ppermute | solution.py:360

commit v11 on v10

--- a/solution.py
+++ b/solution.py
@@ -74,11 +74,11 @@
     return y, x // size, x % size
 
 
-def edge_kernel(obj, joined, edge_l, edge_r, meta):
-    beams, scans = joined.shape[0] - 3, joined.shape[1]
-    values = [joined[axis, slot] for slot in range(scans) for axis in range(2)]
-    values += [joined[2 + beams, at] for at in range(3)]
-    values += [joined[2 + beam, slot] for slot in range(scans) for beam in range(beams)]
+def edge_kernel(obj, positions, counts, offsets, place_of, edge_l, edge_r, meta):
+    scans = positions.shape[2]
+    values = [positions[0, 0, slot, axis] for slot in range(scans) for axis in range(2)]
+    values += [counts[0, 0], place_of[0], place_of[1]]
+    values += [offsets[slot, beam] for slot in range(scans) for beam in range(offsets.shape[1])]
     assert len(values) <= meta.shape[1]
     lane = lax.broadcasted_iota(jnp.int32, meta.shape, 1)
     row = jnp.zeros(meta.shape, jnp.int32)
@@ -397,9 +397,6 @@
     at_row, at_col = lax.axis_index("row").astype(jnp.int32), lax.axis_index("col").astype(jnp.int32)
     odd_row, odd_col = lax.rem(at_row, 2) == 1, lax.rem(at_col, 2) == 1
     ends = jnp.where(odd_row, 0, tile_rows - half), jnp.where(odd_row, tile_rows - half, 0)
-    which = lax.broadcasted_iota(jnp.int32, (1, scans), 1)
-    places = jnp.where(which == 0, counts[0, 0], jnp.where(which == 1, at_row, at_col))
-    joined = jnp.concatenate([positions[0, 0].T, offsets.T, places])
     rows_1, rows_2 = (
         move(lax.dynamic_slice_in_dim(obj, ends[i], half, axis=1), "row", swap("row", i))
         for i in range(2)
@@ -408,8 +405,8 @@
     edge_l, edge_r, meta = call(
         edge_kernel,
         [(tile_rows, size)] * 2 + [jax.ShapeDtypeStruct((1, size), jnp.int32)],
-        [VMEM, SMEM],
-        (obj, joined),
+        [VMEM, SMEM, SMEM, SMEM, SMEM],
+        (obj, positions, counts, offsets, jnp.stack([at_row, at_col])),
         10**6,
     )
 

time: 123 us -> 123 us (level)
  local copies, waits for them, and re-layouts: 3.12 us -> 4.64 us
    unnamed x10 -> x12, local copies, waits for them, and re-layouts: 1.84 us -> 3.35 us
  transfers between devices with their start and end apart: 24 -> 24, of which waited for: 11 -> 10; matrix products, arithmetic and copies ran while one was open for 1% -> 2% of each run, Pallas kernels for 26% -> 26%
where the time goes in v11:
time: 123 us; the launch traced here: 122 us
  starting transfers between devices  44.3 us (36%)
  Pallas kernels  36.1 us (29%)
  waiting for transfers between devices  35.6 us (29%)
  local copies, waits for them, and re-layouts  4.64 us (4%)
    ppermute x24, starting transfers between devices, move(): return lax.ppermute(x, axis, pairs)  44.3 us
    pallas_call x22, Pallas kernels, call(): pl.pallas_call(kernel, out_shape=[s if hasattr(s, 'dtype') else jax.Shape...  36.1 us
    ppermute x24, waiting for transfers between devices, move(): return lax.ppermute(x, axis, pairs)  35.6 us
    unnamed x12, local copies, waits for them, and re-layouts  3.35 us
  transfers between devices with their start and end apart: 24, of which 10 were waited for; matrix products, arithmetic and copies ran while one was open for 2% of the time, Pallas kernels for 26%

profile of v11, /device:TPU:1, one launch (start us, length us, event | category | flops | bytes accessed | tf_op | source)
XLA Modules:
  0.0 122.4 jit_solution(6957807738593278647)
XLA Ops:
  1.7 4.7 %collective-permute-start.1 = (f32[2,64,384]{2,1,0:T(8,128)S(1)}, f32[2,64,384]{2,1,0:T(8,128)S(1)}, u32[]{:S(2)}, u32[]{:S(2)}) collective-permute-start(f32[2,64,384]{2,1,0:T(8,128)S(1)} %get-tuple-element.84), channel_id=1, source_target_pairs={{0,8},{16,24},{8,0},{24,16},{1,9},{17,25},{9,1},{25,17},{2,10},{18... | collective-permute-start | bytes 589832 | tf_op jit(solution)/shard_map/ppermute | solution.py:360
  11.2 4.5 %collective-permute-start.4 = (f32[520,128]{1,0:T(8,128)S(1)}, f32[520,128]{1,0:T(8,128)S(1)}, u32[]{:S(2)}, u32[]{:S(2)}) collective-permute-start(f32[520,128]{1,0:T(8,128)S(1)} %broadcast_select_fusion.2), channel_id=1, source_target_pairs={{1,2},{3,4},{5,6},{2,1},{4,3},{6,5},{9,10},{11,12},{13,14},{10,9},... | collective-permute-start | bytes 798728 | tf_op jit(solution)/shard_map/ppermute | solution.py:360
  16.9 4.8 %collective-permute-done.4 = f32[520,128]{1,0:T(8,128)S(1)} collective-permute-done((f32[520,128]{1,0:T(8,128)S(1)}, f32[520,128]{1,0:T(8,128)S(1)}, u32[]{:S(2)}, u32[]{:S(2)}) %collective-permute-start.4) | collective-permute-done | bytes 266272 | tf_op jit(solution)/shard_map/ppermute | solution.py:360
  23.0 1.6 %shard_map.75 = (f32[256,512]{1,0:T(8,128)S(1)}, f32[4,2,128,128]{3,2,1,0:T(8,128)S(1)}, f32[520,128]{1,0:T(8,128)S(1)}) custom-call(s32[1,128]{1,0:T(1,128)S(1)} %collective-permute-done.refs_0_, f32[2,4,512,128]{3,2,1,0:T(8,128)S(1)} %shard_map.74.refs_1_, f32[4,2,128,128]{3,2,1,0:T(8,128)S(1)} %copy-done, bf16[4,256,256]{2,1,0:T(8,128)(2,1)S(1)} %copy-done.1), custom_call_target="tpu_custom_call" | custom-call | flops 402653184 | bytes 1048576 | tf_op jit(solution)/shard_map/pallas_call | solution.py:23
  25.8 1.6 %shard_map.80 = (f32[256,512]{1,0:T(8,128)S(1)}, f32[4,2,128,128]{3,2,1,0:T(8,128)S(1)}, f32[512,128]{1,0:T(8,128)S(1)}) custom-call(s32[1,128]{1,0:T(1,128)S(1)} %collective-permute-done.refs_0_, f32[2,4,512,128]{3,2,1,0:T(8,128)S(1)} %shard_map.74.refs_1_, f32[4,2,128,128]{3,2,1,0:T(8,128)S(1)} %copy-done, bf16[4,256,256]{2,1,0:T(8,128)(2,1)S(1)} %copy-done.1), custom_call_target="tpu_custom_call" | custom-call | flops 402653184 | bytes 1048576 | tf_op jit(solution)/shard_map/pallas_call | solution.py:23
  29.0 3.0 %collective-permute-done.5.refs_4_ = f32[520,128]{1,0:T(8,128)S(1)} collective-permute-done((f32[520,128]{1,0:T(8,128)S(1)}, f32[520,128]{1,0:T(8,128)S(1)}, u32[]{:S(2)}, u32[]{:S(2)}) %collective-permute-start.5) | collective-permute-done | bytes 266272 | tf_op jit(solution)/shard_map/ppermute | solution.py:360
  32.0 1.6 %shard_map.76 = (f32[256,512]{1,0:T(8,128)S(1)}, f32[4,2,128,128]{3,2,1,0:T(8,128)S(1)}, f32[520,128]{1,0:T(8,128)S(1)}) custom-call(s32[1,128]{1,0:T(1,128)S(1)} %slice_convert_fusion.4.refs_0_, f32[2,4,512,128]{3,2,1,0:T(8,128)S(1)} %shard_map.74.refs_1_, f32[4,2,128,128]{3,2,1,0:T(8,128)S(1)} %copy-done, bf16[4,256,256]{2,1,0:T(8,128)(2,1)S(1)} %copy-done.1, ...), custom_call_target="tpu_custom_call" | custom-call | flops 402653184 | bytes 1048576 | tf_op jit(solution)/shard_map/pallas_call | solution.py:23
  33.6 4.1 %collective-permute-start.6 = (f32[520,128]{1,0:T(8,128)S(1)}, f32[520,128]{1,0:T(8,128)S(1)}, u32[]{:S(2)}, u32[]{:S(2)}) collective-permute-start(f32[520,128]{1,0:T(8,128)S(1)} %get-tuple-element.48), channel_id=1, source_target_pairs={{0,24},{8,0},{16,8},{24,16},{1,25},{9,1},{17,9},{25,17},{2,26},{10... | collective-permute-start | bytes 798728 | tf_op jit(solution)/shard_map/ppermute | solution.py:360
  37.7 1.6 %shard_map.81 = (f32[256,512]{1,0:T(8,128)S(1)}, f32[4,2,128,128]{3,2,1,0:T(8,128)S(1)}, f32[512,128]{1,0:T(8,128)S(1)}) custom-call(s32[1,128]{1,0:T(1,128)S(1)} %slice_convert_fusion.4.refs_0_, f32[2,4,512,128]{3,2,1,0:T(8,128)S(1)} %shard_map.74.refs_1_, f32[4,2,128,128]{3,2,1,0:T(8,128)S(1)} %copy-done, bf16[4,256,256]{2,1,0:T(8,128)(2,1)S(1)} %copy-done.1, ...), custom_call_target="tpu_custom_call" | custom-call | flops 402653184 | bytes 1048576 | tf_op jit(solution)/shard_map/pallas_call | solution.py:23
  39.3 2.7 %collective-permute-start.10 = (f32[512,128]{1,0:T(8,128)S(1)}, f32[512,128]{1,0:T(8,128)S(1)}, u32[]{:S(2)}, u32[]{:S(2)}) collective-permute-start(f32[512,128]{1,0:T(8,128)S(1)} %get-tuple-element.56), channel_id=1, source_target_pairs={{0,24},{8,0},{16,8},{24,16},{1,25},{9,1},{17,9},{25,17},{2,26},{10... | collective-permute-start | bytes 786440 | tf_op jit(solution)/shard_map/ppermute | solution.py:360
  42.9 1.6 %shard_map.77 = (f32[256,512]{1,0:T(8,128)S(1)}, f32[4,2,128,128]{3,2,1,0:T(8,128)S(1)}, f32[520,128]{1,0:T(8,128)S(1)}) custom-call(s32[1,128]{1,0:T(1,128)S(1)} %slice_convert_fusion.3.refs_0_, f32[2,4,512,128]{3,2,1,0:T(8,128)S(1)} %shard_map.74.refs_1_, f32[4,2,128,128]{3,2,1,0:T(8,128)S(1)} %copy-done, bf16[4,256,256]{2,1,0:T(8,128)(2,1)S(1)} %copy-done.1, ...), custom_call_target="tpu_custom_call" | custom-call | flops 402653184 | bytes 1048576 | tf_op jit(solution)/shard_map/pallas_call | solution.py:23
  44.6 4.1 %collective-permute-start.7 = (f32[520,128]{1,0:T(8,128)S(1)}, f32[520,128]{1,0:T(8,128)S(1)}, u32[]{:S(2)}, u32[]{:S(2)}) collective-permute-start(f32[520,128]{1,0:T(8,128)S(1)} %get-tuple-element.49), channel_id=1, source_target_pairs={{0,24},{8,0},{16,8},{24,16},{1,25},{9,1},{17,9},{25,17},{2,26},{10... | collective-permute-start | bytes 798728 | tf_op jit(solution)/shard_map/ppermute | solution.py:360
  48.7 1.6 %shard_map.82 = (f32[256,512]{1,0:T(8,128)S(1)}, f32[4,2,128,128]{3,2,1,0:T(8,128)S(1)}, f32[512,128]{1,0:T(8,128)S(1)}) custom-call(s32[1,128]{1,0:T(1,128)S(1)} %slice_convert_fusion.3.refs_0_, f32[2,4,512,128]{3,2,1,0:T(8,128)S(1)} %shard_map.74.refs_1_, f32[4,2,128,128]{3,2,1,0:T(8,128)S(1)} %copy-done, bf16[4,256,256]{2,1,0:T(8,128)(2,1)S(1)} %copy-done.1, ...), custom_call_target="tpu_custom_call" | custom-call | flops 402653184 | bytes 1048576 | tf_op jit(solution)/shard_map/pallas_call | solution.py:23
  50.4 3.8 %collective-permute-start.11 = (f32[512,128]{1,0:T(8,128)S(1)}, f32[512,128]{1,0:T(8,128)S(1)}, u32[]{:S(2)}, u32[]{:S(2)}) collective-permute-start(f32[512,128]{1,0:T(8,128)S(1)} %get-tuple-element.57), channel_id=1, source_target_pairs={{0,24},{8,0},{16,8},{24,16},{1,25},{9,1},{17,9},{25,17},{2,26},{10... | collective-permute-start | bytes 786440 | tf_op jit(solution)/shard_map/ppermute | solution.py:360
  54.1 2.1 %shard_map.78 = (f32[256,512]{1,0:T(8,128)S(1)}, f32[4,2,128,128]{3,2,1,0:T(8,128)S(1)}, f32[512,128]{1,0:T(8,128)S(1)}, f32[256,512]{1,0:T(8,128)S(1)}, f32[4,2...) custom-call(s32[1,128]{1,0:T(1,128)S(1)} %get-tuple-element.44.refs_0_, f32[2,4,512,128]{3,2,1,0:T(8,128)S(1)} %shard_map.74.refs_1_, ...), custom_call_target="tpu_custom_call" | custom-call | flops 805306368 | bytes 1048576 | tf_op jit(solution)/shard_map/pallas_call | solution.py:23
  56.3 3.3 %collective-permute-done.11.arrived = f32[512,128]{1,0:T(8,128)S(1)} collective-permute-done((f32[512,128]{1,0:T(8,128)S(1)}, f32[512,128]{1,0:T(8,128)S(1)}, u32[]{:S(2)}, u32[]{:S(2)}) %collective-permute-start.11) | collective-permute-done | bytes 262176 | tf_op jit(solution)/shard_map/ppermute | solution.py:360
  61.4 2.5 %shard_map.86.refs_2_ = f32[1,5,640,128]{3,2,1,0:T(8,128)S(1)} custom-call(s32[3,128]{1,0:T(4,128)S(1)} %pad_add_fusion.3.refs_0_, f32[4,2,128,128]{3,2,1,0:T(8,128)S(1)} %copy-done), custom_call_target="tpu_custom_call" | custom-call | flops 402653184 | bytes 1048576 | tf_op jit(solution)/shard_map/pallas_call | solution.py:23
  63.9 2.3 %shard_map.84.refs_9_ = f32[2,4,512,128]{3,2,1,0:T(8,128)S(1)} custom-call(s32[1,128]{1,0:T(1,128)S(1)} %get-tuple-element.44.refs_0_, f32[4,2,128,128]{3,2,1,0:T(8,128)S(1)} %copy-done, bf16[4,256,256]{2,1,0:T(8,128)(2,1)S(1)} %copy-done.1, f32[256,512]{1,0:T(8,128)S(1)} %get-tuple-element.51.refs_3_, f32[4,2,128,128]{3,2,1,0:T(8,128)S(1)} %get-tuple-element.52.refs_4_, ...), custom_call_target="tpu_custom_call" | custom-call | flops 805306368 | bytes 1048576 | tf_op jit(solution)/shard_map/pallas_call | solution.py:23
  66.2 3.1 %collective-permute-done.13.refs_8_ = f32[512,128]{1,0:T(8,128)S(1)} collective-permute-done((f32[512,128]{1,0:T(8,128)S(1)}, f32[512,128]{1,0:T(8,128)S(1)}, u32[]{:S(2)}, u32[]{:S(2)}) %collective-permute-start.13) | collective-permute-done | bytes 262176 | tf_op jit(solution)/shard_map/ppermute | solution.py:360
  69.6 5.4 %collective-permute-done.8.refs_5_ = f32[520,128]{1,0:T(8,128)S(1)} collective-permute-done((f32[520,128]{1,0:T(8,128)S(1)}, f32[520,128]{1,0:T(8,128)S(1)}, u32[]{:S(2)}, u32[]{:S(2)}) %collective-permute-start.8) | collective-permute-done | bytes 266272 | tf_op jit(solution)/shard_map/ppermute | solution.py:360
  75.0 2.8 %shard_map.87.refs_2_ = f32[1,5,640,128]{3,2,1,0:T(8,128)S(1)} custom-call(s32[3,128]{1,0:T(4,128)S(1)} %pad_add_fusion.2.refs_0_, f32[4,2,128,128]{3,2,1,0:T(8,128)S(1)} %copy-done, f32[1,5,640,128]{3,2,1,0:T(8,128)S(1)} %shard_map.86.refs_2_), custom_call_target="tpu_custom_call", output_to_operand_aliasing={{}: (2, {})} | custom-call | flops 402653184 | bytes 1048576 | tf_op jit(solution)/shard_map/pallas_call | solution.py:23
  77.8 2.1 %shard_map.85.refs_9_ = f32[2,4,512,128]{3,2,1,0:T(8,128)S(1)} custom-call(s32[1,128]{1,0:T(1,128)S(1)} %slice_convert_fusion.3.refs_0_, f32[4,2,128,128]{3,2,1,0:T(8,128)S(1)} %copy-done, bf16[4,256,256]{2,1,0:T(8,128)(2,1)S(1)} %copy-done.1, f32[256,512]{1,0:T(8,128)S(1)} %get-tuple-element.60.refs_3_, ...), custom_call_target="tpu_custom_call", output_to_operand_aliasing={{}: (9, {})} | custom-call | flops 805306368 | bytes 1048576 | tf_op jit(solution)/shard_map/pallas_call | solution.py:23
  80.6 5.7 %collective-permute-done.12.refs_5_ = f32[520,128]{1,0:T(8,128)S(1)} collective-permute-done((f32[520,128]{1,0:T(8,128)S(1)}, f32[520,128]{1,0:T(8,128)S(1)}, u32[]{:S(2)}, u32[]{:S(2)}) %collective-permute-start.12) | collective-permute-done | bytes 266272 | tf_op jit(solution)/shard_map/ppermute | solution.py:360
  86.4 2.9 %shard_map.88.refs_2_ = f32[1,5,640,128]{3,2,1,0:T(8,128)S(1)} custom-call(s32[3,128]{1,0:T(4,128)S(1)} %pad_add_fusion.1.refs_0_, f32[4,2,128,128]{3,2,1,0:T(8,128)S(1)} %copy-done, f32[1,5,640,128]{3,2,1,0:T(8,128)S(1)} %shard_map.87.refs_2_), custom_call_target="tpu_custom_call", output_to_operand_aliasing={{}: (2, {})} | custom-call | flops 402653184 | bytes 1048576 | tf_op jit(solution)/shard_map/pallas_call | solution.py:23
  89.2 2.1 %shard_map.90.refs_6_ = f32[2,4,512,128]{3,2,1,0:T(8,128)S(1)} custom-call(s32[1,128]{1,0:T(1,128)S(1)} %slice_convert_fusion.4.refs_0_, f32[4,2,128,128]{3,2,1,0:T(8,128)S(1)} %copy-done, bf16[4,256,256]{2,1,0:T(8,128)(2,1)S(1)} %copy-done.1, f32[256,512]{1,0:T(8,128)S(1)} %get-tuple-element.70.refs_3_, ...), custom_call_target="tpu_custom_call", output_to_operand_aliasing={{}: (9, {})} | custom-call | flops 805306368 | bytes 1048576 | tf_op jit(solution)/shard_map/pallas_call | solution.py:23
  91.4 6.3 %collective-permute-done.14.refs_5_ = f32[520,128]{1,0:T(8,128)S(1)} collective-permute-done((f32[520,128]{1,0:T(8,128)S(1)}, f32[520,128]{1,0:T(8,128)S(1)}, u32[]{:S(2)}, u32[]{:S(2)}) %collective-permute-start.14) | collective-permute-done | bytes 266272 | tf_op jit(solution)/shard_map/ppermute | solution.py:360
  99.2 1.9 %shard_map.92 = (f32[2,4,512,128]{3,2,1,0:T(8,128)S(1)}, f32[512,128]{1,0:T(8,128)S(1)}, f32[384,128]{1,0:T(8,128)S(1)}, f32[128,128]{1,0:T(8,128)S(1)}, f32[2,6...) custom-call(s32[1,128]{1,0:T(1,128)S(1)} %collective-permute-done.refs_0_, ...), custom_call_target="tpu_custom_call", output_to_operand_aliasing={{0}: (6, {})} | custom-call | flops 402653184 | bytes 1048576 | tf_op jit(solution)/shard_map/pallas_call | solution.py:23
  101.1 4.7 %collective-permute-start.18 = (f32[384,128]{1,0:T(8,128)S(1)}, f32[384,128]{1,0:T(8,128)S(1)}, u32[]{:S(2)}, u32[]{:S(2)}) collective-permute-start(f32[384,128]{1,0:T(8,128)S(1)} %get-tuple-element.79), channel_id=1, source_target_pairs={{1,2},{3,4},{5,6},{2,1},{4,3},{6,5},{9,10},{11,12},{13,14},{10,9},... | collective-permute-start | bytes 589832 | tf_op jit(solution)/shard_map/ppermute | solution.py:360
  107.9 5.1 %collective-permute-start.21 = (f32[128,128]{1,0:T(8,128)S(1)}, f32[128,128]{1,0:T(8,128)S(1)}, u32[]{:S(2)}, u32[]{:S(2)}) collective-permute-start(f32[128,128]{1,0:T(8,128)S(1)} %get-tuple-element.82), channel_id=1, source_target_pairs={{1,2},{3,4},{5,6},{2,1},{4,3},{6,5},{9,10},{11,12},{13,14},{10,9},... | collective-permute-start | bytes 196616 | tf_op jit(solution)/shard_map/ppermute | solution.py:360
  113.0 2.6 %shard_map.89.weight = f32[1,5,640,128]{3,2,1,0:T(8,128)S(1)} custom-call(s32[3,128]{1,0:T(4,128)S(1)} %pad_add_fusion.refs_0_, f32[4,2,128,128]{3,2,1,0:T(8,128)S(1)} %copy-done, f32[1,5,640,128]{3,2,1,0:T(8,128)S(1)} %shard_map.88.refs_2_), custom_call_target="tpu_custom_call", output_to_operand_aliasing={{}: (2, {})} | custom-call | flops 402653184 | bytes 1048576 | tf_op jit(solution)/shard_map/pallas_call | solution.py:23
  116.9 1.7 %collective-permute-start.22 = (f32[2,64,128]{2,1,0:T(8,128)S(1)}, f32[2,64,128]{2,1,0:T(8,128)S(1)}, u32[]{:S(2)}, u32[]{:S(2)}) collective-permute-start(f32[2,64,128]{2,1,0:T(8,128)S(1)} %get-tuple-element.108), channel_id=1, source_target_pairs={{0,8},{16,24},{8,0},{24,16},{1,9},{17,25},{9,1},{25,17},{2,10},{18... | collective-permute-start | bytes 196616 | tf_op jit(solution)/shard_map/ppermute | solution.py:360
  118.7 2.5 %collective-permute-done.22 = f32[2,64,128]{2,1,0:T(8,128)S(1)} collective-permute-done((f32[2,64,128]{2,1,0:T(8,128)S(1)}, f32[2,64,128]{2,1,0:T(8,128)S(1)}, u32[]{:S(2)}, u32[]{:S(2)}) %collective-permute-start.22) | collective-permute-done | bytes 65568 | tf_op jit(solution)/shard_map/ppermute | solution.py:360
  (81 shorter events, 20.8 us)
Async XLA Ops:
  1.1 9.8 %collective-permute-start.2 = (f32[2,64,384]{2,1,0:T(8,128)S(1)}, f32[2,64,384]{2,1,0:T(8,128)S(1)}, u32[]{:S(2)}, u32[]{:S(2)}) collective-permute-start(f32[2,64,384]{2,1,0:T(8,128)S(1)} %get-tuple-element.83), channel_id=1, source_target_pairs={{8,16},{16,8},{9,17},{17,9},{10,18},{18,10},{11,19},{19,11},{12,20... | collective-permute-start | bytes 589832 | tf_op jit(solution)/shard_map/ppermute | solution.py:360
  1.7 9.1 %collective-permute-start.1 = (f32[2,64,384]{2,1,0:T(8,128)S(1)}, f32[2,64,384]{2,1,0:T(8,128)S(1)}, u32[]{:S(2)}, u32[]{:S(2)}) collective-permute-start(f32[2,64,384]{2,1,0:T(8,128)S(1)} %get-tuple-element.84), channel_id=1, source_target_pairs={{0,8},{16,24},{8,0},{24,16},{1,9},{17,25},{9,1},{25,17},{2,10},{18... | collective-permute-start | bytes 589832 | tf_op jit(solution)/shard_map/ppermute | solution.py:360
  8.7 1.3 %copy-start.2 = (f32[2,384,384]{2,1,0:T(8,128)S(1)}, f32[2,384,384]{2,1,0:T(8,128)}, u32[]{:S(2)}) copy-start(f32[2,384,384]{2,1,0:T(8,128)} %obj.5) | copy-start | bytes 3538948
  11.2 10.5 %collective-permute-start.4 = (f32[520,128]{1,0:T(8,128)S(1)}, f32[520,128]{1,0:T(8,128)S(1)}, u32[]{:S(2)}, u32[]{:S(2)}) collective-permute-start(f32[520,128]{1,0:T(8,128)S(1)} %broadcast_select_fusion.2), channel_id=1, source_target_pairs={{1,2},{3,4},{5,6},{2,1},{4,3},{6,5},{9,10},{11,12},{13,14},{10,9},... | collective-permute-start | bytes 798728 | tf_op jit(solution)/shard_map/ppermute | solution.py:360
  15.7 6.0 %collective-permute-start.3 = (f32[520,128]{1,0:T(8,128)S(1)}, f32[520,128]{1,0:T(8,128)S(1)}, u32[]{:S(2)}, u32[]{:S(2)}) collective-permute-start(f32[520,128]{1,0:T(8,128)S(1)} %broadcast_select_fusion.3), channel_id=1, source_target_pairs={{0,1},{2,3},{4,5},{6,7},{1,0},{3,2},{5,4},{7,6},{8,9},{10,11},{12,... | collective-permute-start | bytes 798728 | tf_op jit(solution)/shard_map/ppermute | solution.py:360
  15.8 6.7 %collective-permute-start = (s32[1,128]{1,0:T(1,128)S(1)}, s32[1,128]{1,0:T(1,128)S(1)}, u32[]{:S(2)}, u32[]{:S(2)}) collective-permute-start(s32[1,128]{1,0:T(1,128)S(1)} %get-tuple-element.44.refs_0_), channel_id=1, source_target_pairs={{0,24},{8,0},{16,8},{24,16},{1,25},{9,1},{17,9},{25,17},{2,26},{10... | collective-permute-start | bytes 1544 | tf_op jit(solution)/shard_map/ppermute | solution.py:360
  21.8 1.0 copy-start
  21.8 1.2 copy-start.1
  24.6 7.3 %collective-permute-start.5 = (f32[520,128]{1,0:T(8,128)S(1)}, f32[520,128]{1,0:T(8,128)S(1)}, u32[]{:S(2)}, u32[]{:S(2)}) collective-permute-start(f32[520,128]{1,0:T(8,128)S(1)} %get-tuple-element.47), channel_id=1, source_target_pairs={{0,24},{8,0},{16,8},{24,16},{1,25},{9,1},{17,9},{25,17},{2,26},{10... | collective-permute-start | bytes 798728 | tf_op jit(solution)/shard_map/ppermute | solution.py:360
  27.5 10.2 %collective-permute-start.9 = (f32[512,128]{1,0:T(8,128)S(1)}, f32[512,128]{1,0:T(8,128)S(1)}, u32[]{:S(2)}, u32[]{:S(2)}) collective-permute-start(f32[512,128]{1,0:T(8,128)S(1)} %get-tuple-element.55), channel_id=1, source_target_pairs={{0,24},{8,0},{16,8},{24,16},{1,25},{9,1},{17,9},{25,17},{2,26},{10... | collective-permute-start | bytes 786440 | tf_op jit(solution)/shard_map/ppermute | solution.py:360
  32.0 5.7 %copy-start.4 = (f32[1,1,8,128,128]{4,3,2,1,0:T(8,128)S(1)}, f32[1,1,8,128,128]{4,3,2,1,0:T(8,128)}, u32[]{:S(2)}) copy-start(f32[1,1,8,128,128]{4,3,2,1,0:T(8,128)} %param.12) | copy-start | bytes 1572868
  33.6 9.3 %collective-permute-start.6 = (f32[520,128]{1,0:T(8,128)S(1)}, f32[520,128]{1,0:T(8,128)S(1)}, u32[]{:S(2)}, u32[]{:S(2)}) collective-permute-start(f32[520,128]{1,0:T(8,128)S(1)} %get-tuple-element.48), channel_id=1, source_target_pairs={{0,24},{8,0},{16,8},{24,16},{1,25},{9,1},{17,9},{25,17},{2,26},{10... | collective-permute-start | bytes 798728 | tf_op jit(solution)/shard_map/ppermute | solution.py:360
  39.3 9.4 %collective-permute-start.10 = (f32[512,128]{1,0:T(8,128)S(1)}, f32[512,128]{1,0:T(8,128)S(1)}, u32[]{:S(2)}, u32[]{:S(2)}) collective-permute-start(f32[512,128]{1,0:T(8,128)S(1)} %get-tuple-element.56), channel_id=1, source_target_pairs={{0,24},{8,0},{16,8},{24,16},{1,25},{9,1},{17,9},{25,17},{2,26},{10... | collective-permute-start | bytes 786440 | tf_op jit(solution)/shard_map/ppermute | solution.py:360
  44.6 15.4 %collective-permute-start.7 = (f32[520,128]{1,0:T(8,128)S(1)}, f32[520,128]{1,0:T(8,128)S(1)}, u32[]{:S(2)}, u32[]{:S(2)}) collective-permute-start(f32[520,128]{1,0:T(8,128)S(1)} %get-tuple-element.49), channel_id=1, source_target_pairs={{0,24},{8,0},{16,8},{24,16},{1,25},{9,1},{17,9},{25,17},{2,26},{10... | collective-permute-start | bytes 798728 | tf_op jit(solution)/shard_map/ppermute | solution.py:360
  50.4 9.3 %collective-permute-start.11 = (f32[512,128]{1,0:T(8,128)S(1)}, f32[512,128]{1,0:T(8,128)S(1)}, u32[]{:S(2)}, u32[]{:S(2)}) collective-permute-start(f32[512,128]{1,0:T(8,128)S(1)} %get-tuple-element.57), channel_id=1, source_target_pairs={{0,24},{8,0},{16,8},{24,16},{1,25},{9,1},{17,9},{25,17},{2,26},{10... | collective-permute-start | bytes 786440 | tf_op jit(solution)/shard_map/ppermute | solution.py:360
  59.7 9.6 %collective-permute-start.13 = (f32[512,128]{1,0:T(8,128)S(1)}, f32[512,128]{1,0:T(8,128)S(1)}, u32[]{:S(2)}, u32[]{:S(2)}) collective-permute-start(f32[512,128]{1,0:T(8,128)S(1)} %shard_map.83.refs_8_), channel_id=1, source_target_pairs={{0,8},{8,16},{16,24},{24,0},{1,9},{9,17},{17,25},{25,1},{2,10},{10... | collective-permute-start | bytes 786440 | tf_op jit(solution)/shard_map/ppermute | solution.py:360
  60.1 14.9 %collective-permute-start.8 = (f32[520,128]{1,0:T(8,128)S(1)}, f32[520,128]{1,0:T(8,128)S(1)}, u32[]{:S(2)}, u32[]{:S(2)}) collective-permute-start(f32[520,128]{1,0:T(8,128)S(1)} %shard_map.79.refs_5_), channel_id=1, source_target_pairs={{0,8},{8,16},{16,24},{24,0},{1,9},{9,17},{17,25},{25,1},{2,10},{10... | collective-permute-start | bytes 798728 | tf_op jit(solution)/shard_map/ppermute | solution.py:360
  69.3 11.3 %collective-permute-start.15 = (f32[512,128]{1,0:T(8,128)S(1)}, f32[512,128]{1,0:T(8,128)S(1)}, u32[]{:S(2)}, u32[]{:S(2)}) collective-permute-start(f32[512,128]{1,0:T(8,128)S(1)} %collective-permute-done.13.refs_8_), channel_id=1, source_target_pairs={{0,8},{8,16},{16,24},{24,0},{1,9},{9,17},{17,25},{25,1},{2,10},{10... | collective-permute-start | bytes 786440 | tf_op jit(solution)/shard_map/ppermute | solution.py:360
  75.0 11.3 %collective-permute-start.12 = (f32[520,128]{1,0:T(8,128)S(1)}, f32[520,128]{1,0:T(8,128)S(1)}, u32[]{:S(2)}, u32[]{:S(2)}) collective-permute-start(f32[520,128]{1,0:T(8,128)S(1)} %collective-permute-done.8.refs_5_), channel_id=1, source_target_pairs={{0,8},{8,16},{16,24},{24,0},{1,9},{9,17},{17,25},{25,1},{2,10},{10... | collective-permute-start | bytes 798728 | tf_op jit(solution)/shard_map/ppermute | solution.py:360
  80.6 18.6 %collective-permute-start.16 = (f32[512,128]{1,0:T(8,128)S(1)}, f32[512,128]{1,0:T(8,128)S(1)}, u32[]{:S(2)}, u32[]{:S(2)}) collective-permute-start(f32[512,128]{1,0:T(8,128)S(1)} %collective-permute-done.15.refs_8_), channel_id=1, source_target_pairs={{0,8},{8,16},{16,24},{24,0},{1,9},{9,17},{17,25},{25,1},{2,10},{10... | collective-permute-start | bytes 786440 | tf_op jit(solution)/shard_map/ppermute | solution.py:360
  86.3 11.3 %collective-permute-start.14 = (f32[520,128]{1,0:T(8,128)S(1)}, f32[520,128]{1,0:T(8,128)S(1)}, u32[]{:S(2)}, u32[]{:S(2)}) collective-permute-start(f32[520,128]{1,0:T(8,128)S(1)} %collective-permute-done.12.refs_5_), channel_id=1, source_target_pairs={{0,8},{8,16},{16,24},{24,0},{1,9},{9,17},{17,25},{25,1},{2,10},{10... | collective-permute-start | bytes 798728 | tf_op jit(solution)/shard_map/ppermute | solution.py:360
  101.1 17.5 %collective-permute-start.18 = (f32[384,128]{1,0:T(8,128)S(1)}, f32[384,128]{1,0:T(8,128)S(1)}, u32[]{:S(2)}, u32[]{:S(2)}) collective-permute-start(f32[384,128]{1,0:T(8,128)S(1)} %get-tuple-element.79), channel_id=1, source_target_pairs={{1,2},{3,4},{5,6},{2,1},{4,3},{6,5},{9,10},{11,12},{13,14},{10,9},... | collective-permute-start | bytes 589832 | tf_op jit(solution)/shard_map/ppermute | solution.py:360
  105.8 10.4 %collective-permute-start.17 = (f32[512,128]{1,0:T(8,128)S(1)}, f32[512,128]{1,0:T(8,128)S(1)}, u32[]{:S(2)}, u32[]{:S(2)}) collective-permute-start(f32[512,128]{1,0:T(8,128)S(1)} %get-tuple-element.78), channel_id=1, source_target_pairs={{0,1},{2,3},{4,5},{6,7},{1,0},{3,2},{5,4},{7,6},{8,9},{10,11},{12,... | collective-permute-start | bytes 786440 | tf_op jit(solution)/shard_map/ppermute | solution.py:360
  105.9 10.3 %collective-permute-start.20 = (f32[2,64,384]{2,1,0:T(8,128)S(1)}, f32[2,64,384]{2,1,0:T(8,128)S(1)}, u32[]{:S(2)}, u32[]{:S(2)}) collective-permute-start(f32[2,64,384]{2,1,0:T(8,128)S(1)} %get-tuple-element.81), channel_id=1, source_target_pairs={{8,16},{16,8},{9,17},{17,9},{10,18},{18,10},{11,19},{19,11},{12,20... | collective-permute-start | bytes 589832 | tf_op jit(solution)/shard_map/ppermute | solution.py:360
  106.6 9.6 %collective-permute-start.19 = (f32[2,64,384]{2,1,0:T(8,128)S(1)}, f32[2,64,384]{2,1,0:T(8,128)S(1)}, u32[]{:S(2)}, u32[]{:S(2)}) collective-permute-start(f32[2,64,384]{2,1,0:T(8,128)S(1)} %get-tuple-element.80), channel_id=1, source_target_pairs={{0,8},{16,24},{8,0},{24,16},{1,9},{17,25},{9,1},{25,17},{2,10},{18... | collective-permute-start | bytes 589832 | tf_op jit(solution)/shard_map/ppermute | solution.py:360
  107.9 8.2 %collective-permute-start.21 = (f32[128,128]{1,0:T(8,128)S(1)}, f32[128,128]{1,0:T(8,128)S(1)}, u32[]{:S(2)}, u32[]{:S(2)}) collective-permute-start(f32[128,128]{1,0:T(8,128)S(1)} %get-tuple-element.82), channel_id=1, source_target_pairs={{1,2},{3,4},{5,6},{2,1},{4,3},{6,5},{9,10},{11,12},{13,14},{10,9},... | collective-permute-start | bytes 196616 | tf_op jit(solution)/shard_map/ppermute | solution.py:360
  113.0 2.6 %copy-start.3 = (f32[2,384,384]{2,1,0:T(8,128)S(1)}, f32[2,384,384]{2,1,0:T(8,128)}, u32[]{:S(2)}) copy-start(f32[2,384,384]{2,1,0:T(8,128)} %obj.5) | copy-start | bytes 3538948
  116.3 2.4 %collective-permute-start.23 = (f32[2,64,128]{2,1,0:T(8,128)S(1)}, f32[2,64,128]{2,1,0:T(8,128)S(1)}, u32[]{:S(2)}, u32[]{:S(2)}) collective-permute-start(f32[2,64,128]{2,1,0:T(8,128)S(1)} %get-tuple-element.107), channel_id=1, source_target_pairs={{8,16},{16,8},{9,17},{17,9},{10,18},{18,10},{11,19},{19,11},{12,20... | collective-permute-start | bytes 196616 | tf_op jit(solution)/shard_map/ppermute | solution.py:360
  116.9 4.2 %collective-permute-start.22 = (f32[2,64,128]{2,1,0:T(8,128)S(1)}, f32[2,64,128]{2,1,0:T(8,128)S(1)}, u32[]{:S(2)}, u32[]{:S(2)}) collective-permute-start(f32[2,64,128]{2,1,0:T(8,128)S(1)} %get-tuple-element.108), channel_id=1, source_target_pairs={{0,8},{16,24},{8,0},{24,16},{1,9},{17,25},{9,1},{25,17},{2,10},{18... | collective-permute-start | bytes 196616 | tf_op jit(solution)/shard_map/ppermute | solution.py:360
